TPU v7x, 32 devices: a whole 2x2x4 slice. The times are simulated.
32 devices in a mesh: section: 4 (over y, x), slab: 2 (over core), img: 4 (over z).
Axes of the slice: x: 2, y: 2, z: 4, core: 2. Of those that a mesh axis runs over, the one named last changes fastest.
Arguments:
- strips: bfloat16 [4, 4, 8, 16, 320], P('img', None, None, 'slab'), may hold values from -6 to 6
- kernels: bfloat16 [4, 2, 9, 320, 320], P('section'), may hold values from -0.109375 to 0.109375
- cotangent: bfloat16 [4, 4, 8, 16, 320], P('img', None, None, 'slab'), may hold values from -18 to 18
Outputs:
- grad_kernels: float32 [4, 2, 9, 320, 320], P('section', None, None, 'slab', 'img')
- grad_inputs: bfloat16 [4, 4, 4, 8, 16, 320], P('section', 'img', None, None, 'slab')
All inputs are finite; a program needn't handle non-finite values.
Results may differ from a plain program's by a relative error of at most 0.023.
Values may be sent and summed in bfloat16 or wider, within the bound.
No kernel may reach another device: no remote copies, remote signals or barrier semaphores. Data moves between devices by JAX's collectives and lax.ppermute only.
A program may use at most 128 MiB of HBM per device.

v0:
```python
import math

import jax
import jax.numpy as jnp
from jax import lax
from jax.experimental import pallas as pl
from jax.experimental.pallas import tpu as pltpu
from jax.sharding import PartitionSpec as P


def passed_along(value, axis, steps):
    count = lax.axis_size(axis)
    initial, last = (max(0, -steps), min(count, count - steps))
    return lax.ppermute(value, axis, [(source, source + steps) for source in range(initial, last)])


def padded_2(cells, sides, width):
    for axis, dim in sides:
        count = lax.axis_size(axis)
        ends = count - 1
        head = lax.slice_in_dim(cells, 0, width, axis=dim)
        tail = lax.slice_in_dim(cells, cells.shape[dim] - width, cells.shape[dim], axis=dim)
        cells = jnp.concatenate(
            [
                lax.ppermute(tail, axis, [(i, (i + 1) % count) for i in range(ends)]),
                cells,
                lax.ppermute(head, axis, [((i + 1) % count, i) for i in range(ends)]),
            ],
            axis=dim,
        )
    return cells


def unfold(padded, row_count, col_count):
    tap_list = [
        padded[:, down_at : down_at + row_count, right_at : right_at + col_count, :]
        for down_at in range(3)
        for right_at in range(3)
    ]
    stacked = jnp.concatenate(tap_list, axis=3)
    return stacked.reshape(-1, stacked.shape[3])


def columns_of(wide_field):
    row_count = wide_field.shape[1]
    col_count = wide_field.shape[2] - 2
    padded = jnp.pad(wide_field, ((0, 0), (1, 1), (0, 0), (0, 0)))
    return unfold(padded, row_count, col_count)


def convolve(matrix, wide_field):
    count, row_count = (wide_field.shape[0], wide_field.shape[1])
    col_count = wide_field.shape[2] - 2
    flat_out = jnp.dot(columns_of(wide_field), matrix, preferred_element_type=jnp.float32)
    return flat_out.reshape(count, row_count, col_count, matrix.shape[1])


def contract(wide_field, grad_out):
    flat_grad = grad_out.reshape(-1, grad_out.shape[3])
    return lax.dot_general(
        columns_of(wide_field),
        flat_grad,
        (((0,), (0,)), ((), ())),
        preferred_element_type=jnp.float32,
    )


def silu_slope(hidden):
    sigmoid_at = jax.nn.sigmoid(hidden)
    return sigmoid_at * (1.0 + hidden * (1.0 - sigmoid_at))


def store(buffer, value, slot_index, is_valid, axis_at):
    current = lax.dynamic_index_in_dim(buffer, slot_index, axis_at, keepdims=False)
    return lax.dynamic_update_index_in_dim(
        buffer, jnp.where(is_valid, value, current), slot_index, axis_at
    )


def column_shards(strips, kernels, cotangent):
    section_count = lax.axis_size("section")
    section_index = lax.axis_index("section")
    slab_count = lax.axis_size("slab")
    slab_index = lax.axis_index("slab")
    images, strip_count, row_count, col_count, channels = strips.shape
    weights = kernels[0]
    first_forward = weights[0].reshape(9 * channels, channels)
    second_forward = weights[1].reshape(9 * channels, channels)
    first_backward = jnp.transpose(weights[0][::-1], (0, 2, 1)).reshape(9 * channels, channels)
    second_backward = jnp.transpose(weights[1][::-1], (0, 2, 1)).reshape(9 * channels, channels)
    scaling = 1.0 / math.sqrt(
        images * lax.axis_size("img") * strip_count * row_count * col_count * slab_count
    )
    position = slab_index * col_count - 1 + jnp.arange(col_count + 2, dtype=jnp.int32)
    inside = ((position >= 0) & (position < slab_count * col_count))[None, None, :, None]
    tick_count = strip_count + section_count - 1
    hidden_cols = col_count + 2
    empty_field = jnp.zeros((images, row_count, col_count, channels), jnp.bfloat16)
    saved_field = jnp.zeros((strip_count, images, row_count, col_count + 2, channels), jnp.bfloat16)
    saved_hidden = jnp.zeros((strip_count, images, row_count, hidden_cols, channels), jnp.float32)
    saved_active = jnp.zeros(
        (strip_count, images, row_count, col_count + 2, channels), jnp.bfloat16
    )
    outgoing = empty_field
    for step_no in range(tick_count):
        micro_index = step_no - section_index
        is_valid = (micro_index >= 0) & (micro_index < strip_count)
        slot_index = jnp.clip(micro_index, 0, strip_count - 1)
        if step_no == 0:
            incoming = empty_field
        else:
            incoming = passed_along(outgoing, "section", 1)
        first_strip = lax.dynamic_index_in_dim(strips, slot_index, 1, keepdims=False)
        field_in = jnp.where(section_index == 0, first_strip, incoming)
        wide_deep = padded_2(field_in, (("slab", 2),), 2)
        hidden = convolve(first_forward, wide_deep)
        wide_active = jnp.where(inside, jax.nn.silu(hidden), 0.0).astype(jnp.bfloat16)
        wide_field = wide_deep[:, :, 1:-1, :]
        outgoing = (field_in.astype(jnp.float32) + convolve(second_forward, wide_active)).astype(
            jnp.bfloat16
        )
        saved_field = store(saved_field, wide_field, slot_index, is_valid, 0)
        saved_hidden = store(saved_hidden, hidden, slot_index, is_valid, 0)
        saved_active = store(saved_active, wide_active, slot_index, is_valid, 0)
    grad_slots = jnp.zeros((images, strip_count, row_count, col_count, channels), jnp.bfloat16)
    saved_grad_out = jnp.zeros((strip_count, images, row_count, col_count, channels), jnp.bfloat16)
    saved_grad_hidden = jnp.zeros(
        (strip_count, images, row_count, col_count, channels), jnp.bfloat16
    )
    sending = empty_field
    for step_no in range(tick_count):
        micro_index = step_no - (section_count - 1 - section_index)
        is_valid = (micro_index >= 0) & (micro_index < strip_count)
        slot_index = jnp.clip(micro_index, 0, strip_count - 1)
        if step_no == 0:
            arriving = empty_field
        else:
            arriving = passed_along(sending, "section", -1)
        top_grad = lax.dynamic_index_in_dim(cotangent, slot_index, 1, keepdims=False)
        grad_out = jnp.where(section_index == section_count - 1, top_grad, arriving)
        grad_out = jnp.where(is_valid, grad_out, jnp.zeros_like(grad_out))
        hidden = lax.dynamic_index_in_dim(saved_hidden, slot_index, 0, keepdims=False)
        wide_grad = padded_2(grad_out, (("slab", 2),), 2)
        grad_active = convolve(second_backward, wide_grad)
        wide_hidden_grad = jnp.where(inside, grad_active * silu_slope(hidden), 0.0).astype(
            jnp.bfloat16
        )
        grad_hidden = wide_hidden_grad[:, :, 1:-1, :]
        sending = (
            grad_out.astype(jnp.float32) + convolve(first_backward, wide_hidden_grad)
        ).astype(jnp.bfloat16)
        saved_grad_out = store(saved_grad_out, grad_out, slot_index, is_valid, 0)
        saved_grad_hidden = store(saved_grad_hidden, grad_hidden, slot_index, is_valid, 0)
        grad_slots = store(grad_slots, sending, slot_index, is_valid, 1)
    flat_count = strip_count * images
    lower_part = contract(
        saved_field.reshape(flat_count, row_count, col_count + 2, channels),
        saved_grad_hidden.reshape(flat_count, row_count, col_count, channels),
    )
    upper_part = contract(
        saved_active.reshape(flat_count, row_count, col_count + 2, channels),
        saved_grad_out.reshape(flat_count, row_count, col_count, channels),
    )
    grad_terms = jnp.stack([lower_part, upper_part]).reshape(2, 9, channels, channels)
    row_share = lax.psum_scatter(
        grad_terms.astype(jnp.bfloat16), "slab", scatter_dimension=2, tiled=True
    )
    own_share = lax.psum_scatter(row_share, "img", scatter_dimension=3, tiled=True).astype(
        jnp.float32
    )
    grad_kernels = (own_share * scaling)[None]
    return (grad_kernels, grad_slots[None])


def call(kernel, outs, operands, unread, scratch, aliases):
    return pl.pallas_call(
        kernel,
        out_shape=outs,
        in_specs=[
            pl.BlockSpec(memory_space=pl.ANY if place in unread else pltpu.VMEM)
            for place in range(len(operands))
        ],
        out_specs=[pl.BlockSpec(memory_space=pltpu.VMEM)] * len(outs),
        scratch_shapes=scratch,
        input_output_aliases=aliases,
        compiler_params=pltpu.CompilerParams(vmem_limit_bytes=8 << 20),
    )(*operands)


def neighbours(value, shifted, width):
    count, channels = value.shape
    shifted[8 : 8 + count, :] = value
    column = lax.rem(lax.broadcasted_iota(jnp.int32, (count, channels), 0), width)
    before = jnp.where(column == 0, 0.0, shifted[7 : 7 + count, :])
    after = jnp.where(column == width - 1, 0.0, shifted[9 : 9 + count, :])
    return before, after


def convolved(value, matrix, taps, shifted, width):
    count, channels = value.shape
    before, after = neighbours(value, shifted, width)
    for place, part in enumerate((before, value, after)):
        taps[width : width + count, place * channels : (place + 1) * channels] = part.astype(
            jnp.bfloat16
        )
    edge = jnp.zeros((width, 3 * channels), jnp.bfloat16)
    taps[0:width, :] = edge
    taps[width + count : 2 * width + count, :] = edge
    total = jnp.dot(taps[0:count, :], matrix[0], preferred_element_type=jnp.float32)
    for down in (1, 2):
        total = total + jnp.dot(
            taps[down * width : down * width + count, :],
            matrix[down],
            preferred_element_type=jnp.float32,
        )
    return total


def forward_call(field, weights, state, section, crop, crops, width, last, after):
    count, channels = field.shape

    def kernel(field_ref, weights_ref, after_ref, *refs):
        *_, saved_ref, hidden_ref, taps, shifted = refs

        @pl.when(lax.axis_index("section") == section)
        def _():
            field_in = field_ref[...]
            wide = field_in.astype(jnp.float32)
            saved_ref[0, crop] = field_in
            hidden = convolved(wide, weights_ref.at[0], taps, shifted, width)
            hidden_ref[crop] = hidden
            active = (hidden * jax.nn.sigmoid(hidden)).astype(jnp.bfloat16)
            saved_ref[1, crop] = active
            if not last:
                added = convolved(
                    active.astype(jnp.float32), weights_ref.at[1], taps, shifted, width
                )
                refs[-5][...] = (wide + added).astype(jnp.bfloat16)

    outs = [
        jax.ShapeDtypeStruct((count, channels), jnp.bfloat16),
        jax.ShapeDtypeStruct((2, crops, count, channels), jnp.bfloat16),
        jax.ShapeDtypeStruct((crops, count, channels), jnp.float32),
    ][1 if last else 0 :]
    scratch = [
        pltpu.VMEM((count + 2 * width, 3 * channels), jnp.bfloat16),
        pltpu.VMEM((count + 16, channels), jnp.float32),
    ]
    aliases = {3 + k: k + (0 if last else 1) for k in range(len(state))}
    outputs = call(kernel, outs, [field, weights, after, *state], (2,), scratch, aliases)
    return (None if last else outputs[0]), outputs[-2:]


def backward_call(
    grad, turned, hidden, state, section, crop, crops, width, parts, after
):
    count, channels = grad.shape
    share = channels // parts
    first = section == 0

    def kernel(grad_ref, turned_ref, hidden_ref, after_ref, *refs):
        *_, kept_ref, sent_ref, taps, shifted = refs

        @pl.when(lax.axis_index("section") == section)
        def _():
            wide = grad_ref[...].astype(jnp.float32)
            kept_ref[0, crop] = grad_ref[...]
            grad_active = convolved(wide, turned_ref.at[1], taps, shifted, width)
            hidden = hidden_ref[crop]
            gate = jax.nn.sigmoid(hidden)
            grad_hidden = (grad_active * (gate * (1.0 + hidden * (1.0 - gate)))).astype(
                jnp.bfloat16
            )
            place_parts(sent_ref, (), grad_hidden, crop, parts, lax.axis_index("img"))
            added = convolved(
                grad_hidden.astype(jnp.float32), turned_ref.at[0], taps, shifted, width
            )
            result = (wide + added).astype(jnp.bfloat16)
            kept_ref[1, crop] = result
            if not first:
                refs[-5][...] = result

    outs = [
        jax.ShapeDtypeStruct((count, channels), jnp.bfloat16),
        jax.ShapeDtypeStruct((2, crops, count, channels), jnp.bfloat16),
        jax.ShapeDtypeStruct((parts, share, crops * count), jnp.bfloat16),
    ][1 if first else 0 :]
    scratch = [
        pltpu.VMEM((count + 2 * width, 3 * channels), jnp.bfloat16),
        pltpu.VMEM((count + 16, channels), jnp.float32),
    ]
    aliases = {4 + k: k + (0 if first else 1) for k in range(len(state))}
    operands = [grad, turned, hidden, after, *state]
    outputs = call(kernel, outs, operands, (3,), scratch, aliases)
    return (None if first else outputs[0]), outputs[-2:]


def place_parts(target, lead, value, crop, parts, own):
    count, channels = value.shape
    share = channels // parts
    flipped = value.T
    for part in range(parts):
        slot = lax.rem(part + parts - own, parts)
        target[(slot, *lead, slice(None), slice(crop * count, (crop + 1) * count))] = flipped[
            part * share : (part + 1) * share, :
        ]


def flip_call(kept, kinds, parts, axis, after):
    _, crops, count, channels = kept.shape

    def kernel(kept_ref, after_ref, flipped_ref):
        for place, kind in enumerate(kinds):
            for crop in range(crops):
                place_parts(
                    flipped_ref, (place,), kept_ref[kind, crop], crop, parts, lax.axis_index(axis)
                )

    shape = (parts, len(kinds), channels // parts, crops * count)
    (flipped,) = call(kernel, [jax.ShapeDtypeStruct(shape, kept.dtype)], [kept, after], (1,), [], {})
    return flipped


def turn_call(weights, after):
    two, _, _, channels = weights.shape

    def kernel(weights_ref, after_ref, turned_ref):
        for which in range(two):
            for tap in range(9):
                down, right = divmod(tap, 3)
                flipped = weights_ref[which, down, right * channels : (right + 1) * channels, :].T
                down, right = divmod(8 - tap, 3)
                turned_ref[which, down, right * channels : (right + 1) * channels, :] = flipped

    out = jax.ShapeDtypeStruct(weights.shape, weights.dtype)
    (turned,) = call(kernel, [out], [weights, after], (1,), [], {})
    return turned


def split_call(strips, cotangent, last):
    images, strip_count, rows, cols, channels = strips.shape
    share = strip_count // 2

    def kernel(strips_ref, cotangent_ref, own_ref, other_ref):
        own = lax.axis_index("slab")
        is_last = lax.axis_index("section") == last
        for image in range(images):
            for crop in range(share):
                at = image * share + crop
                for ref, half in ((own_ref, own), (other_ref, 1 - own)):
                    top = cotangent_ref[image, half * share + crop]
                    ref[at] = jnp.where(is_last, top, strips_ref[image, half * share + crop])

    out = jax.ShapeDtypeStruct((images * share, rows, cols, channels), strips.dtype)
    return call(kernel, [out, out], [strips, cotangent], (), [], {})


def join_call(own, other):
    crops, rows, cols, channels = own.shape

    def kernel(own_ref, other_ref, *out_refs):
        is_left = lax.axis_index("slab") == 0
        for crop, out_ref in enumerate(out_refs):
            mine = own_ref[crop].astype(jnp.float32)
            theirs = other_ref[crop].astype(jnp.float32)
            left = jnp.where(is_left, mine, theirs)
            right = jnp.where(is_left, theirs, mine)
            whole = jnp.concatenate([left, right], axis=1)
            out_ref[...] = whole.reshape(rows * 2 * cols, channels).astype(jnp.bfloat16)

    out = jax.ShapeDtypeStruct((rows * 2 * cols, channels), own.dtype)
    return call(kernel, [out] * crops, [own, other], (), [], {})


def part_call(kept, rows, after):
    _, crops, count, channels = kept.shape
    cols = count // rows // 2

    def kernel(kept_ref, after_ref, own_ref, other_ref):
        is_left = lax.axis_index("slab") == 0
        for crop in range(crops):
            whole = kept_ref[1, crop].astype(jnp.float32).reshape(rows, 2 * cols, channels)
            left, right = whole[:, :cols], whole[:, cols:]
            own_ref[crop] = jnp.where(is_left, left, right).astype(jnp.bfloat16)
            other_ref[crop] = jnp.where(is_left, right, left).astype(jnp.bfloat16)

    out = jax.ShapeDtypeStruct((crops, rows, cols, channels), kept.dtype)
    return call(kernel, [out, out], [kept, after], (1,), [], {})


def merge_call(own, other, images):
    crops, rows, cols, channels = own.shape
    share = crops // images

    def kernel(own_ref, other_ref, out_ref):
        place = lax.axis_index("slab")
        for image in range(images):
            for crop in range(share):
                out_ref[image, place * share + crop] = own_ref[image * share + crop]
                out_ref[image, (1 - place) * share + crop] = other_ref[image * share + crop]

    out = jax.ShapeDtypeStruct((images, 2 * share, rows, cols, channels), own.dtype)
    (merged,) = call(kernel, [out], [own, other], (), [], {})
    return merged


def choose_call(home, early, late, slot, last):
    blocks = 1 + len(early)

    def kernel(*refs):
        home_ref, out_ref = refs[0], refs[-1]
        early_refs, late_refs = refs[1:blocks], refs[blocks:-1]
        is_last = lax.axis_index("section") == last
        out_ref[0] = home_ref[slot]
        for block in range(1, blocks):
            out_ref[block] = jnp.where(
                is_last, late_refs[block - 1][slot], early_refs[block - 1][slot]
            )

    out = jax.ShapeDtypeStruct((blocks, *home.shape[1:]), home.dtype)
    (chosen,) = call(kernel, [out], [home, *early, *late], (), [], {})
    return chosen


def stack_call(inner, outer):
    blocks = len(outer)

    def kernel(*refs):
        out_ref = refs[-1]
        for block in range(blocks):
            value = refs[block][...]
            if inner:
                is_first = lax.axis_index("section") == 0
                value = jnp.where(is_first, refs[blocks + block][...], value)
            out_ref[block] = value

    out = jax.ShapeDtypeStruct((blocks, *outer[0].shape), outer[0].dtype)
    (stacked,) = call(kernel, [out], [*outer, *inner], (), [], {})
    return stacked


def spread_call(own, other, count, width):
    blocks, two, share, cells = own.shape
    crops = cells // count
    stride = count + width
    total = 2 * blocks * crops * stride + width

    def kernel(own_ref, other_ref, out_ref, done_ref, shifted):
        done_ref[...] = jnp.zeros_like(done_ref)
        edge = jnp.zeros((width, 3 * share), jnp.bfloat16)
        for kind in range(two):
            out_ref[kind, total - width : total, :] = edge
            for block in range(2 * blocks):
                ref = own_ref if block < blocks else other_ref
                for crop in range(crops):
                    value = ref[block % blocks, kind, :, crop * count : (crop + 1) * count]
                    value = value.T.astype(jnp.float32)
                    before, after = neighbours(value, shifted, width)
                    at = (block * crops + crop) * stride
                    out_ref[kind, at : at + width, :] = edge
                    for place, part in enumerate((before, value, after)):
                        lanes = slice(place * share, (place + 1) * share)
                        out_ref[kind, at + width : at + stride, lanes] = part.astype(jnp.bfloat16)

    outs = [
        jax.ShapeDtypeStruct((two, total, 3 * share), jnp.bfloat16),
        jax.ShapeDtypeStruct((8, 128), jnp.float32),
    ]
    scratch = [pltpu.VMEM((count + 16, share), jnp.float32)]
    return call(kernel, outs, [own, other], (), scratch, {})


def terms_call(around, kind, own, other, others, count, width, scaling):
    blocks, columns, cells = own.shape
    rows = around.shape[2] // 3
    stride = count + width
    crops = cells // count

    def kernel(around_ref, own_ref, other_ref, *refs):
        out_ref = refs[-1]
        if others:
            refs[-1][1] = refs[0][...]
            out_ref = refs[-1].at[0]
        for down in range(3):
            total = None
            for block in range(2 * blocks):
                left = own_ref[block] if block < blocks else other_ref[block - blocks]
                at = [(block * crops + k) * stride + down * width for k in range(crops)]
                right = jnp.concatenate(
                    [around_ref[kind, start : start + count, :] for start in at], axis=0
                )
                term = jnp.dot(left, right, preferred_element_type=jnp.float32)
                total = term if total is None else total + term
            total = (total * scaling).T.reshape(3, rows, columns)
            for place in range(3):
                out_ref[3 * down + place] = total[place]

    shape = (9, rows, columns)
    out = jax.ShapeDtypeStruct((2, *shape) if others else shape, jnp.float32)
    (terms,) = call(kernel, [out], [around, own, other, *others], (), [], {})
    return terms


def rotated(value, axis, steps):
    count = lax.axis_size(axis)
    return lax.ppermute(value, axis, [(source, (source + steps) % count) for source in range(count)])


def crop_shards(strips, kernels, cotangent):
    sections = lax.axis_size("section")
    slabs, groups = lax.axis_size("slab"), lax.axis_size("img")
    images, strip_count, row_count, col_count, channels = strips.shape
    width = col_count * slabs
    count = row_count * width
    crops = images * strip_count // slabs
    last = sections - 1
    scaling = 1.0 / math.sqrt(images * groups * strip_count * count)
    weights = kernels[0].reshape(2, 3, 3 * channels, channels)

    def hop(value, source, target):
        return lax.ppermute(value, "section", [(source, target)])

    def shared(values, step, routes):
        pairs = [
            (source * groups + i, target * groups + (i + step) % groups)
            for source, target in routes
            for i in range(groups)
        ]
        return lax.ppermute(values, ("section", "img"), pairs)

    own, other = split_call(strips, cotangent, last)
    fields = join_call(own, rotated(other, "slab", 1))
    incoming = fields
    state, saved_sets = [], []
    turned, after = None, weights
    for place in range(sections):
        outgoing = []
        for crop in range(crops):
            out, state = forward_call(
                incoming[crop], weights, state, place, crop, crops, width, place == last, after
            )
            outgoing.append(out)
        if place == 0:
            turned = turn_call(weights, state[0])
        if place < last:
            incoming = [hop(out, place, place + 1) for out in outgoing]
        if place == last - 1:
            flipped = flip_call(state[0], (0, 1), slabs, "slab", state[1])
            after = flipped
            routes = [(source, source) for source in range(last)]
            saved_sets.append([shared(flipped, step, routes) for step in range(1, groups)])
    saved, hidden = state
    incoming = fields
    grads = []
    around, after = None, hidden
    for place in reversed(range(sections)):
        outgoing = []
        for crop in range(crops):
            out, grads = backward_call(
                incoming[crop], turned, hidden, grads, place, crop, crops, width, groups, after
            )
            outgoing.append(out)
        if place:
            incoming = [hop(out, place, place - 1) for out in outgoing]
        if place == last:
            flipped = flip_call(saved, (0, 1), slabs, "slab", grads[0])
            saved_sets.append([shared(flipped, step, [(last, last)]) for step in range(1, groups)])
        if place == 1:
            handed = flip_call(grads[0], (0, 1), groups, "img", grads[1])
            routes = [(source, source) for source in range(1, sections)]
            later = [handed[0, 0]]
            for step in range(1, groups):
                later.append(shared(handed[step, 0], step, routes))
            first = [shared(handed[step, 1], step, [(1, 0)]) for step in range(groups)]
            own = choose_call(flipped, *saved_sets, 0, last)
            other = choose_call(flipped, *saved_sets, 1, last)
            other = rotated(other, "slab", 1)
            around, after = spread_call(own, other, count, width)
    kept, sent = grads
    hidden_grads = [sent[0]]
    for step in range(1, groups):
        hidden_grads.append(shared(sent[step], step, [(place, place) for place in range(sections)]))
    out_grads = stack_call(first, later)
    other = rotated(out_grads, "slab", 1)
    upper = terms_call(around, 1, out_grads, other, [], count, width, scaling)
    hidden_grads = stack_call([], hidden_grads)
    other = rotated(hidden_grads, "slab", 1)
    terms = terms_call(around, 0, hidden_grads, other, [upper], count, width, scaling)
    own, other = part_call(kept, row_count, hidden_grads)
    grad_inputs = merge_call(own, rotated(other, "slab", 1), images)
    return (terms[None], grad_inputs[None])


def shards(strips, kernels, cotangent):
    slabs, groups = lax.axis_size("slab"), lax.axis_size("img")
    strip_count, row_count, col_count, channels = strips.shape[1:]
    width = col_count * slabs
    whole_crops = strip_count % slabs == 0 and width % 16 == 0 and (row_count * width) % 128 == 0
    whole_crops = whole_crops and slabs == 2 and lax.axis_size("section") > 1
    if whole_crops and channels % (16 * slabs) == 0 and channels % (16 * groups) == 0:
        return crop_shards(strips, kernels, cotangent)
    return column_shards(strips, kernels, cotangent)


def solution(mesh):
    in_specs = (
        P("img", None, None, "slab", None),
        P("section", None, None, None, None),
        P("img", None, None, "slab", None),
    )
    out_specs = (
        P("section", None, None, "slab", "img"),
        P("section", "img", None, None, "slab", None),
    )
    return jax.shard_map(shards, mesh=mesh, in_specs=in_specs, out_specs=out_specs, check_vma=False)
```

profile of v0, /device:TPU:27, one launch (start us, length us, event | category | flops | bytes accessed | tf_op | source)
XLA Modules:
  0.0 115.9 jit_solution(7368181140249410544)
XLA Ops:
  0.6 0.9 copy-done.1
  1.6 0.9 copy-done.2
  2.5 0.7 collective-permute-start
  3.3 0.9 collective-permute-done.other_ref
  4.2 0.1 shard_map.51
  4.3 0.0 copy-start
  4.3 2.2 %copy-done = bf16[1,2,9,320,320]{4,3,2,1,0:T(8,128)(2,1)S(1)} copy-done((bf16[1,2,9,320,320]{4,3,2,1,0:T(8,128)(2,1)S(1)}, bf16[1,2,9,320,320]{4,3,2,1,0:T(8,128)(2,1)}, u32[]{:S(2)}) %copy-start) | copy-done | bytes 3686424
  6.5 1.5 %collective-permute-start.2 = (bf16[128,320]{1,0:T(8,128)(2,1)S(1)}, bf16[128,320]{1,0:T(8,128)(2,1)S(1)}, u32[]{:S(2)}, u32[]{:S(2)}) collective-permute-start(bf16[128,320]{1,0:T(8,128)(2,1)S(1)} %get-tuple-element.61), channel_id=1, source_target_pairs={{0,8},{1,9},{2,10},{3,11},{4,12},{5,13},{6,14},{7,15}} | collective-permute-start | bytes 245768 | tf_op jit(solution)/shard_map/ppermute | solution.py:521
  8.1 0.0 slice-start.1
  8.1 1.4 %collective-permute-start.1 = (bf16[128,320]{1,0:T(8,128)(2,1)S(1)}, bf16[128,320]{1,0:T(8,128)(2,1)S(1)}, u32[]{:S(2)}, u32[]{:S(2)}) collective-permute-start(bf16[128,320]{1,0:T(8,128)(2,1)S(1)} %get-tuple-element.60), channel_id=1, source_target_pairs={{0,8},{1,9},{2,10},{3,11},{4,12},{5,13},{6,14},{7,15}} | collective-permute-start | bytes 245768 | tf_op jit(solution)/shard_map/ppermute | solution.py:521
  9.6 1.4 %shard_map.61.turned_ref = bf16[2,3,960,320]{3,2,1,0:T(8,128)(2,1)S(1)} custom-call(bf16[2,3,960,320]{3,2,1,0:T(8,128)(2,1)S(1)} %bitcast.33, bf16[2,2,128,320]{3,2,1,0:T(8,128)(2,1)S(1)} %get-tuple-element.62.refs_0_.after_ref), custom_call_target="tpu_custom_call" | custom-call | tf_op jit(solution)/shard_map/pallas_call | solution.py:176
  10.9 1.7 %collective-permute-done.2.field_ref = bf16[128,320]{1,0:T(8,128)(2,1)S(1)} collective-permute-done((bf16[128,320]{1,0:T(8,128)(2,1)S(1)}, bf16[128,320]{1,0:T(8,128)(2,1)S(1)}, u32[]{:S(2)}, u32[]{:S(2)}) %collective-permute-start.2) | collective-permute-done | bytes 81952 | tf_op jit(solution)/shard_map/ppermute | solution.py:521
  12.7 1.3 %shard_map.54 = (bf16[128,320]{1,0:T(8,128)(2,1)S(1)}, bf16[2,2,128,320]{3,2,1,0:T(8,128)(2,1)S(1)}, f32[2,128,320]{2,1,0:T(8,128)S(1)}) custom-call(bf16[128,320]{1,0:T(8,128)(2,1)S(1)} %collective-permute-done.2.field_ref, bf16[2,3,960,320]{3,2,1,0:T(8,128)(2,1)S(1)} %bitcast.34, ...), custom_call_target="tpu_custom_call", output_to_operand_aliasing={{1}: (3, {}), {2}: (4, {})} | custom-call | tf_op jit(solution)/shard_map/pallas_call | solution.py:176
  14.0 1.3 %collective-permute-start.4 = (bf16[128,320]{1,0:T(8,128)(2,1)S(1)}, bf16[128,320]{1,0:T(8,128)(2,1)S(1)}, u32[]{:S(2)}, u32[]{:S(2)}) collective-permute-start(bf16[128,320]{1,0:T(8,128)(2,1)S(1)} %get-tuple-element.67), channel_id=1, source_target_pairs={{8,16},{9,17},{10,18},{11,19},{12,20},{13,21},{14,22},{15,23}} | collective-permute-start | bytes 245768 | tf_op jit(solution)/shard_map/ppermute | solution.py:521
  15.3 0.0 collective-permute-done.1.field_ref
  15.3 1.3 %shard_map.55 = (bf16[128,320]{1,0:T(8,128)(2,1)S(1)}, bf16[2,2,128,320]{3,2,1,0:T(8,128)(2,1)S(1)}, f32[2,128,320]{2,1,0:T(8,128)S(1)}) custom-call(bf16[128,320]{1,0:T(8,128)(2,1)S(1)} %collective-permute-done.1.field_ref, bf16[2,3,960,320]{3,2,1,0:T(8,128)(2,1)S(1)} %bitcast.36, ...), custom_call_target="tpu_custom_call", output_to_operand_aliasing={{1}: (3, {}), {2}: (4, {})} | custom-call | tf_op jit(solution)/shard_map/pallas_call | solution.py:176
  16.6 1.3 %collective-permute-start.3 = (bf16[128,320]{1,0:T(8,128)(2,1)S(1)}, bf16[128,320]{1,0:T(8,128)(2,1)S(1)}, u32[]{:S(2)}, u32[]{:S(2)}) collective-permute-start(bf16[128,320]{1,0:T(8,128)(2,1)S(1)} %get-tuple-element.66), channel_id=1, source_target_pairs={{8,16},{9,17},{10,18},{11,19},{12,20},{13,21},{14,22},{15,23}} | collective-permute-start | bytes 245768 | tf_op jit(solution)/shard_map/ppermute | solution.py:521
  17.9 0.0 collective-permute-done.4.field_ref
  17.9 1.6 %collective-permute-done.3.field_ref = bf16[128,320]{1,0:T(8,128)(2,1)S(1)} collective-permute-done((bf16[128,320]{1,0:T(8,128)(2,1)S(1)}, bf16[128,320]{1,0:T(8,128)(2,1)S(1)}, u32[]{:S(2)}, u32[]{:S(2)}) %collective-permute-start.3) | collective-permute-done | bytes 81952 | tf_op jit(solution)/shard_map/ppermute | solution.py:521
  19.5 0.2 shard_map.58.after_ref
  19.7 1.9 %collective-permute-start.7 = (bf16[2,2,160,256]{3,2,1,0:T(8,128)(2,1)S(1)}, bf16[2,2,160,256]{3,2,1,0:T(8,128)(2,1)S(1)}, u32[]{:S(2)}, u32[]{:S(2)}) collective-permute-start(bf16[2,2,160,256]{3,2,1,0:T(8,128)(2,1)S(1)} %shard_map.58.after_ref), channel_id=1, source_target_pairs={{0,1},{1,2},{2,3},{3,0},{8,9},{9,10},{10,11},{11,8},{16,17},{17,18... | collective-permute-start | bytes 983048 | tf_op jit(solution)/shard_map/ppermute | solution.py:529
  21.6 0.7 collective-permute-start.6
  22.3 0.7 collective-permute-start.5
  22.9 3.3 %collective-permute-start.8 = (bf16[2,2,160,256]{3,2,1,0:T(8,128)(2,1)S(1)}, bf16[2,2,160,256]{3,2,1,0:T(8,128)(2,1)S(1)}, u32[]{:S(2)}, u32[]{:S(2)}) collective-permute-start(bf16[2,2,160,256]{3,2,1,0:T(8,128)(2,1)S(1)} %shard_map.58.after_ref), channel_id=1, source_target_pairs={{0,2},{1,3},{2,0},{3,1},{8,10},{9,11},{10,8},{11,9},{16,18},{17,19... | collective-permute-start | bytes 983048 | tf_op jit(solution)/shard_map/ppermute | solution.py:529
  26.2 2.0 %collective-permute-start.9 = (bf16[2,2,160,256]{3,2,1,0:T(8,128)(2,1)S(1)}, bf16[2,2,160,256]{3,2,1,0:T(8,128)(2,1)S(1)}, u32[]{:S(2)}, u32[]{:S(2)}) collective-permute-start(bf16[2,2,160,256]{3,2,1,0:T(8,128)(2,1)S(1)} %shard_map.58.after_ref), channel_id=1, source_target_pairs={{0,3},{1,0},{2,1},{3,2},{8,11},{9,8},{10,9},{11,10},{16,19},{17,16... | collective-permute-start | bytes 983048 | tf_op jit(solution)/shard_map/ppermute | solution.py:529
  28.4 0.2 shard_map.63
  28.6 0.2 shard_map.64.refs_0_
  28.7 0.7 collective-permute-start.10
  29.4 0.7 collective-permute-start.11
  30.1 0.7 collective-permute-start.12
  30.8 19.3 %collective-permute-done.8.refs_2_ = bf16[2,2,160,256]{3,2,1,0:T(8,128)(2,1)S(1)} collective-permute-done((bf16[2,2,160,256]{3,2,1,0:T(8,128)(2,1)S(1)}, bf16[2,2,160,256]{3,2,1,0:T(8,128)(2,1)S(1)}, u32[]{:S(2)}, u32[]{:S(2)}) %collective-permute-start.8) | collective-permute-done | bytes 327712 | tf_op jit(solution)/shard_map/ppermute | solution.py:529
  50.1 0.1 shard_map.66
  50.2 2.7 %collective-permute-start.13 = (bf16[4,2,160,256]{3,2,1,0:T(8,128)(2,1)S(1)}, bf16[4,2,160,256]{3,2,1,0:T(8,128)(2,1)S(1)}, u32[]{:S(2)}, u32[]{:S(2)}) collective-permute-start(bf16[4,2,160,256]{3,2,1,0:T(8,128)(2,1)S(1)} %shard_map.66), channel_id=1, source_target_pairs={{0,4},{4,0},{1,5},{5,1},{2,6},{6,2},{3,7},{7,3},{8,12},{12,8},{9,1... | collective-permute-start | bytes 1966088 | tf_op jit(solution)/shard_map/ppermute | solution.py:506
  52.8 0.7 collective-permute-start.15
  53.5 0.7 collective-permute-start.14
  54.2 1.3 %collective-permute-start.17 = (bf16[128,320]{1,0:T(8,128)(2,1)S(1)}, bf16[128,320]{1,0:T(8,128)(2,1)S(1)}, u32[]{:S(2)}, u32[]{:S(2)}) collective-permute-start(bf16[128,320]{1,0:T(8,128)(2,1)S(1)} %get-tuple-element.90), channel_id=1, source_target_pairs={{16,8},{17,9},{18,10},{19,11},{20,12},{21,13},{22,14},{23,15}} | collective-permute-start | bytes 245768 | tf_op jit(solution)/shard_map/ppermute | solution.py:521
  55.5 1.3 %collective-permute-start.16 = (bf16[128,320]{1,0:T(8,128)(2,1)S(1)}, bf16[128,320]{1,0:T(8,128)(2,1)S(1)}, u32[]{:S(2)}, u32[]{:S(2)}) collective-permute-start(bf16[128,320]{1,0:T(8,128)(2,1)S(1)} %get-tuple-element.89), channel_id=1, source_target_pairs={{16,8},{17,9},{18,10},{19,11},{20,12},{21,13},{22,14},{23,15}} | collective-permute-start | bytes 245768 | tf_op jit(solution)/shard_map/ppermute | solution.py:521
  56.8 22.0 %collective-permute-done.17.grad_ref = bf16[128,320]{1,0:T(8,128)(2,1)S(1)} collective-permute-done((bf16[128,320]{1,0:T(8,128)(2,1)S(1)}, bf16[128,320]{1,0:T(8,128)(2,1)S(1)}, u32[]{:S(2)}, u32[]{:S(2)}) %collective-permute-start.17) | collective-permute-done | bytes 81952 | tf_op jit(solution)/shard_map/ppermute | solution.py:521
  78.8 1.2 %shard_map.70 = (bf16[128,320]{1,0:T(8,128)(2,1)S(1)}, bf16[2,2,128,320]{3,2,1,0:T(8,128)(2,1)S(1)}, bf16[4,80,256]{2,1,0:T(8,128)(2,1)S(1)}) custom-call(bf16[128,320]{1,0:T(8,128)(2,1)S(1)} %collective-permute-done.17.grad_ref, bf16[2,3,960,320]{3,2,1,0:T(8,128)(2,1)S(1)} %shard_map.61.turned_ref, ...), custom_call_target="tpu_custom_call", output_to_operand_aliasing={{1}: (4, {}), {2}: (5, {})} | custom-call | tf_op jit(solution)/shard_map/pallas_call | solution.py:176
  80.1 1.3 %collective-permute-done.16.grad_ref = bf16[128,320]{1,0:T(8,128)(2,1)S(1)} collective-permute-done((bf16[128,320]{1,0:T(8,128)(2,1)S(1)}, bf16[128,320]{1,0:T(8,128)(2,1)S(1)}, u32[]{:S(2)}, u32[]{:S(2)}) %collective-permute-start.16) | collective-permute-done | bytes 81952 | tf_op jit(solution)/shard_map/ppermute | solution.py:521
  81.4 1.2 %shard_map.71 = (bf16[128,320]{1,0:T(8,128)(2,1)S(1)}, bf16[2,2,128,320]{3,2,1,0:T(8,128)(2,1)S(1)}, bf16[4,80,256]{2,1,0:T(8,128)(2,1)S(1)}) custom-call(bf16[128,320]{1,0:T(8,128)(2,1)S(1)} %collective-permute-done.16.grad_ref, bf16[2,3,960,320]{3,2,1,0:T(8,128)(2,1)S(1)} %shard_map.61.turned_ref, ...), custom_call_target="tpu_custom_call", output_to_operand_aliasing={{1}: (4, {}), {2}: (5, {})} | custom-call | tf_op jit(solution)/shard_map/pallas_call | solution.py:176
  82.7 1.3 %collective-permute-start.18 = (bf16[128,320]{1,0:T(8,128)(2,1)S(1)}, bf16[128,320]{1,0:T(8,128)(2,1)S(1)}, u32[]{:S(2)}, u32[]{:S(2)}) collective-permute-start(bf16[128,320]{1,0:T(8,128)(2,1)S(1)} %get-tuple-element.95), channel_id=1, source_target_pairs={{8,0},{9,1},{10,2},{11,3},{12,4},{13,5},{14,6},{15,7}} | collective-permute-start | bytes 245768 | tf_op jit(solution)/shard_map/ppermute | solution.py:521
  84.0 1.3 %collective-permute-start.19 = (bf16[128,320]{1,0:T(8,128)(2,1)S(1)}, bf16[128,320]{1,0:T(8,128)(2,1)S(1)}, u32[]{:S(2)}, u32[]{:S(2)}) collective-permute-start(bf16[128,320]{1,0:T(8,128)(2,1)S(1)} %get-tuple-element.97), channel_id=1, source_target_pairs={{8,0},{9,1},{10,2},{11,3},{12,4},{13,5},{14,6},{15,7}} | collective-permute-start | bytes 245768 | tf_op jit(solution)/shard_map/ppermute | solution.py:521
  85.3 0.2 shard_map.75
  85.5 1.9 %collective-permute-start.24 = (bf16[80,256]{1,0:T(8,128)(2,1)S(1)}, bf16[80,256]{1,0:T(8,128)(2,1)S(1)}, u32[]{:S(2)}, u32[]{:S(2)}) collective-permute-start(bf16[80,256]{1,0:T(8,128)(2,1)S(1)} %get-tuple-element.112), channel_id=1, source_target_pairs={{8,9},{9,10},{10,11},{11,8},{16,17},{17,18},{18,19},{19,16},{24,25... | collective-permute-start | bytes 122888 | tf_op jit(solution)/shard_map/ppermute | solution.py:529
  87.4 2.7 %collective-permute-start.25 = (bf16[80,256]{1,0:T(8,128)(2,1)S(1)}, bf16[80,256]{1,0:T(8,128)(2,1)S(1)}, u32[]{:S(2)}, u32[]{:S(2)}) collective-permute-start(bf16[80,256]{1,0:T(8,128)(2,1)S(1)} %get-tuple-element.111), channel_id=1, source_target_pairs={{8,10},{9,11},{10,8},{11,9},{16,18},{17,19},{18,16},{19,17},{24,26... | collective-permute-start | bytes 122888 | tf_op jit(solution)/shard_map/ppermute | solution.py:529
  90.1 0.1 shard_map.65.own_ref
  90.2 3.4 %collective-permute-start.26 = (bf16[80,256]{1,0:T(8,128)(2,1)S(1)}, bf16[80,256]{1,0:T(8,128)(2,1)S(1)}, u32[]{:S(2)}, u32[]{:S(2)}) collective-permute-start(bf16[80,256]{1,0:T(8,128)(2,1)S(1)} %get-tuple-element.110), channel_id=1, source_target_pairs={{8,11},{9,8},{10,9},{11,10},{16,19},{17,16},{18,17},{19,18},{24,27... | collective-permute-start | bytes 122888 | tf_op jit(solution)/shard_map/ppermute | solution.py:529
  93.6 2.3 %shard_map.67 = (bf16[2,2320,480]{2,1,0:T(8,128)(2,1)S(1)}, f32[8,128]{1,0:T(8,128)S(1)}) custom-call(bf16[4,2,160,256]{3,2,1,0:T(8,128)(2,1)S(1)} %shard_map.65.own_ref, bf16[4,2,160,256]{3,2,1,0:T(8,128)(2,1)S(1)} %collective-permute-done.13.other_ref), custom_call_target="tpu_custom_call" | custom-call | tf_op jit(solution)/shard_map/pallas_call | solution.py:176
  95.9 1.3 %collective-permute-start.27 = (bf16[80,256]{1,0:T(8,128)(2,1)S(1)}, bf16[80,256]{1,0:T(8,128)(2,1)S(1)}, u32[]{:S(2)}, u32[]{:S(2)}) collective-permute-start(bf16[80,256]{1,0:T(8,128)(2,1)S(1)} %get-tuple-element.109), channel_id=1, source_target_pairs={{8,0},{9,1},{10,2},{11,3},{12,4},{13,5},{14,6},{15,7}} | collective-permute-start | bytes 122888 | tf_op jit(solution)/shard_map/ppermute | solution.py:529
  97.2 1.3 %collective-permute-start.28 = (bf16[80,256]{1,0:T(8,128)(2,1)S(1)}, bf16[80,256]{1,0:T(8,128)(2,1)S(1)}, u32[]{:S(2)}, u32[]{:S(2)}) collective-permute-start(bf16[80,256]{1,0:T(8,128)(2,1)S(1)} %get-tuple-element.108), channel_id=1, source_target_pairs={{8,1},{9,2},{10,3},{11,0},{12,5},{13,6},{14,7},{15,4}} | collective-permute-start | bytes 122888 | tf_op jit(solution)/shard_map/ppermute | solution.py:529
  98.6 1.3 %collective-permute-start.29 = (bf16[80,256]{1,0:T(8,128)(2,1)S(1)}, bf16[80,256]{1,0:T(8,128)(2,1)S(1)}, u32[]{:S(2)}, u32[]{:S(2)}) collective-permute-start(bf16[80,256]{1,0:T(8,128)(2,1)S(1)} %get-tuple-element.107), channel_id=1, source_target_pairs={{8,2},{9,3},{10,0},{11,1},{12,6},{13,7},{14,4},{15,5}} | collective-permute-start | bytes 122888 | tf_op jit(solution)/shard_map/ppermute | solution.py:529
  99.9 1.3 %collective-permute-start.30 = (bf16[80,256]{1,0:T(8,128)(2,1)S(1)}, bf16[80,256]{1,0:T(8,128)(2,1)S(1)}, u32[]{:S(2)}, u32[]{:S(2)}) collective-permute-start(bf16[80,256]{1,0:T(8,128)(2,1)S(1)} %get-tuple-element.106), channel_id=1, source_target_pairs={{8,3},{9,0},{10,1},{11,2},{12,7},{13,4},{14,5},{15,6}} | collective-permute-start | bytes 122888 | tf_op jit(solution)/shard_map/ppermute | solution.py:529
  101.2 1.9 %collective-permute-start.20 = (bf16[80,256]{1,0:T(8,128)(2,1)S(1)}, bf16[80,256]{1,0:T(8,128)(2,1)S(1)}, u32[]{:S(2)}, u32[]{:S(2)}) collective-permute-start(bf16[80,256]{1,0:T(8,128)(2,1)S(1)} %get-tuple-element.116), channel_id=1, source_target_pairs={{0,1},{1,2},{2,3},{3,0},{8,9},{9,10},{10,11},{11,8},{16,17},{17,18... | collective-permute-start | bytes 122888 | tf_op jit(solution)/shard_map/ppermute | solution.py:529
  103.1 1.2 %collective-permute-start.22 = (bf16[80,256]{1,0:T(8,128)(2,1)S(1)}, bf16[80,256]{1,0:T(8,128)(2,1)S(1)}, u32[]{:S(2)}, u32[]{:S(2)}) collective-permute-start(bf16[80,256]{1,0:T(8,128)(2,1)S(1)} %get-tuple-element.114), channel_id=1, source_target_pairs={{0,3},{1,0},{2,1},{3,2},{8,11},{9,8},{10,9},{11,10},{16,19},{17,16... | collective-permute-start | bytes 122888 | tf_op jit(solution)/shard_map/ppermute | solution.py:529
  104.3 3.1 %collective-permute-start.31 = (bf16[4,80,256]{2,1,0:T(8,128)(2,1)S(1)}, bf16[4,80,256]{2,1,0:T(8,128)(2,1)S(1)}, u32[]{:S(2)}, u32[]{:S(2)}) collective-permute-start(bf16[4,80,256]{2,1,0:T(8,128)(2,1)S(1)} %shard_map.76.own_ref), channel_id=1, source_target_pairs={{0,4},{4,0},{1,5},{5,1},{2,6},{6,2},{3,7},{7,3},{8,12},{12,8},{9,1... | collective-permute-start | bytes 491528 | tf_op jit(solution)/shard_map/ppermute | solution.py:506
  107.4 0.5 collective-permute-done.21.refs_2_
  107.9 0.1 collective-permute-done.22.refs_3_
  108.0 3.3 %collective-permute-start.23 = (bf16[4,80,256]{2,1,0:T(8,128)(2,1)S(1)}, bf16[4,80,256]{2,1,0:T(8,128)(2,1)S(1)}, u32[]{:S(2)}, u32[]{:S(2)}) collective-permute-start(bf16[4,80,256]{2,1,0:T(8,128)(2,1)S(1)} %shard_map.74.own_ref.after_ref), channel_id=1, source_target_pairs={{0,4},{4,0},{1,5},{5,1},{2,6},{6,2},{3,7},{7,3},{8,12},{12,8},{9,1... | collective-permute-start | bytes 491528 | tf_op jit(solution)/shard_map/ppermute | solution.py:506
  111.2 0.1 shard_map.79
  111.3 0.1 collective-permute-start.32
  111.4 1.3 %shard_map.77.refs_0_ = f32[9,160,80]{2,1,0:T(8,128)S(1)} custom-call(bf16[2,2320,480]{2,1,0:T(8,128)(2,1)S(1)} %get-tuple-element.83.around_ref, bf16[4,80,256]{2,1,0:T(8,128)(2,1)S(1)} %shard_map.76.own_ref, bf16[4,80,256]{2,1,0:T(8,128)(2,1)S(1)} %collective-permute-done.31.other_ref), custom_call_target="tpu_custom_call" | custom-call | tf_op jit(solution)/shard_map/pallas_call | solution.py:176
  112.7 0.7 shard_map.80
  113.4 2.4 %shard_map.78 = f32[2,9,160,80]{3,2,1,0:T(8,128)} custom-call(bf16[2,2320,480]{2,1,0:T(8,128)(2,1)S(1)} %get-tuple-element.83.around_ref, bf16[4,80,256]{2,1,0:T(8,128)(2,1)S(1)} %shard_map.74.own_ref.after_ref, bf16[4,80,256]{2,1,0:T(8,128)(2,1)S(1)} %collective-permute-done.23.other_ref, f32[9,160,80]{2,1,0:T(8,128)S(1)} %shard_map.77.refs_0_), custom_call_target="tpu_custom_call" | custom-call | tf_op jit(solution)/shard_map/pallas_call | solution.py:176
  (46 shorter events, 0.3 us)
Async XLA Ops:
  0.6 0.9 copy-start.1
  1.6 0.9 copy-start.2
  2.5 1.7 %collective-permute-start = (bf16[2,8,8,320]{3,2,1,0:T(8,128)(2,1)S(1)}, bf16[2,8,8,320]{3,2,1,0:T(8,128)(2,1)S(1)}, u32[]{:S(2)}, u32[]{:S(2)}) collective-permute-start(bf16[2,8,8,320]{3,2,1,0:T(8,128)(2,1)S(1)} %get-tuple-element.55), channel_id=1, source_target_pairs={{0,4},{4,0},{1,5},{5,1},{2,6},{6,2},{3,7},{7,3},{8,12},{12,8},{9,1... | collective-permute-start | bytes 245768 | tf_op jit(solution)/shard_map/ppermute | solution.py:506
  4.3 2.3 %copy-start = (bf16[1,2,9,320,320]{4,3,2,1,0:T(8,128)(2,1)S(1)}, bf16[1,2,9,320,320]{4,3,2,1,0:T(8,128)(2,1)}, u32[]{:S(2)}) copy-start(bf16[1,2,9,320,320]{4,3,2,1,0:T(8,128)(2,1)} %param.4) | copy-start | bytes 11059204
  6.5 3.0 %slice-start = ((s8[4423680]{0:T(1024)(128)(4,1)}), s8[4194304]{0:T(1024)(128)(4,1)S(1)}, s32[]{:S(2)}) async-start(s8[4423680]{0:T(1024)(128)(4,1)} %bitcast.31), calls=%async_computation | async-start | bytes 8388608
  6.5 6.1 %collective-permute-start.2 = (bf16[128,320]{1,0:T(8,128)(2,1)S(1)}, bf16[128,320]{1,0:T(8,128)(2,1)S(1)}, u32[]{:S(2)}, u32[]{:S(2)}) collective-permute-start(bf16[128,320]{1,0:T(8,128)(2,1)S(1)} %get-tuple-element.61), channel_id=1, source_target_pairs={{0,8},{1,9},{2,10},{3,11},{4,12},{5,13},{6,14},{7,15}} | collective-permute-start | bytes 245768 | tf_op jit(solution)/shard_map/ppermute | solution.py:521
  8.1 1.5 %slice-start.1 = ((s8[4423680]{0:T(1024)(128)(4,1)}), s8[229376]{0:T(1024)(128)(4,1)S(1)}, s32[]{:S(2)}) async-start(s8[4423680]{0:T(1024)(128)(4,1)} %bitcast.31), calls=%async_computation.1 | async-start | bytes 458752
  8.1 7.2 %collective-permute-start.1 = (bf16[128,320]{1,0:T(8,128)(2,1)S(1)}, bf16[128,320]{1,0:T(8,128)(2,1)S(1)}, u32[]{:S(2)}, u32[]{:S(2)}) collective-permute-start(bf16[128,320]{1,0:T(8,128)(2,1)S(1)} %get-tuple-element.60), channel_id=1, source_target_pairs={{0,8},{1,9},{2,10},{3,11},{4,12},{5,13},{6,14},{7,15}} | collective-permute-start | bytes 245768 | tf_op jit(solution)/shard_map/ppermute | solution.py:521
  14.0 3.9 %collective-permute-start.4 = (bf16[128,320]{1,0:T(8,128)(2,1)S(1)}, bf16[128,320]{1,0:T(8,128)(2,1)S(1)}, u32[]{:S(2)}, u32[]{:S(2)}) collective-permute-start(bf16[128,320]{1,0:T(8,128)(2,1)S(1)} %get-tuple-element.67), channel_id=1, source_target_pairs={{8,16},{9,17},{10,18},{11,19},{12,20},{13,21},{14,22},{15,23}} | collective-permute-start | bytes 245768 | tf_op jit(solution)/shard_map/ppermute | solution.py:521
  16.6 2.9 %collective-permute-start.3 = (bf16[128,320]{1,0:T(8,128)(2,1)S(1)}, bf16[128,320]{1,0:T(8,128)(2,1)S(1)}, u32[]{:S(2)}, u32[]{:S(2)}) collective-permute-start(bf16[128,320]{1,0:T(8,128)(2,1)S(1)} %get-tuple-element.66), channel_id=1, source_target_pairs={{8,16},{9,17},{10,18},{11,19},{12,20},{13,21},{14,22},{15,23}} | collective-permute-start | bytes 245768 | tf_op jit(solution)/shard_map/ppermute | solution.py:521
  19.7 10.4 %collective-permute-start.7 = (bf16[2,2,160,256]{3,2,1,0:T(8,128)(2,1)S(1)}, bf16[2,2,160,256]{3,2,1,0:T(8,128)(2,1)S(1)}, u32[]{:S(2)}, u32[]{:S(2)}) collective-permute-start(bf16[2,2,160,256]{3,2,1,0:T(8,128)(2,1)S(1)} %shard_map.58.after_ref), channel_id=1, source_target_pairs={{0,1},{1,2},{2,3},{3,0},{8,9},{9,10},{10,11},{11,8},{16,17},{17,18... | collective-permute-start | bytes 983048 | tf_op jit(solution)/shard_map/ppermute | solution.py:529
  21.6 6.7 %collective-permute-start.6 = (bf16[128,320]{1,0:T(8,128)(2,1)S(1)}, bf16[128,320]{1,0:T(8,128)(2,1)S(1)}, u32[]{:S(2)}, u32[]{:S(2)}) collective-permute-start(bf16[128,320]{1,0:T(8,128)(2,1)S(1)} %get-tuple-element.75), channel_id=1, source_target_pairs={{16,24},{17,25},{18,26},{19,27},{20,28},{21,29},{22,30},{23,31}} | collective-permute-start | bytes 245768 | tf_op jit(solution)/shard_map/ppermute | solution.py:521
  22.3 6.0 %collective-permute-start.5 = (bf16[128,320]{1,0:T(8,128)(2,1)S(1)}, bf16[128,320]{1,0:T(8,128)(2,1)S(1)}, u32[]{:S(2)}, u32[]{:S(2)}) collective-permute-start(bf16[128,320]{1,0:T(8,128)(2,1)S(1)} %get-tuple-element.72), channel_id=1, source_target_pairs={{16,24},{17,25},{18,26},{19,27},{20,28},{21,29},{22,30},{23,31}} | collective-permute-start | bytes 245768 | tf_op jit(solution)/shard_map/ppermute | solution.py:521
  22.9 27.1 %collective-permute-start.8 = (bf16[2,2,160,256]{3,2,1,0:T(8,128)(2,1)S(1)}, bf16[2,2,160,256]{3,2,1,0:T(8,128)(2,1)S(1)}, u32[]{:S(2)}, u32[]{:S(2)}) collective-permute-start(bf16[2,2,160,256]{3,2,1,0:T(8,128)(2,1)S(1)} %shard_map.58.after_ref), channel_id=1, source_target_pairs={{0,2},{1,3},{2,0},{3,1},{8,10},{9,11},{10,8},{11,9},{16,18},{17,19... | collective-permute-start | bytes 983048 | tf_op jit(solution)/shard_map/ppermute | solution.py:529
  26.2 23.8 %collective-permute-start.9 = (bf16[2,2,160,256]{3,2,1,0:T(8,128)(2,1)S(1)}, bf16[2,2,160,256]{3,2,1,0:T(8,128)(2,1)S(1)}, u32[]{:S(2)}, u32[]{:S(2)}) collective-permute-start(bf16[2,2,160,256]{3,2,1,0:T(8,128)(2,1)S(1)} %shard_map.58.after_ref), channel_id=1, source_target_pairs={{0,3},{1,0},{2,1},{3,2},{8,11},{9,8},{10,9},{11,10},{16,19},{17,16... | collective-permute-start | bytes 983048 | tf_op jit(solution)/shard_map/ppermute | solution.py:529
  28.7 21.4 %collective-permute-start.10 = (bf16[2,2,160,256]{3,2,1,0:T(8,128)(2,1)S(1)}, bf16[2,2,160,256]{3,2,1,0:T(8,128)(2,1)S(1)}, u32[]{:S(2)}, u32[]{:S(2)}) collective-permute-start(bf16[2,2,160,256]{3,2,1,0:T(8,128)(2,1)S(1)} %shard_map.64.refs_0_), channel_id=1, source_target_pairs={{24,25},{25,26},{26,27},{27,24},{28,29},{29,30},{30,31},{31,28}} | collective-permute-start | bytes 983048 | tf_op jit(solution)/shard_map/ppermute | solution.py:529
  29.4 20.7 %collective-permute-start.11 = (bf16[2,2,160,256]{3,2,1,0:T(8,128)(2,1)S(1)}, bf16[2,2,160,256]{3,2,1,0:T(8,128)(2,1)S(1)}, u32[]{:S(2)}, u32[]{:S(2)}) collective-permute-start(bf16[2,2,160,256]{3,2,1,0:T(8,128)(2,1)S(1)} %shard_map.64.refs_0_), channel_id=1, source_target_pairs={{24,26},{25,27},{26,24},{27,25},{28,30},{29,31},{30,28},{31,29}} | collective-permute-start | bytes 983048 | tf_op jit(solution)/shard_map/ppermute | solution.py:529
  30.1 20.0 %collective-permute-start.12 = (bf16[2,2,160,256]{3,2,1,0:T(8,128)(2,1)S(1)}, bf16[2,2,160,256]{3,2,1,0:T(8,128)(2,1)S(1)}, u32[]{:S(2)}, u32[]{:S(2)}) collective-permute-start(bf16[2,2,160,256]{3,2,1,0:T(8,128)(2,1)S(1)} %shard_map.64.refs_0_), channel_id=1, source_target_pairs={{24,27},{25,24},{26,25},{27,26},{28,31},{29,28},{30,29},{31,30}} | collective-permute-start | bytes 983048 | tf_op jit(solution)/shard_map/ppermute | solution.py:529
  50.2 40.0 %collective-permute-start.13 = (bf16[4,2,160,256]{3,2,1,0:T(8,128)(2,1)S(1)}, bf16[4,2,160,256]{3,2,1,0:T(8,128)(2,1)S(1)}, u32[]{:S(2)}, u32[]{:S(2)}) collective-permute-start(bf16[4,2,160,256]{3,2,1,0:T(8,128)(2,1)S(1)} %shard_map.66), channel_id=1, source_target_pairs={{0,4},{4,0},{1,5},{5,1},{2,6},{6,2},{3,7},{7,3},{8,12},{12,8},{9,1... | collective-permute-start | bytes 1966088 | tf_op jit(solution)/shard_map/ppermute | solution.py:506
  52.8 1.3 %collective-permute-start.15 = (bf16[128,320]{1,0:T(8,128)(2,1)S(1)}, bf16[128,320]{1,0:T(8,128)(2,1)S(1)}, u32[]{:S(2)}, u32[]{:S(2)}) collective-permute-start(bf16[128,320]{1,0:T(8,128)(2,1)S(1)} %get-tuple-element.85), channel_id=1, source_target_pairs={{24,16},{25,17},{26,18},{27,19},{28,20},{29,21},{30,22},{31,23}} | collective-permute-start | bytes 245768 | tf_op jit(solution)/shard_map/ppermute | solution.py:521
  53.5 2.0 %collective-permute-start.14 = (bf16[128,320]{1,0:T(8,128)(2,1)S(1)}, bf16[128,320]{1,0:T(8,128)(2,1)S(1)}, u32[]{:S(2)}, u32[]{:S(2)}) collective-permute-start(bf16[128,320]{1,0:T(8,128)(2,1)S(1)} %get-tuple-element.84), channel_id=1, source_target_pairs={{24,16},{25,17},{26,18},{27,19},{28,20},{29,21},{30,22},{31,23}} | collective-permute-start | bytes 245768 | tf_op jit(solution)/shard_map/ppermute | solution.py:521
  54.2 24.6 %collective-permute-start.17 = (bf16[128,320]{1,0:T(8,128)(2,1)S(1)}, bf16[128,320]{1,0:T(8,128)(2,1)S(1)}, u32[]{:S(2)}, u32[]{:S(2)}) collective-permute-start(bf16[128,320]{1,0:T(8,128)(2,1)S(1)} %get-tuple-element.90), channel_id=1, source_target_pairs={{16,8},{17,9},{18,10},{19,11},{20,12},{21,13},{22,14},{23,15}} | collective-permute-start | bytes 245768 | tf_op jit(solution)/shard_map/ppermute | solution.py:521
  55.5 25.9 %collective-permute-start.16 = (bf16[128,320]{1,0:T(8,128)(2,1)S(1)}, bf16[128,320]{1,0:T(8,128)(2,1)S(1)}, u32[]{:S(2)}, u32[]{:S(2)}) collective-permute-start(bf16[128,320]{1,0:T(8,128)(2,1)S(1)} %get-tuple-element.89), channel_id=1, source_target_pairs={{16,8},{17,9},{18,10},{19,11},{20,12},{21,13},{22,14},{23,15}} | collective-permute-start | bytes 245768 | tf_op jit(solution)/shard_map/ppermute | solution.py:521
  82.7 14.5 %collective-permute-start.18 = (bf16[128,320]{1,0:T(8,128)(2,1)S(1)}, bf16[128,320]{1,0:T(8,128)(2,1)S(1)}, u32[]{:S(2)}, u32[]{:S(2)}) collective-permute-start(bf16[128,320]{1,0:T(8,128)(2,1)S(1)} %get-tuple-element.95), channel_id=1, source_target_pairs={{8,0},{9,1},{10,2},{11,3},{12,4},{13,5},{14,6},{15,7}} | collective-permute-start | bytes 245768 | tf_op jit(solution)/shard_map/ppermute | solution.py:521
  84.0 11.9 %collective-permute-start.19 = (bf16[128,320]{1,0:T(8,128)(2,1)S(1)}, bf16[128,320]{1,0:T(8,128)(2,1)S(1)}, u32[]{:S(2)}, u32[]{:S(2)}) collective-permute-start(bf16[128,320]{1,0:T(8,128)(2,1)S(1)} %get-tuple-element.97), channel_id=1, source_target_pairs={{8,0},{9,1},{10,2},{11,3},{12,4},{13,5},{14,6},{15,7}} | collective-permute-start | bytes 245768 | tf_op jit(solution)/shard_map/ppermute | solution.py:521
  85.5 13.1 %collective-permute-start.24 = (bf16[80,256]{1,0:T(8,128)(2,1)S(1)}, bf16[80,256]{1,0:T(8,128)(2,1)S(1)}, u32[]{:S(2)}, u32[]{:S(2)}) collective-permute-start(bf16[80,256]{1,0:T(8,128)(2,1)S(1)} %get-tuple-element.112), channel_id=1, source_target_pairs={{8,9},{9,10},{10,11},{11,8},{16,17},{17,18},{18,19},{19,16},{24,25... | collective-permute-start | bytes 122888 | tf_op jit(solution)/shard_map/ppermute | solution.py:529
  87.4 12.5 %collective-permute-start.25 = (bf16[80,256]{1,0:T(8,128)(2,1)S(1)}, bf16[80,256]{1,0:T(8,128)(2,1)S(1)}, u32[]{:S(2)}, u32[]{:S(2)}) collective-permute-start(bf16[80,256]{1,0:T(8,128)(2,1)S(1)} %get-tuple-element.111), channel_id=1, source_target_pairs={{8,10},{9,11},{10,8},{11,9},{16,18},{17,19},{18,16},{19,17},{24,26... | collective-permute-start | bytes 122888 | tf_op jit(solution)/shard_map/ppermute | solution.py:529
  90.2 11.0 %collective-permute-start.26 = (bf16[80,256]{1,0:T(8,128)(2,1)S(1)}, bf16[80,256]{1,0:T(8,128)(2,1)S(1)}, u32[]{:S(2)}, u32[]{:S(2)}) collective-permute-start(bf16[80,256]{1,0:T(8,128)(2,1)S(1)} %get-tuple-element.110), channel_id=1, source_target_pairs={{8,11},{9,8},{10,9},{11,10},{16,19},{17,16},{18,17},{19,18},{24,27... | collective-permute-start | bytes 122888 | tf_op jit(solution)/shard_map/ppermute | solution.py:529
  95.9 7.2 %collective-permute-start.27 = (bf16[80,256]{1,0:T(8,128)(2,1)S(1)}, bf16[80,256]{1,0:T(8,128)(2,1)S(1)}, u32[]{:S(2)}, u32[]{:S(2)}) collective-permute-start(bf16[80,256]{1,0:T(8,128)(2,1)S(1)} %get-tuple-element.109), channel_id=1, source_target_pairs={{8,0},{9,1},{10,2},{11,3},{12,4},{13,5},{14,6},{15,7}} | collective-permute-start | bytes 122888 | tf_op jit(solution)/shard_map/ppermute | solution.py:529
  97.2 5.9 %collective-permute-start.28 = (bf16[80,256]{1,0:T(8,128)(2,1)S(1)}, bf16[80,256]{1,0:T(8,128)(2,1)S(1)}, u32[]{:S(2)}, u32[]{:S(2)}) collective-permute-start(bf16[80,256]{1,0:T(8,128)(2,1)S(1)} %get-tuple-element.108), channel_id=1, source_target_pairs={{8,1},{9,2},{10,3},{11,0},{12,5},{13,6},{14,7},{15,4}} | collective-permute-start | bytes 122888 | tf_op jit(solution)/shard_map/ppermute | solution.py:529
  98.6 5.7 %collective-permute-start.29 = (bf16[80,256]{1,0:T(8,128)(2,1)S(1)}, bf16[80,256]{1,0:T(8,128)(2,1)S(1)}, u32[]{:S(2)}, u32[]{:S(2)}) collective-permute-start(bf16[80,256]{1,0:T(8,128)(2,1)S(1)} %get-tuple-element.107), channel_id=1, source_target_pairs={{8,2},{9,3},{10,0},{11,1},{12,6},{13,7},{14,4},{15,5}} | collective-permute-start | bytes 122888 | tf_op jit(solution)/shard_map/ppermute | solution.py:529
  99.9 4.4 %collective-permute-start.30 = (bf16[80,256]{1,0:T(8,128)(2,1)S(1)}, bf16[80,256]{1,0:T(8,128)(2,1)S(1)}, u32[]{:S(2)}, u32[]{:S(2)}) collective-permute-start(bf16[80,256]{1,0:T(8,128)(2,1)S(1)} %get-tuple-element.106), channel_id=1, source_target_pairs={{8,3},{9,0},{10,1},{11,2},{12,7},{13,4},{14,5},{15,6}} | collective-permute-start | bytes 122888 | tf_op jit(solution)/shard_map/ppermute | solution.py:529
  101.2 6.2 %collective-permute-start.20 = (bf16[80,256]{1,0:T(8,128)(2,1)S(1)}, bf16[80,256]{1,0:T(8,128)(2,1)S(1)}, u32[]{:S(2)}, u32[]{:S(2)}) collective-permute-start(bf16[80,256]{1,0:T(8,128)(2,1)S(1)} %get-tuple-element.116), channel_id=1, source_target_pairs={{0,1},{1,2},{2,3},{3,0},{8,9},{9,10},{10,11},{11,8},{16,17},{17,18... | collective-permute-start | bytes 122888 | tf_op jit(solution)/shard_map/ppermute | solution.py:529
  103.0 4.8 %collective-permute-start.21 = (bf16[80,256]{1,0:T(8,128)(2,1)S(1)}, bf16[80,256]{1,0:T(8,128)(2,1)S(1)}, u32[]{:S(2)}, u32[]{:S(2)}) collective-permute-start(bf16[80,256]{1,0:T(8,128)(2,1)S(1)} %get-tuple-element.115), channel_id=1, source_target_pairs={{0,2},{1,3},{2,0},{3,1},{8,10},{9,11},{10,8},{11,9},{16,18},{17,19... | collective-permute-start | bytes 122888 | tf_op jit(solution)/shard_map/ppermute | solution.py:529
  103.1 4.9 %collective-permute-start.22 = (bf16[80,256]{1,0:T(8,128)(2,1)S(1)}, bf16[80,256]{1,0:T(8,128)(2,1)S(1)}, u32[]{:S(2)}, u32[]{:S(2)}) collective-permute-start(bf16[80,256]{1,0:T(8,128)(2,1)S(1)} %get-tuple-element.114), channel_id=1, source_target_pairs={{0,3},{1,0},{2,1},{3,2},{8,11},{9,8},{10,9},{11,10},{16,19},{17,16... | collective-permute-start | bytes 122888 | tf_op jit(solution)/shard_map/ppermute | solution.py:529
  104.3 7.1 %collective-permute-start.31 = (bf16[4,80,256]{2,1,0:T(8,128)(2,1)S(1)}, bf16[4,80,256]{2,1,0:T(8,128)(2,1)S(1)}, u32[]{:S(2)}, u32[]{:S(2)}) collective-permute-start(bf16[4,80,256]{2,1,0:T(8,128)(2,1)S(1)} %shard_map.76.own_ref), channel_id=1, source_target_pairs={{0,4},{4,0},{1,5},{5,1},{2,6},{6,2},{3,7},{7,3},{8,12},{12,8},{9,1... | collective-permute-start | bytes 491528 | tf_op jit(solution)/shard_map/ppermute | solution.py:506
  108.0 5.5 %collective-permute-start.23 = (bf16[4,80,256]{2,1,0:T(8,128)(2,1)S(1)}, bf16[4,80,256]{2,1,0:T(8,128)(2,1)S(1)}, u32[]{:S(2)}, u32[]{:S(2)}) collective-permute-start(bf16[4,80,256]{2,1,0:T(8,128)(2,1)S(1)} %shard_map.74.own_ref.after_ref), channel_id=1, source_target_pairs={{0,4},{4,0},{1,5},{5,1},{2,6},{6,2},{3,7},{7,3},{8,12},{12,8},{9,1... | collective-permute-start | bytes 491528 | tf_op jit(solution)/shard_map/ppermute | solution.py:506
  111.3 1.4 %collective-permute-start.32 = (bf16[2,8,8,320]{3,2,1,0:T(8,128)(2,1)S(1)}, bf16[2,8,8,320]{3,2,1,0:T(8,128)(2,1)S(1)}, u32[]{:S(2)}, u32[]{:S(2)}) collective-permute-start(bf16[2,8,8,320]{3,2,1,0:T(8,128)(2,1)S(1)} %get-tuple-element.105), channel_id=1, source_target_pairs={{0,4},{4,0},{1,5},{5,1},{2,6},{6,2},{3,7},{7,3},{8,12},{12,8},{9,1... | collective-permute-start | bytes 245768 | tf_op jit(solution)/shard_map/ppermute | solution.py:506
where the time goes:
time: 118 us; the launch traced here: 116 us
  starting transfers between devices  48.8 us (41%)
  waiting for transfers between devices  47.5 us (40%)
  Pallas kernels  14.2 us (12%)
  local copies, waits for them, and re-layouts  4.15 us (4%)
  between operations  1.19 us (1%)
    ppermute x12, waiting for transfers between devices, hop(): return lax.ppermute(value, 'section', [(source, target)])  26.7 us
    ppermute x16, starting transfers between devices, shared(): return lax.ppermute(values, ('section', 'img'), pairs)  25.5 us
    ppermute x16, waiting for transfers between devices, shared(): return lax.ppermute(values, ('section', 'img'), pairs)  19.9 us
    pallas_call x31, Pallas kernels, call(): pl.pallas_call(kernel, out_shape=outs, in_specs=[pl.BlockSpec(memory_spac...  14.2 us
    ppermute x12, starting transfers between devices, hop(): return lax.ppermute(value, 'section', [(source, target)])  13.4 us
    ppermute x5, starting transfers between devices, rotated(): lax.ppermute(value, axis, [(source, (source + steps) % count) for source...  9.86 us
    unnamed x10, local copies, waits for them, and re-layouts  4.11 us
  transfers between devices with their start and end apart: 33, of which 8 were waited for; matrix products, arithmetic and copies ran while one was open for 0% of the time, Pallas kernels for 10%

commit v1 on v0

--- a/solution.py
+++ b/solution.py
@@ -172,12 +172,13 @@
     return (grad_kernels, grad_slots[None])
 
 
-def call(kernel, outs, operands, unread, scratch, aliases):
+def call(kernel, outs, operands, unread, scratch, aliases, apart=()):
+    spaces = {**dict.fromkeys(unread, pl.ANY), **dict.fromkeys(apart, pltpu.HBM)}
     return pl.pallas_call(
         kernel,
         out_shape=outs,
         in_specs=[
-            pl.BlockSpec(memory_space=pl.ANY if place in unread else pltpu.VMEM)
+            pl.BlockSpec(memory_space=spaces.get(place, pltpu.VMEM))
             for place in range(len(operands))
         ],
         out_specs=[pl.BlockSpec(memory_space=pltpu.VMEM)] * len(outs),
@@ -264,26 +265,27 @@
         @pl.when(lax.axis_index("section") == section)
         def _():
             wide = grad_ref[...].astype(jnp.float32)
-            kept_ref[0, crop] = grad_ref[...]
+            own = lax.axis_index("img")
+            place_parts(sent_ref, (0,), grad_ref[...], crop, parts, own)
             grad_active = convolved(wide, turned_ref.at[1], taps, shifted, width)
             hidden = hidden_ref[crop]
             gate = jax.nn.sigmoid(hidden)
             grad_hidden = (grad_active * (gate * (1.0 + hidden * (1.0 - gate)))).astype(
                 jnp.bfloat16
             )
-            place_parts(sent_ref, (), grad_hidden, crop, parts, lax.axis_index("img"))
+            place_parts(sent_ref, (1,), grad_hidden, crop, parts, own)
             added = convolved(
                 grad_hidden.astype(jnp.float32), turned_ref.at[0], taps, shifted, width
             )
             result = (wide + added).astype(jnp.bfloat16)
-            kept_ref[1, crop] = result
+            kept_ref[crop] = result
             if not first:
                 refs[-5][...] = result
 
     outs = [
         jax.ShapeDtypeStruct((count, channels), jnp.bfloat16),
-        jax.ShapeDtypeStruct((2, crops, count, channels), jnp.bfloat16),
-        jax.ShapeDtypeStruct((parts, share, crops * count), jnp.bfloat16),
+        jax.ShapeDtypeStruct((crops, count, channels), jnp.bfloat16),
+        jax.ShapeDtypeStruct((parts, 2, share, crops * count), jnp.bfloat16),
     ][1 if first else 0 :]
     scratch = [
         pltpu.VMEM((count + 2 * width, 3 * channels), jnp.bfloat16),
@@ -341,18 +343,50 @@
     images, strip_count, rows, cols, channels = strips.shape
     share = strip_count // 2
 
-    def kernel(strips_ref, cotangent_ref, own_ref, other_ref):
+    def kernel(strips_ref, cotangent_ref, own_ref, other_ref, sems):
         own = lax.axis_index("slab")
         is_last = lax.axis_index("section") == last
-        for image in range(images):
-            for crop in range(share):
-                at = image * share + crop
-                for ref, half in ((own_ref, own), (other_ref, 1 - own)):
-                    top = cotangent_ref[image, half * share + crop]
-                    ref[at] = jnp.where(is_last, top, strips_ref[image, half * share + crop])
+
+        def fetch(source_ref):
+            copies = []
+            for image in range(images):
+                at = pl.ds(image * share, share)
+                for side, (ref, half) in enumerate(((own_ref, own), (other_ref, 1 - own))):
+                    source = source_ref.at[image, pl.ds(half * share, share)]
+                    copies.append(pltpu.make_async_copy(source, ref.at[at], sems.at[2 * image + side]))
+            for copy in copies:
+                copy.start()
+            for copy in copies:
+                copy.wait()
+
+        @pl.when(is_last)
+        def _():
+            fetch(cotangent_ref)
+
+        @pl.when(jnp.logical_not(is_last))
+        def _():
+            fetch(strips_ref)
 
     out = jax.ShapeDtypeStruct((images * share, rows, cols, channels), strips.dtype)
-    return call(kernel, [out, out], [strips, cotangent], (), [], {})
+    sems = [pltpu.SemaphoreType.DMA((2 * images,))]
+    return call(kernel, [out, out], [strips, cotangent], (), sems, {}, (0, 1))
+
+
+def load_call(weights):
+    def kernel(weights_ref, out_ref, sems):
+        copies = [
+            pltpu.make_async_copy(weights_ref.at[which], out_ref.at[which], sems.at[which])
+            for which in range(2)
+        ]
+        for copy in copies:
+            copy.start()
+        for copy in copies:
+            copy.wait()
+
+    out = jax.ShapeDtypeStruct(weights.shape, weights.dtype)
+    sems = [pltpu.SemaphoreType.DMA((2,))]
+    (loaded,) = call(kernel, [out], [weights], (), sems, {}, (0,))
+    return loaded
 
 
 def join_call(own, other):
@@ -373,13 +407,13 @@
 
 
 def part_call(kept, rows, after):
-    _, crops, count, channels = kept.shape
+    crops, count, channels = kept.shape
     cols = count // rows // 2
 
     def kernel(kept_ref, after_ref, own_ref, other_ref):
         is_left = lax.axis_index("slab") == 0
         for crop in range(crops):
-            whole = kept_ref[1, crop].astype(jnp.float32).reshape(rows, 2 * cols, channels)
+            whole = kept_ref[crop].astype(jnp.float32).reshape(rows, 2 * cols, channels)
             left, right = whole[:, :cols], whole[:, cols:]
             own_ref[crop] = jnp.where(is_left, left, right).astype(jnp.bfloat16)
             other_ref[crop] = jnp.where(is_left, right, left).astype(jnp.bfloat16)
@@ -404,100 +438,79 @@
     return merged
 
 
-def choose_call(home, early, late, slot, last):
-    blocks = 1 + len(early)
-
+def stack_call(blocks, slot, after):
     def kernel(*refs):
-        home_ref, out_ref = refs[0], refs[-1]
-        early_refs, late_refs = refs[1:blocks], refs[blocks:-1]
-        is_last = lax.axis_index("section") == last
-        out_ref[0] = home_ref[slot]
-        for block in range(1, blocks):
-            out_ref[block] = jnp.where(
-                is_last, late_refs[block - 1][slot], early_refs[block - 1][slot]
-            )
-
-    out = jax.ShapeDtypeStruct((blocks, *home.shape[1:]), home.dtype)
-    (chosen,) = call(kernel, [out], [home, *early, *late], (), [], {})
-    return chosen
-
-
-def stack_call(inner, outer):
-    blocks = len(outer)
-
-    def kernel(*refs):
-        out_ref = refs[-1]
-        for block in range(blocks):
-            value = refs[block][...]
-            if inner:
-                is_first = lax.axis_index("section") == 0
-                value = jnp.where(is_first, refs[blocks + block][...], value)
-            out_ref[block] = value
-
-    out = jax.ShapeDtypeStruct((blocks, *outer[0].shape), outer[0].dtype)
-    (stacked,) = call(kernel, [out], [*outer, *inner], (), [], {})
+        for place in range(len(blocks)):
+            refs[-1][place] = refs[place][...] if slot is None else refs[place][slot]
+
+    shape = blocks[0].shape if slot is None else blocks[0].shape[1:]
+    out = jax.ShapeDtypeStruct((len(blocks), *shape), blocks[0].dtype)
+    (stacked,) = call(kernel, [out], [*blocks, after], (len(blocks),), [], {})
     return stacked
 
 
-def spread_call(own, other, count, width):
-    blocks, two, share, cells = own.shape
+def spread_call(sources, slots, blocks, around, is_last, last, count, width):
+    two, share, cells = sources[0].shape[-3:]
     crops = cells // count
     stride = count + width
-    total = 2 * blocks * crops * stride + width
-
-    def kernel(own_ref, other_ref, out_ref, done_ref, shifted):
-        done_ref[...] = jnp.zeros_like(done_ref)
-        edge = jnp.zeros((width, 3 * share), jnp.bfloat16)
-        for kind in range(two):
-            out_ref[kind, total - width : total, :] = edge
-            for block in range(2 * blocks):
-                ref = own_ref if block < blocks else other_ref
-                for crop in range(crops):
-                    value = ref[block % blocks, kind, :, crop * count : (crop + 1) * count]
-                    value = value.T.astype(jnp.float32)
-                    before, after = neighbours(value, shifted, width)
-                    at = (block * crops + crop) * stride
-                    out_ref[kind, at : at + width, :] = edge
-                    for place, part in enumerate((before, value, after)):
-                        lanes = slice(place * share, (place + 1) * share)
-                        out_ref[kind, at + width : at + stride, lanes] = part.astype(jnp.bfloat16)
-
-    outs = [
-        jax.ShapeDtypeStruct((two, total, 3 * share), jnp.bfloat16),
-        jax.ShapeDtypeStruct((8, 128), jnp.float32),
-    ]
+    fresh = isinstance(around, jax.ShapeDtypeStruct)
+    total = around.shape[1]
+
+    def kernel(*refs):
+        out_ref, shifted = refs[-2:]
+        mine = (lax.axis_index("section") == last) == is_last
+
+        @pl.when(mine)
+        def _():
+            edge = jnp.zeros((width, 3 * share), jnp.bfloat16)
+            for kind in range(two):
+                out_ref[kind, total - width : total, :] = edge
+                for ref, slot, block in zip(refs, slots, blocks):
+                    for crop in range(crops):
+                        cell = slice(crop * count, (crop + 1) * count)
+                        value = ref[(*slot, kind, slice(None), cell)].T.astype(jnp.float32)
+                        before, after = neighbours(value, shifted, width)
+                        at = (block * crops + crop) * stride
+                        out_ref[kind, at : at + width, :] = edge
+                        for place, part in enumerate((before, value, after)):
+                            lanes = slice(place * share, (place + 1) * share)
+                            out_ref[kind, at + width : at + stride, lanes] = part.astype(
+                                jnp.bfloat16
+                            )
+
+    operands = [*sources] if fresh else [*sources, around]
+    aliases = {} if fresh else {len(sources): 0}
+    out = jax.ShapeDtypeStruct(around.shape, around.dtype)
     scratch = [pltpu.VMEM((count + 16, share), jnp.float32)]
-    return call(kernel, outs, [own, other], (), scratch, {})
-
-
-def terms_call(around, kind, own, other, others, count, width, scaling):
-    blocks, columns, cells = own.shape
+    (spread,) = call(kernel, [out], operands, (), scratch, aliases)
+    return spread
+
+
+def terms_call(around, own, other, count, width, scaling):
+    blocks, _, columns, cells = own.shape
     rows = around.shape[2] // 3
     stride = count + width
     crops = cells // count
 
-    def kernel(around_ref, own_ref, other_ref, *refs):
-        out_ref = refs[-1]
-        if others:
-            refs[-1][1] = refs[0][...]
-            out_ref = refs[-1].at[0]
-        for down in range(3):
-            total = None
-            for block in range(2 * blocks):
-                left = own_ref[block] if block < blocks else other_ref[block - blocks]
-                at = [(block * crops + k) * stride + down * width for k in range(crops)]
-                right = jnp.concatenate(
-                    [around_ref[kind, start : start + count, :] for start in at], axis=0
-                )
-                term = jnp.dot(left, right, preferred_element_type=jnp.float32)
-                total = term if total is None else total + term
-            total = (total * scaling).T.reshape(3, rows, columns)
-            for place in range(3):
-                out_ref[3 * down + place] = total[place]
-
-    shape = (9, rows, columns)
-    out = jax.ShapeDtypeStruct((2, *shape) if others else shape, jnp.float32)
-    (terms,) = call(kernel, [out], [around, own, other, *others], (), [], {})
+    def kernel(around_ref, own_ref, other_ref, out_ref):
+        for kind in range(2):
+            for down in range(3):
+                total = None
+                for block in range(2 * blocks):
+                    left = own_ref if block < blocks else other_ref
+                    left = left[block % blocks, 1 - kind]
+                    at = [(block * crops + k) * stride + down * width for k in range(crops)]
+                    right = jnp.concatenate(
+                        [around_ref[kind, start : start + count, :] for start in at], axis=0
+                    )
+                    term = jnp.dot(left, right, preferred_element_type=jnp.float32)
+                    total = term if total is None else total + term
+                total = (total * scaling).T.reshape(3, rows, columns)
+                for place in range(3):
+                    out_ref[kind, 3 * down + place] = total[place]
+
+    out = jax.ShapeDtypeStruct((2, 9, rows, columns), jnp.float32)
+    (terms,) = call(kernel, [out], [around, own, other], (), [], {})
     return terms
 
 
@@ -515,23 +528,25 @@
     crops = images * strip_count // slabs
     last = sections - 1
     scaling = 1.0 / math.sqrt(images * groups * strip_count * count)
-    weights = kernels[0].reshape(2, 3, 3 * channels, channels)
 
     def hop(value, source, target):
         return lax.ppermute(value, "section", [(source, target)])
 
     def shared(values, step, routes):
         pairs = [
-            (source * groups + i, target * groups + (i + step) % groups)
-            for source, target in routes
+            (source * groups + i, source * groups + (i + step) % groups)
+            for source in routes
             for i in range(groups)
         ]
         return lax.ppermute(values, ("section", "img"), pairs)
 
+    everywhere = range(sections)
     own, other = split_call(strips, cotangent, last)
-    fields = join_call(own, rotated(other, "slab", 1))
+    other = rotated(other, "slab", 1)
+    weights = load_call(kernels[0].reshape(2, 3, 3 * channels, channels))
+    fields = join_call(own, other)
     incoming = fields
-    state, saved_sets = [], []
+    state, early = [], []
     turned, after = None, weights
     for place in range(sections):
         outgoing = []
@@ -547,12 +562,14 @@
         if place == last - 1:
             flipped = flip_call(state[0], (0, 1), slabs, "slab", state[1])
             after = flipped
-            routes = [(source, source) for source in range(last)]
-            saved_sets.append([shared(flipped, step, routes) for step in range(1, groups)])
+            early = [flipped]
+            for step in range(1, groups):
+                early.append(shared(flipped, step, everywhere))
     saved, hidden = state
     incoming = fields
     grads = []
     around, after = None, hidden
+    late = []
     for place in reversed(range(sections)):
         outgoing = []
         for crop in range(crops):
@@ -564,30 +581,50 @@
             incoming = [hop(out, place, place - 1) for out in outgoing]
         if place == last:
             flipped = flip_call(saved, (0, 1), slabs, "slab", grads[0])
-            saved_sets.append([shared(flipped, step, [(last, last)]) for step in range(1, groups)])
+            pairs = [(last * slabs + i, last * slabs + (i + 1) % slabs) for i in range(slabs)]
+            other = lax.ppermute(flipped[1], ("section", "slab"), pairs)
+            both = stack_call([flipped[0], other], None, grads[0])
+            late = [both]
+            for step in range(1, groups):
+                late.append(shared(both, step, [last]))
         if place == 1:
-            handed = flip_call(grads[0], (0, 1), groups, "img", grads[1])
-            routes = [(source, source) for source in range(1, sections)]
-            later = [handed[0, 0]]
-            for step in range(1, groups):
-                later.append(shared(handed[step, 0], step, routes))
-            first = [shared(handed[step, 1], step, [(1, 0)]) for step in range(groups)]
-            own = choose_call(flipped, *saved_sets, 0, last)
-            other = choose_call(flipped, *saved_sets, 1, last)
+            other = stack_call(early, 1, outgoing[-1])
             other = rotated(other, "slab", 1)
-            around, after = spread_call(own, other, count, width)
+            stride = count + width
+            shape = (2, slabs * groups * crops * stride + width, 3 * (channels // slabs))
+            around = spread_call(
+                [*early, *([other] * groups)],
+                [(0,)] * groups + [(block,) for block in range(groups)],
+                list(range(slabs * groups)),
+                jax.ShapeDtypeStruct(shape, jnp.bfloat16),
+                False,
+                last,
+                count,
+                width,
+            )
+            after = around
     kept, sent = grads
-    hidden_grads = [sent[0]]
+    own = [sent[0]]
     for step in range(1, groups):
-        hidden_grads.append(shared(sent[step], step, [(place, place) for place in range(sections)]))
-    out_grads = stack_call(first, later)
-    other = rotated(out_grads, "slab", 1)
-    upper = terms_call(around, 1, out_grads, other, [], count, width, scaling)
-    hidden_grads = stack_call([], hidden_grads)
-    other = rotated(hidden_grads, "slab", 1)
-    terms = terms_call(around, 0, hidden_grads, other, [upper], count, width, scaling)
-    own, other = part_call(kept, row_count, hidden_grads)
-    grad_inputs = merge_call(own, rotated(other, "slab", 1), images)
+        own.append(shared(sent[step], step, everywhere))
+    around, sent = lax.optimization_barrier((around, sent))
+    for block in range(groups):
+        around = spread_call(
+            [late[block]] * slabs,
+            [(slab,) for slab in range(slabs)],
+            [slab * groups + block for slab in range(slabs)],
+            around,
+            True,
+            last,
+            count,
+            width,
+        )
+    own = stack_call(own, None, around)
+    other = rotated(own, "slab", 1)
+    terms = terms_call(around, own, other, count, width, scaling)
+    own, other = part_call(kept, row_count, sent)
+    other = rotated(other, "slab", 1)
+    grad_inputs = merge_call(own, other, images)
     return (terms[None], grad_inputs[None])
 
 

time: 118 us -> 112 us (0.949)
  the two profiles are of different devices: /device:TPU:27 before, /device:TPU:15 now
where the time goes in v1:
time: 112 us
  waiting for transfers between devices  61.4 us (55%)
  starting transfers between devices  31.8 us (28%)
  Pallas kernels  13.3 us (12%)
  local copies, waits for them, and re-layouts  4.15 us (4%)
    ppermute x9, waiting for transfers between devices, shared(): return lax.ppermute(values, ('section', 'img'), pairs)  46.1 us
    ppermute x9, starting transfers between devices, shared(): return lax.ppermute(values, ('section', 'img'), pairs)  15.3 us
    ppermute x12, waiting for transfers between devices, hop(): return lax.ppermute(value, 'section', [(source, target)])  14 us
    pallas_call x33, Pallas kernels, call(): pl.pallas_call(kernel, out_shape=outs, in_specs=[pl.BlockSpec(memory_spac...  13.3 us
    ppermute x12, starting transfers between devices, hop(): return lax.ppermute(value, 'section', [(source, target)])  10.5 us
    ppermute x1, starting transfers between devices, crop_shards(): other = lax.ppermute(flipped[1], ('section', 'slab'), pairs)  4.14 us
    unnamed x6, local copies, waits for them, and re-layouts  4.1 us
  transfers between devices with their start and end apart: 26, of which 11 were waited for; matrix products, arithmetic and copies ran while one was open for 0% of the time, Pallas kernels for 5%

profile of v1, /device:TPU:15, one launch (start us, length us, event | category | flops | bytes accessed | tf_op | source)
XLA Modules:
  0.0 111.8 jit_solution(13028212640835410061)
XLA Ops:
  0.6 0.9 copy-done.1
  1.6 0.9 copy-done.2
  2.5 0.2 shard_map.50
  2.7 0.7 collective-permute-start
  3.5 2.3 %copy-done = bf16[1,2,9,320,320]{4,3,2,1,0:T(8,128)(2,1)S(1)} copy-done((bf16[1,2,9,320,320]{4,3,2,1,0:T(8,128)(2,1)S(1)}, bf16[1,2,9,320,320]{4,3,2,1,0:T(8,128)(2,1)}, u32[]{:S(2)}) %copy-start) | copy-done | bytes 3686424
  5.7 0.6 shard_map.52.weights_ref.after_ref
  6.3 0.0 collective-permute-done.other_ref
  6.3 0.1 shard_map.51
  6.4 0.7 collective-permute-start.2
  7.1 0.7 collective-permute-start.1
  7.8 1.4 %shard_map.62.turned_ref = bf16[2,3,960,320]{3,2,1,0:T(8,128)(2,1)S(1)} custom-call(bf16[2,3,960,320]{3,2,1,0:T(8,128)(2,1)S(1)} %shard_map.52.weights_ref.after_ref, bf16[2,2,128,320]{3,2,1,0:T(8,128)(2,1)S(1)} %get-tuple-element.62.refs_0_.after_ref), custom_call_target="tpu_custom_call" | custom-call | tf_op jit(solution)/shard_map/pallas_call | solution.py:177
  9.2 0.0 collective-permute-done.2.field_ref
  9.2 0.7 collective-permute-start.4
  9.9 0.0 collective-permute-done.1.field_ref
  9.9 0.7 collective-permute-start.3
  10.6 1.3 %collective-permute-start.6 = (bf16[128,320]{1,0:T(8,128)(2,1)S(1)}, bf16[128,320]{1,0:T(8,128)(2,1)S(1)}, u32[]{:S(2)}, u32[]{:S(2)}) collective-permute-start(bf16[128,320]{1,0:T(8,128)(2,1)S(1)} %get-tuple-element.75), channel_id=1, source_target_pairs={{16,24},{17,25},{18,26},{19,27},{20,28},{21,29},{22,30},{23,31}} | collective-permute-start | bytes 245768 | tf_op jit(solution)/shard_map/ppermute | solution.py:533
  11.9 0.0 collective-permute-done.3.field_ref
  12.0 1.3 %collective-permute-start.5 = (bf16[128,320]{1,0:T(8,128)(2,1)S(1)}, bf16[128,320]{1,0:T(8,128)(2,1)S(1)}, u32[]{:S(2)}, u32[]{:S(2)}) collective-permute-start(bf16[128,320]{1,0:T(8,128)(2,1)S(1)} %get-tuple-element.72), channel_id=1, source_target_pairs={{16,24},{17,25},{18,26},{19,27},{20,28},{21,29},{22,30},{23,31}} | collective-permute-start | bytes 245768 | tf_op jit(solution)/shard_map/ppermute | solution.py:533
  13.3 0.2 shard_map.59.after_ref.refs_0_
  13.4 9.8 %collective-permute-done.6.field_ref = bf16[128,320]{1,0:T(8,128)(2,1)S(1)} collective-permute-done((bf16[128,320]{1,0:T(8,128)(2,1)S(1)}, bf16[128,320]{1,0:T(8,128)(2,1)S(1)}, u32[]{:S(2)}, u32[]{:S(2)}) %collective-permute-start.6) | collective-permute-done | bytes 81952 | tf_op jit(solution)/shard_map/ppermute | solution.py:533
  23.2 0.6 shard_map.60
  23.8 2.3 %collective-permute-done.5.field_ref = bf16[128,320]{1,0:T(8,128)(2,1)S(1)} collective-permute-done((bf16[128,320]{1,0:T(8,128)(2,1)S(1)}, bf16[128,320]{1,0:T(8,128)(2,1)S(1)}, u32[]{:S(2)}, u32[]{:S(2)}) %collective-permute-start.5) | collective-permute-done | bytes 81952 | tf_op jit(solution)/shard_map/ppermute | solution.py:533
  26.2 0.6 shard_map.61
  26.8 1.2 %shard_map.63 = (bf16[128,320]{1,0:T(8,128)(2,1)S(1)}, bf16[2,128,320]{2,1,0:T(8,128)(2,1)S(1)}, bf16[4,2,80,256]{3,2,1,0:T(8,128)(2,1)S(1)}) custom-call(bf16[128,320]{1,0:T(8,128)(2,1)S(1)} %get-tuple-element.57.field_ref.grad_ref, bf16[2,3,960,320]{3,2,1,0:T(8,128)(2,1)S(1)} %shard_map.62.turned_ref, ...), custom_call_target="tpu_custom_call" | custom-call | tf_op jit(solution)/shard_map/pallas_call | solution.py:177
  28.0 1.4 %shard_map.64 = (bf16[128,320]{1,0:T(8,128)(2,1)S(1)}, bf16[2,128,320]{2,1,0:T(8,128)(2,1)S(1)}, bf16[4,2,80,256]{3,2,1,0:T(8,128)(2,1)S(1)}) custom-call(bf16[128,320]{1,0:T(8,128)(2,1)S(1)} %get-tuple-element.56.field_ref.grad_ref, bf16[2,3,960,320]{3,2,1,0:T(8,128)(2,1)S(1)} %shard_map.62.turned_ref, ...), custom_call_target="tpu_custom_call", output_to_operand_aliasing={{1}: (4, {}), {2}: (5, {})} | custom-call | tf_op jit(solution)/shard_map/pallas_call | solution.py:177
  29.5 0.2 shard_map.65
  29.7 4.1 %collective-permute-start.7 = (bf16[2,160,256]{2,1,0:T(8,128)(2,1)S(1)}, bf16[2,160,256]{2,1,0:T(8,128)(2,1)S(1)}, u32[]{:S(2)}, u32[]{:S(2)}) collective-permute-start(bf16[2,160,256]{2,1,0:T(8,128)(2,1)S(1)} %get-tuple-element.110), channel_id=1, source_target_pairs={{24,28},{28,24},{25,29},{29,25},{26,30},{30,26},{27,31},{31,27}} | collective-permute-start | bytes 491528 | tf_op jit(solution)/shard_map/ppermute | solution.py:585
  33.8 1.4 %collective-permute-start.11 = (bf16[2,2,160,256]{3,2,1,0:T(8,128)(2,1)S(1)}, bf16[2,2,160,256]{3,2,1,0:T(8,128)(2,1)S(1)}, u32[]{:S(2)}, u32[]{:S(2)}) collective-permute-start(bf16[2,2,160,256]{3,2,1,0:T(8,128)(2,1)S(1)} %shard_map.59.after_ref.refs_0_), channel_id=1, source_target_pairs={{0,1},{1,2},{2,3},{3,0},{8,9},{9,10},{10,11},{11,8},{16,17},{17,18... | collective-permute-start | bytes 983048 | tf_op jit(solution)/shard_map/ppermute | solution.py:541
  35.2 1.1 collective-permute-start.12
  36.3 1.4 %collective-permute-start.13 = (bf16[2,2,160,256]{3,2,1,0:T(8,128)(2,1)S(1)}, bf16[2,2,160,256]{3,2,1,0:T(8,128)(2,1)S(1)}, u32[]{:S(2)}, u32[]{:S(2)}) collective-permute-start(bf16[2,2,160,256]{3,2,1,0:T(8,128)(2,1)S(1)} %shard_map.59.after_ref.refs_0_), channel_id=1, source_target_pairs={{0,3},{1,0},{2,1},{3,2},{8,11},{9,8},{10,9},{11,10},{16,19},{17,16... | collective-permute-start | bytes 983048 | tf_op jit(solution)/shard_map/ppermute | solution.py:541
  37.7 1.3 %collective-permute-start.15 = (bf16[128,320]{1,0:T(8,128)(2,1)S(1)}, bf16[128,320]{1,0:T(8,128)(2,1)S(1)}, u32[]{:S(2)}, u32[]{:S(2)}) collective-permute-start(bf16[128,320]{1,0:T(8,128)(2,1)S(1)} %get-tuple-element.84), channel_id=1, source_target_pairs={{24,16},{25,17},{26,18},{27,19},{28,20},{29,21},{30,22},{31,23}} | collective-permute-start | bytes 245768 | tf_op jit(solution)/shard_map/ppermute | solution.py:533
  38.9 0.0 collective-permute-done.7.refs_1_
  39.0 1.3 %collective-permute-start.14 = (bf16[128,320]{1,0:T(8,128)(2,1)S(1)}, bf16[128,320]{1,0:T(8,128)(2,1)S(1)}, u32[]{:S(2)}, u32[]{:S(2)}) collective-permute-start(bf16[128,320]{1,0:T(8,128)(2,1)S(1)} %get-tuple-element.83), channel_id=1, source_target_pairs={{24,16},{25,17},{26,18},{27,19},{28,20},{29,21},{30,22},{31,23}} | collective-permute-start | bytes 245768 | tf_op jit(solution)/shard_map/ppermute | solution.py:533
  40.3 0.3 collective-permute-done.15.grad_ref
  40.6 0.7 collective-permute-start.17
  41.2 1.6 %collective-permute-done.14.grad_ref = bf16[128,320]{1,0:T(8,128)(2,1)S(1)} collective-permute-done((bf16[128,320]{1,0:T(8,128)(2,1)S(1)}, bf16[128,320]{1,0:T(8,128)(2,1)S(1)}, u32[]{:S(2)}, u32[]{:S(2)}) %collective-permute-start.14) | collective-permute-done | bytes 81952 | tf_op jit(solution)/shard_map/ppermute | solution.py:533
  42.8 0.7 collective-permute-start.16
  43.5 0.0 collective-permute-done.17.grad_ref
  43.5 0.0 collective-permute-done.16.grad_ref
  43.6 19.7 %collective-permute-done.12.refs_2_ = bf16[2,2,160,256]{3,2,1,0:T(8,128)(2,1)S(1)} collective-permute-done((bf16[2,2,160,256]{3,2,1,0:T(8,128)(2,1)S(1)}, bf16[2,2,160,256]{3,2,1,0:T(8,128)(2,1)S(1)}, u32[]{:S(2)}, u32[]{:S(2)}) %collective-permute-start.12) | collective-permute-done | bytes 327712 | tf_op jit(solution)/shard_map/ppermute | solution.py:541
  63.3 2.2 %collective-permute-done.13.refs_3_ = bf16[2,2,160,256]{3,2,1,0:T(8,128)(2,1)S(1)} collective-permute-done((bf16[2,2,160,256]{3,2,1,0:T(8,128)(2,1)S(1)}, bf16[2,2,160,256]{3,2,1,0:T(8,128)(2,1)S(1)}, u32[]{:S(2)}, u32[]{:S(2)}) %collective-permute-start.13) | collective-permute-done | bytes 327712 | tf_op jit(solution)/shard_map/ppermute | solution.py:541
  65.5 0.5 collective-permute-start.18
  66.1 1.9 %collective-permute-start.10 = (bf16[2,2,160,256]{3,2,1,0:T(8,128)(2,1)S(1)}, bf16[2,2,160,256]{3,2,1,0:T(8,128)(2,1)S(1)}, u32[]{:S(2)}, u32[]{:S(2)}) collective-permute-start(bf16[2,2,160,256]{3,2,1,0:T(8,128)(2,1)S(1)} %shard_map.66.refs_0_.refs_1_), channel_id=1, source_target_pairs={{24,25},{25,26},{26,27},{27,24},{28,29},{29,30},{30,31},{31,28}} | collective-permute-start | bytes 983048 | tf_op jit(solution)/shard_map/ppermute | solution.py:541
  68.0 0.7 collective-permute-start.20
  68.7 0.7 collective-permute-start.19
  69.3 3.2 %collective-permute-start.9 = (bf16[2,2,160,256]{3,2,1,0:T(8,128)(2,1)S(1)}, bf16[2,2,160,256]{3,2,1,0:T(8,128)(2,1)S(1)}, u32[]{:S(2)}, u32[]{:S(2)}) collective-permute-start(bf16[2,2,160,256]{3,2,1,0:T(8,128)(2,1)S(1)} %shard_map.66.refs_0_.refs_1_), channel_id=1, source_target_pairs={{24,26},{25,27},{26,24},{27,25},{28,30},{29,31},{30,28},{31,29}} | collective-permute-start | bytes 983048 | tf_op jit(solution)/shard_map/ppermute | solution.py:541
  72.6 3.4 %collective-permute-start.8 = (bf16[2,2,160,256]{3,2,1,0:T(8,128)(2,1)S(1)}, bf16[2,2,160,256]{3,2,1,0:T(8,128)(2,1)S(1)}, u32[]{:S(2)}, u32[]{:S(2)}) collective-permute-start(bf16[2,2,160,256]{3,2,1,0:T(8,128)(2,1)S(1)} %shard_map.66.refs_0_.refs_1_), channel_id=1, source_target_pairs={{24,27},{25,24},{26,25},{27,26},{28,31},{29,28},{30,29},{31,30}} | collective-permute-start | bytes 983048 | tf_op jit(solution)/shard_map/ppermute | solution.py:541
  76.0 0.0 collective-permute-done.19.grad_ref
  76.1 0.1 collective-permute-start.21
  76.1 2.9 %collective-permute-start.22 = (bf16[2,80,256]{2,1,0:T(8,128)(2,1)S(1)}, bf16[2,80,256]{2,1,0:T(8,128)(2,1)S(1)}, u32[]{:S(2)}, u32[]{:S(2)}) collective-permute-start(bf16[2,80,256]{2,1,0:T(8,128)(2,1)S(1)} %get-tuple-element.107), channel_id=1, source_target_pairs={{0,2},{1,3},{2,0},{3,1},{8,10},{9,11},{10,8},{11,9},{16,18},{17,19... | collective-permute-start | bytes 245768 | tf_op jit(solution)/shard_map/ppermute | solution.py:541
  79.0 0.6 shard_map.75.refs_2_
  79.6 0.6 shard_map.76.refs_2_
  80.2 19.7 %collective-permute-done.9.refs_0_.refs_1_ = bf16[2,2,160,256]{3,2,1,0:T(8,128)(2,1)S(1)} collective-permute-done((bf16[2,2,160,256]{3,2,1,0:T(8,128)(2,1)S(1)}, bf16[2,2,160,256]{3,2,1,0:T(8,128)(2,1)S(1)}, u32[]{:S(2)}, u32[]{:S(2)}) %collective-permute-start.9) | collective-permute-done | bytes 327712 | tf_op jit(solution)/shard_map/ppermute | solution.py:541
  99.9 0.6 shard_map.77.refs_2_
  100.4 1.6 %collective-permute-done.8.refs_0_.refs_1_ = bf16[2,2,160,256]{3,2,1,0:T(8,128)(2,1)S(1)} collective-permute-done((bf16[2,2,160,256]{3,2,1,0:T(8,128)(2,1)S(1)}, bf16[2,2,160,256]{3,2,1,0:T(8,128)(2,1)S(1)}, u32[]{:S(2)}, u32[]{:S(2)}) %collective-permute-start.8) | collective-permute-done | bytes 327712 | tf_op jit(solution)/shard_map/ppermute | solution.py:541
  102.1 0.6 shard_map.78.refs_4_.around_ref
  102.7 0.7 collective-permute-done.22.refs_2_
  103.4 2.2 %collective-permute-done.23.refs_3_ = bf16[2,80,256]{2,1,0:T(8,128)(2,1)S(1)} collective-permute-done((bf16[2,80,256]{2,1,0:T(8,128)(2,1)S(1)}, bf16[2,80,256]{2,1,0:T(8,128)(2,1)S(1)}, u32[]{:S(2)}, u32[]{:S(2)}) %collective-permute-start.23) | collective-permute-done | bytes 81952 | tf_op jit(solution)/shard_map/ppermute | solution.py:541
  105.6 0.5 collective-permute-start.24
  106.1 0.1 shard_map.81
  106.2 0.1 collective-permute-start.25
  106.3 1.3 %collective-permute-done.25.other_ref = bf16[2,8,8,320]{3,2,1,0:T(8,128)(2,1)S(1)} collective-permute-done((bf16[2,8,8,320]{3,2,1,0:T(8,128)(2,1)S(1)}, bf16[2,8,8,320]{3,2,1,0:T(8,128)(2,1)S(1)}, u32[]{:S(2)}, u32[]{:S(2)}) %collective-permute-start.25) | collective-permute-done | bytes 81952 | tf_op jit(solution)/shard_map/ppermute | solution.py:519
  107.6 0.7 shard_map.82
  108.3 3.5 %shard_map.80 = f32[2,9,160,80]{3,2,1,0:T(8,128)} custom-call(bf16[2,2320,480]{2,1,0:T(8,128)(2,1)S(1)} %shard_map.78.refs_4_.around_ref, bf16[4,2,80,256]{3,2,1,0:T(8,128)(2,1)S(1)} %shard_map.79.own_ref, bf16[4,2,80,256]{3,2,1,0:T(8,128)(2,1)S(1)} %collective-permute-done.24.other_ref), custom_call_target="tpu_custom_call" | custom-call | tf_op jit(solution)/shard_map/pallas_call | solution.py:177
  (29 shorter events, 0.4 us)
Async XLA Ops:
  0.6 0.9 copy-start.1
  1.6 0.9 copy-start.2
  2.7 3.6 %collective-permute-start = (bf16[2,8,8,320]{3,2,1,0:T(8,128)(2,1)S(1)}, bf16[2,8,8,320]{3,2,1,0:T(8,128)(2,1)S(1)}, u32[]{:S(2)}, u32[]{:S(2)}) collective-permute-start(bf16[2,8,8,320]{3,2,1,0:T(8,128)(2,1)S(1)} %get-tuple-element.55), channel_id=1, source_target_pairs={{0,4},{4,0},{1,5},{5,1},{2,6},{6,2},{3,7},{7,3},{8,12},{12,8},{9,1... | collective-permute-start | bytes 245768 | tf_op jit(solution)/shard_map/ppermute | solution.py:519
  3.5 2.3 %copy-start = (bf16[1,2,9,320,320]{4,3,2,1,0:T(8,128)(2,1)S(1)}, bf16[1,2,9,320,320]{4,3,2,1,0:T(8,128)(2,1)}, u32[]{:S(2)}) copy-start(bf16[1,2,9,320,320]{4,3,2,1,0:T(8,128)(2,1)} %param.4) | copy-start | bytes 11059204
  6.4 2.7 %collective-permute-start.2 = (bf16[128,320]{1,0:T(8,128)(2,1)S(1)}, bf16[128,320]{1,0:T(8,128)(2,1)S(1)}, u32[]{:S(2)}, u32[]{:S(2)}) collective-permute-start(bf16[128,320]{1,0:T(8,128)(2,1)S(1)} %get-tuple-element.61), channel_id=1, source_target_pairs={{0,8},{1,9},{2,10},{3,11},{4,12},{5,13},{6,14},{7,15}} | collective-permute-start | bytes 245768 | tf_op jit(solution)/shard_map/ppermute | solution.py:533
  7.1 2.7 %collective-permute-start.1 = (bf16[128,320]{1,0:T(8,128)(2,1)S(1)}, bf16[128,320]{1,0:T(8,128)(2,1)S(1)}, u32[]{:S(2)}, u32[]{:S(2)}) collective-permute-start(bf16[128,320]{1,0:T(8,128)(2,1)S(1)} %get-tuple-element.60), channel_id=1, source_target_pairs={{0,8},{1,9},{2,10},{3,11},{4,12},{5,13},{6,14},{7,15}} | collective-permute-start | bytes 245768 | tf_op jit(solution)/shard_map/ppermute | solution.py:533
  9.2 1.4 %collective-permute-start.4 = (bf16[128,320]{1,0:T(8,128)(2,1)S(1)}, bf16[128,320]{1,0:T(8,128)(2,1)S(1)}, u32[]{:S(2)}, u32[]{:S(2)}) collective-permute-start(bf16[128,320]{1,0:T(8,128)(2,1)S(1)} %get-tuple-element.67), channel_id=1, source_target_pairs={{8,16},{9,17},{10,18},{11,19},{12,20},{13,21},{14,22},{15,23}} | collective-permute-start | bytes 245768 | tf_op jit(solution)/shard_map/ppermute | solution.py:533
  9.9 2.0 %collective-permute-start.3 = (bf16[128,320]{1,0:T(8,128)(2,1)S(1)}, bf16[128,320]{1,0:T(8,128)(2,1)S(1)}, u32[]{:S(2)}, u32[]{:S(2)}) collective-permute-start(bf16[128,320]{1,0:T(8,128)(2,1)S(1)} %get-tuple-element.66), channel_id=1, source_target_pairs={{8,16},{9,17},{10,18},{11,19},{12,20},{13,21},{14,22},{15,23}} | collective-permute-start | bytes 245768 | tf_op jit(solution)/shard_map/ppermute | solution.py:533
  10.6 12.6 %collective-permute-start.6 = (bf16[128,320]{1,0:T(8,128)(2,1)S(1)}, bf16[128,320]{1,0:T(8,128)(2,1)S(1)}, u32[]{:S(2)}, u32[]{:S(2)}) collective-permute-start(bf16[128,320]{1,0:T(8,128)(2,1)S(1)} %get-tuple-element.75), channel_id=1, source_target_pairs={{16,24},{17,25},{18,26},{19,27},{20,28},{21,29},{22,30},{23,31}} | collective-permute-start | bytes 245768 | tf_op jit(solution)/shard_map/ppermute | solution.py:533
  12.0 14.2 %collective-permute-start.5 = (bf16[128,320]{1,0:T(8,128)(2,1)S(1)}, bf16[128,320]{1,0:T(8,128)(2,1)S(1)}, u32[]{:S(2)}, u32[]{:S(2)}) collective-permute-start(bf16[128,320]{1,0:T(8,128)(2,1)S(1)} %get-tuple-element.72), channel_id=1, source_target_pairs={{16,24},{17,25},{18,26},{19,27},{20,28},{21,29},{22,30},{23,31}} | collective-permute-start | bytes 245768 | tf_op jit(solution)/shard_map/ppermute | solution.py:533
  29.7 9.3 %collective-permute-start.7 = (bf16[2,160,256]{2,1,0:T(8,128)(2,1)S(1)}, bf16[2,160,256]{2,1,0:T(8,128)(2,1)S(1)}, u32[]{:S(2)}, u32[]{:S(2)}) collective-permute-start(bf16[2,160,256]{2,1,0:T(8,128)(2,1)S(1)} %get-tuple-element.110), channel_id=1, source_target_pairs={{24,28},{28,24},{25,29},{29,25},{26,30},{30,26},{27,31},{31,27}} | collective-permute-start | bytes 491528 | tf_op jit(solution)/shard_map/ppermute | solution.py:585
  33.8 9.8 %collective-permute-start.11 = (bf16[2,2,160,256]{3,2,1,0:T(8,128)(2,1)S(1)}, bf16[2,2,160,256]{3,2,1,0:T(8,128)(2,1)S(1)}, u32[]{:S(2)}, u32[]{:S(2)}) collective-permute-start(bf16[2,2,160,256]{3,2,1,0:T(8,128)(2,1)S(1)} %shard_map.59.after_ref.refs_0_), channel_id=1, source_target_pairs={{0,1},{1,2},{2,3},{3,0},{8,9},{9,10},{10,11},{11,8},{16,17},{17,18... | collective-permute-start | bytes 983048 | tf_op jit(solution)/shard_map/ppermute | solution.py:541
  35.2 28.1 %collective-permute-start.12 = (bf16[2,2,160,256]{3,2,1,0:T(8,128)(2,1)S(1)}, bf16[2,2,160,256]{3,2,1,0:T(8,128)(2,1)S(1)}, u32[]{:S(2)}, u32[]{:S(2)}) collective-permute-start(bf16[2,2,160,256]{3,2,1,0:T(8,128)(2,1)S(1)} %shard_map.59.after_ref.refs_0_), channel_id=1, source_target_pairs={{0,2},{1,3},{2,0},{3,1},{8,10},{9,11},{10,8},{11,9},{16,18},{17,19... | collective-permute-start | bytes 983048 | tf_op jit(solution)/shard_map/ppermute | solution.py:541
  36.3 29.2 %collective-permute-start.13 = (bf16[2,2,160,256]{3,2,1,0:T(8,128)(2,1)S(1)}, bf16[2,2,160,256]{3,2,1,0:T(8,128)(2,1)S(1)}, u32[]{:S(2)}, u32[]{:S(2)}) collective-permute-start(bf16[2,2,160,256]{3,2,1,0:T(8,128)(2,1)S(1)} %shard_map.59.after_ref.refs_0_), channel_id=1, source_target_pairs={{0,3},{1,0},{2,1},{3,2},{8,11},{9,8},{10,9},{11,10},{16,19},{17,16... | collective-permute-start | bytes 983048 | tf_op jit(solution)/shard_map/ppermute | solution.py:541
  37.7 2.9 %collective-permute-start.15 = (bf16[128,320]{1,0:T(8,128)(2,1)S(1)}, bf16[128,320]{1,0:T(8,128)(2,1)S(1)}, u32[]{:S(2)}, u32[]{:S(2)}) collective-permute-start(bf16[128,320]{1,0:T(8,128)(2,1)S(1)} %get-tuple-element.84), channel_id=1, source_target_pairs={{24,16},{25,17},{26,18},{27,19},{28,20},{29,21},{30,22},{31,23}} | collective-permute-start | bytes 245768 | tf_op jit(solution)/shard_map/ppermute | solution.py:533
  39.0 3.9 %collective-permute-start.14 = (bf16[128,320]{1,0:T(8,128)(2,1)S(1)}, bf16[128,320]{1,0:T(8,128)(2,1)S(1)}, u32[]{:S(2)}, u32[]{:S(2)}) collective-permute-start(bf16[128,320]{1,0:T(8,128)(2,1)S(1)} %get-tuple-element.83), channel_id=1, source_target_pairs={{24,16},{25,17},{26,18},{27,19},{28,20},{29,21},{30,22},{31,23}} | collective-permute-start | bytes 245768 | tf_op jit(solution)/shard_map/ppermute | solution.py:533
  40.6 3.0 %collective-permute-start.17 = (bf16[128,320]{1,0:T(8,128)(2,1)S(1)}, bf16[128,320]{1,0:T(8,128)(2,1)S(1)}, u32[]{:S(2)}, u32[]{:S(2)}) collective-permute-start(bf16[128,320]{1,0:T(8,128)(2,1)S(1)} %get-tuple-element.89), channel_id=1, source_target_pairs={{16,8},{17,9},{18,10},{19,11},{20,12},{21,13},{22,14},{23,15}} | collective-permute-start | bytes 245768 | tf_op jit(solution)/shard_map/ppermute | solution.py:533
  42.8 0.7 collective-permute-start.16
  65.5 7.0 %collective-permute-start.18 = (bf16[4,2,160,256]{3,2,1,0:T(8,128)(2,1)S(1)}, bf16[4,2,160,256]{3,2,1,0:T(8,128)(2,1)S(1)}, u32[]{:S(2)}, u32[]{:S(2)}) collective-permute-start(bf16[4,2,160,256]{3,2,1,0:T(8,128)(2,1)S(1)} %shard_map.71), channel_id=1, source_target_pairs={{0,4},{4,0},{1,5},{5,1},{2,6},{6,2},{3,7},{7,3},{8,12},{12,8},{9,1... | collective-permute-start | bytes 1966088 | tf_op jit(solution)/shard_map/ppermute | solution.py:519
  66.1 12.9 %collective-permute-start.10 = (bf16[2,2,160,256]{3,2,1,0:T(8,128)(2,1)S(1)}, bf16[2,2,160,256]{3,2,1,0:T(8,128)(2,1)S(1)}, u32[]{:S(2)}, u32[]{:S(2)}) collective-permute-start(bf16[2,2,160,256]{3,2,1,0:T(8,128)(2,1)S(1)} %shard_map.66.refs_0_.refs_1_), channel_id=1, source_target_pairs={{24,25},{25,26},{26,27},{27,24},{28,29},{29,30},{30,31},{31,28}} | collective-permute-start | bytes 983048 | tf_op jit(solution)/shard_map/ppermute | solution.py:541
  68.0 8.0 %collective-permute-start.20 = (bf16[128,320]{1,0:T(8,128)(2,1)S(1)}, bf16[128,320]{1,0:T(8,128)(2,1)S(1)}, u32[]{:S(2)}, u32[]{:S(2)}) collective-permute-start(bf16[128,320]{1,0:T(8,128)(2,1)S(1)} %get-tuple-element.95), channel_id=1, source_target_pairs={{8,0},{9,1},{10,2},{11,3},{12,4},{13,5},{14,6},{15,7}} | collective-permute-start | bytes 245768 | tf_op jit(solution)/shard_map/ppermute | solution.py:533
  68.7 7.3 %collective-permute-start.19 = (bf16[128,320]{1,0:T(8,128)(2,1)S(1)}, bf16[128,320]{1,0:T(8,128)(2,1)S(1)}, u32[]{:S(2)}, u32[]{:S(2)}) collective-permute-start(bf16[128,320]{1,0:T(8,128)(2,1)S(1)} %get-tuple-element.94.refs_4_), channel_id=1, source_target_pairs={{8,0},{9,1},{10,2},{11,3},{12,4},{13,5},{14,6},{15,7}} | collective-permute-start | bytes 245768 | tf_op jit(solution)/shard_map/ppermute | solution.py:533
  69.3 30.5 %collective-permute-start.9 = (bf16[2,2,160,256]{3,2,1,0:T(8,128)(2,1)S(1)}, bf16[2,2,160,256]{3,2,1,0:T(8,128)(2,1)S(1)}, u32[]{:S(2)}, u32[]{:S(2)}) collective-permute-start(bf16[2,2,160,256]{3,2,1,0:T(8,128)(2,1)S(1)} %shard_map.66.refs_0_.refs_1_), channel_id=1, source_target_pairs={{24,26},{25,27},{26,24},{27,25},{28,30},{29,31},{30,28},{31,29}} | collective-permute-start | bytes 983048 | tf_op jit(solution)/shard_map/ppermute | solution.py:541
  72.6 29.5 %collective-permute-start.8 = (bf16[2,2,160,256]{3,2,1,0:T(8,128)(2,1)S(1)}, bf16[2,2,160,256]{3,2,1,0:T(8,128)(2,1)S(1)}, u32[]{:S(2)}, u32[]{:S(2)}) collective-permute-start(bf16[2,2,160,256]{3,2,1,0:T(8,128)(2,1)S(1)} %shard_map.66.refs_0_.refs_1_), channel_id=1, source_target_pairs={{24,27},{25,24},{26,25},{27,26},{28,31},{29,28},{30,29},{31,30}} | collective-permute-start | bytes 983048 | tf_op jit(solution)/shard_map/ppermute | solution.py:541
  76.1 26.6 %collective-permute-start.21 = (bf16[2,80,256]{2,1,0:T(8,128)(2,1)S(1)}, bf16[2,80,256]{2,1,0:T(8,128)(2,1)S(1)}, u32[]{:S(2)}, u32[]{:S(2)}) collective-permute-start(bf16[2,80,256]{2,1,0:T(8,128)(2,1)S(1)} %get-tuple-element.108), channel_id=1, source_target_pairs={{0,1},{1,2},{2,3},{3,0},{8,9},{9,10},{10,11},{11,8},{16,17},{17,18... | collective-permute-start | bytes 245768 | tf_op jit(solution)/shard_map/ppermute | solution.py:541
  76.1 27.2 %collective-permute-start.22 = (bf16[2,80,256]{2,1,0:T(8,128)(2,1)S(1)}, bf16[2,80,256]{2,1,0:T(8,128)(2,1)S(1)}, u32[]{:S(2)}, u32[]{:S(2)}) collective-permute-start(bf16[2,80,256]{2,1,0:T(8,128)(2,1)S(1)} %get-tuple-element.107), channel_id=1, source_target_pairs={{0,2},{1,3},{2,0},{3,1},{8,10},{9,11},{10,8},{11,9},{16,18},{17,19... | collective-permute-start | bytes 245768 | tf_op jit(solution)/shard_map/ppermute | solution.py:541
  79.0 26.6 %collective-permute-start.23 = (bf16[2,80,256]{2,1,0:T(8,128)(2,1)S(1)}, bf16[2,80,256]{2,1,0:T(8,128)(2,1)S(1)}, u32[]{:S(2)}, u32[]{:S(2)}) collective-permute-start(bf16[2,80,256]{2,1,0:T(8,128)(2,1)S(1)} %get-tuple-element.106), channel_id=1, source_target_pairs={{0,3},{1,0},{2,1},{3,2},{8,11},{9,8},{10,9},{11,10},{16,19},{17,16... | collective-permute-start | bytes 245768 | tf_op jit(solution)/shard_map/ppermute | solution.py:541
  105.6 2.7 %collective-permute-start.24 = (bf16[4,2,80,256]{3,2,1,0:T(8,128)(2,1)S(1)}, bf16[4,2,80,256]{3,2,1,0:T(8,128)(2,1)S(1)}, u32[]{:S(2)}, u32[]{:S(2)}) collective-permute-start(bf16[4,2,80,256]{3,2,1,0:T(8,128)(2,1)S(1)} %shard_map.79.own_ref), channel_id=1, source_target_pairs={{0,4},{4,0},{1,5},{5,1},{2,6},{6,2},{3,7},{7,3},{8,12},{12,8},{9,1... | collective-permute-start | bytes 983048 | tf_op jit(solution)/shard_map/ppermute | solution.py:519
  106.2 1.4 %collective-permute-start.25 = (bf16[2,8,8,320]{3,2,1,0:T(8,128)(2,1)S(1)}, bf16[2,8,8,320]{3,2,1,0:T(8,128)(2,1)S(1)}, u32[]{:S(2)}, u32[]{:S(2)}) collective-permute-start(bf16[2,8,8,320]{3,2,1,0:T(8,128)(2,1)S(1)} %get-tuple-element.105), channel_id=1, source_target_pairs={{0,4},{4,0},{1,5},{5,1},{2,6},{6,2},{3,7},{7,3},{8,12},{12,8},{9,1... | collective-permute-start | bytes 245768 | tf_op jit(solution)/shard_map/ppermute | solution.py:519

commit v2 on v1

--- a/solution.py
+++ b/solution.py
@@ -308,18 +308,23 @@
         ]
 
 
-def flip_call(kept, kinds, parts, axis, after):
-    _, crops, count, channels = kept.shape
-
-    def kernel(kept_ref, after_ref, flipped_ref):
-        for place, kind in enumerate(kinds):
-            for crop in range(crops):
-                place_parts(
-                    flipped_ref, (place,), kept_ref[kind, crop], crop, parts, lax.axis_index(axis)
-                )
-
-    shape = (parts, len(kinds), channels // parts, crops * count)
-    (flipped,) = call(kernel, [jax.ShapeDtypeStruct(shape, kept.dtype)], [kept, after], (1,), [], {})
+def flip_call(kept, parts, axis, after):
+    def kernel(*refs):
+        flipped_ref = refs[-1]
+        for crop, (place, index) in enumerate(kept):
+            value = refs[place][index]
+            place_parts(flipped_ref, (), value, crop, parts, lax.axis_index(axis))
+
+    operands = []
+    for array, index in kept:
+        if all(array is not other for other in operands):
+            operands.append(array)
+    kept = [
+        ([array is other for other in operands].index(True), index) for array, index in kept
+    ]
+    count, channels = operands[0].shape[-2:]
+    out = jax.ShapeDtypeStruct((parts, channels // parts, len(kept) * count), operands[0].dtype)
+    (flipped,) = call(kernel, [out], [*operands, after], (len(operands),), [], {})
     return flipped
 
 
@@ -449,8 +454,29 @@
     return stacked
 
 
-def spread_call(sources, slots, blocks, around, is_last, last, count, width):
-    two, share, cells = sources[0].shape[-3:]
+def pick_call(home, received, sections, after):
+    slots = home.shape[0]
+    arrays = [array for section in range(sections) for array in received[section]]
+    each = len(arrays) // sections
+
+    def kernel(home_ref, *refs):
+        for slot in range(slots):
+            refs[-slots + slot][0] = home_ref[slot]
+        for section in range(sections):
+
+            @pl.when(lax.axis_index("section") == section)
+            def _():
+                for block in range(each):
+                    for slot in range(slots):
+                        refs[-slots + slot][1 + block] = refs[section * each + block][slot]
+
+    out = jax.ShapeDtypeStruct((1 + each, *home.shape[1:]), home.dtype)
+    operands = [home, *arrays, after]
+    return call(kernel, [out] * slots, operands, (len(operands) - 1,), [], {})
+
+
+def spread_call(sources, slots, blocks, kind, around, sections, count, width):
+    share, cells = sources[0].shape[-2:]
     crops = cells // count
     stride = count + width
     fresh = isinstance(around, jax.ShapeDtypeStruct)
@@ -458,25 +484,22 @@
 
     def kernel(*refs):
         out_ref, shifted = refs[-2:]
-        mine = (lax.axis_index("section") == last) == is_last
-
-        @pl.when(mine)
+        section = lax.axis_index("section")
+
+        @pl.when((section >= sections[0]) & (section <= sections[1]))
         def _():
             edge = jnp.zeros((width, 3 * share), jnp.bfloat16)
-            for kind in range(two):
-                out_ref[kind, total - width : total, :] = edge
-                for ref, slot, block in zip(refs, slots, blocks):
-                    for crop in range(crops):
-                        cell = slice(crop * count, (crop + 1) * count)
-                        value = ref[(*slot, kind, slice(None), cell)].T.astype(jnp.float32)
-                        before, after = neighbours(value, shifted, width)
-                        at = (block * crops + crop) * stride
-                        out_ref[kind, at : at + width, :] = edge
-                        for place, part in enumerate((before, value, after)):
-                            lanes = slice(place * share, (place + 1) * share)
-                            out_ref[kind, at + width : at + stride, lanes] = part.astype(
-                                jnp.bfloat16
-                            )
+            out_ref[kind, total - width : total, :] = edge
+            for ref, slot, block in zip(refs, slots, blocks):
+                for crop in range(crops):
+                    cell = slice(crop * count, (crop + 1) * count)
+                    value = ref[(*slot, slice(None), cell)].T.astype(jnp.float32)
+                    before, after = neighbours(value, shifted, width)
+                    at = (block * crops + crop) * stride
+                    out_ref[kind, at : at + width, :] = edge
+                    for place, part in enumerate((before, value, after)):
+                        lanes = slice(place * share, (place + 1) * share)
+                        out_ref[kind, at + width : at + stride, lanes] = part.astype(jnp.bfloat16)
 
     operands = [*sources] if fresh else [*sources, around]
     aliases = {} if fresh else {len(sources): 0}
@@ -534,19 +557,26 @@
 
     def shared(values, step, routes):
         pairs = [
-            (source * groups + i, source * groups + (i + step) % groups)
-            for source in routes
+            (source * groups + i, target * groups + (i + step) % groups)
+            for source, target in routes
             for i in range(groups)
         ]
         return lax.ppermute(values, ("section", "img"), pairs)
 
-    everywhere = range(sections)
-    own, other = split_call(strips, cotangent, last)
+    steps = range(1, groups)
+    everywhere = [(place, place) for place in range(sections)]
+    soon, late_from = everywhere[: max(1, sections - 2)], max(1, sections - 2)
+    own, other = split_call(
+        pltpu.with_memory_space_constraint(strips, pltpu.HBM),
+        pltpu.with_memory_space_constraint(cotangent, pltpu.HBM),
+        last,
+    )
     other = rotated(other, "slab", 1)
-    weights = load_call(kernels[0].reshape(2, 3, 3 * channels, channels))
+    weights = kernels[0].reshape(2, 3, 3 * channels, channels)
+    weights = load_call(pltpu.with_memory_space_constraint(weights, pltpu.HBM))
     fields = join_call(own, other)
     incoming = fields
-    state, early = [], []
+    state, handed = [], {}
     turned, after = None, weights
     for place in range(sections):
         outgoing = []
@@ -559,12 +589,15 @@
             turned = turn_call(weights, state[0])
         if place < last:
             incoming = [hop(out, place, place + 1) for out in outgoing]
-        if place == last - 1:
-            flipped = flip_call(state[0], (0, 1), slabs, "slab", state[1])
+        if 0 < place < last:
+            flipped = flip_call([(out, Ellipsis) for out in outgoing], slabs, "slab", state[1])
+            handed[place + 1] = [shared(flipped, step, [(place, place + 1)]) for step in steps]
             after = flipped
-            early = [flipped]
-            for step in range(1, groups):
-                early.append(shared(flipped, step, everywhere))
+        if place == 0:
+            flipped_outgoing = outgoing
+        if place == min(1, last - 1):
+            flipped = flip_call([(field, Ellipsis) for field in fields], slabs, "slab", state[1])
+            handed[0] = [shared(flipped, step, [(0, 0)]) for step in steps]
     saved, hidden = state
     incoming = fields
     grads = []
@@ -579,33 +612,55 @@
             outgoing.append(out)
         if place:
             incoming = [hop(out, place, place - 1) for out in outgoing]
-        if place == last:
-            flipped = flip_call(saved, (0, 1), slabs, "slab", grads[0])
-            pairs = [(last * slabs + i, last * slabs + (i + 1) % slabs) for i in range(slabs)]
-            other = lax.ppermute(flipped[1], ("section", "slab"), pairs)
-            both = stack_call([flipped[0], other], None, grads[0])
+        if place == min(last, 2):
+            active = flip_call([(saved, (1, crop)) for crop in range(crops)], slabs, "slab", grads[0])
+            pairs = [
+                (source * slabs + i, source * slabs + (i + 1) % slabs)
+                for source in range(late_from, sections)
+                for i in range(slabs)
+            ]
+            other = lax.ppermute(active[1], ("section", "slab"), pairs)
+            both = stack_call([active[0], other], None, grads[0])
             late = [both]
-            for step in range(1, groups):
-                late.append(shared(both, step, [last]))
+            for step in steps:
+                late.append(shared(both, step, everywhere[late_from:]))
+            flipped = flip_call([(out, Ellipsis) for out in flipped_outgoing], slabs, "slab", both)
+            handed[1] = [shared(flipped, step, [(0, 1)]) for step in steps]
+            early = [shared(active, step, soon) for step in steps]
         if place == 1:
-            other = stack_call(early, 1, outgoing[-1])
+            mine = flip_call([(saved, (0, crop)) for crop in range(crops)], slabs, "slab", outgoing[-1])
+            inputs = pick_call(mine, handed, sections, outgoing[-1])
+            active = [active, *early]
+            other = stack_call(active, 1, outgoing[-1])
             other = rotated(other, "slab", 1)
+            outer = rotated(inputs[1], "slab", 1)
             stride = count + width
             shape = (2, slabs * groups * crops * stride + width, 3 * (channels // slabs))
+            slots = [(block,) for block in range(groups)]
             around = spread_call(
-                [*early, *([other] * groups)],
-                [(0,)] * groups + [(block,) for block in range(groups)],
+                [inputs[0]] * groups + [outer] * groups,
+                slots + slots,
                 list(range(slabs * groups)),
+                0,
                 jax.ShapeDtypeStruct(shape, jnp.bfloat16),
-                False,
-                last,
+                (0, last),
+                count,
+                width,
+            )
+            around = spread_call(
+                active + [other] * groups,
+                [(0,)] * groups + slots,
+                list(range(slabs * groups)),
+                1,
+                around,
+                (0, late_from - 1),
                 count,
                 width,
             )
             after = around
     kept, sent = grads
     own = [sent[0]]
-    for step in range(1, groups):
+    for step in steps:
         own.append(shared(sent[step], step, everywhere))
     around, sent = lax.optimization_barrier((around, sent))
     for block in range(groups):
@@ -613,9 +668,9 @@
             [late[block]] * slabs,
             [(slab,) for slab in range(slabs)],
             [slab * groups + block for slab in range(slabs)],
+            1,
             around,
-            True,
-            last,
+            (late_from, last),
             count,
             width,
         )

time: 112 us -> 110 us (0.982)
  the two profiles are of different devices: /device:TPU:15 before, /device:TPU:0 now
where the time goes in v2:
time: 110 us; the launch traced here: 109 us
  starting transfers between devices  69.9 us (64%)
  waiting for transfers between devices  20.3 us (18%)
  Pallas kernels  17.4 us (16%)
  between operations  1.33 us (1%)
    ppermute x21, starting transfers between devices, shared(): return lax.ppermute(values, ('section', 'img'), pairs)  55.6 us
    pallas_call x39, Pallas kernels, call(): pl.pallas_call(kernel, out_shape=outs, in_specs=[pl.BlockSpec(memory_spac...  17.4 us
    ppermute x21, waiting for transfers between devices, shared(): return lax.ppermute(values, ('section', 'img'), pairs)  17 us
    ppermute x12, starting transfers between devices, hop(): return lax.ppermute(value, 'section', [(source, target)])  12.3 us
  transfers between devices with their start and end apart: 39, of which 11 were waited for; matrix products, arithmetic and copies ran while one was open for 0% of the time, Pallas kernels for 11%

profile of v2, /device:TPU:0, one launch (start us, length us, event | category | flops | bytes accessed | tf_op | source)
XLA Modules:
  0.0 108.9 jit_solution(898843354680850579)
XLA Ops:
  0.6 1.0 shard_map.50
  1.6 0.6 collective-permute-start
  2.2 2.3 %shard_map.52.weights_ref.after_ref = bf16[2,3,960,320]{3,2,1,0:T(8,128)(2,1)S(1)} custom-call(bf16[2,3,960,320]{3,2,1,0:T(8,128)(2,1)} %bitcast.15), custom_call_target="tpu_custom_call" | custom-call | tf_op jit(solution)/shard_map/pallas_call | solution.py:177
  4.6 1.3 %shard_map.53 = (bf16[128,320]{1,0:T(8,128)(2,1)S(1)}, bf16[2,2,128,320]{3,2,1,0:T(8,128)(2,1)S(1)}, f32[2,128,320]{2,1,0:T(8,128)S(1)}) custom-call(bf16[128,320]{1,0:T(8,128)(2,1)S(1)} %get-tuple-element.59.field_ref.grad_ref.refs_0_, bf16[2,3,960,320]{3,2,1,0:T(8,128)(2,1)S(1)} %shard_map.52.weights_ref.after_ref, ...), custom_call_target="tpu_custom_call" | custom-call | tf_op jit(solution)/shard_map/pallas_call | solution.py:177
  5.9 3.1 %collective-permute-start.2 = (bf16[128,320]{1,0:T(8,128)(2,1)S(1)}, bf16[128,320]{1,0:T(8,128)(2,1)S(1)}, u32[]{:S(2)}, u32[]{:S(2)}) collective-permute-start(bf16[128,320]{1,0:T(8,128)(2,1)S(1)} %get-tuple-element.63.refs_0_), channel_id=1, source_target_pairs={{0,8},{1,9},{2,10},{3,11},{4,12},{5,13},{6,14},{7,15}} | collective-permute-start | bytes 245768 | tf_op jit(solution)/shard_map/ppermute | solution.py:556
  9.0 1.3 %shard_map.54 = (bf16[128,320]{1,0:T(8,128)(2,1)S(1)}, bf16[2,2,128,320]{3,2,1,0:T(8,128)(2,1)S(1)}, f32[2,128,320]{2,1,0:T(8,128)S(1)}) custom-call(bf16[128,320]{1,0:T(8,128)(2,1)S(1)} %get-tuple-element.58.field_ref.grad_ref.refs_1_, bf16[2,3,960,320]{3,2,1,0:T(8,128)(2,1)S(1)} %shard_map.52.weights_ref.after_ref, ...), custom_call_target="tpu_custom_call", output_to_operand_aliasing={{1}: (3, {}), {2}: (4, {})} | custom-call | tf_op jit(solution)/shard_map/pallas_call | solution.py:177
  10.3 1.3 %collective-permute-start.1 = (bf16[128,320]{1,0:T(8,128)(2,1)S(1)}, bf16[128,320]{1,0:T(8,128)(2,1)S(1)}, u32[]{:S(2)}, u32[]{:S(2)}) collective-permute-start(bf16[128,320]{1,0:T(8,128)(2,1)S(1)} %get-tuple-element.62.refs_1_), channel_id=1, source_target_pairs={{0,8},{1,9},{2,10},{3,11},{4,12},{5,13},{6,14},{7,15}} | collective-permute-start | bytes 245768 | tf_op jit(solution)/shard_map/ppermute | solution.py:556
  11.6 1.4 %shard_map.63.turned_ref = bf16[2,3,960,320]{3,2,1,0:T(8,128)(2,1)S(1)} custom-call(bf16[2,3,960,320]{3,2,1,0:T(8,128)(2,1)S(1)} %shard_map.52.weights_ref.after_ref, bf16[2,2,128,320]{3,2,1,0:T(8,128)(2,1)S(1)} %get-tuple-element.64.refs_0_.after_ref), custom_call_target="tpu_custom_call" | custom-call | tf_op jit(solution)/shard_map/pallas_call | solution.py:177
  13.0 0.7 collective-permute-start.4
  13.7 0.6 collective-permute-done.1.field_ref
  14.3 0.7 collective-permute-start.3
  15.0 0.1 shard_map.74
  15.1 0.1 shard_map.57.after_ref
  15.2 0.7 collective-permute-start.6
  15.9 0.7 collective-permute-start.5
  16.6 0.1 shard_map.60.after_ref
  16.8 0.7 collective-permute-start.8
  17.5 0.2 shard_map.65
  17.7 0.7 collective-permute-start.7
  18.3 3.5 %collective-permute-start.19 = (bf16[2,160,256]{2,1,0:T(8,128)(2,1)S(1)}, bf16[2,160,256]{2,1,0:T(8,128)(2,1)S(1)}, u32[]{:S(2)}, u32[]{:S(2)}) collective-permute-start(bf16[2,160,256]{2,1,0:T(8,128)(2,1)S(1)} %shard_map.74), channel_id=1, source_target_pairs={{0,1},{1,2},{2,3},{3,0},{4,5},{5,6},{6,7},{7,4}} | collective-permute-start | bytes 491528 | tf_op jit(solution)/shard_map/ppermute | solution.py:564
  21.8 4.5 %collective-permute-start.20 = (bf16[2,160,256]{2,1,0:T(8,128)(2,1)S(1)}, bf16[2,160,256]{2,1,0:T(8,128)(2,1)S(1)}, u32[]{:S(2)}, u32[]{:S(2)}) collective-permute-start(bf16[2,160,256]{2,1,0:T(8,128)(2,1)S(1)} %shard_map.74), channel_id=1, source_target_pairs={{0,2},{1,3},{2,0},{3,1},{4,6},{5,7},{6,4},{7,5}} | collective-permute-start | bytes 491528 | tf_op jit(solution)/shard_map/ppermute | solution.py:564
  26.3 3.3 %collective-permute-start.21 = (bf16[2,160,256]{2,1,0:T(8,128)(2,1)S(1)}, bf16[2,160,256]{2,1,0:T(8,128)(2,1)S(1)}, u32[]{:S(2)}, u32[]{:S(2)}) collective-permute-start(bf16[2,160,256]{2,1,0:T(8,128)(2,1)S(1)} %shard_map.74), channel_id=1, source_target_pairs={{0,3},{1,0},{2,1},{3,2},{4,7},{5,4},{6,5},{7,6}} | collective-permute-start | bytes 491528 | tf_op jit(solution)/shard_map/ppermute | solution.py:564
  29.6 0.7 collective-permute-start.25
  30.3 0.7 collective-permute-start.26
  31.0 0.1 shard_map.68.refs_0_
  31.2 0.7 collective-permute-start.27
  31.9 3.1 %collective-permute-done.20.refs_1_ = bf16[2,160,256]{2,1,0:T(8,128)(2,1)S(1)} collective-permute-done((bf16[2,160,256]{2,1,0:T(8,128)(2,1)S(1)}, bf16[2,160,256]{2,1,0:T(8,128)(2,1)S(1)}, u32[]{:S(2)}, u32[]{:S(2)}) %collective-permute-start.20) | collective-permute-done | bytes 163872 | tf_op jit(solution)/shard_map/ppermute | solution.py:564
  35.0 0.7 collective-permute-start.9
  35.6 1.2 %collective-permute-done.21.refs_2_ = bf16[2,160,256]{2,1,0:T(8,128)(2,1)S(1)} collective-permute-done((bf16[2,160,256]{2,1,0:T(8,128)(2,1)S(1)}, bf16[2,160,256]{2,1,0:T(8,128)(2,1)S(1)}, u32[]{:S(2)}, u32[]{:S(2)}) %collective-permute-start.21) | collective-permute-done | bytes 163872 | tf_op jit(solution)/shard_map/ppermute | solution.py:564
  36.8 0.7 collective-permute-start.28
  37.5 0.7 collective-permute-start.29
  38.2 0.7 collective-permute-start.30
  39.0 18.7 %collective-permute-start.22 = (bf16[2,160,256]{2,1,0:T(8,128)(2,1)S(1)}, bf16[2,160,256]{2,1,0:T(8,128)(2,1)S(1)}, u32[]{:S(2)}, u32[]{:S(2)}) collective-permute-start(bf16[2,160,256]{2,1,0:T(8,128)(2,1)S(1)} %shard_map.75), channel_id=1, source_target_pairs={{0,9},{1,10},{2,11},{3,8},{4,13},{5,14},{6,15},{7,12}} | collective-permute-start | bytes 491528 | tf_op jit(solution)/shard_map/ppermute | solution.py:564
  57.7 0.7 collective-permute-start.17
  58.4 0.7 collective-permute-start.16
  59.1 1.3 %collective-permute-start.23 = (bf16[2,160,256]{2,1,0:T(8,128)(2,1)S(1)}, bf16[2,160,256]{2,1,0:T(8,128)(2,1)S(1)}, u32[]{:S(2)}, u32[]{:S(2)}) collective-permute-start(bf16[2,160,256]{2,1,0:T(8,128)(2,1)S(1)} %shard_map.75), channel_id=1, source_target_pairs={{0,10},{1,11},{2,8},{3,9},{4,14},{5,15},{6,12},{7,13}} | collective-permute-start | bytes 491528 | tf_op jit(solution)/shard_map/ppermute | solution.py:564
  60.4 1.3 %collective-permute-start.24 = (bf16[2,160,256]{2,1,0:T(8,128)(2,1)S(1)}, bf16[2,160,256]{2,1,0:T(8,128)(2,1)S(1)}, u32[]{:S(2)}, u32[]{:S(2)}) collective-permute-start(bf16[2,160,256]{2,1,0:T(8,128)(2,1)S(1)} %shard_map.75), channel_id=1, source_target_pairs={{0,11},{1,8},{2,9},{3,10},{4,15},{5,12},{6,13},{7,14}} | collective-permute-start | bytes 491528 | tf_op jit(solution)/shard_map/ppermute | solution.py:564
  61.7 1.9 %collective-permute-start.13 = (bf16[2,160,256]{2,1,0:T(8,128)(2,1)S(1)}, bf16[2,160,256]{2,1,0:T(8,128)(2,1)S(1)}, u32[]{:S(2)}, u32[]{:S(2)}) collective-permute-start(bf16[2,160,256]{2,1,0:T(8,128)(2,1)S(1)} %shard_map.68.refs_0_), channel_id=1, source_target_pairs={{0,1},{1,2},{2,3},{3,0},{8,9},{9,10},{10,11},{11,8},{4,5},{5,6},{6... | collective-permute-start | bytes 491528 | tf_op jit(solution)/shard_map/ppermute | solution.py:564
  63.6 6.1 %collective-permute-start.14 = (bf16[2,160,256]{2,1,0:T(8,128)(2,1)S(1)}, bf16[2,160,256]{2,1,0:T(8,128)(2,1)S(1)}, u32[]{:S(2)}, u32[]{:S(2)}) collective-permute-start(bf16[2,160,256]{2,1,0:T(8,128)(2,1)S(1)} %shard_map.68.refs_0_), channel_id=1, source_target_pairs={{0,2},{1,3},{2,0},{3,1},{8,10},{9,11},{10,8},{11,9},{4,6},{5,7},{6... | collective-permute-start | bytes 491528 | tf_op jit(solution)/shard_map/ppermute | solution.py:564
  69.7 3.4 %collective-permute-start.15 = (bf16[2,160,256]{2,1,0:T(8,128)(2,1)S(1)}, bf16[2,160,256]{2,1,0:T(8,128)(2,1)S(1)}, u32[]{:S(2)}, u32[]{:S(2)}) collective-permute-start(bf16[2,160,256]{2,1,0:T(8,128)(2,1)S(1)} %shard_map.68.refs_0_), channel_id=1, source_target_pairs={{0,3},{1,0},{2,1},{3,2},{8,11},{9,8},{10,9},{11,10},{4,7},{5,4},{6... | collective-permute-start | bytes 491528 | tf_op jit(solution)/shard_map/ppermute | solution.py:564
  73.1 0.1 shard_map.73.home_ref
  73.4 2.6 %collective-permute-done.13.refs_1_ = bf16[2,160,256]{2,1,0:T(8,128)(2,1)S(1)} collective-permute-done((bf16[2,160,256]{2,1,0:T(8,128)(2,1)S(1)}, bf16[2,160,256]{2,1,0:T(8,128)(2,1)S(1)}, u32[]{:S(2)}, u32[]{:S(2)}) %collective-permute-start.13) | collective-permute-done | bytes 163872 | tf_op jit(solution)/shard_map/ppermute | solution.py:564
  76.0 5.5 %collective-permute-done.14.refs_2_ = bf16[2,160,256]{2,1,0:T(8,128)(2,1)S(1)} collective-permute-done((bf16[2,160,256]{2,1,0:T(8,128)(2,1)S(1)}, bf16[2,160,256]{2,1,0:T(8,128)(2,1)S(1)}, u32[]{:S(2)}, u32[]{:S(2)}) %collective-permute-start.14) | collective-permute-done | bytes 163872 | tf_op jit(solution)/shard_map/ppermute | solution.py:564
  81.6 1.3 %collective-permute-start.33 = (bf16[128,320]{1,0:T(8,128)(2,1)S(1)}, bf16[128,320]{1,0:T(8,128)(2,1)S(1)}, u32[]{:S(2)}, u32[]{:S(2)}) collective-permute-start(bf16[128,320]{1,0:T(8,128)(2,1)S(1)} %get-tuple-element.99), channel_id=1, source_target_pairs={{8,0},{9,1},{10,2},{11,3},{12,4},{13,5},{14,6},{15,7}} | collective-permute-start | bytes 245768 | tf_op jit(solution)/shard_map/ppermute | solution.py:556
  82.9 1.3 %collective-permute-start.32 = (bf16[128,320]{1,0:T(8,128)(2,1)S(1)}, bf16[128,320]{1,0:T(8,128)(2,1)S(1)}, u32[]{:S(2)}, u32[]{:S(2)}) collective-permute-start(bf16[128,320]{1,0:T(8,128)(2,1)S(1)} %get-tuple-element.96.refs_4_.refs_1_.refs_12_), channel_id=1, source_target_pairs={{8,0},{9,1},{10,2},{11,3},{12,4},{13,5},{14,6},{15,7}} | collective-permute-start | bytes 245768 | tf_op jit(solution)/shard_map/ppermute | solution.py:556
  84.2 0.7 collective-permute-start.12
  84.9 0.7 collective-permute-start.11
  85.6 1.1 %shard_map.77.refs_8_ = bf16[2,2320,480]{2,1,0:T(8,128)(2,1)S(1)} custom-call(bf16[4,160,256]{2,1,0:T(8,128)(2,1)S(1)} %get-tuple-element.97.refs_0_.refs_1_.refs_2_.refs_3_, bf16[4,160,256]{2,1,0:T(8,128)(2,1)S(1)} %get-tuple-element.97.refs_0_.refs_1_.refs_2_.refs_3_, bf16[4,160,256]{2,1,0:T(8,128)(2,1)S(1)} %get-tuple-element.97.refs_0_.refs_1_.refs_2_.refs_3_, ...), custom_call_target="tpu_custom_call" | custom-call | tf_op jit(solution)/shard_map/pallas_call | solution.py:177
  86.7 0.7 collective-permute-start.10
  87.4 1.1 %shard_map.78.after_ref.refs_2_ = bf16[2,2320,480]{2,1,0:T(8,128)(2,1)S(1)} custom-call(bf16[2,160,256]{2,1,0:T(8,128)(2,1)S(1)} %shard_map.68.refs_0_, bf16[2,160,256]{2,1,0:T(8,128)(2,1)S(1)} %collective-permute-done.13.refs_1_, bf16[2,160,256]{2,1,0:T(8,128)(2,1)S(1)} %collective-permute-done.14.refs_2_, ...), custom_call_target="tpu_custom_call", output_to_operand_aliasing={{}: (8, {})} | custom-call | tf_op jit(solution)/shard_map/pallas_call | solution.py:177
  88.5 0.8 collective-permute-done.33.grad_ref
  89.3 1.2 %shard_map.79 = (bf16[2,128,320]{2,1,0:T(8,128)(2,1)S(1)}, bf16[4,2,80,256]{3,2,1,0:T(8,128)(2,1)S(1)}) custom-call(bf16[128,320]{1,0:T(8,128)(2,1)S(1)} %collective-permute-done.33.grad_ref, bf16[2,3,960,320]{3,2,1,0:T(8,128)(2,1)S(1)} %shard_map.63.turned_ref, ...), custom_call_target="tpu_custom_call", output_to_operand_aliasing={{0}: (4, {}), {1}: (5, {})} | custom-call | tf_op jit(solution)/shard_map/pallas_call | solution.py:177
  90.5 0.7 collective-permute-done.32.grad_ref
  91.2 1.2 %shard_map.80 = (bf16[2,128,320]{2,1,0:T(8,128)(2,1)S(1)}, bf16[4,2,80,256]{3,2,1,0:T(8,128)(2,1)S(1)}) custom-call(bf16[128,320]{1,0:T(8,128)(2,1)S(1)} %collective-permute-done.32.grad_ref, bf16[2,3,960,320]{3,2,1,0:T(8,128)(2,1)S(1)} %shard_map.63.turned_ref, ...), custom_call_target="tpu_custom_call", output_to_operand_aliasing={{0}: (4, {}), {1}: (5, {})} | custom-call | tf_op jit(solution)/shard_map/pallas_call | solution.py:177
  92.5 3.2 %collective-permute-start.34 = (bf16[2,80,256]{2,1,0:T(8,128)(2,1)S(1)}, bf16[2,80,256]{2,1,0:T(8,128)(2,1)S(1)}, u32[]{:S(2)}, u32[]{:S(2)}) collective-permute-start(bf16[2,80,256]{2,1,0:T(8,128)(2,1)S(1)} %get-tuple-element.112), channel_id=1, source_target_pairs={{0,1},{1,2},{2,3},{3,0},{8,9},{9,10},{10,11},{11,8},{16,17},{17,18... | collective-permute-start | bytes 245768 | tf_op jit(solution)/shard_map/ppermute | solution.py:564
  95.7 1.3 %collective-permute-start.35 = (bf16[2,80,256]{2,1,0:T(8,128)(2,1)S(1)}, bf16[2,80,256]{2,1,0:T(8,128)(2,1)S(1)}, u32[]{:S(2)}, u32[]{:S(2)}) collective-permute-start(bf16[2,80,256]{2,1,0:T(8,128)(2,1)S(1)} %get-tuple-element.111), channel_id=1, source_target_pairs={{0,2},{1,3},{2,0},{3,1},{8,10},{9,11},{10,8},{11,9},{16,18},{17,19... | collective-permute-start | bytes 245768 | tf_op jit(solution)/shard_map/ppermute | solution.py:564
  97.0 1.1 %collective-permute-start.36 = (bf16[2,80,256]{2,1,0:T(8,128)(2,1)S(1)}, bf16[2,80,256]{2,1,0:T(8,128)(2,1)S(1)}, u32[]{:S(2)}, u32[]{:S(2)}) collective-permute-start(bf16[2,80,256]{2,1,0:T(8,128)(2,1)S(1)} %get-tuple-element.110), channel_id=1, source_target_pairs={{0,3},{1,0},{2,1},{3,2},{8,11},{9,8},{10,9},{11,10},{16,19},{17,16... | collective-permute-start | bytes 245768 | tf_op jit(solution)/shard_map/ppermute | solution.py:564
  98.2 1.2 %collective-permute-done.34.refs_1_ = bf16[2,80,256]{2,1,0:T(8,128)(2,1)S(1)} collective-permute-done((bf16[2,80,256]{2,1,0:T(8,128)(2,1)S(1)}, bf16[2,80,256]{2,1,0:T(8,128)(2,1)S(1)}, u32[]{:S(2)}, u32[]{:S(2)}) %collective-permute-start.34) | collective-permute-done | bytes 81952 | tf_op jit(solution)/shard_map/ppermute | solution.py:564
  99.4 3.2 %collective-permute-done.35.refs_2_ = bf16[2,80,256]{2,1,0:T(8,128)(2,1)S(1)} collective-permute-done((bf16[2,80,256]{2,1,0:T(8,128)(2,1)S(1)}, bf16[2,80,256]{2,1,0:T(8,128)(2,1)S(1)}, u32[]{:S(2)}, u32[]{:S(2)}) %collective-permute-start.35) | collective-permute-done | bytes 81952 | tf_op jit(solution)/shard_map/ppermute | solution.py:564
  102.5 0.3 collective-permute-done.36.refs_3_
  103.0 0.6 collective-permute-start.38
  103.6 1.1 %collective-permute-done.38.other_ref = bf16[2,8,8,320]{3,2,1,0:T(8,128)(2,1)S(1)} collective-permute-done((bf16[2,8,8,320]{3,2,1,0:T(8,128)(2,1)S(1)}, bf16[2,8,8,320]{3,2,1,0:T(8,128)(2,1)S(1)}, u32[]{:S(2)}, u32[]{:S(2)}) %collective-permute-start.38) | collective-permute-done | bytes 81952 | tf_op jit(solution)/shard_map/ppermute | solution.py:542
  104.7 0.7 shard_map.88
  105.4 3.5 %shard_map.86 = f32[2,9,160,80]{3,2,1,0:T(8,128)} custom-call(bf16[2,2320,480]{2,1,0:T(8,128)(2,1)S(1)} %shard_map.84.refs_4_.around_ref, bf16[4,2,80,256]{3,2,1,0:T(8,128)(2,1)S(1)} %shard_map.85.own_ref, bf16[4,2,80,256]{3,2,1,0:T(8,128)(2,1)S(1)} %collective-permute-done.37.other_ref), custom_call_target="tpu_custom_call" | custom-call | tf_op jit(solution)/shard_map/pallas_call | solution.py:177
  (55 shorter events, 0.9 us)
Async XLA Ops:
  1.6 2.9 %collective-permute-start = (bf16[2,8,8,320]{3,2,1,0:T(8,128)(2,1)S(1)}, bf16[2,8,8,320]{3,2,1,0:T(8,128)(2,1)S(1)}, u32[]{:S(2)}, u32[]{:S(2)}) collective-permute-start(bf16[2,8,8,320]{3,2,1,0:T(8,128)(2,1)S(1)} %get-tuple-element.57), channel_id=1, source_target_pairs={{0,4},{4,0},{1,5},{5,1},{2,6},{6,2},{3,7},{7,3},{8,12},{12,8},{9,1... | collective-permute-start | bytes 245768 | tf_op jit(solution)/shard_map/ppermute | solution.py:542
  5.9 7.1 %collective-permute-start.2 = (bf16[128,320]{1,0:T(8,128)(2,1)S(1)}, bf16[128,320]{1,0:T(8,128)(2,1)S(1)}, u32[]{:S(2)}, u32[]{:S(2)}) collective-permute-start(bf16[128,320]{1,0:T(8,128)(2,1)S(1)} %get-tuple-element.63.refs_0_), channel_id=1, source_target_pairs={{0,8},{1,9},{2,10},{3,11},{4,12},{5,13},{6,14},{7,15}} | collective-permute-start | bytes 245768 | tf_op jit(solution)/shard_map/ppermute | solution.py:556
  10.3 4.0 %collective-permute-start.1 = (bf16[128,320]{1,0:T(8,128)(2,1)S(1)}, bf16[128,320]{1,0:T(8,128)(2,1)S(1)}, u32[]{:S(2)}, u32[]{:S(2)}) collective-permute-start(bf16[128,320]{1,0:T(8,128)(2,1)S(1)} %get-tuple-element.62.refs_1_), channel_id=1, source_target_pairs={{0,8},{1,9},{2,10},{3,11},{4,12},{5,13},{6,14},{7,15}} | collective-permute-start | bytes 245768 | tf_op jit(solution)/shard_map/ppermute | solution.py:556
  13.0 2.2 %collective-permute-start.4 = (bf16[128,320]{1,0:T(8,128)(2,1)S(1)}, bf16[128,320]{1,0:T(8,128)(2,1)S(1)}, u32[]{:S(2)}, u32[]{:S(2)}) collective-permute-start(bf16[128,320]{1,0:T(8,128)(2,1)S(1)} %get-tuple-element.69.refs_0_), channel_id=1, source_target_pairs={{8,16},{9,17},{10,18},{11,19},{12,20},{13,21},{14,22},{15,23}} | collective-permute-start | bytes 245768 | tf_op jit(solution)/shard_map/ppermute | solution.py:556
  14.3 1.6 %collective-permute-start.3 = (bf16[128,320]{1,0:T(8,128)(2,1)S(1)}, bf16[128,320]{1,0:T(8,128)(2,1)S(1)}, u32[]{:S(2)}, u32[]{:S(2)}) collective-permute-start(bf16[128,320]{1,0:T(8,128)(2,1)S(1)} %get-tuple-element.68.refs_1_), channel_id=1, source_target_pairs={{8,16},{9,17},{10,18},{11,19},{12,20},{13,21},{14,22},{15,23}} | collective-permute-start | bytes 245768 | tf_op jit(solution)/shard_map/ppermute | solution.py:556
  15.2 1.5 %collective-permute-start.6 = (bf16[128,320]{1,0:T(8,128)(2,1)S(1)}, bf16[128,320]{1,0:T(8,128)(2,1)S(1)}, u32[]{:S(2)}, u32[]{:S(2)}) collective-permute-start(bf16[128,320]{1,0:T(8,128)(2,1)S(1)} %get-tuple-element.75.refs_0_), channel_id=1, source_target_pairs={{16,24},{17,25},{18,26},{19,27},{20,28},{21,29},{22,30},{23,31}} | collective-permute-start | bytes 245768 | tf_op jit(solution)/shard_map/ppermute | solution.py:556
  15.9 0.8 collective-permute-start.5
  16.8 12.8 %collective-permute-start.8 = (bf16[128,320]{1,0:T(8,128)(2,1)S(1)}, bf16[128,320]{1,0:T(8,128)(2,1)S(1)}, u32[]{:S(2)}, u32[]{:S(2)}) collective-permute-start(bf16[128,320]{1,0:T(8,128)(2,1)S(1)} %get-tuple-element.85), channel_id=1, source_target_pairs={{24,16},{25,17},{26,18},{27,19},{28,20},{29,21},{30,22},{31,23}} | collective-permute-start | bytes 245768 | tf_op jit(solution)/shard_map/ppermute | solution.py:556
  17.7 12.6 %collective-permute-start.7 = (bf16[128,320]{1,0:T(8,128)(2,1)S(1)}, bf16[128,320]{1,0:T(8,128)(2,1)S(1)}, u32[]{:S(2)}, u32[]{:S(2)}) collective-permute-start(bf16[128,320]{1,0:T(8,128)(2,1)S(1)} %get-tuple-element.84), channel_id=1, source_target_pairs={{24,16},{25,17},{26,18},{27,19},{28,20},{29,21},{30,22},{31,23}} | collective-permute-start | bytes 245768 | tf_op jit(solution)/shard_map/ppermute | solution.py:556
  18.3 12.8 %collective-permute-start.19 = (bf16[2,160,256]{2,1,0:T(8,128)(2,1)S(1)}, bf16[2,160,256]{2,1,0:T(8,128)(2,1)S(1)}, u32[]{:S(2)}, u32[]{:S(2)}) collective-permute-start(bf16[2,160,256]{2,1,0:T(8,128)(2,1)S(1)} %shard_map.74), channel_id=1, source_target_pairs={{0,1},{1,2},{2,3},{3,0},{4,5},{5,6},{6,7},{7,4}} | collective-permute-start | bytes 491528 | tf_op jit(solution)/shard_map/ppermute | solution.py:564
  21.8 13.1 %collective-permute-start.20 = (bf16[2,160,256]{2,1,0:T(8,128)(2,1)S(1)}, bf16[2,160,256]{2,1,0:T(8,128)(2,1)S(1)}, u32[]{:S(2)}, u32[]{:S(2)}) collective-permute-start(bf16[2,160,256]{2,1,0:T(8,128)(2,1)S(1)} %shard_map.74), channel_id=1, source_target_pairs={{0,2},{1,3},{2,0},{3,1},{4,6},{5,7},{6,4},{7,5}} | collective-permute-start | bytes 491528 | tf_op jit(solution)/shard_map/ppermute | solution.py:564
  26.3 10.5 %collective-permute-start.21 = (bf16[2,160,256]{2,1,0:T(8,128)(2,1)S(1)}, bf16[2,160,256]{2,1,0:T(8,128)(2,1)S(1)}, u32[]{:S(2)}, u32[]{:S(2)}) collective-permute-start(bf16[2,160,256]{2,1,0:T(8,128)(2,1)S(1)} %shard_map.74), channel_id=1, source_target_pairs={{0,3},{1,0},{2,1},{3,2},{4,7},{5,4},{6,5},{7,6}} | collective-permute-start | bytes 491528 | tf_op jit(solution)/shard_map/ppermute | solution.py:564
  29.6 7.9 %collective-permute-start.25 = (bf16[2,160,256]{2,1,0:T(8,128)(2,1)S(1)}, bf16[2,160,256]{2,1,0:T(8,128)(2,1)S(1)}, u32[]{:S(2)}, u32[]{:S(2)}) collective-permute-start(bf16[2,160,256]{2,1,0:T(8,128)(2,1)S(1)} %shard_map.57.after_ref), channel_id=1, source_target_pairs={{8,17},{9,18},{10,19},{11,16},{12,21},{13,22},{14,23},{15,20}} | collective-permute-start | bytes 491528 | tf_op jit(solution)/shard_map/ppermute | solution.py:564
  30.3 8.6 %collective-permute-start.26 = (bf16[2,160,256]{2,1,0:T(8,128)(2,1)S(1)}, bf16[2,160,256]{2,1,0:T(8,128)(2,1)S(1)}, u32[]{:S(2)}, u32[]{:S(2)}) collective-permute-start(bf16[2,160,256]{2,1,0:T(8,128)(2,1)S(1)} %shard_map.57.after_ref), channel_id=1, source_target_pairs={{8,18},{9,19},{10,16},{11,17},{12,22},{13,23},{14,20},{15,21}} | collective-permute-start | bytes 491528 | tf_op jit(solution)/shard_map/ppermute | solution.py:564
  31.2 26.5 %collective-permute-start.27 = (bf16[2,160,256]{2,1,0:T(8,128)(2,1)S(1)}, bf16[2,160,256]{2,1,0:T(8,128)(2,1)S(1)}, u32[]{:S(2)}, u32[]{:S(2)}) collective-permute-start(bf16[2,160,256]{2,1,0:T(8,128)(2,1)S(1)} %shard_map.57.after_ref), channel_id=1, source_target_pairs={{8,19},{9,16},{10,17},{11,18},{12,23},{13,20},{14,21},{15,22}} | collective-permute-start | bytes 491528 | tf_op jit(solution)/shard_map/ppermute | solution.py:564
  35.0 3.2 %collective-permute-start.9 = (bf16[160,256]{1,0:T(8,128)(2,1)S(1)}, bf16[160,256]{1,0:T(8,128)(2,1)S(1)}, u32[]{:S(2)}, u32[]{:S(2)}) collective-permute-start(bf16[160,256]{1,0:T(8,128)(2,1)S(1)} %get-tuple-element.114), channel_id=1, source_target_pairs={{16,20},{20,16},{24,28},{28,24},{17,21},{21,17},{25,29},{29,25},{1... | collective-permute-start | bytes 245768 | tf_op jit(solution)/shard_map/ppermute | solution.py:622
  36.8 21.6 %collective-permute-start.28 = (bf16[2,160,256]{2,1,0:T(8,128)(2,1)S(1)}, bf16[2,160,256]{2,1,0:T(8,128)(2,1)S(1)}, u32[]{:S(2)}, u32[]{:S(2)}) collective-permute-start(bf16[2,160,256]{2,1,0:T(8,128)(2,1)S(1)} %shard_map.60.after_ref), channel_id=1, source_target_pairs={{16,25},{17,26},{18,27},{19,24},{20,29},{21,30},{22,31},{23,28}} | collective-permute-start | bytes 491528 | tf_op jit(solution)/shard_map/ppermute | solution.py:564
  37.5 21.6 %collective-permute-start.29 = (bf16[2,160,256]{2,1,0:T(8,128)(2,1)S(1)}, bf16[2,160,256]{2,1,0:T(8,128)(2,1)S(1)}, u32[]{:S(2)}, u32[]{:S(2)}) collective-permute-start(bf16[2,160,256]{2,1,0:T(8,128)(2,1)S(1)} %shard_map.60.after_ref), channel_id=1, source_target_pairs={{16,26},{17,27},{18,24},{19,25},{20,30},{21,31},{22,28},{23,29}} | collective-permute-start | bytes 491528 | tf_op jit(solution)/shard_map/ppermute | solution.py:564
  38.2 22.2 %collective-permute-start.30 = (bf16[2,160,256]{2,1,0:T(8,128)(2,1)S(1)}, bf16[2,160,256]{2,1,0:T(8,128)(2,1)S(1)}, u32[]{:S(2)}, u32[]{:S(2)}) collective-permute-start(bf16[2,160,256]{2,1,0:T(8,128)(2,1)S(1)} %shard_map.60.after_ref), channel_id=1, source_target_pairs={{16,27},{17,24},{18,25},{19,26},{20,31},{21,28},{22,29},{23,30}} | collective-permute-start | bytes 491528 | tf_op jit(solution)/shard_map/ppermute | solution.py:564
  39.0 30.7 %collective-permute-start.22 = (bf16[2,160,256]{2,1,0:T(8,128)(2,1)S(1)}, bf16[2,160,256]{2,1,0:T(8,128)(2,1)S(1)}, u32[]{:S(2)}, u32[]{:S(2)}) collective-permute-start(bf16[2,160,256]{2,1,0:T(8,128)(2,1)S(1)} %shard_map.75), channel_id=1, source_target_pairs={{0,9},{1,10},{2,11},{3,8},{4,13},{5,14},{6,15},{7,12}} | collective-permute-start | bytes 491528 | tf_op jit(solution)/shard_map/ppermute | solution.py:564
  57.7 4.0 %collective-permute-start.17 = (bf16[128,320]{1,0:T(8,128)(2,1)S(1)}, bf16[128,320]{1,0:T(8,128)(2,1)S(1)}, u32[]{:S(2)}, u32[]{:S(2)}) collective-permute-start(bf16[128,320]{1,0:T(8,128)(2,1)S(1)} %get-tuple-element.92), channel_id=1, source_target_pairs={{16,8},{17,9},{18,10},{19,11},{20,12},{21,13},{22,14},{23,15}} | collective-permute-start | bytes 245768 | tf_op jit(solution)/shard_map/ppermute | solution.py:556
  58.4 5.3 %collective-permute-start.16 = (bf16[128,320]{1,0:T(8,128)(2,1)S(1)}, bf16[128,320]{1,0:T(8,128)(2,1)S(1)}, u32[]{:S(2)}, u32[]{:S(2)}) collective-permute-start(bf16[128,320]{1,0:T(8,128)(2,1)S(1)} %get-tuple-element.91), channel_id=1, source_target_pairs={{16,8},{17,9},{18,10},{19,11},{20,12},{21,13},{22,14},{23,15}} | collective-permute-start | bytes 245768 | tf_op jit(solution)/shard_map/ppermute | solution.py:556
  59.1 14.2 %collective-permute-start.23 = (bf16[2,160,256]{2,1,0:T(8,128)(2,1)S(1)}, bf16[2,160,256]{2,1,0:T(8,128)(2,1)S(1)}, u32[]{:S(2)}, u32[]{:S(2)}) collective-permute-start(bf16[2,160,256]{2,1,0:T(8,128)(2,1)S(1)} %shard_map.75), channel_id=1, source_target_pairs={{0,10},{1,11},{2,8},{3,9},{4,14},{5,15},{6,12},{7,13}} | collective-permute-start | bytes 491528 | tf_op jit(solution)/shard_map/ppermute | solution.py:564
  60.4 12.9 %collective-permute-start.24 = (bf16[2,160,256]{2,1,0:T(8,128)(2,1)S(1)}, bf16[2,160,256]{2,1,0:T(8,128)(2,1)S(1)}, u32[]{:S(2)}, u32[]{:S(2)}) collective-permute-start(bf16[2,160,256]{2,1,0:T(8,128)(2,1)S(1)} %shard_map.75), channel_id=1, source_target_pairs={{0,11},{1,8},{2,9},{3,10},{4,15},{5,12},{6,13},{7,14}} | collective-permute-start | bytes 491528 | tf_op jit(solution)/shard_map/ppermute | solution.py:564
  61.7 14.3 %collective-permute-start.13 = (bf16[2,160,256]{2,1,0:T(8,128)(2,1)S(1)}, bf16[2,160,256]{2,1,0:T(8,128)(2,1)S(1)}, u32[]{:S(2)}, u32[]{:S(2)}) collective-permute-start(bf16[2,160,256]{2,1,0:T(8,128)(2,1)S(1)} %shard_map.68.refs_0_), channel_id=1, source_target_pairs={{0,1},{1,2},{2,3},{3,0},{8,9},{9,10},{10,11},{11,8},{4,5},{5,6},{6... | collective-permute-start | bytes 491528 | tf_op jit(solution)/shard_map/ppermute | solution.py:564
  63.6 17.8 %collective-permute-start.14 = (bf16[2,160,256]{2,1,0:T(8,128)(2,1)S(1)}, bf16[2,160,256]{2,1,0:T(8,128)(2,1)S(1)}, u32[]{:S(2)}, u32[]{:S(2)}) collective-permute-start(bf16[2,160,256]{2,1,0:T(8,128)(2,1)S(1)} %shard_map.68.refs_0_), channel_id=1, source_target_pairs={{0,2},{1,3},{2,0},{3,1},{8,10},{9,11},{10,8},{11,9},{4,6},{5,7},{6... | collective-permute-start | bytes 491528 | tf_op jit(solution)/shard_map/ppermute | solution.py:564
  69.7 11.8 %collective-permute-start.15 = (bf16[2,160,256]{2,1,0:T(8,128)(2,1)S(1)}, bf16[2,160,256]{2,1,0:T(8,128)(2,1)S(1)}, u32[]{:S(2)}, u32[]{:S(2)}) collective-permute-start(bf16[2,160,256]{2,1,0:T(8,128)(2,1)S(1)} %shard_map.68.refs_0_), channel_id=1, source_target_pairs={{0,3},{1,0},{2,1},{3,2},{8,11},{9,8},{10,9},{11,10},{4,7},{5,4},{6... | collective-permute-start | bytes 491528 | tf_op jit(solution)/shard_map/ppermute | solution.py:564
  73.3 11.5 %collective-permute-start.31 = (bf16[4,160,256]{2,1,0:T(8,128)(2,1)S(1)}, bf16[4,160,256]{2,1,0:T(8,128)(2,1)S(1)}, u32[]{:S(2)}, u32[]{:S(2)}) collective-permute-start(bf16[4,160,256]{2,1,0:T(8,128)(2,1)S(1)} %get-tuple-element.98), channel_id=1, source_target_pairs={{0,4},{4,0},{1,5},{5,1},{2,6},{6,2},{3,7},{7,3},{8,12},{12,8},{9,1... | collective-permute-start | bytes 983048 | tf_op jit(solution)/shard_map/ppermute | solution.py:542
  81.5 5.2 %collective-permute-start.18 = (bf16[4,160,256]{2,1,0:T(8,128)(2,1)S(1)}, bf16[4,160,256]{2,1,0:T(8,128)(2,1)S(1)}, u32[]{:S(2)}, u32[]{:S(2)}) collective-permute-start(bf16[4,160,256]{2,1,0:T(8,128)(2,1)S(1)} %shard_map.72), channel_id=1, source_target_pairs={{0,4},{4,0},{1,5},{5,1},{2,6},{6,2},{3,7},{7,3},{8,12},{12,8},{9,1... | collective-permute-start | bytes 983048 | tf_op jit(solution)/shard_map/ppermute | solution.py:542
  81.6 7.7 %collective-permute-start.33 = (bf16[128,320]{1,0:T(8,128)(2,1)S(1)}, bf16[128,320]{1,0:T(8,128)(2,1)S(1)}, u32[]{:S(2)}, u32[]{:S(2)}) collective-permute-start(bf16[128,320]{1,0:T(8,128)(2,1)S(1)} %get-tuple-element.99), channel_id=1, source_target_pairs={{8,0},{9,1},{10,2},{11,3},{12,4},{13,5},{14,6},{15,7}} | collective-permute-start | bytes 245768 | tf_op jit(solution)/shard_map/ppermute | solution.py:556
  82.9 8.3 %collective-permute-start.32 = (bf16[128,320]{1,0:T(8,128)(2,1)S(1)}, bf16[128,320]{1,0:T(8,128)(2,1)S(1)}, u32[]{:S(2)}, u32[]{:S(2)}) collective-permute-start(bf16[128,320]{1,0:T(8,128)(2,1)S(1)} %get-tuple-element.96.refs_4_.refs_1_.refs_12_), channel_id=1, source_target_pairs={{8,0},{9,1},{10,2},{11,3},{12,4},{13,5},{14,6},{15,7}} | collective-permute-start | bytes 245768 | tf_op jit(solution)/shard_map/ppermute | solution.py:556
  84.2 12.8 %collective-permute-start.12 = (bf16[2,160,256]{2,1,0:T(8,128)(2,1)S(1)}, bf16[2,160,256]{2,1,0:T(8,128)(2,1)S(1)}, u32[]{:S(2)}, u32[]{:S(2)}) collective-permute-start(bf16[2,160,256]{2,1,0:T(8,128)(2,1)S(1)} %shard_map.69.refs_2_.refs_0_.refs_1_), channel_id=1, source_target_pairs={{16,17},{17,18},{18,19},{19,16},{24,25},{25,26},{26,27},{27,24},{2... | collective-permute-start | bytes 491528 | tf_op jit(solution)/shard_map/ppermute | solution.py:564
  84.9 13.3 %collective-permute-start.11 = (bf16[2,160,256]{2,1,0:T(8,128)(2,1)S(1)}, bf16[2,160,256]{2,1,0:T(8,128)(2,1)S(1)}, u32[]{:S(2)}, u32[]{:S(2)}) collective-permute-start(bf16[2,160,256]{2,1,0:T(8,128)(2,1)S(1)} %shard_map.69.refs_2_.refs_0_.refs_1_), channel_id=1, source_target_pairs={{16,18},{17,19},{18,16},{19,17},{24,26},{25,27},{26,24},{27,25},{2... | collective-permute-start | bytes 491528 | tf_op jit(solution)/shard_map/ppermute | solution.py:564
  86.7 11.4 %collective-permute-start.10 = (bf16[2,160,256]{2,1,0:T(8,128)(2,1)S(1)}, bf16[2,160,256]{2,1,0:T(8,128)(2,1)S(1)}, u32[]{:S(2)}, u32[]{:S(2)}) collective-permute-start(bf16[2,160,256]{2,1,0:T(8,128)(2,1)S(1)} %shard_map.69.refs_2_.refs_0_.refs_1_), channel_id=1, source_target_pairs={{16,19},{17,16},{18,17},{19,18},{24,27},{25,24},{26,25},{27,26},{2... | collective-permute-start | bytes 491528 | tf_op jit(solution)/shard_map/ppermute | solution.py:564
  92.5 6.9 %collective-permute-start.34 = (bf16[2,80,256]{2,1,0:T(8,128)(2,1)S(1)}, bf16[2,80,256]{2,1,0:T(8,128)(2,1)S(1)}, u32[]{:S(2)}, u32[]{:S(2)}) collective-permute-start(bf16[2,80,256]{2,1,0:T(8,128)(2,1)S(1)} %get-tuple-element.112), channel_id=1, source_target_pairs={{0,1},{1,2},{2,3},{3,0},{8,9},{9,10},{10,11},{11,8},{16,17},{17,18... | collective-permute-start | bytes 245768 | tf_op jit(solution)/shard_map/ppermute | solution.py:564
  95.7 6.8 %collective-permute-start.35 = (bf16[2,80,256]{2,1,0:T(8,128)(2,1)S(1)}, bf16[2,80,256]{2,1,0:T(8,128)(2,1)S(1)}, u32[]{:S(2)}, u32[]{:S(2)}) collective-permute-start(bf16[2,80,256]{2,1,0:T(8,128)(2,1)S(1)} %get-tuple-element.111), channel_id=1, source_target_pairs={{0,2},{1,3},{2,0},{3,1},{8,10},{9,11},{10,8},{11,9},{16,18},{17,19... | collective-permute-start | bytes 245768 | tf_op jit(solution)/shard_map/ppermute | solution.py:564
  97.0 5.8 %collective-permute-start.36 = (bf16[2,80,256]{2,1,0:T(8,128)(2,1)S(1)}, bf16[2,80,256]{2,1,0:T(8,128)(2,1)S(1)}, u32[]{:S(2)}, u32[]{:S(2)}) collective-permute-start(bf16[2,80,256]{2,1,0:T(8,128)(2,1)S(1)} %get-tuple-element.110), channel_id=1, source_target_pairs={{0,3},{1,0},{2,1},{3,2},{8,11},{9,8},{10,9},{11,10},{16,19},{17,16... | collective-permute-start | bytes 245768 | tf_op jit(solution)/shard_map/ppermute | solution.py:564
  102.8 2.5 %collective-permute-start.37 = (bf16[4,2,80,256]{3,2,1,0:T(8,128)(2,1)S(1)}, bf16[4,2,80,256]{3,2,1,0:T(8,128)(2,1)S(1)}, u32[]{:S(2)}, u32[]{:S(2)}) collective-permute-start(bf16[4,2,80,256]{3,2,1,0:T(8,128)(2,1)S(1)} %shard_map.85.own_ref), channel_id=1, source_target_pairs={{0,4},{4,0},{1,5},{5,1},{2,6},{6,2},{3,7},{7,3},{8,12},{12,8},{9,1... | collective-permute-start | bytes 983048 | tf_op jit(solution)/shard_map/ppermute | solution.py:542
  103.0 1.7 %collective-permute-start.38 = (bf16[2,8,8,320]{3,2,1,0:T(8,128)(2,1)S(1)}, bf16[2,8,8,320]{3,2,1,0:T(8,128)(2,1)S(1)}, u32[]{:S(2)}, u32[]{:S(2)}) collective-permute-start(bf16[2,8,8,320]{3,2,1,0:T(8,128)(2,1)S(1)} %get-tuple-element.109), channel_id=1, source_target_pairs={{0,4},{4,0},{1,5},{5,1},{2,6},{6,2},{3,7},{7,3},{8,12},{12,8},{9,1... | collective-permute-start | bytes 245768 | tf_op jit(solution)/shard_map/ppermute | solution.py:542

commit v3 on v2

--- a/solution.py
+++ b/solution.py
@@ -443,57 +443,76 @@
     return merged
 
 
-def stack_call(blocks, slot, after):
+def stack_call(blocks):
     def kernel(*refs):
         for place in range(len(blocks)):
-            refs[-1][place] = refs[place][...] if slot is None else refs[place][slot]
-
-    shape = blocks[0].shape if slot is None else blocks[0].shape[1:]
-    out = jax.ShapeDtypeStruct((len(blocks), *shape), blocks[0].dtype)
-    (stacked,) = call(kernel, [out], [*blocks, after], (len(blocks),), [], {})
+            refs[-1][place] = refs[place][...]
+
+    out = jax.ShapeDtypeStruct((len(blocks), *blocks[0].shape), blocks[0].dtype)
+    (stacked,) = call(kernel, [out], [*blocks], (), [], {})
     return stacked
 
 
-def pick_call(home, received, sections, after):
-    slots = home.shape[0]
-    arrays = [array for section in range(sections) for array in received[section]]
-    each = len(arrays) // sections
-
-    def kernel(home_ref, *refs):
-        for slot in range(slots):
-            refs[-slots + slot][0] = home_ref[slot]
+def remake_call(saved, weights, received, width):
+    _, crops, count, channels = saved.shape
+    share = channels // 2
+    sections, each = len(received), len(received[0])
+
+    def kernel(saved_ref, weights_ref, *refs):
+        home_ref, outer_ref, taps, shifted = refs[-4:]
+        is_left = lax.axis_index("slab") == 0
+
+        def put(kind, block, crop, value):
+            cells = slice(crop * count, (crop + 1) * count)
+            flipped = value.T
+            low, high = flipped[:share], flipped[share:]
+            home_ref[kind, block, :, cells] = jnp.where(is_left, low, high)
+            outer_ref[kind, block, :, cells] = jnp.where(is_left, high, low)
+
+        for crop in range(crops):
+            for kind in range(2):
+                put(kind, 0, crop, saved_ref[kind, crop])
         for section in range(sections):
 
             @pl.when(lax.axis_index("section") == section)
             def _():
                 for block in range(each):
-                    for slot in range(slots):
-                        refs[-slots + slot][1 + block] = refs[section * each + block][slot]
-
-    out = jax.ShapeDtypeStruct((1 + each, *home.shape[1:]), home.dtype)
-    operands = [home, *arrays, after]
-    return call(kernel, [out] * slots, operands, (len(operands) - 1,), [], {})
-
-
-def spread_call(sources, slots, blocks, kind, around, sections, count, width):
-    share, cells = sources[0].shape[-2:]
+                    home_ref[0, 1 + block] = refs[section * each + block][0]
+                    outer_ref[0, 1 + block] = refs[section * each + block][1]
+
+        for block in range(1, 1 + each):
+            for crop in range(crops):
+                cells = slice(crop * count, (crop + 1) * count)
+                mine, theirs = home_ref[0, block, :, cells], outer_ref[0, block, :, cells]
+                low, high = jnp.where(is_left, mine, theirs), jnp.where(is_left, theirs, mine)
+                field = jnp.concatenate([low, high], axis=0).T.astype(jnp.float32)
+                hidden = convolved(field, weights_ref.at[0], taps, shifted, width)
+                put(1, block, crop, (hidden * jax.nn.sigmoid(hidden)).astype(jnp.bfloat16))
+
+    out = jax.ShapeDtypeStruct((2, 1 + each, share, crops * count), saved.dtype)
+    scratch = [
+        pltpu.VMEM((count + 2 * width, 3 * channels), jnp.bfloat16),
+        pltpu.VMEM((count + 16, channels), jnp.float32),
+    ]
+    operands = [saved, weights, *[array for arrays in received for array in arrays]]
+    return call(kernel, [out, out], operands, (), scratch, {})
+
+
+def spread_call(own, other, count, width, after):
+    two, blocks, share, cells = own.shape
     crops = cells // count
     stride = count + width
-    fresh = isinstance(around, jax.ShapeDtypeStruct)
-    total = around.shape[1]
-
-    def kernel(*refs):
-        out_ref, shifted = refs[-2:]
-        section = lax.axis_index("section")
-
-        @pl.when((section >= sections[0]) & (section <= sections[1]))
-        def _():
-            edge = jnp.zeros((width, 3 * share), jnp.bfloat16)
+    total = 2 * blocks * crops * stride + width
+
+    def kernel(own_ref, other_ref, after_ref, out_ref, shifted):
+        edge = jnp.zeros((width, 3 * share), jnp.bfloat16)
+        for kind in range(two):
             out_ref[kind, total - width : total, :] = edge
-            for ref, slot, block in zip(refs, slots, blocks):
+            for block in range(2 * blocks):
+                ref = own_ref if block < blocks else other_ref
                 for crop in range(crops):
                     cell = slice(crop * count, (crop + 1) * count)
-                    value = ref[(*slot, slice(None), cell)].T.astype(jnp.float32)
+                    value = ref[kind, block % blocks, :, cell].T.astype(jnp.float32)
                     before, after = neighbours(value, shifted, width)
                     at = (block * crops + crop) * stride
                     out_ref[kind, at : at + width, :] = edge
@@ -501,11 +520,9 @@
                         lanes = slice(place * share, (place + 1) * share)
                         out_ref[kind, at + width : at + stride, lanes] = part.astype(jnp.bfloat16)
 
-    operands = [*sources] if fresh else [*sources, around]
-    aliases = {} if fresh else {len(sources): 0}
-    out = jax.ShapeDtypeStruct(around.shape, around.dtype)
+    out = jax.ShapeDtypeStruct((two, total, 3 * share), jnp.bfloat16)
     scratch = [pltpu.VMEM((count + 16, share), jnp.float32)]
-    (spread,) = call(kernel, [out], operands, (), scratch, aliases)
+    (spread,) = call(kernel, [out], [own, other, after], (2,), scratch, {})
     return spread
 
 
@@ -550,10 +567,15 @@
     count = row_count * width
     crops = images * strip_count // slabs
     last = sections - 1
+    early, middle = min(1, last - 1), min(2, last)
+    steps = range(1, groups)
     scaling = 1.0 / math.sqrt(images * groups * strip_count * count)
 
-    def hop(value, source, target):
-        return lax.ppermute(value, "section", [(source, target)])
+    def hop(values, source, target):
+        arrived = []
+        for value in values:
+            arrived.append(lax.ppermute(value, "section", [(source, target)]))
+        return arrived
 
     def shared(values, step, routes):
         pairs = [
@@ -563,20 +585,23 @@
         ]
         return lax.ppermute(values, ("section", "img"), pairs)
 
-    steps = range(1, groups)
-    everywhere = [(place, place) for place in range(sections)]
-    soon, late_from = everywhere[: max(1, sections - 2)], max(1, sections - 2)
+    def swapped(value):
+        return rotated(value, "slab", 1)
+
+    def flipped(values):
+        return flip_call([(value, Ellipsis) for value in values], slabs, "slab", values[-1])
+
     own, other = split_call(
         pltpu.with_memory_space_constraint(strips, pltpu.HBM),
         pltpu.with_memory_space_constraint(cotangent, pltpu.HBM),
         last,
     )
-    other = rotated(other, "slab", 1)
+    other = swapped(other)
     weights = kernels[0].reshape(2, 3, 3 * channels, channels)
     weights = load_call(pltpu.with_memory_space_constraint(weights, pltpu.HBM))
     fields = join_call(own, other)
     incoming = fields
-    state, handed = [], {}
+    state, received = [], [None] * sections
     turned, after = None, weights
     for place in range(sections):
         outgoing = []
@@ -585,24 +610,20 @@
                 incoming[crop], weights, state, place, crop, crops, width, place == last, after
             )
             outgoing.append(out)
-        if place == 0:
+        if place < last:
+            incoming = hop(outgoing, place, place + 1)
+            handed = flipped(outgoing)
+            routes = [(place, place + 1)]
+            received[place + 1] = [shared(handed, step, routes) for step in steps]
+        if place == early:
+            handed = flipped(fields)
+            received[0] = [shared(handed, step, [(0, 0)]) for step in steps]
             turned = turn_call(weights, state[0])
-        if place < last:
-            incoming = [hop(out, place, place + 1) for out in outgoing]
-        if 0 < place < last:
-            flipped = flip_call([(out, Ellipsis) for out in outgoing], slabs, "slab", state[1])
-            handed[place + 1] = [shared(flipped, step, [(place, place + 1)]) for step in steps]
-            after = flipped
-        if place == 0:
-            flipped_outgoing = outgoing
-        if place == min(1, last - 1):
-            flipped = flip_call([(field, Ellipsis) for field in fields], slabs, "slab", state[1])
-            handed[0] = [shared(flipped, step, [(0, 0)]) for step in steps]
+            after = turned
     saved, hidden = state
     incoming = fields
     grads = []
     around, after = None, hidden
-    late = []
     for place in reversed(range(sections)):
         outgoing = []
         for crop in range(crops):
@@ -611,74 +632,24 @@
             )
             outgoing.append(out)
         if place:
-            incoming = [hop(out, place, place - 1) for out in outgoing]
-        if place == min(last, 2):
-            active = flip_call([(saved, (1, crop)) for crop in range(crops)], slabs, "slab", grads[0])
-            pairs = [
-                (source * slabs + i, source * slabs + (i + 1) % slabs)
-                for source in range(late_from, sections)
-                for i in range(slabs)
-            ]
-            other = lax.ppermute(active[1], ("section", "slab"), pairs)
-            both = stack_call([active[0], other], None, grads[0])
-            late = [both]
-            for step in steps:
-                late.append(shared(both, step, everywhere[late_from:]))
-            flipped = flip_call([(out, Ellipsis) for out in flipped_outgoing], slabs, "slab", both)
-            handed[1] = [shared(flipped, step, [(0, 1)]) for step in steps]
-            early = [shared(active, step, soon) for step in steps]
+            incoming = hop(outgoing, place, place - 1)
+        if place == middle:
+            home, outer = remake_call(saved, weights, received, width)
+            after = home
+            outer = swapped(outer)
         if place == 1:
-            mine = flip_call([(saved, (0, crop)) for crop in range(crops)], slabs, "slab", outgoing[-1])
-            inputs = pick_call(mine, handed, sections, outgoing[-1])
-            active = [active, *early]
-            other = stack_call(active, 1, outgoing[-1])
-            other = rotated(other, "slab", 1)
-            outer = rotated(inputs[1], "slab", 1)
-            stride = count + width
-            shape = (2, slabs * groups * crops * stride + width, 3 * (channels // slabs))
-            slots = [(block,) for block in range(groups)]
-            around = spread_call(
-                [inputs[0]] * groups + [outer] * groups,
-                slots + slots,
-                list(range(slabs * groups)),
-                0,
-                jax.ShapeDtypeStruct(shape, jnp.bfloat16),
-                (0, last),
-                count,
-                width,
-            )
-            around = spread_call(
-                active + [other] * groups,
-                [(0,)] * groups + slots,
-                list(range(slabs * groups)),
-                1,
-                around,
-                (0, late_from - 1),
-                count,
-                width,
-            )
+            around = spread_call(home, outer, count, width, outgoing[-1])
             after = around
     kept, sent = grads
     own = [sent[0]]
+    everywhere = [(place, place) for place in range(sections)]
     for step in steps:
         own.append(shared(sent[step], step, everywhere))
-    around, sent = lax.optimization_barrier((around, sent))
-    for block in range(groups):
-        around = spread_call(
-            [late[block]] * slabs,
-            [(slab,) for slab in range(slabs)],
-            [slab * groups + block for slab in range(slabs)],
-            1,
-            around,
-            (late_from, last),
-            count,
-            width,
-        )
-    own = stack_call(own, None, around)
-    other = rotated(own, "slab", 1)
+    own = stack_call(own)
+    other = swapped(own)
     terms = terms_call(around, own, other, count, width, scaling)
     own, other = part_call(kept, row_count, sent)
-    other = rotated(other, "slab", 1)
+    other = swapped(other)
     grad_inputs = merge_call(own, other, images)
     return (terms[None], grad_inputs[None])
 

time: 110 us -> 100 us (0.909)
  starting transfers between devices: 69.9 us -> 40.8 us
  waiting for transfers between devices: 20.3 us -> 37.5 us
  Pallas kernels: 17.4 us -> 20.2 us
    ppermute x21 -> x15, starting transfers between devices: 55.6 us -> 28.8 us  [shared(): return lax.ppermute(values, ('section', 'img'), pairs)]
    ppermute x13 -> x12, waiting for transfers between devices: 2.11 us -> 25.2 us  [hop(): arrived.append(lax.ppermute(value, 'section', [(source, target)]))]
    ppermute x21 -> x15, waiting for transfers between devices: 17 us -> 10.2 us  [shared(): return lax.ppermute(values, ('section', 'img'), pairs)]
    pallas_call x39 -> x30, Pallas kernels: 17.4 us -> 20.2 us  [call(): pl.pallas_call(kernel, out_shape=outs, in_specs=[pl.BlockSpec(memory_spac...]
    ppermute x13 -> x12, starting transfers between devices: 13 us -> 10.7 us  [hop(): arrived.append(lax.ppermute(value, 'section', [(source, target)]))]
  transfers between devices with their start and end apart: 39 -> 31, of which waited for: 11 -> 7; matrix products, arithmetic and copies ran while one was open for 0% -> 0% of each run, Pallas kernels for 11% -> 11%
where the time goes in v3:
time: 100 us; the launch traced here: 99.7 us
  starting transfers between devices  40.8 us (41%)
  waiting for transfers between devices  37.5 us (38%)
  Pallas kernels  20.2 us (20%)
  between operations  1.2 us (1%)
    ppermute x15, starting transfers between devices, shared(): return lax.ppermute(values, ('section', 'img'), pairs)  28.8 us
    ppermute x12, waiting for transfers between devices, hop(): arrived.append(lax.ppermute(value, 'section', [(source, target)]))  25.2 us
    pallas_call x30, Pallas kernels, call(): pl.pallas_call(kernel, out_shape=outs, in_specs=[pl.BlockSpec(memory_spac...  20.2 us
    ppermute x12, starting transfers between devices, hop(): arrived.append(lax.ppermute(value, 'section', [(source, target)]))  10.7 us
    ppermute x15, waiting for transfers between devices, shared(): return lax.ppermute(values, ('section', 'img'), pairs)  10.2 us
    ppermute x4, waiting for transfers between devices, rotated(): lax.ppermute(value, axis, [(source, (source + steps) % count) for source...  2.08 us
  transfers between devices with their start and end apart: 31, of which 7 were waited for; matrix products, arithmetic and copies ran while one was open for 0% of the time, Pallas kernels for 11%

profile of v3, /device:TPU:0, one launch (start us, length us, event | category | flops | bytes accessed | tf_op | source)
XLA Modules:
  0.0 99.7 jit_solution(7638233191014745948)
XLA Ops:
  0.6 1.0 shard_map.50
  1.6 0.6 collective-permute-start
  2.2 0.9 collective-permute-done.other_ref
  3.1 0.1 shard_map.51
  3.2 0.1 shard_map.62
  3.3 6.9 %collective-permute-start.9 = (bf16[2,160,256]{2,1,0:T(8,128)(2,1)S(1)}, bf16[2,160,256]{2,1,0:T(8,128)(2,1)S(1)}, u32[]{:S(2)}, u32[]{:S(2)}) collective-permute-start(bf16[2,160,256]{2,1,0:T(8,128)(2,1)S(1)} %shard_map.62), channel_id=1, source_target_pairs={{0,3},{1,0},{2,1},{3,2},{4,7},{5,4},{6,5},{7,6}} | collective-permute-start | bytes 491528 | tf_op jit(solution)/shard_map/ppermute | solution.py:586
  10.1 2.3 %shard_map.52.weights_ref.after_ref = bf16[2,3,960,320]{3,2,1,0:T(8,128)(2,1)S(1)} custom-call(bf16[2,3,960,320]{3,2,1,0:T(8,128)(2,1)} %bitcast.11), custom_call_target="tpu_custom_call" | custom-call | tf_op jit(solution)/shard_map/pallas_call | solution.py:177
  12.5 1.3 %shard_map.53 = (bf16[128,320]{1,0:T(8,128)(2,1)S(1)}, bf16[2,2,128,320]{3,2,1,0:T(8,128)(2,1)S(1)}, f32[2,128,320]{2,1,0:T(8,128)S(1)}) custom-call(bf16[128,320]{1,0:T(8,128)(2,1)S(1)} %get-tuple-element.57.field_ref.refs_0_.grad_ref, bf16[2,3,960,320]{3,2,1,0:T(8,128)(2,1)S(1)} %shard_map.52.weights_ref.after_ref, ...), custom_call_target="tpu_custom_call" | custom-call | tf_op jit(solution)/shard_map/pallas_call | solution.py:177
  13.8 1.3 %collective-permute-start.2 = (bf16[128,320]{1,0:T(8,128)(2,1)S(1)}, bf16[128,320]{1,0:T(8,128)(2,1)S(1)}, u32[]{:S(2)}, u32[]{:S(2)}) collective-permute-start(bf16[128,320]{1,0:T(8,128)(2,1)S(1)} %get-tuple-element.61.refs_0_), channel_id=1, source_target_pairs={{0,8},{1,9},{2,10},{3,11},{4,12},{5,13},{6,14},{7,15}} | collective-permute-start | bytes 245768 | tf_op jit(solution)/shard_map/ppermute | solution.py:577
  15.1 1.3 %shard_map.54 = (bf16[128,320]{1,0:T(8,128)(2,1)S(1)}, bf16[2,2,128,320]{3,2,1,0:T(8,128)(2,1)S(1)}, f32[2,128,320]{2,1,0:T(8,128)S(1)}) custom-call(bf16[128,320]{1,0:T(8,128)(2,1)S(1)} %get-tuple-element.56.field_ref.refs_1_.refs_2_.grad_ref, ...), custom_call_target="tpu_custom_call", output_to_operand_aliasing={{1}: (3, {}), {2}: (4, {})} | custom-call | tf_op jit(solution)/shard_map/pallas_call | solution.py:177
  16.3 1.3 %collective-permute-start.1 = (bf16[128,320]{1,0:T(8,128)(2,1)S(1)}, bf16[128,320]{1,0:T(8,128)(2,1)S(1)}, u32[]{:S(2)}, u32[]{:S(2)}) collective-permute-start(bf16[128,320]{1,0:T(8,128)(2,1)S(1)} %get-tuple-element.60.refs_1_.refs_2_), channel_id=1, source_target_pairs={{0,8},{1,9},{2,10},{3,11},{4,12},{5,13},{6,14},{7,15}} | collective-permute-start | bytes 245768 | tf_op jit(solution)/shard_map/ppermute | solution.py:577
  17.7 1.9 %collective-permute-start.8 = (bf16[2,160,256]{2,1,0:T(8,128)(2,1)S(1)}, bf16[2,160,256]{2,1,0:T(8,128)(2,1)S(1)}, u32[]{:S(2)}, u32[]{:S(2)}) collective-permute-start(bf16[2,160,256]{2,1,0:T(8,128)(2,1)S(1)} %shard_map.62), channel_id=1, source_target_pairs={{0,2},{1,3},{2,0},{3,1},{4,6},{5,7},{6,4},{7,5}} | collective-permute-start | bytes 491528 | tf_op jit(solution)/shard_map/ppermute | solution.py:586
  19.6 2.9 %collective-permute-start.7 = (bf16[2,160,256]{2,1,0:T(8,128)(2,1)S(1)}, bf16[2,160,256]{2,1,0:T(8,128)(2,1)S(1)}, u32[]{:S(2)}, u32[]{:S(2)}) collective-permute-start(bf16[2,160,256]{2,1,0:T(8,128)(2,1)S(1)} %shard_map.62), channel_id=1, source_target_pairs={{0,1},{1,2},{2,3},{3,0},{4,5},{5,6},{6,7},{7,4}} | collective-permute-start | bytes 491528 | tf_op jit(solution)/shard_map/ppermute | solution.py:586
  22.5 0.0 collective-permute-done.1.field_ref
  22.6 0.7 collective-permute-start.3
  23.2 0.7 collective-permute-start.4
  23.9 0.1 shard_map.63
  24.0 4.2 %collective-permute-start.12 = (bf16[2,160,256]{2,1,0:T(8,128)(2,1)S(1)}, bf16[2,160,256]{2,1,0:T(8,128)(2,1)S(1)}, u32[]{:S(2)}, u32[]{:S(2)}) collective-permute-start(bf16[2,160,256]{2,1,0:T(8,128)(2,1)S(1)} %shard_map.63), channel_id=1, source_target_pairs={{0,11},{1,8},{2,9},{3,10},{4,15},{5,12},{6,13},{7,14}} | collective-permute-start | bytes 491528 | tf_op jit(solution)/shard_map/ppermute | solution.py:586
  28.3 0.1 shard_map.64
  28.4 3.0 %collective-permute-done.8.refs_1_ = bf16[2,160,256]{2,1,0:T(8,128)(2,1)S(1)} collective-permute-done((bf16[2,160,256]{2,1,0:T(8,128)(2,1)S(1)}, bf16[2,160,256]{2,1,0:T(8,128)(2,1)S(1)}, u32[]{:S(2)}, u32[]{:S(2)}) %collective-permute-start.8) | collective-permute-done | bytes 163872 | tf_op jit(solution)/shard_map/ppermute | solution.py:586
  31.3 1.3 %collective-permute-start.11 = (bf16[2,160,256]{2,1,0:T(8,128)(2,1)S(1)}, bf16[2,160,256]{2,1,0:T(8,128)(2,1)S(1)}, u32[]{:S(2)}, u32[]{:S(2)}) collective-permute-start(bf16[2,160,256]{2,1,0:T(8,128)(2,1)S(1)} %shard_map.63), channel_id=1, source_target_pairs={{0,10},{1,11},{2,8},{3,9},{4,14},{5,15},{6,12},{7,13}} | collective-permute-start | bytes 491528 | tf_op jit(solution)/shard_map/ppermute | solution.py:586
  32.6 1.3 %collective-permute-start.10 = (bf16[2,160,256]{2,1,0:T(8,128)(2,1)S(1)}, bf16[2,160,256]{2,1,0:T(8,128)(2,1)S(1)}, u32[]{:S(2)}, u32[]{:S(2)}) collective-permute-start(bf16[2,160,256]{2,1,0:T(8,128)(2,1)S(1)} %shard_map.63), channel_id=1, source_target_pairs={{0,9},{1,10},{2,11},{3,8},{4,13},{5,14},{6,15},{7,12}} | collective-permute-start | bytes 491528 | tf_op jit(solution)/shard_map/ppermute | solution.py:586
  33.9 0.0 collective-permute-done.4.field_ref
  34.0 0.7 collective-permute-start.15
  34.6 1.4 %shard_map.57.after_ref.turned_ref = bf16[2,3,960,320]{3,2,1,0:T(8,128)(2,1)S(1)} custom-call(bf16[2,3,960,320]{3,2,1,0:T(8,128)(2,1)S(1)} %shard_map.52.weights_ref.after_ref, bf16[2,2,128,320]{3,2,1,0:T(8,128)(2,1)S(1)} %get-tuple-element.67.after_ref.refs_0_), custom_call_target="tpu_custom_call" | custom-call | tf_op jit(solution)/shard_map/pallas_call | solution.py:177
  36.0 0.7 collective-permute-start.5
  36.7 0.0 collective-permute-done.12.refs_5_
  36.7 0.7 collective-permute-start.6
  37.4 0.1 shard_map.65
  37.5 0.7 collective-permute-start.14
  38.2 2.7 %collective-permute-done.10.refs_3_ = bf16[2,160,256]{2,1,0:T(8,128)(2,1)S(1)} collective-permute-done((bf16[2,160,256]{2,1,0:T(8,128)(2,1)S(1)}, bf16[2,160,256]{2,1,0:T(8,128)(2,1)S(1)}, u32[]{:S(2)}, u32[]{:S(2)}) %collective-permute-start.10) | collective-permute-done | bytes 163872 | tf_op jit(solution)/shard_map/ppermute | solution.py:586
  40.9 0.7 collective-permute-start.13
  41.6 0.0 collective-permute-done.15.refs_8_
  41.6 0.7 collective-permute-start.18
  42.3 0.0 collective-permute-done.5.field_ref
  42.3 0.7 collective-permute-start.17
  43.0 0.7 collective-permute-start.16
  43.7 0.0 collective-permute-done.13.refs_6_
  43.7 0.0 collective-permute-done.18.refs_11_
  43.8 0.0 collective-permute-done.16.refs_9_
  43.8 3.3 %shard_map.66 = (bf16[2,4,160,256]{3,2,1,0:T(8,128)(2,1)S(1)}, bf16[2,4,160,256]{3,2,1,0:T(8,128)(2,1)S(1)}) custom-call(bf16[2,2,128,320]{3,2,1,0:T(8,128)(2,1)S(1)} %get-tuple-element.78.saved_ref, bf16[2,3,960,320]{3,2,1,0:T(8,128)(2,1)S(1)} %shard_map.52.weights_ref.after_ref, bf16[2,160,256]{2,1,0:T(8,128)(2,1)S(1)} %collective-permute-done.7.refs_0_, ...), custom_call_target="tpu_custom_call" | custom-call | tf_op jit(solution)/shard_map/pallas_call | solution.py:177
  47.1 0.1 collective-permute-start.19
  47.2 0.7 collective-permute-start.21
  47.9 0.7 collective-permute-start.20
  48.6 0.7 collective-permute-start.23
  49.3 0.0 collective-permute-done.20.grad_ref
  49.3 0.7 collective-permute-start.22
  50.0 1.3 %collective-permute-start.25 = (bf16[128,320]{1,0:T(8,128)(2,1)S(1)}, bf16[128,320]{1,0:T(8,128)(2,1)S(1)}, u32[]{:S(2)}, u32[]{:S(2)}) collective-permute-start(bf16[128,320]{1,0:T(8,128)(2,1)S(1)} %get-tuple-element.97), channel_id=1, source_target_pairs={{8,0},{9,1},{10,2},{11,3},{12,4},{13,5},{14,6},{15,7}} | collective-permute-start | bytes 245768 | tf_op jit(solution)/shard_map/ppermute | solution.py:577
  51.4 1.5 %collective-permute-start.24 = (bf16[128,320]{1,0:T(8,128)(2,1)S(1)}, bf16[128,320]{1,0:T(8,128)(2,1)S(1)}, u32[]{:S(2)}, u32[]{:S(2)}) collective-permute-start(bf16[128,320]{1,0:T(8,128)(2,1)S(1)} %get-tuple-element.96.after_ref), channel_id=1, source_target_pairs={{8,0},{9,1},{10,2},{11,3},{12,4},{13,5},{14,6},{15,7}} | collective-permute-start | bytes 245768 | tf_op jit(solution)/shard_map/ppermute | solution.py:577
  52.9 2.3 %shard_map.73.after_ref.around_ref = bf16[2,2320,480]{2,1,0:T(8,128)(2,1)S(1)} custom-call(bf16[2,4,160,256]{3,2,1,0:T(8,128)(2,1)S(1)} %get-tuple-element.79.after_ref.own_ref, bf16[2,4,160,256]{3,2,1,0:T(8,128)(2,1)S(1)} %collective-permute-done.19.other_ref, bf16[128,320]{1,0:T(8,128)(2,1)S(1)} %get-tuple-element.96.after_ref), custom_call_target="tpu_custom_call" | custom-call | tf_op jit(solution)/shard_map/pallas_call | solution.py:177
  55.1 23.8 %collective-permute-done.25.grad_ref = bf16[128,320]{1,0:T(8,128)(2,1)S(1)} collective-permute-done((bf16[128,320]{1,0:T(8,128)(2,1)S(1)}, bf16[128,320]{1,0:T(8,128)(2,1)S(1)}, u32[]{:S(2)}, u32[]{:S(2)}) %collective-permute-start.25) | collective-permute-done | bytes 81952 | tf_op jit(solution)/shard_map/ppermute | solution.py:577
  79.0 1.2 %shard_map.74 = (bf16[2,128,320]{2,1,0:T(8,128)(2,1)S(1)}, bf16[4,2,80,256]{3,2,1,0:T(8,128)(2,1)S(1)}) custom-call(bf16[128,320]{1,0:T(8,128)(2,1)S(1)} %collective-permute-done.25.grad_ref, bf16[2,3,960,320]{3,2,1,0:T(8,128)(2,1)S(1)} %shard_map.57.after_ref.turned_ref, ...), custom_call_target="tpu_custom_call", output_to_operand_aliasing={{0}: (4, {}), {1}: (5, {})} | custom-call | tf_op jit(solution)/shard_map/pallas_call | solution.py:177
  80.2 1.3 %collective-permute-done.24.grad_ref = bf16[128,320]{1,0:T(8,128)(2,1)S(1)} collective-permute-done((bf16[128,320]{1,0:T(8,128)(2,1)S(1)}, bf16[128,320]{1,0:T(8,128)(2,1)S(1)}, u32[]{:S(2)}, u32[]{:S(2)}) %collective-permute-start.24) | collective-permute-done | bytes 81952 | tf_op jit(solution)/shard_map/ppermute | solution.py:577
  81.6 1.2 %shard_map.75 = (bf16[2,128,320]{2,1,0:T(8,128)(2,1)S(1)}, bf16[4,2,80,256]{3,2,1,0:T(8,128)(2,1)S(1)}) custom-call(bf16[128,320]{1,0:T(8,128)(2,1)S(1)} %collective-permute-done.24.grad_ref, bf16[2,3,960,320]{3,2,1,0:T(8,128)(2,1)S(1)} %shard_map.57.after_ref.turned_ref, ...), custom_call_target="tpu_custom_call", output_to_operand_aliasing={{0}: (4, {}), {1}: (5, {})} | custom-call | tf_op jit(solution)/shard_map/pallas_call | solution.py:177
  82.8 2.7 %collective-permute-start.28 = (bf16[2,80,256]{2,1,0:T(8,128)(2,1)S(1)}, bf16[2,80,256]{2,1,0:T(8,128)(2,1)S(1)}, u32[]{:S(2)}, u32[]{:S(2)}) collective-permute-start(bf16[2,80,256]{2,1,0:T(8,128)(2,1)S(1)} %get-tuple-element.106), channel_id=1, source_target_pairs={{0,3},{1,0},{2,1},{3,2},{8,11},{9,8},{10,9},{11,10},{16,19},{17,16... | collective-permute-start | bytes 245768 | tf_op jit(solution)/shard_map/ppermute | solution.py:586
  85.5 1.6 %collective-permute-start.27 = (bf16[2,80,256]{2,1,0:T(8,128)(2,1)S(1)}, bf16[2,80,256]{2,1,0:T(8,128)(2,1)S(1)}, u32[]{:S(2)}, u32[]{:S(2)}) collective-permute-start(bf16[2,80,256]{2,1,0:T(8,128)(2,1)S(1)} %get-tuple-element.107), channel_id=1, source_target_pairs={{0,2},{1,3},{2,0},{3,1},{8,10},{9,11},{10,8},{11,9},{16,18},{17,19... | collective-permute-start | bytes 245768 | tf_op jit(solution)/shard_map/ppermute | solution.py:586
  87.2 1.9 %collective-permute-start.26 = (bf16[2,80,256]{2,1,0:T(8,128)(2,1)S(1)}, bf16[2,80,256]{2,1,0:T(8,128)(2,1)S(1)}, u32[]{:S(2)}, u32[]{:S(2)}) collective-permute-start(bf16[2,80,256]{2,1,0:T(8,128)(2,1)S(1)} %get-tuple-element.108), channel_id=1, source_target_pairs={{0,1},{1,2},{2,3},{3,0},{8,9},{9,10},{10,11},{11,8},{16,17},{17,18... | collective-permute-start | bytes 245768 | tf_op jit(solution)/shard_map/ppermute | solution.py:586
  89.1 4.5 %collective-permute-done.27.refs_2_ = bf16[2,80,256]{2,1,0:T(8,128)(2,1)S(1)} collective-permute-done((bf16[2,80,256]{2,1,0:T(8,128)(2,1)S(1)}, bf16[2,80,256]{2,1,0:T(8,128)(2,1)S(1)}, u32[]{:S(2)}, u32[]{:S(2)}) %collective-permute-start.27) | collective-permute-done | bytes 81952 | tf_op jit(solution)/shard_map/ppermute | solution.py:586
  93.6 0.1 collective-permute-start.29
  93.7 0.1 shard_map.78
  93.7 0.6 collective-permute-start.30
  94.3 1.1 %collective-permute-done.30.other_ref = bf16[2,8,8,320]{3,2,1,0:T(8,128)(2,1)S(1)} collective-permute-done((bf16[2,8,8,320]{3,2,1,0:T(8,128)(2,1)S(1)}, bf16[2,8,8,320]{3,2,1,0:T(8,128)(2,1)S(1)}, u32[]{:S(2)}, u32[]{:S(2)}) %collective-permute-start.30) | collective-permute-done | bytes 81952 | tf_op jit(solution)/shard_map/ppermute | solution.py:559
  95.4 0.7 shard_map.79
  96.1 3.5 %shard_map.77 = f32[2,9,160,80]{3,2,1,0:T(8,128)} custom-call(bf16[2,2320,480]{2,1,0:T(8,128)(2,1)S(1)} %shard_map.73.after_ref.around_ref, bf16[4,2,80,256]{3,2,1,0:T(8,128)(2,1)S(1)} %shard_map.76.own_ref, bf16[4,2,80,256]{3,2,1,0:T(8,128)(2,1)S(1)} %collective-permute-done.29.other_ref), custom_call_target="tpu_custom_call" | custom-call | tf_op jit(solution)/shard_map/pallas_call | solution.py:177
  (29 shorter events, 0.3 us)
Async XLA Ops:
  1.6 1.5 %collective-permute-start = (bf16[2,8,8,320]{3,2,1,0:T(8,128)(2,1)S(1)}, bf16[2,8,8,320]{3,2,1,0:T(8,128)(2,1)S(1)}, u32[]{:S(2)}, u32[]{:S(2)}) collective-permute-start(bf16[2,8,8,320]{3,2,1,0:T(8,128)(2,1)S(1)} %get-tuple-element.55), channel_id=1, source_target_pairs={{0,4},{4,0},{1,5},{5,1},{2,6},{6,2},{3,7},{7,3},{8,12},{12,8},{9,1... | collective-permute-start | bytes 245768 | tf_op jit(solution)/shard_map/ppermute | solution.py:559
  3.3 20.7 %collective-permute-start.9 = (bf16[2,160,256]{2,1,0:T(8,128)(2,1)S(1)}, bf16[2,160,256]{2,1,0:T(8,128)(2,1)S(1)}, u32[]{:S(2)}, u32[]{:S(2)}) collective-permute-start(bf16[2,160,256]{2,1,0:T(8,128)(2,1)S(1)} %shard_map.62), channel_id=1, source_target_pairs={{0,3},{1,0},{2,1},{3,2},{4,7},{5,4},{6,5},{7,6}} | collective-permute-start | bytes 491528 | tf_op jit(solution)/shard_map/ppermute | solution.py:586
  13.8 8.7 %collective-permute-start.2 = (bf16[128,320]{1,0:T(8,128)(2,1)S(1)}, bf16[128,320]{1,0:T(8,128)(2,1)S(1)}, u32[]{:S(2)}, u32[]{:S(2)}) collective-permute-start(bf16[128,320]{1,0:T(8,128)(2,1)S(1)} %get-tuple-element.61.refs_0_), channel_id=1, source_target_pairs={{0,8},{1,9},{2,10},{3,11},{4,12},{5,13},{6,14},{7,15}} | collective-permute-start | bytes 245768 | tf_op jit(solution)/shard_map/ppermute | solution.py:577
  16.3 6.2 %collective-permute-start.1 = (bf16[128,320]{1,0:T(8,128)(2,1)S(1)}, bf16[128,320]{1,0:T(8,128)(2,1)S(1)}, u32[]{:S(2)}, u32[]{:S(2)}) collective-permute-start(bf16[128,320]{1,0:T(8,128)(2,1)S(1)} %get-tuple-element.60.refs_1_.refs_2_), channel_id=1, source_target_pairs={{0,8},{1,9},{2,10},{3,11},{4,12},{5,13},{6,14},{7,15}} | collective-permute-start | bytes 245768 | tf_op jit(solution)/shard_map/ppermute | solution.py:577
  17.7 13.7 %collective-permute-start.8 = (bf16[2,160,256]{2,1,0:T(8,128)(2,1)S(1)}, bf16[2,160,256]{2,1,0:T(8,128)(2,1)S(1)}, u32[]{:S(2)}, u32[]{:S(2)}) collective-permute-start(bf16[2,160,256]{2,1,0:T(8,128)(2,1)S(1)} %shard_map.62), channel_id=1, source_target_pairs={{0,2},{1,3},{2,0},{3,1},{4,6},{5,7},{6,4},{7,5}} | collective-permute-start | bytes 491528 | tf_op jit(solution)/shard_map/ppermute | solution.py:586
  19.6 16.5 %collective-permute-start.7 = (bf16[2,160,256]{2,1,0:T(8,128)(2,1)S(1)}, bf16[2,160,256]{2,1,0:T(8,128)(2,1)S(1)}, u32[]{:S(2)}, u32[]{:S(2)}) collective-permute-start(bf16[2,160,256]{2,1,0:T(8,128)(2,1)S(1)} %shard_map.62), channel_id=1, source_target_pairs={{0,1},{1,2},{2,3},{3,0},{4,5},{5,6},{6,7},{7,4}} | collective-permute-start | bytes 491528 | tf_op jit(solution)/shard_map/ppermute | solution.py:586
  22.6 10.1 %collective-permute-start.3 = (bf16[128,320]{1,0:T(8,128)(2,1)S(1)}, bf16[128,320]{1,0:T(8,128)(2,1)S(1)}, u32[]{:S(2)}, u32[]{:S(2)}) collective-permute-start(bf16[128,320]{1,0:T(8,128)(2,1)S(1)} %get-tuple-element.66.refs_1_.refs_2_), channel_id=1, source_target_pairs={{8,16},{9,17},{10,18},{11,19},{12,20},{13,21},{14,22},{15,23}} | collective-permute-start | bytes 245768 | tf_op jit(solution)/shard_map/ppermute | solution.py:577
  23.2 10.7 %collective-permute-start.4 = (bf16[128,320]{1,0:T(8,128)(2,1)S(1)}, bf16[128,320]{1,0:T(8,128)(2,1)S(1)}, u32[]{:S(2)}, u32[]{:S(2)}) collective-permute-start(bf16[128,320]{1,0:T(8,128)(2,1)S(1)} %get-tuple-element.68.refs_0_), channel_id=1, source_target_pairs={{8,16},{9,17},{10,18},{11,19},{12,20},{13,21},{14,22},{15,23}} | collective-permute-start | bytes 245768 | tf_op jit(solution)/shard_map/ppermute | solution.py:577
  24.0 12.7 %collective-permute-start.12 = (bf16[2,160,256]{2,1,0:T(8,128)(2,1)S(1)}, bf16[2,160,256]{2,1,0:T(8,128)(2,1)S(1)}, u32[]{:S(2)}, u32[]{:S(2)}) collective-permute-start(bf16[2,160,256]{2,1,0:T(8,128)(2,1)S(1)} %shard_map.63), channel_id=1, source_target_pairs={{0,11},{1,8},{2,9},{3,10},{4,15},{5,12},{6,13},{7,14}} | collective-permute-start | bytes 491528 | tf_op jit(solution)/shard_map/ppermute | solution.py:586
  31.3 6.2 %collective-permute-start.11 = (bf16[2,160,256]{2,1,0:T(8,128)(2,1)S(1)}, bf16[2,160,256]{2,1,0:T(8,128)(2,1)S(1)}, u32[]{:S(2)}, u32[]{:S(2)}) collective-permute-start(bf16[2,160,256]{2,1,0:T(8,128)(2,1)S(1)} %shard_map.63), channel_id=1, source_target_pairs={{0,10},{1,11},{2,8},{3,9},{4,14},{5,15},{6,12},{7,13}} | collective-permute-start | bytes 491528 | tf_op jit(solution)/shard_map/ppermute | solution.py:586
  32.6 8.3 %collective-permute-start.10 = (bf16[2,160,256]{2,1,0:T(8,128)(2,1)S(1)}, bf16[2,160,256]{2,1,0:T(8,128)(2,1)S(1)}, u32[]{:S(2)}, u32[]{:S(2)}) collective-permute-start(bf16[2,160,256]{2,1,0:T(8,128)(2,1)S(1)} %shard_map.63), channel_id=1, source_target_pairs={{0,9},{1,10},{2,11},{3,8},{4,13},{5,14},{6,15},{7,12}} | collective-permute-start | bytes 491528 | tf_op jit(solution)/shard_map/ppermute | solution.py:586
  34.0 7.7 %collective-permute-start.15 = (bf16[2,160,256]{2,1,0:T(8,128)(2,1)S(1)}, bf16[2,160,256]{2,1,0:T(8,128)(2,1)S(1)}, u32[]{:S(2)}, u32[]{:S(2)}) collective-permute-start(bf16[2,160,256]{2,1,0:T(8,128)(2,1)S(1)} %shard_map.64), channel_id=1, source_target_pairs={{8,19},{9,16},{10,17},{11,18},{12,23},{13,20},{14,21},{15,22}} | collective-permute-start | bytes 491528 | tf_op jit(solution)/shard_map/ppermute | solution.py:586
  36.0 6.3 %collective-permute-start.5 = (bf16[128,320]{1,0:T(8,128)(2,1)S(1)}, bf16[128,320]{1,0:T(8,128)(2,1)S(1)}, u32[]{:S(2)}, u32[]{:S(2)}) collective-permute-start(bf16[128,320]{1,0:T(8,128)(2,1)S(1)} %get-tuple-element.72.refs_1_.refs_2_), channel_id=1, source_target_pairs={{16,24},{17,25},{18,26},{19,27},{20,28},{21,29},{22,30},{23,31}} | collective-permute-start | bytes 245768 | tf_op jit(solution)/shard_map/ppermute | solution.py:577
  36.7 6.3 %collective-permute-start.6 = (bf16[128,320]{1,0:T(8,128)(2,1)S(1)}, bf16[128,320]{1,0:T(8,128)(2,1)S(1)}, u32[]{:S(2)}, u32[]{:S(2)}) collective-permute-start(bf16[128,320]{1,0:T(8,128)(2,1)S(1)} %get-tuple-element.73.refs_0_), channel_id=1, source_target_pairs={{16,24},{17,25},{18,26},{19,27},{20,28},{21,29},{22,30},{23,31}} | collective-permute-start | bytes 245768 | tf_op jit(solution)/shard_map/ppermute | solution.py:577
  37.5 6.2 %collective-permute-start.14 = (bf16[2,160,256]{2,1,0:T(8,128)(2,1)S(1)}, bf16[2,160,256]{2,1,0:T(8,128)(2,1)S(1)}, u32[]{:S(2)}, u32[]{:S(2)}) collective-permute-start(bf16[2,160,256]{2,1,0:T(8,128)(2,1)S(1)} %shard_map.64), channel_id=1, source_target_pairs={{8,18},{9,19},{10,16},{11,17},{12,22},{13,23},{14,20},{15,21}} | collective-permute-start | bytes 491528 | tf_op jit(solution)/shard_map/ppermute | solution.py:586
  40.9 2.8 %collective-permute-start.13 = (bf16[2,160,256]{2,1,0:T(8,128)(2,1)S(1)}, bf16[2,160,256]{2,1,0:T(8,128)(2,1)S(1)}, u32[]{:S(2)}, u32[]{:S(2)}) collective-permute-start(bf16[2,160,256]{2,1,0:T(8,128)(2,1)S(1)} %shard_map.64), channel_id=1, source_target_pairs={{8,17},{9,18},{10,19},{11,16},{12,21},{13,22},{14,23},{15,20}} | collective-permute-start | bytes 491528 | tf_op jit(solution)/shard_map/ppermute | solution.py:586
  41.6 2.1 %collective-permute-start.18 = (bf16[2,160,256]{2,1,0:T(8,128)(2,1)S(1)}, bf16[2,160,256]{2,1,0:T(8,128)(2,1)S(1)}, u32[]{:S(2)}, u32[]{:S(2)}) collective-permute-start(bf16[2,160,256]{2,1,0:T(8,128)(2,1)S(1)} %shard_map.65), channel_id=1, source_target_pairs={{16,27},{17,24},{18,25},{19,26},{20,31},{21,28},{22,29},{23,30}} | collective-permute-start | bytes 491528 | tf_op jit(solution)/shard_map/ppermute | solution.py:586
  42.3 1.5 %collective-permute-start.17 = (bf16[2,160,256]{2,1,0:T(8,128)(2,1)S(1)}, bf16[2,160,256]{2,1,0:T(8,128)(2,1)S(1)}, u32[]{:S(2)}, u32[]{:S(2)}) collective-permute-start(bf16[2,160,256]{2,1,0:T(8,128)(2,1)S(1)} %shard_map.65), channel_id=1, source_target_pairs={{16,26},{17,27},{18,24},{19,25},{20,30},{21,31},{22,28},{23,29}} | collective-permute-start | bytes 491528 | tf_op jit(solution)/shard_map/ppermute | solution.py:586
  43.0 0.8 collective-permute-start.16
  47.1 5.8 %collective-permute-start.19 = (bf16[2,4,160,256]{3,2,1,0:T(8,128)(2,1)S(1)}, bf16[2,4,160,256]{3,2,1,0:T(8,128)(2,1)S(1)}, u32[]{:S(2)}, u32[]{:S(2)}) collective-permute-start(bf16[2,4,160,256]{3,2,1,0:T(8,128)(2,1)S(1)} %get-tuple-element.80), channel_id=1, source_target_pairs={{0,4},{4,0},{1,5},{5,1},{2,6},{6,2},{3,7},{7,3},{8,12},{12,8},{9,1... | collective-permute-start | bytes 1966088 | tf_op jit(solution)/shard_map/ppermute | solution.py:559
  47.2 1.4 %collective-permute-start.21 = (bf16[128,320]{1,0:T(8,128)(2,1)S(1)}, bf16[128,320]{1,0:T(8,128)(2,1)S(1)}, u32[]{:S(2)}, u32[]{:S(2)}) collective-permute-start(bf16[128,320]{1,0:T(8,128)(2,1)S(1)} %get-tuple-element.85), channel_id=1, source_target_pairs={{24,16},{25,17},{26,18},{27,19},{28,20},{29,21},{30,22},{31,23}} | collective-permute-start | bytes 245768 | tf_op jit(solution)/shard_map/ppermute | solution.py:577
  47.9 1.4 %collective-permute-start.20 = (bf16[128,320]{1,0:T(8,128)(2,1)S(1)}, bf16[128,320]{1,0:T(8,128)(2,1)S(1)}, u32[]{:S(2)}, u32[]{:S(2)}) collective-permute-start(bf16[128,320]{1,0:T(8,128)(2,1)S(1)} %get-tuple-element.84), channel_id=1, source_target_pairs={{24,16},{25,17},{26,18},{27,19},{28,20},{29,21},{30,22},{31,23}} | collective-permute-start | bytes 245768 | tf_op jit(solution)/shard_map/ppermute | solution.py:577
  48.6 1.4 %collective-permute-start.23 = (bf16[128,320]{1,0:T(8,128)(2,1)S(1)}, bf16[128,320]{1,0:T(8,128)(2,1)S(1)}, u32[]{:S(2)}, u32[]{:S(2)}) collective-permute-start(bf16[128,320]{1,0:T(8,128)(2,1)S(1)} %get-tuple-element.91), channel_id=1, source_target_pairs={{16,8},{17,9},{18,10},{19,11},{20,12},{21,13},{22,14},{23,15}} | collective-permute-start | bytes 245768 | tf_op jit(solution)/shard_map/ppermute | solution.py:577
  49.3 2.0 %collective-permute-start.22 = (bf16[128,320]{1,0:T(8,128)(2,1)S(1)}, bf16[128,320]{1,0:T(8,128)(2,1)S(1)}, u32[]{:S(2)}, u32[]{:S(2)}) collective-permute-start(bf16[128,320]{1,0:T(8,128)(2,1)S(1)} %get-tuple-element.90), channel_id=1, source_target_pairs={{16,8},{17,9},{18,10},{19,11},{20,12},{21,13},{22,14},{23,15}} | collective-permute-start | bytes 245768 | tf_op jit(solution)/shard_map/ppermute | solution.py:577
  50.0 29.0 %collective-permute-start.25 = (bf16[128,320]{1,0:T(8,128)(2,1)S(1)}, bf16[128,320]{1,0:T(8,128)(2,1)S(1)}, u32[]{:S(2)}, u32[]{:S(2)}) collective-permute-start(bf16[128,320]{1,0:T(8,128)(2,1)S(1)} %get-tuple-element.97), channel_id=1, source_target_pairs={{8,0},{9,1},{10,2},{11,3},{12,4},{13,5},{14,6},{15,7}} | collective-permute-start | bytes 245768 | tf_op jit(solution)/shard_map/ppermute | solution.py:577
  51.4 30.2 %collective-permute-start.24 = (bf16[128,320]{1,0:T(8,128)(2,1)S(1)}, bf16[128,320]{1,0:T(8,128)(2,1)S(1)}, u32[]{:S(2)}, u32[]{:S(2)}) collective-permute-start(bf16[128,320]{1,0:T(8,128)(2,1)S(1)} %get-tuple-element.96.after_ref), channel_id=1, source_target_pairs={{8,0},{9,1},{10,2},{11,3},{12,4},{13,5},{14,6},{15,7}} | collective-permute-start | bytes 245768 | tf_op jit(solution)/shard_map/ppermute | solution.py:577
  82.8 6.3 %collective-permute-start.28 = (bf16[2,80,256]{2,1,0:T(8,128)(2,1)S(1)}, bf16[2,80,256]{2,1,0:T(8,128)(2,1)S(1)}, u32[]{:S(2)}, u32[]{:S(2)}) collective-permute-start(bf16[2,80,256]{2,1,0:T(8,128)(2,1)S(1)} %get-tuple-element.106), channel_id=1, source_target_pairs={{0,3},{1,0},{2,1},{3,2},{8,11},{9,8},{10,9},{11,10},{16,19},{17,16... | collective-permute-start | bytes 245768 | tf_op jit(solution)/shard_map/ppermute | solution.py:586
  85.5 8.0 %collective-permute-start.27 = (bf16[2,80,256]{2,1,0:T(8,128)(2,1)S(1)}, bf16[2,80,256]{2,1,0:T(8,128)(2,1)S(1)}, u32[]{:S(2)}, u32[]{:S(2)}) collective-permute-start(bf16[2,80,256]{2,1,0:T(8,128)(2,1)S(1)} %get-tuple-element.107), channel_id=1, source_target_pairs={{0,2},{1,3},{2,0},{3,1},{8,10},{9,11},{10,8},{11,9},{16,18},{17,19... | collective-permute-start | bytes 245768 | tf_op jit(solution)/shard_map/ppermute | solution.py:586
  87.2 6.4 %collective-permute-start.26 = (bf16[2,80,256]{2,1,0:T(8,128)(2,1)S(1)}, bf16[2,80,256]{2,1,0:T(8,128)(2,1)S(1)}, u32[]{:S(2)}, u32[]{:S(2)}) collective-permute-start(bf16[2,80,256]{2,1,0:T(8,128)(2,1)S(1)} %get-tuple-element.108), channel_id=1, source_target_pairs={{0,1},{1,2},{2,3},{3,0},{8,9},{9,10},{10,11},{11,8},{16,17},{17,18... | collective-permute-start | bytes 245768 | tf_op jit(solution)/shard_map/ppermute | solution.py:586
  93.6 2.5 %collective-permute-start.29 = (bf16[4,2,80,256]{3,2,1,0:T(8,128)(2,1)S(1)}, bf16[4,2,80,256]{3,2,1,0:T(8,128)(2,1)S(1)}, u32[]{:S(2)}, u32[]{:S(2)}) collective-permute-start(bf16[4,2,80,256]{3,2,1,0:T(8,128)(2,1)S(1)} %shard_map.76.own_ref), channel_id=1, source_target_pairs={{0,4},{4,0},{1,5},{5,1},{2,6},{6,2},{3,7},{7,3},{8,12},{12,8},{9,1... | collective-permute-start | bytes 983048 | tf_op jit(solution)/shard_map/ppermute | solution.py:559
  93.7 1.7 %collective-permute-start.30 = (bf16[2,8,8,320]{3,2,1,0:T(8,128)(2,1)S(1)}, bf16[2,8,8,320]{3,2,1,0:T(8,128)(2,1)S(1)}, u32[]{:S(2)}, u32[]{:S(2)}) collective-permute-start(bf16[2,8,8,320]{3,2,1,0:T(8,128)(2,1)S(1)} %get-tuple-element.105), channel_id=1, source_target_pairs={{0,4},{4,0},{1,5},{5,1},{2,6},{6,2},{3,7},{7,3},{8,12},{12,8},{9,1... | collective-permute-start | bytes 245768 | tf_op jit(solution)/shard_map/ppermute | solution.py:559

commit v4 on v3

--- a/solution.py
+++ b/solution.py
@@ -498,31 +498,33 @@
     return call(kernel, [out, out], operands, (), scratch, {})
 
 
-def spread_call(own, other, count, width, after):
-    two, blocks, share, cells = own.shape
+def spread_call(cells_of, around, place, count, width):
+    two, blocks, share, cells = cells_of.shape
     crops = cells // count
     stride = count + width
     total = 2 * blocks * crops * stride + width
 
-    def kernel(own_ref, other_ref, after_ref, out_ref, shifted):
+    def kernel(cells_ref, *refs):
+        out_ref, shifted = refs[-2:]
         edge = jnp.zeros((width, 3 * share), jnp.bfloat16)
         for kind in range(two):
             out_ref[kind, total - width : total, :] = edge
-            for block in range(2 * blocks):
-                ref = own_ref if block < blocks else other_ref
+            for block in range(blocks):
                 for crop in range(crops):
                     cell = slice(crop * count, (crop + 1) * count)
-                    value = ref[kind, block % blocks, :, cell].T.astype(jnp.float32)
+                    value = cells_ref[kind, block, :, cell].T.astype(jnp.float32)
                     before, after = neighbours(value, shifted, width)
-                    at = (block * crops + crop) * stride
+                    at = ((place * blocks + block) * crops + crop) * stride
                     out_ref[kind, at : at + width, :] = edge
-                    for place, part in enumerate((before, value, after)):
-                        lanes = slice(place * share, (place + 1) * share)
+                    for side, part in enumerate((before, value, after)):
+                        lanes = slice(side * share, (side + 1) * share)
                         out_ref[kind, at + width : at + stride, lanes] = part.astype(jnp.bfloat16)
 
     out = jax.ShapeDtypeStruct((two, total, 3 * share), jnp.bfloat16)
     scratch = [pltpu.VMEM((count + 16, share), jnp.float32)]
-    (spread,) = call(kernel, [out], [own, other, after], (2,), scratch, {})
+    operands = [cells_of] if around is None else [cells_of, around]
+    aliases = {} if around is None else {1: 0}
+    (spread,) = call(kernel, [out], operands, (), scratch, aliases)
     return spread
 
 
@@ -567,7 +569,7 @@
     count = row_count * width
     crops = images * strip_count // slabs
     last = sections - 1
-    early, middle = min(1, last - 1), min(2, last)
+    early = min(1, last - 1)
     steps = range(1, groups)
     scaling = 1.0 / math.sqrt(images * groups * strip_count * count)
 
@@ -623,7 +625,7 @@
     saved, hidden = state
     incoming = fields
     grads = []
-    around, after = None, hidden
+    after = hidden
     for place in reversed(range(sections)):
         outgoing = []
         for crop in range(crops):
@@ -633,18 +635,15 @@
             outgoing.append(out)
         if place:
             incoming = hop(outgoing, place, place - 1)
-        if place == middle:
-            home, outer = remake_call(saved, weights, received, width)
-            after = home
-            outer = swapped(outer)
-        if place == 1:
-            around = spread_call(home, outer, count, width, outgoing[-1])
-            after = around
     kept, sent = grads
     own = [sent[0]]
     everywhere = [(place, place) for place in range(sections)]
     for step in steps:
         own.append(shared(sent[step], step, everywhere))
+    home, outer = remake_call(saved, weights, received, width)
+    outer = swapped(outer)
+    around = spread_call(home, None, 0, count, width)
+    around = spread_call(outer, around, 1, count, width)
     own = stack_call(own)
     other = swapped(own)
     terms = terms_call(around, own, other, count, width, scaling)

time: 100 us -> 92 us (0.920)
  waiting for transfers between devices: 37.5 us -> 22.6 us
  starting transfers between devices: 40.8 us -> 47.4 us
    ppermute x12, waiting for transfers between devices: 25.2 us -> 14.7 us  [hop(): arrived.append(lax.ppermute(value, 'section', [(source, target)]))]
    ppermute x15, starting transfers between devices: 28.8 us -> 33.8 us  [shared(): return lax.ppermute(values, ('section', 'img'), pairs)]
    ppermute x15, waiting for transfers between devices: 10.2 us -> 7.85 us  [shared(): return lax.ppermute(values, ('section', 'img'), pairs)]
    ppermute x4, waiting for transfers between devices: 2.08 us -> 0.01 us  [rotated(): lax.ppermute(value, axis, [(source, (source + steps) % count) for source...]
    ppermute x12, starting transfers between devices: 10.7 us -> 12.3 us  [hop(): arrived.append(lax.ppermute(value, 'section', [(source, target)]))]
    pallas_call x30 -> x31, Pallas kernels: 20.2 us -> 20.3 us  [call(): pl.pallas_call(kernel, out_shape=outs, in_specs=[pl.BlockSpec(memory_spac...]
  transfers between devices with their start and end apart: 31 -> 31, of which waited for: 7 -> 7; matrix products, arithmetic and copies ran while one was open for 0% -> 0% of each run, Pallas kernels for 11% -> 16%
where the time goes in v4:
time: 92 us; the launch traced here: 91.5 us
  starting transfers between devices  47.4 us (52%)
  waiting for transfers between devices  22.6 us (25%)
  Pallas kernels  20.3 us (22%)
  between operations  1.21 us (1%)
    ppermute x15, starting transfers between devices, shared(): return lax.ppermute(values, ('section', 'img'), pairs)  33.8 us
    pallas_call x31, Pallas kernels, call(): pl.pallas_call(kernel, out_shape=outs, in_specs=[pl.BlockSpec(memory_spac...  20.3 us
    ppermute x12, waiting for transfers between devices, hop(): arrived.append(lax.ppermute(value, 'section', [(source, target)]))  14.7 us
    ppermute x12, starting transfers between devices, hop(): arrived.append(lax.ppermute(value, 'section', [(source, target)]))  12.3 us
    ppermute x15, waiting for transfers between devices, shared(): return lax.ppermute(values, ('section', 'img'), pairs)  7.85 us
  transfers between devices with their start and end apart: 31, of which 7 were waited for; matrix products, arithmetic and copies ran while one was open for 0% of the time, Pallas kernels for 16%

profile of v4, /device:TPU:0, one launch (start us, length us, event | category | flops | bytes accessed | tf_op | source)
XLA Modules:
  0.0 91.5 jit_solution(12504624437950109327)
XLA Ops:
  0.6 1.0 %shard_map.50 = (bf16[2,8,8,320]{3,2,1,0:T(8,128)(2,1)S(1)}, bf16[2,8,8,320]{3,2,1,0:T(8,128)(2,1)S(1)}) custom-call(bf16[1,4,8,8,320]{4,3,2,1,0:T(8,128)(2,1)} %strips_ref.1, bf16[1,4,8,8,320]{4,3,2,1,0:T(8,128)(2,1)} %cotangent_ref.1), custom_call_target="tpu_custom_call" | custom-call | tf_op jit(solution)/shard_map/pallas_call | solution.py:177
  1.6 0.6 collective-permute-start
  2.2 2.3 %shard_map.52.weights_ref.after_ref = bf16[2,3,960,320]{3,2,1,0:T(8,128)(2,1)S(1)} custom-call(bf16[2,3,960,320]{3,2,1,0:T(8,128)(2,1)} %bitcast.11), custom_call_target="tpu_custom_call" | custom-call | tf_op jit(solution)/shard_map/pallas_call | solution.py:177
  4.5 0.0 collective-permute-done.other_ref
  4.5 0.1 shard_map.51
  4.6 1.3 %shard_map.53 = (bf16[128,320]{1,0:T(8,128)(2,1)S(1)}, bf16[2,2,128,320]{3,2,1,0:T(8,128)(2,1)S(1)}, f32[2,128,320]{2,1,0:T(8,128)S(1)}) custom-call(bf16[128,320]{1,0:T(8,128)(2,1)S(1)} %get-tuple-element.57.field_ref.refs_0_.grad_ref, bf16[2,3,960,320]{3,2,1,0:T(8,128)(2,1)S(1)} %shard_map.52.weights_ref.after_ref, ...), custom_call_target="tpu_custom_call" | custom-call | tf_op jit(solution)/shard_map/pallas_call | solution.py:177
  5.9 3.1 %collective-permute-start.2 = (bf16[128,320]{1,0:T(8,128)(2,1)S(1)}, bf16[128,320]{1,0:T(8,128)(2,1)S(1)}, u32[]{:S(2)}, u32[]{:S(2)}) collective-permute-start(bf16[128,320]{1,0:T(8,128)(2,1)S(1)} %get-tuple-element.61.refs_0_), channel_id=1, source_target_pairs={{0,8},{1,9},{2,10},{3,11},{4,12},{5,13},{6,14},{7,15}} | collective-permute-start | bytes 245768 | tf_op jit(solution)/shard_map/ppermute | solution.py:579
  9.0 1.3 %shard_map.54 = (bf16[128,320]{1,0:T(8,128)(2,1)S(1)}, bf16[2,2,128,320]{3,2,1,0:T(8,128)(2,1)S(1)}, f32[2,128,320]{2,1,0:T(8,128)S(1)}) custom-call(bf16[128,320]{1,0:T(8,128)(2,1)S(1)} %get-tuple-element.56.field_ref.refs_1_.refs_2_.grad_ref, ...), custom_call_target="tpu_custom_call", output_to_operand_aliasing={{1}: (3, {}), {2}: (4, {})} | custom-call | tf_op jit(solution)/shard_map/pallas_call | solution.py:177
  10.3 1.3 %collective-permute-start.1 = (bf16[128,320]{1,0:T(8,128)(2,1)S(1)}, bf16[128,320]{1,0:T(8,128)(2,1)S(1)}, u32[]{:S(2)}, u32[]{:S(2)}) collective-permute-start(bf16[128,320]{1,0:T(8,128)(2,1)S(1)} %get-tuple-element.60.refs_1_.refs_2_), channel_id=1, source_target_pairs={{0,8},{1,9},{2,10},{3,11},{4,12},{5,13},{6,14},{7,15}} | collective-permute-start | bytes 245768 | tf_op jit(solution)/shard_map/ppermute | solution.py:579
  11.6 0.1 shard_map.63
  11.7 1.3 %collective-permute-start.10 = (bf16[2,160,256]{2,1,0:T(8,128)(2,1)S(1)}, bf16[2,160,256]{2,1,0:T(8,128)(2,1)S(1)}, u32[]{:S(2)}, u32[]{:S(2)}) collective-permute-start(bf16[2,160,256]{2,1,0:T(8,128)(2,1)S(1)} %shard_map.63), channel_id=1, source_target_pairs={{0,9},{1,10},{2,11},{3,8},{4,13},{5,14},{6,15},{7,12}} | collective-permute-start | bytes 491528 | tf_op jit(solution)/shard_map/ppermute | solution.py:588
  13.0 0.0 collective-permute-done.2.field_ref
  13.0 0.7 collective-permute-start.4
  13.7 0.6 collective-permute-done.1.field_ref
  14.3 0.7 collective-permute-start.3
  15.0 11.9 %collective-permute-start.11 = (bf16[2,160,256]{2,1,0:T(8,128)(2,1)S(1)}, bf16[2,160,256]{2,1,0:T(8,128)(2,1)S(1)}, u32[]{:S(2)}, u32[]{:S(2)}) collective-permute-start(bf16[2,160,256]{2,1,0:T(8,128)(2,1)S(1)} %shard_map.63), channel_id=1, source_target_pairs={{0,10},{1,11},{2,8},{3,9},{4,14},{5,15},{6,12},{7,13}} | collective-permute-start | bytes 491528 | tf_op jit(solution)/shard_map/ppermute | solution.py:588
  26.8 2.3 %collective-permute-start.12 = (bf16[2,160,256]{2,1,0:T(8,128)(2,1)S(1)}, bf16[2,160,256]{2,1,0:T(8,128)(2,1)S(1)}, u32[]{:S(2)}, u32[]{:S(2)}) collective-permute-start(bf16[2,160,256]{2,1,0:T(8,128)(2,1)S(1)} %shard_map.63), channel_id=1, source_target_pairs={{0,11},{1,8},{2,9},{3,10},{4,15},{5,12},{6,13},{7,14}} | collective-permute-start | bytes 491528 | tf_op jit(solution)/shard_map/ppermute | solution.py:588
  29.1 0.1 shard_map.62
  29.2 0.0 collective-permute-done.4.field_ref
  29.2 2.5 %collective-permute-start.7 = (bf16[2,160,256]{2,1,0:T(8,128)(2,1)S(1)}, bf16[2,160,256]{2,1,0:T(8,128)(2,1)S(1)}, u32[]{:S(2)}, u32[]{:S(2)}) collective-permute-start(bf16[2,160,256]{2,1,0:T(8,128)(2,1)S(1)} %shard_map.62), channel_id=1, source_target_pairs={{0,1},{1,2},{2,3},{3,0},{4,5},{5,6},{6,7},{7,4}} | collective-permute-start | bytes 491528 | tf_op jit(solution)/shard_map/ppermute | solution.py:588
  31.7 1.4 %shard_map.57.after_ref.turned_ref = bf16[2,3,960,320]{3,2,1,0:T(8,128)(2,1)S(1)} custom-call(bf16[2,3,960,320]{3,2,1,0:T(8,128)(2,1)S(1)} %shard_map.52.weights_ref.after_ref, bf16[2,2,128,320]{3,2,1,0:T(8,128)(2,1)S(1)} %get-tuple-element.67.after_ref.refs_0_), custom_call_target="tpu_custom_call" | custom-call | tf_op jit(solution)/shard_map/pallas_call | solution.py:177
  33.1 0.7 collective-permute-start.6
  33.8 0.0 collective-permute-done.10.refs_3_
  33.8 0.7 collective-permute-start.5
  34.5 0.0 collective-permute-done.6.field_ref
  34.5 2.4 %collective-permute-start.8 = (bf16[2,160,256]{2,1,0:T(8,128)(2,1)S(1)}, bf16[2,160,256]{2,1,0:T(8,128)(2,1)S(1)}, u32[]{:S(2)}, u32[]{:S(2)}) collective-permute-start(bf16[2,160,256]{2,1,0:T(8,128)(2,1)S(1)} %shard_map.62), channel_id=1, source_target_pairs={{0,2},{1,3},{2,0},{3,1},{4,6},{5,7},{6,4},{7,5}} | collective-permute-start | bytes 491528 | tf_op jit(solution)/shard_map/ppermute | solution.py:588
  36.9 0.0 collective-permute-done.5.field_ref
  36.9 4.7 %collective-permute-start.9 = (bf16[2,160,256]{2,1,0:T(8,128)(2,1)S(1)}, bf16[2,160,256]{2,1,0:T(8,128)(2,1)S(1)}, u32[]{:S(2)}, u32[]{:S(2)}) collective-permute-start(bf16[2,160,256]{2,1,0:T(8,128)(2,1)S(1)} %shard_map.62), channel_id=1, source_target_pairs={{0,3},{1,0},{2,1},{3,2},{4,7},{5,4},{6,5},{7,6}} | collective-permute-start | bytes 491528 | tf_op jit(solution)/shard_map/ppermute | solution.py:588
  41.6 0.1 shard_map.64
  41.8 0.0 collective-permute-done.11.refs_4_
  41.8 0.7 collective-permute-start.13
  42.5 0.0 collective-permute-done.12.refs_5_
  42.5 0.7 collective-permute-start.21
  43.2 0.7 collective-permute-start.14
  43.8 0.2 shard_map.70
  44.0 0.7 collective-permute-start.20
  44.8 1.9 %collective-permute-done.8.refs_1_ = bf16[2,160,256]{2,1,0:T(8,128)(2,1)S(1)} collective-permute-done((bf16[2,160,256]{2,1,0:T(8,128)(2,1)S(1)}, bf16[2,160,256]{2,1,0:T(8,128)(2,1)S(1)}, u32[]{:S(2)}, u32[]{:S(2)}) %collective-permute-start.8) | collective-permute-done | bytes 163872 | tf_op jit(solution)/shard_map/ppermute | solution.py:588
  46.6 0.7 collective-permute-start.23
  47.3 1.4 %collective-permute-done.9.refs_2_ = bf16[2,160,256]{2,1,0:T(8,128)(2,1)S(1)} collective-permute-done((bf16[2,160,256]{2,1,0:T(8,128)(2,1)S(1)}, bf16[2,160,256]{2,1,0:T(8,128)(2,1)S(1)}, u32[]{:S(2)}, u32[]{:S(2)}) %collective-permute-start.9) | collective-permute-done | bytes 163872 | tf_op jit(solution)/shard_map/ppermute | solution.py:588
  48.6 0.7 collective-permute-start.15
  49.3 0.1 shard_map.65
  49.4 0.7 collective-permute-start.16
  50.1 0.7 collective-permute-start.17
  50.8 0.7 collective-permute-start.18
  51.5 0.7 collective-permute-start.22
  52.2 1.3 %collective-permute-start.25 = (bf16[128,320]{1,0:T(8,128)(2,1)S(1)}, bf16[128,320]{1,0:T(8,128)(2,1)S(1)}, u32[]{:S(2)}, u32[]{:S(2)}) collective-permute-start(bf16[128,320]{1,0:T(8,128)(2,1)S(1)} %get-tuple-element.97), channel_id=1, source_target_pairs={{8,0},{9,1},{10,2},{11,3},{12,4},{13,5},{14,6},{15,7}} | collective-permute-start | bytes 245768 | tf_op jit(solution)/shard_map/ppermute | solution.py:579
  53.6 1.3 %collective-permute-start.24 = (bf16[128,320]{1,0:T(8,128)(2,1)S(1)}, bf16[128,320]{1,0:T(8,128)(2,1)S(1)}, u32[]{:S(2)}, u32[]{:S(2)}) collective-permute-start(bf16[128,320]{1,0:T(8,128)(2,1)S(1)} %get-tuple-element.96), channel_id=1, source_target_pairs={{8,0},{9,1},{10,2},{11,3},{12,4},{13,5},{14,6},{15,7}} | collective-permute-start | bytes 245768 | tf_op jit(solution)/shard_map/ppermute | solution.py:579
  54.9 3.1 %shard_map.66 = (bf16[2,4,160,256]{3,2,1,0:T(8,128)(2,1)S(1)}, bf16[2,4,160,256]{3,2,1,0:T(8,128)(2,1)S(1)}) custom-call(bf16[2,2,128,320]{3,2,1,0:T(8,128)(2,1)S(1)} %get-tuple-element.78.saved_ref, bf16[2,3,960,320]{3,2,1,0:T(8,128)(2,1)S(1)} %shard_map.52.weights_ref.after_ref, bf16[2,160,256]{2,1,0:T(8,128)(2,1)S(1)} %collective-permute-done.7.refs_0_, ...), custom_call_target="tpu_custom_call" | custom-call | tf_op jit(solution)/shard_map/pallas_call | solution.py:177
  58.1 0.1 collective-permute-start.19
  58.1 12.8 %collective-permute-done.25.grad_ref = bf16[128,320]{1,0:T(8,128)(2,1)S(1)} collective-permute-done((bf16[128,320]{1,0:T(8,128)(2,1)S(1)}, bf16[128,320]{1,0:T(8,128)(2,1)S(1)}, u32[]{:S(2)}, u32[]{:S(2)}) %collective-permute-start.25) | collective-permute-done | bytes 81952 | tf_op jit(solution)/shard_map/ppermute | solution.py:579
  70.9 1.2 %shard_map.75 = (bf16[2,128,320]{2,1,0:T(8,128)(2,1)S(1)}, bf16[4,2,80,256]{3,2,1,0:T(8,128)(2,1)S(1)}) custom-call(bf16[128,320]{1,0:T(8,128)(2,1)S(1)} %collective-permute-done.25.grad_ref, bf16[2,3,960,320]{3,2,1,0:T(8,128)(2,1)S(1)} %shard_map.57.after_ref.turned_ref, ...), custom_call_target="tpu_custom_call", output_to_operand_aliasing={{0}: (4, {}), {1}: (5, {})} | custom-call | tf_op jit(solution)/shard_map/pallas_call | solution.py:177
  72.2 1.3 %collective-permute-done.24.grad_ref = bf16[128,320]{1,0:T(8,128)(2,1)S(1)} collective-permute-done((bf16[128,320]{1,0:T(8,128)(2,1)S(1)}, bf16[128,320]{1,0:T(8,128)(2,1)S(1)}, u32[]{:S(2)}, u32[]{:S(2)}) %collective-permute-start.24) | collective-permute-done | bytes 81952 | tf_op jit(solution)/shard_map/ppermute | solution.py:579
  73.5 1.2 %shard_map.76 = (bf16[2,128,320]{2,1,0:T(8,128)(2,1)S(1)}, bf16[4,2,80,256]{3,2,1,0:T(8,128)(2,1)S(1)}) custom-call(bf16[128,320]{1,0:T(8,128)(2,1)S(1)} %collective-permute-done.24.grad_ref, bf16[2,3,960,320]{3,2,1,0:T(8,128)(2,1)S(1)} %shard_map.57.after_ref.turned_ref, ...), custom_call_target="tpu_custom_call", output_to_operand_aliasing={{0}: (4, {}), {1}: (5, {})} | custom-call | tf_op jit(solution)/shard_map/pallas_call | solution.py:177
  74.8 2.1 %collective-permute-start.26 = (bf16[2,80,256]{2,1,0:T(8,128)(2,1)S(1)}, bf16[2,80,256]{2,1,0:T(8,128)(2,1)S(1)}, u32[]{:S(2)}, u32[]{:S(2)}) collective-permute-start(bf16[2,80,256]{2,1,0:T(8,128)(2,1)S(1)} %get-tuple-element.108), channel_id=1, source_target_pairs={{0,1},{1,2},{2,3},{3,0},{8,9},{9,10},{10,11},{11,8},{16,17},{17,18... | collective-permute-start | bytes 245768 | tf_op jit(solution)/shard_map/ppermute | solution.py:588
  76.9 2.7 %collective-permute-start.28 = (bf16[2,80,256]{2,1,0:T(8,128)(2,1)S(1)}, bf16[2,80,256]{2,1,0:T(8,128)(2,1)S(1)}, u32[]{:S(2)}, u32[]{:S(2)}) collective-permute-start(bf16[2,80,256]{2,1,0:T(8,128)(2,1)S(1)} %get-tuple-element.106), channel_id=1, source_target_pairs={{0,3},{1,0},{2,1},{3,2},{8,11},{9,8},{10,9},{11,10},{16,19},{17,16... | collective-permute-start | bytes 245768 | tf_op jit(solution)/shard_map/ppermute | solution.py:588
  79.6 2.6 %collective-permute-done.26.refs_1_ = bf16[2,80,256]{2,1,0:T(8,128)(2,1)S(1)} collective-permute-done((bf16[2,80,256]{2,1,0:T(8,128)(2,1)S(1)}, bf16[2,80,256]{2,1,0:T(8,128)(2,1)S(1)}, u32[]{:S(2)}, u32[]{:S(2)}) %collective-permute-start.26) | collective-permute-done | bytes 81952 | tf_op jit(solution)/shard_map/ppermute | solution.py:588
  82.2 2.0 %collective-permute-done.27.refs_2_ = bf16[2,80,256]{2,1,0:T(8,128)(2,1)S(1)} collective-permute-done((bf16[2,80,256]{2,1,0:T(8,128)(2,1)S(1)}, bf16[2,80,256]{2,1,0:T(8,128)(2,1)S(1)}, u32[]{:S(2)}, u32[]{:S(2)}) %collective-permute-start.27) | collective-permute-done | bytes 81952 | tf_op jit(solution)/shard_map/ppermute | solution.py:588
  84.2 0.1 collective-permute-start.29
  84.3 0.1 shard_map.79
  84.4 0.6 collective-permute-start.30
  84.9 1.1 %shard_map.67.refs_0_ = bf16[2,2320,480]{2,1,0:T(8,128)(2,1)S(1)} custom-call(bf16[2,4,160,256]{3,2,1,0:T(8,128)(2,1)S(1)} %get-tuple-element.80.cells_ref), custom_call_target="tpu_custom_call" | custom-call | tf_op jit(solution)/shard_map/pallas_call | solution.py:177
  86.1 0.7 shard_map.80
  86.8 1.1 %shard_map.68.around_ref = bf16[2,2320,480]{2,1,0:T(8,128)(2,1)S(1)} custom-call(bf16[2,4,160,256]{3,2,1,0:T(8,128)(2,1)S(1)} %collective-permute-done.19.cells_ref, bf16[2,2320,480]{2,1,0:T(8,128)(2,1)S(1)} %shard_map.67.refs_0_), custom_call_target="tpu_custom_call", output_to_operand_aliasing={{}: (1, {})} | custom-call | tf_op jit(solution)/shard_map/pallas_call | solution.py:177
  88.0 3.5 %shard_map.78 = f32[2,9,160,80]{3,2,1,0:T(8,128)} custom-call(bf16[2,2320,480]{2,1,0:T(8,128)(2,1)S(1)} %shard_map.68.around_ref, bf16[4,2,80,256]{3,2,1,0:T(8,128)(2,1)S(1)} %shard_map.77.own_ref, bf16[4,2,80,256]{3,2,1,0:T(8,128)(2,1)S(1)} %collective-permute-done.29.other_ref), custom_call_target="tpu_custom_call" | custom-call | tf_op jit(solution)/shard_map/pallas_call | solution.py:177
  (30 shorter events, 0.3 us)
Async XLA Ops:
  1.6 2.9 %collective-permute-start = (bf16[2,8,8,320]{3,2,1,0:T(8,128)(2,1)S(1)}, bf16[2,8,8,320]{3,2,1,0:T(8,128)(2,1)S(1)}, u32[]{:S(2)}, u32[]{:S(2)}) collective-permute-start(bf16[2,8,8,320]{3,2,1,0:T(8,128)(2,1)S(1)} %get-tuple-element.55), channel_id=1, source_target_pairs={{0,4},{4,0},{1,5},{5,1},{2,6},{6,2},{3,7},{7,3},{8,12},{12,8},{9,1... | collective-permute-start | bytes 245768 | tf_op jit(solution)/shard_map/ppermute | solution.py:561
  5.9 7.2 %collective-permute-start.2 = (bf16[128,320]{1,0:T(8,128)(2,1)S(1)}, bf16[128,320]{1,0:T(8,128)(2,1)S(1)}, u32[]{:S(2)}, u32[]{:S(2)}) collective-permute-start(bf16[128,320]{1,0:T(8,128)(2,1)S(1)} %get-tuple-element.61.refs_0_), channel_id=1, source_target_pairs={{0,8},{1,9},{2,10},{3,11},{4,12},{5,13},{6,14},{7,15}} | collective-permute-start | bytes 245768 | tf_op jit(solution)/shard_map/ppermute | solution.py:579
  10.3 4.0 %collective-permute-start.1 = (bf16[128,320]{1,0:T(8,128)(2,1)S(1)}, bf16[128,320]{1,0:T(8,128)(2,1)S(1)}, u32[]{:S(2)}, u32[]{:S(2)}) collective-permute-start(bf16[128,320]{1,0:T(8,128)(2,1)S(1)} %get-tuple-element.60.refs_1_.refs_2_), channel_id=1, source_target_pairs={{0,8},{1,9},{2,10},{3,11},{4,12},{5,13},{6,14},{7,15}} | collective-permute-start | bytes 245768 | tf_op jit(solution)/shard_map/ppermute | solution.py:579
  11.7 22.1 %collective-permute-start.10 = (bf16[2,160,256]{2,1,0:T(8,128)(2,1)S(1)}, bf16[2,160,256]{2,1,0:T(8,128)(2,1)S(1)}, u32[]{:S(2)}, u32[]{:S(2)}) collective-permute-start(bf16[2,160,256]{2,1,0:T(8,128)(2,1)S(1)} %shard_map.63), channel_id=1, source_target_pairs={{0,9},{1,10},{2,11},{3,8},{4,13},{5,14},{6,15},{7,12}} | collective-permute-start | bytes 491528 | tf_op jit(solution)/shard_map/ppermute | solution.py:588
  13.0 16.2 %collective-permute-start.4 = (bf16[128,320]{1,0:T(8,128)(2,1)S(1)}, bf16[128,320]{1,0:T(8,128)(2,1)S(1)}, u32[]{:S(2)}, u32[]{:S(2)}) collective-permute-start(bf16[128,320]{1,0:T(8,128)(2,1)S(1)} %get-tuple-element.68.refs_0_), channel_id=1, source_target_pairs={{8,16},{9,17},{10,18},{11,19},{12,20},{13,21},{14,22},{15,23}} | collective-permute-start | bytes 245768 | tf_op jit(solution)/shard_map/ppermute | solution.py:579
  14.3 18.8 %collective-permute-start.3 = (bf16[128,320]{1,0:T(8,128)(2,1)S(1)}, bf16[128,320]{1,0:T(8,128)(2,1)S(1)}, u32[]{:S(2)}, u32[]{:S(2)}) collective-permute-start(bf16[128,320]{1,0:T(8,128)(2,1)S(1)} %get-tuple-element.66.refs_1_.refs_2_), channel_id=1, source_target_pairs={{8,16},{9,17},{10,18},{11,19},{12,20},{13,21},{14,22},{15,23}} | collective-permute-start | bytes 245768 | tf_op jit(solution)/shard_map/ppermute | solution.py:579
  15.0 26.8 %collective-permute-start.11 = (bf16[2,160,256]{2,1,0:T(8,128)(2,1)S(1)}, bf16[2,160,256]{2,1,0:T(8,128)(2,1)S(1)}, u32[]{:S(2)}, u32[]{:S(2)}) collective-permute-start(bf16[2,160,256]{2,1,0:T(8,128)(2,1)S(1)} %shard_map.63), channel_id=1, source_target_pairs={{0,10},{1,11},{2,8},{3,9},{4,14},{5,15},{6,12},{7,13}} | collective-permute-start | bytes 491528 | tf_op jit(solution)/shard_map/ppermute | solution.py:588
  26.8 15.7 %collective-permute-start.12 = (bf16[2,160,256]{2,1,0:T(8,128)(2,1)S(1)}, bf16[2,160,256]{2,1,0:T(8,128)(2,1)S(1)}, u32[]{:S(2)}, u32[]{:S(2)}) collective-permute-start(bf16[2,160,256]{2,1,0:T(8,128)(2,1)S(1)} %shard_map.63), channel_id=1, source_target_pairs={{0,11},{1,8},{2,9},{3,10},{4,15},{5,12},{6,13},{7,14}} | collective-permute-start | bytes 491528 | tf_op jit(solution)/shard_map/ppermute | solution.py:588
  29.2 13.9 %collective-permute-start.7 = (bf16[2,160,256]{2,1,0:T(8,128)(2,1)S(1)}, bf16[2,160,256]{2,1,0:T(8,128)(2,1)S(1)}, u32[]{:S(2)}, u32[]{:S(2)}) collective-permute-start(bf16[2,160,256]{2,1,0:T(8,128)(2,1)S(1)} %shard_map.62), channel_id=1, source_target_pairs={{0,1},{1,2},{2,3},{3,0},{4,5},{5,6},{6,7},{7,4}} | collective-permute-start | bytes 491528 | tf_op jit(solution)/shard_map/ppermute | solution.py:588
  33.1 1.4 %collective-permute-start.6 = (bf16[128,320]{1,0:T(8,128)(2,1)S(1)}, bf16[128,320]{1,0:T(8,128)(2,1)S(1)}, u32[]{:S(2)}, u32[]{:S(2)}) collective-permute-start(bf16[128,320]{1,0:T(8,128)(2,1)S(1)} %get-tuple-element.73.refs_0_), channel_id=1, source_target_pairs={{16,24},{17,25},{18,26},{19,27},{20,28},{21,29},{22,30},{23,31}} | collective-permute-start | bytes 245768 | tf_op jit(solution)/shard_map/ppermute | solution.py:579
  33.8 3.1 %collective-permute-start.5 = (bf16[128,320]{1,0:T(8,128)(2,1)S(1)}, bf16[128,320]{1,0:T(8,128)(2,1)S(1)}, u32[]{:S(2)}, u32[]{:S(2)}) collective-permute-start(bf16[128,320]{1,0:T(8,128)(2,1)S(1)} %get-tuple-element.72.refs_1_.refs_2_), channel_id=1, source_target_pairs={{16,24},{17,25},{18,26},{19,27},{20,28},{21,29},{22,30},{23,31}} | collective-permute-start | bytes 245768 | tf_op jit(solution)/shard_map/ppermute | solution.py:579
  34.5 12.1 %collective-permute-start.8 = (bf16[2,160,256]{2,1,0:T(8,128)(2,1)S(1)}, bf16[2,160,256]{2,1,0:T(8,128)(2,1)S(1)}, u32[]{:S(2)}, u32[]{:S(2)}) collective-permute-start(bf16[2,160,256]{2,1,0:T(8,128)(2,1)S(1)} %shard_map.62), channel_id=1, source_target_pairs={{0,2},{1,3},{2,0},{3,1},{4,6},{5,7},{6,4},{7,5}} | collective-permute-start | bytes 491528 | tf_op jit(solution)/shard_map/ppermute | solution.py:588
  36.9 11.8 %collective-permute-start.9 = (bf16[2,160,256]{2,1,0:T(8,128)(2,1)S(1)}, bf16[2,160,256]{2,1,0:T(8,128)(2,1)S(1)}, u32[]{:S(2)}, u32[]{:S(2)}) collective-permute-start(bf16[2,160,256]{2,1,0:T(8,128)(2,1)S(1)} %shard_map.62), channel_id=1, source_target_pairs={{0,3},{1,0},{2,1},{3,2},{4,7},{5,4},{6,5},{7,6}} | collective-permute-start | bytes 491528 | tf_op jit(solution)/shard_map/ppermute | solution.py:588
  41.8 7.6 %collective-permute-start.13 = (bf16[2,160,256]{2,1,0:T(8,128)(2,1)S(1)}, bf16[2,160,256]{2,1,0:T(8,128)(2,1)S(1)}, u32[]{:S(2)}, u32[]{:S(2)}) collective-permute-start(bf16[2,160,256]{2,1,0:T(8,128)(2,1)S(1)} %shard_map.64), channel_id=1, source_target_pairs={{8,17},{9,18},{10,19},{11,16},{12,21},{13,22},{14,23},{15,20}} | collective-permute-start | bytes 491528 | tf_op jit(solution)/shard_map/ppermute | solution.py:588
  42.5 1.6 %collective-permute-start.21 = (bf16[128,320]{1,0:T(8,128)(2,1)S(1)}, bf16[128,320]{1,0:T(8,128)(2,1)S(1)}, u32[]{:S(2)}, u32[]{:S(2)}) collective-permute-start(bf16[128,320]{1,0:T(8,128)(2,1)S(1)} %get-tuple-element.85), channel_id=1, source_target_pairs={{24,16},{25,17},{26,18},{27,19},{28,20},{29,21},{30,22},{31,23}} | collective-permute-start | bytes 245768 | tf_op jit(solution)/shard_map/ppermute | solution.py:579
  43.2 7.0 %collective-permute-start.14 = (bf16[2,160,256]{2,1,0:T(8,128)(2,1)S(1)}, bf16[2,160,256]{2,1,0:T(8,128)(2,1)S(1)}, u32[]{:S(2)}, u32[]{:S(2)}) collective-permute-start(bf16[2,160,256]{2,1,0:T(8,128)(2,1)S(1)} %shard_map.64), channel_id=1, source_target_pairs={{8,18},{9,19},{10,16},{11,17},{12,22},{13,23},{14,20},{15,21}} | collective-permute-start | bytes 491528 | tf_op jit(solution)/shard_map/ppermute | solution.py:588
  44.0 6.8 %collective-permute-start.20 = (bf16[128,320]{1,0:T(8,128)(2,1)S(1)}, bf16[128,320]{1,0:T(8,128)(2,1)S(1)}, u32[]{:S(2)}, u32[]{:S(2)}) collective-permute-start(bf16[128,320]{1,0:T(8,128)(2,1)S(1)} %get-tuple-element.84), channel_id=1, source_target_pairs={{24,16},{25,17},{26,18},{27,19},{28,20},{29,21},{30,22},{31,23}} | collective-permute-start | bytes 245768 | tf_op jit(solution)/shard_map/ppermute | solution.py:579
  46.6 4.9 %collective-permute-start.23 = (bf16[128,320]{1,0:T(8,128)(2,1)S(1)}, bf16[128,320]{1,0:T(8,128)(2,1)S(1)}, u32[]{:S(2)}, u32[]{:S(2)}) collective-permute-start(bf16[128,320]{1,0:T(8,128)(2,1)S(1)} %get-tuple-element.91), channel_id=1, source_target_pairs={{16,8},{17,9},{18,10},{19,11},{20,12},{21,13},{22,14},{23,15}} | collective-permute-start | bytes 245768 | tf_op jit(solution)/shard_map/ppermute | solution.py:579
  48.6 4.9 %collective-permute-start.15 = (bf16[2,160,256]{2,1,0:T(8,128)(2,1)S(1)}, bf16[2,160,256]{2,1,0:T(8,128)(2,1)S(1)}, u32[]{:S(2)}, u32[]{:S(2)}) collective-permute-start(bf16[2,160,256]{2,1,0:T(8,128)(2,1)S(1)} %shard_map.64), channel_id=1, source_target_pairs={{8,19},{9,16},{10,17},{11,18},{12,23},{13,20},{14,21},{15,22}} | collective-permute-start | bytes 491528 | tf_op jit(solution)/shard_map/ppermute | solution.py:588
  49.4 5.4 %collective-permute-start.16 = (bf16[2,160,256]{2,1,0:T(8,128)(2,1)S(1)}, bf16[2,160,256]{2,1,0:T(8,128)(2,1)S(1)}, u32[]{:S(2)}, u32[]{:S(2)}) collective-permute-start(bf16[2,160,256]{2,1,0:T(8,128)(2,1)S(1)} %shard_map.65), channel_id=1, source_target_pairs={{16,25},{17,26},{18,27},{19,24},{20,29},{21,30},{22,31},{23,28}} | collective-permute-start | bytes 491528 | tf_op jit(solution)/shard_map/ppermute | solution.py:588
  50.1 4.8 %collective-permute-start.17 = (bf16[2,160,256]{2,1,0:T(8,128)(2,1)S(1)}, bf16[2,160,256]{2,1,0:T(8,128)(2,1)S(1)}, u32[]{:S(2)}, u32[]{:S(2)}) collective-permute-start(bf16[2,160,256]{2,1,0:T(8,128)(2,1)S(1)} %shard_map.65), channel_id=1, source_target_pairs={{16,26},{17,27},{18,24},{19,25},{20,30},{21,31},{22,28},{23,29}} | collective-permute-start | bytes 491528 | tf_op jit(solution)/shard_map/ppermute | solution.py:588
  50.8 4.1 %collective-permute-start.18 = (bf16[2,160,256]{2,1,0:T(8,128)(2,1)S(1)}, bf16[2,160,256]{2,1,0:T(8,128)(2,1)S(1)}, u32[]{:S(2)}, u32[]{:S(2)}) collective-permute-start(bf16[2,160,256]{2,1,0:T(8,128)(2,1)S(1)} %shard_map.65), channel_id=1, source_target_pairs={{16,27},{17,24},{18,25},{19,26},{20,31},{21,28},{22,29},{23,30}} | collective-permute-start | bytes 491528 | tf_op jit(solution)/shard_map/ppermute | solution.py:588
  51.5 0.7 collective-permute-start.22
  52.2 18.7 %collective-permute-start.25 = (bf16[128,320]{1,0:T(8,128)(2,1)S(1)}, bf16[128,320]{1,0:T(8,128)(2,1)S(1)}, u32[]{:S(2)}, u32[]{:S(2)}) collective-permute-start(bf16[128,320]{1,0:T(8,128)(2,1)S(1)} %get-tuple-element.97), channel_id=1, source_target_pairs={{8,0},{9,1},{10,2},{11,3},{12,4},{13,5},{14,6},{15,7}} | collective-permute-start | bytes 245768 | tf_op jit(solution)/shard_map/ppermute | solution.py:579
  53.6 19.9 %collective-permute-start.24 = (bf16[128,320]{1,0:T(8,128)(2,1)S(1)}, bf16[128,320]{1,0:T(8,128)(2,1)S(1)}, u32[]{:S(2)}, u32[]{:S(2)}) collective-permute-start(bf16[128,320]{1,0:T(8,128)(2,1)S(1)} %get-tuple-element.96), channel_id=1, source_target_pairs={{8,0},{9,1},{10,2},{11,3},{12,4},{13,5},{14,6},{15,7}} | collective-permute-start | bytes 245768 | tf_op jit(solution)/shard_map/ppermute | solution.py:579
  58.1 28.7 %collective-permute-start.19 = (bf16[2,4,160,256]{3,2,1,0:T(8,128)(2,1)S(1)}, bf16[2,4,160,256]{3,2,1,0:T(8,128)(2,1)S(1)}, u32[]{:S(2)}, u32[]{:S(2)}) collective-permute-start(bf16[2,4,160,256]{3,2,1,0:T(8,128)(2,1)S(1)} %get-tuple-element.79), channel_id=1, source_target_pairs={{0,4},{4,0},{1,5},{5,1},{2,6},{6,2},{3,7},{7,3},{8,12},{12,8},{9,1... | collective-permute-start | bytes 1966088 | tf_op jit(solution)/shard_map/ppermute | solution.py:561
  74.8 7.4 %collective-permute-start.26 = (bf16[2,80,256]{2,1,0:T(8,128)(2,1)S(1)}, bf16[2,80,256]{2,1,0:T(8,128)(2,1)S(1)}, u32[]{:S(2)}, u32[]{:S(2)}) collective-permute-start(bf16[2,80,256]{2,1,0:T(8,128)(2,1)S(1)} %get-tuple-element.108), channel_id=1, source_target_pairs={{0,1},{1,2},{2,3},{3,0},{8,9},{9,10},{10,11},{11,8},{16,17},{17,18... | collective-permute-start | bytes 245768 | tf_op jit(solution)/shard_map/ppermute | solution.py:588
  76.9 7.3 %collective-permute-start.27 = (bf16[2,80,256]{2,1,0:T(8,128)(2,1)S(1)}, bf16[2,80,256]{2,1,0:T(8,128)(2,1)S(1)}, u32[]{:S(2)}, u32[]{:S(2)}) collective-permute-start(bf16[2,80,256]{2,1,0:T(8,128)(2,1)S(1)} %get-tuple-element.107), channel_id=1, source_target_pairs={{0,2},{1,3},{2,0},{3,1},{8,10},{9,11},{10,8},{11,9},{16,18},{17,19... | collective-permute-start | bytes 245768 | tf_op jit(solution)/shard_map/ppermute | solution.py:588
  76.9 7.3 %collective-permute-start.28 = (bf16[2,80,256]{2,1,0:T(8,128)(2,1)S(1)}, bf16[2,80,256]{2,1,0:T(8,128)(2,1)S(1)}, u32[]{:S(2)}, u32[]{:S(2)}) collective-permute-start(bf16[2,80,256]{2,1,0:T(8,128)(2,1)S(1)} %get-tuple-element.106), channel_id=1, source_target_pairs={{0,3},{1,0},{2,1},{3,2},{8,11},{9,8},{10,9},{11,10},{16,19},{17,16... | collective-permute-start | bytes 245768 | tf_op jit(solution)/shard_map/ppermute | solution.py:588
  84.2 3.7 %collective-permute-start.29 = (bf16[4,2,80,256]{3,2,1,0:T(8,128)(2,1)S(1)}, bf16[4,2,80,256]{3,2,1,0:T(8,128)(2,1)S(1)}, u32[]{:S(2)}, u32[]{:S(2)}) collective-permute-start(bf16[4,2,80,256]{3,2,1,0:T(8,128)(2,1)S(1)} %shard_map.77.own_ref), channel_id=1, source_target_pairs={{0,4},{4,0},{1,5},{5,1},{2,6},{6,2},{3,7},{7,3},{8,12},{12,8},{9,1... | collective-permute-start | bytes 983048 | tf_op jit(solution)/shard_map/ppermute | solution.py:561
  84.4 1.7 %collective-permute-start.30 = (bf16[2,8,8,320]{3,2,1,0:T(8,128)(2,1)S(1)}, bf16[2,8,8,320]{3,2,1,0:T(8,128)(2,1)S(1)}, u32[]{:S(2)}, u32[]{:S(2)}) collective-permute-start(bf16[2,8,8,320]{3,2,1,0:T(8,128)(2,1)S(1)} %get-tuple-element.105), channel_id=1, source_target_pairs={{0,4},{4,0},{1,5},{5,1},{2,6},{6,2},{3,7},{7,3},{8,12},{12,8},{9,1... | collective-permute-start | bytes 245768 | tf_op jit(solution)/shard_map/ppermute | solution.py:561

commit v5 on v4

--- a/solution.py
+++ b/solution.py
@@ -453,10 +453,10 @@
     return stacked
 
 
-def remake_call(saved, weights, received, width):
+def remake_call(saved, weights, soon, late, late_from, width):
     _, crops, count, channels = saved.shape
     share = channels // 2
-    sections, each = len(received), len(received[0])
+    each = len(soon)
 
     def kernel(saved_ref, weights_ref, *refs):
         home_ref, outer_ref, taps, shifted = refs[-4:]
@@ -472,14 +472,12 @@
         for crop in range(crops):
             for kind in range(2):
                 put(kind, 0, crop, saved_ref[kind, crop])
-        for section in range(sections):
-
-            @pl.when(lax.axis_index("section") == section)
-            def _():
-                for block in range(each):
-                    home_ref[0, 1 + block] = refs[section * each + block][0]
-                    outer_ref[0, 1 + block] = refs[section * each + block][1]
-
+        is_late = lax.axis_index("section") >= late_from
+        for block in range(each):
+            for slot, ref in enumerate((home_ref, outer_ref)):
+                ref[0, 1 + block] = jnp.where(
+                    is_late, refs[each + block][slot], refs[block][slot]
+                )
         for block in range(1, 1 + each):
             for crop in range(crops):
                 cells = slice(crop * count, (crop + 1) * count)
@@ -494,7 +492,7 @@
         pltpu.VMEM((count + 2 * width, 3 * channels), jnp.bfloat16),
         pltpu.VMEM((count + 16, channels), jnp.float32),
     ]
-    operands = [saved, weights, *[array for arrays in received for array in arrays]]
+    operands = [saved, weights, *soon, *late]
     return call(kernel, [out, out], operands, (), scratch, {})
 
 
@@ -569,7 +567,7 @@
     count = row_count * width
     crops = images * strip_count // slabs
     last = sections - 1
-    early = min(1, last - 1)
+    early, middle, late_from = min(1, last - 1), min(2, last), max(1, sections - 2)
     steps = range(1, groups)
     scaling = 1.0 / math.sqrt(images * groups * strip_count * count)
 
@@ -581,8 +579,8 @@
 
     def shared(values, step, routes):
         pairs = [
-            (source * groups + i, target * groups + (i + step) % groups)
-            for source, target in routes
+            (place * groups + i, place * groups + (i + step) % groups)
+            for place in routes
             for i in range(groups)
         ]
         return lax.ppermute(values, ("section", "img"), pairs)
@@ -590,8 +588,8 @@
     def swapped(value):
         return rotated(value, "slab", 1)
 
-    def flipped(values):
-        return flip_call([(value, Ellipsis) for value in values], slabs, "slab", values[-1])
+    def flipped(saved, after):
+        return flip_call([(saved, (0, crop)) for crop in range(crops)], slabs, "slab", after)
 
     own, other = split_call(
         pltpu.with_memory_space_constraint(strips, pltpu.HBM),
@@ -603,7 +601,7 @@
     weights = load_call(pltpu.with_memory_space_constraint(weights, pltpu.HBM))
     fields = join_call(own, other)
     incoming = fields
-    state, received = [], [None] * sections
+    state = []
     turned, after = None, weights
     for place in range(sections):
         outgoing = []
@@ -614,12 +612,9 @@
             outgoing.append(out)
         if place < last:
             incoming = hop(outgoing, place, place + 1)
-            handed = flipped(outgoing)
-            routes = [(place, place + 1)]
-            received[place + 1] = [shared(handed, step, routes) for step in steps]
         if place == early:
-            handed = flipped(fields)
-            received[0] = [shared(handed, step, [(0, 0)]) for step in steps]
+            inputs = flipped(state[0], state[1])
+            soon = [shared(inputs, step, range(late_from)) for step in steps]
             turned = turn_call(weights, state[0])
             after = turned
     saved, hidden = state
@@ -635,12 +630,14 @@
             outgoing.append(out)
         if place:
             incoming = hop(outgoing, place, place - 1)
+        if place == middle:
+            inputs = flipped(saved, outgoing[-1])
+            late = [shared(inputs, step, range(late_from, sections)) for step in steps]
     kept, sent = grads
     own = [sent[0]]
-    everywhere = [(place, place) for place in range(sections)]
     for step in steps:
-        own.append(shared(sent[step], step, everywhere))
-    home, outer = remake_call(saved, weights, received, width)
+        own.append(shared(sent[step], step, range(sections)))
+    home, outer = remake_call(saved, weights, soon, late, late_from, width)
     outer = swapped(outer)
     around = spread_call(home, None, 0, count, width)
     around = spread_call(outer, around, 1, count, width)

time: 92 us -> 81.5 us (0.89)
  starting transfers between devices: 47.4 us -> 30.7 us
  waiting for transfers between devices: 22.6 us -> 29.4 us
    ppermute x15 -> x9, starting transfers between devices: 33.8 us -> 17.1 us  [shared(): return lax.ppermute(values, ('section', 'img'), pairs)]
    ppermute x12, waiting for transfers between devices: 14.7 us -> 23.3 us  [hop(): arrived.append(lax.ppermute(value, 'section', [(source, target)]))]
    ppermute x15 -> x9, waiting for transfers between devices: 7.85 us -> 6.12 us  [shared(): return lax.ppermute(values, ('section', 'img'), pairs)]
    pallas_call x31 -> x29, Pallas kernels: 20.3 us -> 19.9 us  [call(): pl.pallas_call(kernel, out_shape=outs, in_specs=[pl.BlockSpec(memory_spac...]
  transfers between devices with their start and end apart: 31 -> 25, of which waited for: 7 -> 8; matrix products, arithmetic and copies ran while one was open for 0% -> 0% of each run, Pallas kernels for 16% -> 17%
where the time goes in v5:
time: 81.5 us; the launch traced here: 81.1 us
  starting transfers between devices  30.7 us (38%)
  waiting for transfers between devices  29.4 us (36%)
  Pallas kernels  19.9 us (24%)
  between operations  1.08 us (1%)
    ppermute x12, waiting for transfers between devices, hop(): arrived.append(lax.ppermute(value, 'section', [(source, target)]))  23.3 us
    pallas_call x29, Pallas kernels, call(): pl.pallas_call(kernel, out_shape=outs, in_specs=[pl.BlockSpec(memory_spac...  19.9 us
    ppermute x9, starting transfers between devices, shared(): return lax.ppermute(values, ('section', 'img'), pairs)  17.1 us
    ppermute x12, starting transfers between devices, hop(): arrived.append(lax.ppermute(value, 'section', [(source, target)]))  12.3 us
    ppermute x9, waiting for transfers between devices, shared(): return lax.ppermute(values, ('section', 'img'), pairs)  6.12 us
  transfers between devices with their start and end apart: 25, of which 8 were waited for; matrix products, arithmetic and copies ran while one was open for 0% of the time, Pallas kernels for 17%

profile of v5, /device:TPU:0, one launch (start us, length us, event | category | flops | bytes accessed | tf_op | source)
XLA Modules:
  0.0 81.1 jit_solution(3076255130942231088)
XLA Ops:
  0.6 1.0 %shard_map.50 = (bf16[2,8,8,320]{3,2,1,0:T(8,128)(2,1)S(1)}, bf16[2,8,8,320]{3,2,1,0:T(8,128)(2,1)S(1)}) custom-call(bf16[1,4,8,8,320]{4,3,2,1,0:T(8,128)(2,1)} %strips_ref.1, bf16[1,4,8,8,320]{4,3,2,1,0:T(8,128)(2,1)} %cotangent_ref.1), custom_call_target="tpu_custom_call" | custom-call | tf_op jit(solution)/shard_map/pallas_call | solution.py:177
  1.6 0.6 collective-permute-start
  2.2 2.3 %shard_map.52.weights_ref.after_ref = bf16[2,3,960,320]{3,2,1,0:T(8,128)(2,1)S(1)} custom-call(bf16[2,3,960,320]{3,2,1,0:T(8,128)(2,1)} %bitcast.11), custom_call_target="tpu_custom_call" | custom-call | tf_op jit(solution)/shard_map/pallas_call | solution.py:177
  4.5 0.0 collective-permute-done.other_ref
  4.5 0.1 shard_map.51
  4.6 1.3 %shard_map.53 = (bf16[128,320]{1,0:T(8,128)(2,1)S(1)}, bf16[2,2,128,320]{3,2,1,0:T(8,128)(2,1)S(1)}, f32[2,128,320]{2,1,0:T(8,128)S(1)}) custom-call(bf16[128,320]{1,0:T(8,128)(2,1)S(1)} %get-tuple-element.57.field_ref.grad_ref, bf16[2,3,960,320]{3,2,1,0:T(8,128)(2,1)S(1)} %shard_map.52.weights_ref.after_ref, ...), custom_call_target="tpu_custom_call" | custom-call | tf_op jit(solution)/shard_map/pallas_call | solution.py:177
  5.9 3.1 %collective-permute-start.2 = (bf16[128,320]{1,0:T(8,128)(2,1)S(1)}, bf16[128,320]{1,0:T(8,128)(2,1)S(1)}, u32[]{:S(2)}, u32[]{:S(2)}) collective-permute-start(bf16[128,320]{1,0:T(8,128)(2,1)S(1)} %get-tuple-element.61), channel_id=1, source_target_pairs={{0,8},{1,9},{2,10},{3,11},{4,12},{5,13},{6,14},{7,15}} | collective-permute-start | bytes 245768 | tf_op jit(solution)/shard_map/ppermute | solution.py:577
  9.0 1.3 %shard_map.54 = (bf16[128,320]{1,0:T(8,128)(2,1)S(1)}, bf16[2,2,128,320]{3,2,1,0:T(8,128)(2,1)S(1)}, f32[2,128,320]{2,1,0:T(8,128)S(1)}) custom-call(bf16[128,320]{1,0:T(8,128)(2,1)S(1)} %get-tuple-element.56.field_ref.grad_ref, bf16[2,3,960,320]{3,2,1,0:T(8,128)(2,1)S(1)} %shard_map.52.weights_ref.after_ref, ...), custom_call_target="tpu_custom_call", output_to_operand_aliasing={{1}: (3, {}), {2}: (4, {})} | custom-call | tf_op jit(solution)/shard_map/pallas_call | solution.py:177
  10.3 1.3 %collective-permute-start.1 = (bf16[128,320]{1,0:T(8,128)(2,1)S(1)}, bf16[128,320]{1,0:T(8,128)(2,1)S(1)}, u32[]{:S(2)}, u32[]{:S(2)}) collective-permute-start(bf16[128,320]{1,0:T(8,128)(2,1)S(1)} %get-tuple-element.60), channel_id=1, source_target_pairs={{0,8},{1,9},{2,10},{3,11},{4,12},{5,13},{6,14},{7,15}} | collective-permute-start | bytes 245768 | tf_op jit(solution)/shard_map/ppermute | solution.py:577
  11.6 0.1 collective-permute-done.2.field_ref
  11.7 0.7 collective-permute-start.4
  12.3 1.9 %collective-permute-done.1.field_ref = bf16[128,320]{1,0:T(8,128)(2,1)S(1)} collective-permute-done((bf16[128,320]{1,0:T(8,128)(2,1)S(1)}, bf16[128,320]{1,0:T(8,128)(2,1)S(1)}, u32[]{:S(2)}, u32[]{:S(2)}) %collective-permute-start.1) | collective-permute-done | bytes 81952 | tf_op jit(solution)/shard_map/ppermute | solution.py:577
  14.3 0.7 collective-permute-start.3
  15.0 1.4 %shard_map.57.after_ref.turned_ref = bf16[2,3,960,320]{3,2,1,0:T(8,128)(2,1)S(1)} custom-call(bf16[2,3,960,320]{3,2,1,0:T(8,128)(2,1)S(1)} %shard_map.52.weights_ref.after_ref, bf16[2,2,128,320]{3,2,1,0:T(8,128)(2,1)S(1)} %get-tuple-element.67.after_ref.refs_0_), custom_call_target="tpu_custom_call" | custom-call | tf_op jit(solution)/shard_map/pallas_call | solution.py:177
  16.3 0.1 shard_map.62
  16.4 0.0 collective-permute-done.4.field_ref
  16.5 0.7 collective-permute-start.6
  17.1 0.0 collective-permute-done.3.field_ref
  17.2 0.7 collective-permute-start.5
  17.8 3.5 %collective-permute-start.7 = (bf16[2,160,256]{2,1,0:T(8,128)(2,1)S(1)}, bf16[2,160,256]{2,1,0:T(8,128)(2,1)S(1)}, u32[]{:S(2)}, u32[]{:S(2)}) collective-permute-start(bf16[2,160,256]{2,1,0:T(8,128)(2,1)S(1)} %shard_map.62), channel_id=1, source_target_pairs={{0,1},{1,2},{2,3},{3,0},{8,9},{9,10},{10,11},{11,8},{4,5},{5,6},{6... | collective-permute-start | bytes 491528 | tf_op jit(solution)/shard_map/ppermute | solution.py:586
  21.3 4.5 %collective-permute-start.8 = (bf16[2,160,256]{2,1,0:T(8,128)(2,1)S(1)}, bf16[2,160,256]{2,1,0:T(8,128)(2,1)S(1)}, u32[]{:S(2)}, u32[]{:S(2)}) collective-permute-start(bf16[2,160,256]{2,1,0:T(8,128)(2,1)S(1)} %shard_map.62), channel_id=1, source_target_pairs={{0,2},{1,3},{2,0},{3,1},{8,10},{9,11},{10,8},{11,9},{4,6},{5,7},{6... | collective-permute-start | bytes 491528 | tf_op jit(solution)/shard_map/ppermute | solution.py:586
  25.8 0.0 collective-permute-done.6.field_ref
  25.8 0.0 collective-permute-done.5.field_ref
  25.9 0.7 collective-permute-start.11
  26.6 0.2 shard_map.64
  26.8 0.7 collective-permute-start.10
  27.4 0.0 collective-permute-done.11.grad_ref
  27.5 0.7 collective-permute-start.17
  28.2 3.3 %collective-permute-start.9 = (bf16[2,160,256]{2,1,0:T(8,128)(2,1)S(1)}, bf16[2,160,256]{2,1,0:T(8,128)(2,1)S(1)}, u32[]{:S(2)}, u32[]{:S(2)}) collective-permute-start(bf16[2,160,256]{2,1,0:T(8,128)(2,1)S(1)} %shard_map.62), channel_id=1, source_target_pairs={{0,3},{1,0},{2,1},{3,2},{8,11},{9,8},{10,9},{11,10},{4,7},{5,4},{6... | collective-permute-start | bytes 491528 | tf_op jit(solution)/shard_map/ppermute | solution.py:586
  31.5 0.0 collective-permute-done.10.grad_ref
  31.5 0.1 shard_map.67
  31.6 0.7 collective-permute-start.12
  32.3 0.0 collective-permute-done.7.refs_0_
  32.3 0.7 collective-permute-start.13
  33.0 1.5 %collective-permute-done.8.refs_1_ = bf16[2,160,256]{2,1,0:T(8,128)(2,1)S(1)} collective-permute-done((bf16[2,160,256]{2,1,0:T(8,128)(2,1)S(1)}, bf16[2,160,256]{2,1,0:T(8,128)(2,1)S(1)}, u32[]{:S(2)}, u32[]{:S(2)}) %collective-permute-start.8) | collective-permute-done | bytes 163872 | tf_op jit(solution)/shard_map/ppermute | solution.py:586
  34.4 0.7 collective-permute-start.14
  35.1 0.0 collective-permute-done.17.grad_ref
  35.1 0.7 collective-permute-start.16
  35.8 0.0 collective-permute-done.16.grad_ref
  35.8 1.3 %collective-permute-start.19 = (bf16[128,320]{1,0:T(8,128)(2,1)S(1)}, bf16[128,320]{1,0:T(8,128)(2,1)S(1)}, u32[]{:S(2)}, u32[]{:S(2)}) collective-permute-start(bf16[128,320]{1,0:T(8,128)(2,1)S(1)} %get-tuple-element.97), channel_id=1, source_target_pairs={{8,0},{9,1},{10,2},{11,3},{12,4},{13,5},{14,6},{15,7}} | collective-permute-start | bytes 245768 | tf_op jit(solution)/shard_map/ppermute | solution.py:577
  37.2 0.7 collective-permute-done.9.refs_2_
  37.8 1.3 %collective-permute-start.18 = (bf16[128,320]{1,0:T(8,128)(2,1)S(1)}, bf16[128,320]{1,0:T(8,128)(2,1)S(1)}, u32[]{:S(2)}, u32[]{:S(2)}) collective-permute-start(bf16[128,320]{1,0:T(8,128)(2,1)S(1)} %get-tuple-element.96), channel_id=1, source_target_pairs={{8,0},{9,1},{10,2},{11,3},{12,4},{13,5},{14,6},{15,7}} | collective-permute-start | bytes 245768 | tf_op jit(solution)/shard_map/ppermute | solution.py:577
  39.1 0.0 collective-permute-done.12.refs_3_
  39.1 0.0 collective-permute-done.14.refs_5_
  39.1 3.0 %shard_map.68 = (bf16[2,4,160,256]{3,2,1,0:T(8,128)(2,1)S(1)}, bf16[2,4,160,256]{3,2,1,0:T(8,128)(2,1)S(1)}) custom-call(bf16[2,2,128,320]{3,2,1,0:T(8,128)(2,1)S(1)} %get-tuple-element.78.refs_0_.saved_ref, bf16[2,3,960,320]{3,2,1,0:T(8,128)(2,1)S(1)} %shard_map.52.weights_ref.after_ref, bf16[2,160,256]{2,1,0:T(8,128)(2,1)S(1)} %collective-permute-done.7.refs_0_, ...), custom_call_target="tpu_custom_call" | custom-call | tf_op jit(solution)/shard_map/pallas_call | solution.py:177
  42.1 0.1 collective-permute-start.15
  42.2 19.9 %collective-permute-done.19.grad_ref = bf16[128,320]{1,0:T(8,128)(2,1)S(1)} collective-permute-done((bf16[128,320]{1,0:T(8,128)(2,1)S(1)}, bf16[128,320]{1,0:T(8,128)(2,1)S(1)}, u32[]{:S(2)}, u32[]{:S(2)}) %collective-permute-start.19) | collective-permute-done | bytes 81952 | tf_op jit(solution)/shard_map/ppermute | solution.py:577
  62.1 1.2 %shard_map.73 = (bf16[2,128,320]{2,1,0:T(8,128)(2,1)S(1)}, bf16[4,2,80,256]{3,2,1,0:T(8,128)(2,1)S(1)}) custom-call(bf16[128,320]{1,0:T(8,128)(2,1)S(1)} %collective-permute-done.19.grad_ref, bf16[2,3,960,320]{3,2,1,0:T(8,128)(2,1)S(1)} %shard_map.57.after_ref.turned_ref, ...), custom_call_target="tpu_custom_call", output_to_operand_aliasing={{0}: (4, {}), {1}: (5, {})} | custom-call | tf_op jit(solution)/shard_map/pallas_call | solution.py:177
  63.3 1.3 %collective-permute-done.18.grad_ref = bf16[128,320]{1,0:T(8,128)(2,1)S(1)} collective-permute-done((bf16[128,320]{1,0:T(8,128)(2,1)S(1)}, bf16[128,320]{1,0:T(8,128)(2,1)S(1)}, u32[]{:S(2)}, u32[]{:S(2)}) %collective-permute-start.18) | collective-permute-done | bytes 81952 | tf_op jit(solution)/shard_map/ppermute | solution.py:577
  64.7 1.2 %shard_map.74 = (bf16[2,128,320]{2,1,0:T(8,128)(2,1)S(1)}, bf16[4,2,80,256]{3,2,1,0:T(8,128)(2,1)S(1)}) custom-call(bf16[128,320]{1,0:T(8,128)(2,1)S(1)} %collective-permute-done.18.grad_ref, bf16[2,3,960,320]{3,2,1,0:T(8,128)(2,1)S(1)} %shard_map.57.after_ref.turned_ref, ...), custom_call_target="tpu_custom_call", output_to_operand_aliasing={{0}: (4, {}), {1}: (5, {})} | custom-call | tf_op jit(solution)/shard_map/pallas_call | solution.py:177
  65.9 0.8 collective-permute-start.20
  66.7 0.4 collective-permute-start.21
  67.0 2.7 %collective-permute-start.22 = (bf16[2,80,256]{2,1,0:T(8,128)(2,1)S(1)}, bf16[2,80,256]{2,1,0:T(8,128)(2,1)S(1)}, u32[]{:S(2)}, u32[]{:S(2)}) collective-permute-start(bf16[2,80,256]{2,1,0:T(8,128)(2,1)S(1)} %get-tuple-element.106), channel_id=1, source_target_pairs={{0,3},{1,0},{2,1},{3,2},{8,11},{9,8},{10,9},{11,10},{16,19},{17,16... | collective-permute-start | bytes 245768 | tf_op jit(solution)/shard_map/ppermute | solution.py:586
  69.8 2.6 %collective-permute-done.20.refs_1_ = bf16[2,80,256]{2,1,0:T(8,128)(2,1)S(1)} collective-permute-done((bf16[2,80,256]{2,1,0:T(8,128)(2,1)S(1)}, bf16[2,80,256]{2,1,0:T(8,128)(2,1)S(1)}, u32[]{:S(2)}, u32[]{:S(2)}) %collective-permute-start.20) | collective-permute-done | bytes 81952 | tf_op jit(solution)/shard_map/ppermute | solution.py:586
  72.3 1.4 %collective-permute-done.21.refs_2_ = bf16[2,80,256]{2,1,0:T(8,128)(2,1)S(1)} collective-permute-done((bf16[2,80,256]{2,1,0:T(8,128)(2,1)S(1)}, bf16[2,80,256]{2,1,0:T(8,128)(2,1)S(1)}, u32[]{:S(2)}, u32[]{:S(2)}) %collective-permute-start.21) | collective-permute-done | bytes 81952 | tf_op jit(solution)/shard_map/ppermute | solution.py:586
  73.8 0.0 collective-permute-done.22.refs_3_
  73.8 0.1 collective-permute-start.23
  73.9 0.1 shard_map.77
  73.9 0.6 collective-permute-start.24
  74.5 1.1 %shard_map.69.refs_0_ = bf16[2,2320,480]{2,1,0:T(8,128)(2,1)S(1)} custom-call(bf16[2,4,160,256]{3,2,1,0:T(8,128)(2,1)S(1)} %get-tuple-element.90.cells_ref), custom_call_target="tpu_custom_call" | custom-call | tf_op jit(solution)/shard_map/pallas_call | solution.py:177
  75.7 0.7 shard_map.78
  76.4 1.1 %shard_map.70.around_ref = bf16[2,2320,480]{2,1,0:T(8,128)(2,1)S(1)} custom-call(bf16[2,4,160,256]{3,2,1,0:T(8,128)(2,1)S(1)} %collective-permute-done.15.cells_ref, bf16[2,2320,480]{2,1,0:T(8,128)(2,1)S(1)} %shard_map.69.refs_0_), custom_call_target="tpu_custom_call", output_to_operand_aliasing={{}: (1, {})} | custom-call | tf_op jit(solution)/shard_map/pallas_call | solution.py:177
  77.5 0.0 collective-permute-done.23.other_ref
  77.5 3.5 %shard_map.76 = f32[2,9,160,80]{3,2,1,0:T(8,128)} custom-call(bf16[2,2320,480]{2,1,0:T(8,128)(2,1)S(1)} %shard_map.70.around_ref, bf16[4,2,80,256]{3,2,1,0:T(8,128)(2,1)S(1)} %shard_map.75.own_ref, bf16[4,2,80,256]{3,2,1,0:T(8,128)(2,1)S(1)} %collective-permute-done.23.other_ref), custom_call_target="tpu_custom_call" | custom-call | tf_op jit(solution)/shard_map/pallas_call | solution.py:177
  (16 shorter events, 0.2 us)
Async XLA Ops:
  1.6 2.9 %collective-permute-start = (bf16[2,8,8,320]{3,2,1,0:T(8,128)(2,1)S(1)}, bf16[2,8,8,320]{3,2,1,0:T(8,128)(2,1)S(1)}, u32[]{:S(2)}, u32[]{:S(2)}) collective-permute-start(bf16[2,8,8,320]{3,2,1,0:T(8,128)(2,1)S(1)} %get-tuple-element.55), channel_id=1, source_target_pairs={{0,4},{4,0},{1,5},{5,1},{2,6},{6,2},{3,7},{7,3},{8,12},{12,8},{9,1... | collective-permute-start | bytes 245768 | tf_op jit(solution)/shard_map/ppermute | solution.py:559
  5.9 5.8 %collective-permute-start.2 = (bf16[128,320]{1,0:T(8,128)(2,1)S(1)}, bf16[128,320]{1,0:T(8,128)(2,1)S(1)}, u32[]{:S(2)}, u32[]{:S(2)}) collective-permute-start(bf16[128,320]{1,0:T(8,128)(2,1)S(1)} %get-tuple-element.61), channel_id=1, source_target_pairs={{0,8},{1,9},{2,10},{3,11},{4,12},{5,13},{6,14},{7,15}} | collective-permute-start | bytes 245768 | tf_op jit(solution)/shard_map/ppermute | solution.py:577
  10.3 4.0 %collective-permute-start.1 = (bf16[128,320]{1,0:T(8,128)(2,1)S(1)}, bf16[128,320]{1,0:T(8,128)(2,1)S(1)}, u32[]{:S(2)}, u32[]{:S(2)}) collective-permute-start(bf16[128,320]{1,0:T(8,128)(2,1)S(1)} %get-tuple-element.60), channel_id=1, source_target_pairs={{0,8},{1,9},{2,10},{3,11},{4,12},{5,13},{6,14},{7,15}} | collective-permute-start | bytes 245768 | tf_op jit(solution)/shard_map/ppermute | solution.py:577
  11.7 4.7 %collective-permute-start.4 = (bf16[128,320]{1,0:T(8,128)(2,1)S(1)}, bf16[128,320]{1,0:T(8,128)(2,1)S(1)}, u32[]{:S(2)}, u32[]{:S(2)}) collective-permute-start(bf16[128,320]{1,0:T(8,128)(2,1)S(1)} %get-tuple-element.68), channel_id=1, source_target_pairs={{8,16},{9,17},{10,18},{11,19},{12,20},{13,21},{14,22},{15,23}} | collective-permute-start | bytes 245768 | tf_op jit(solution)/shard_map/ppermute | solution.py:577
  14.3 2.8 %collective-permute-start.3 = (bf16[128,320]{1,0:T(8,128)(2,1)S(1)}, bf16[128,320]{1,0:T(8,128)(2,1)S(1)}, u32[]{:S(2)}, u32[]{:S(2)}) collective-permute-start(bf16[128,320]{1,0:T(8,128)(2,1)S(1)} %get-tuple-element.66), channel_id=1, source_target_pairs={{8,16},{9,17},{10,18},{11,19},{12,20},{13,21},{14,22},{15,23}} | collective-permute-start | bytes 245768 | tf_op jit(solution)/shard_map/ppermute | solution.py:577
  16.5 9.3 %collective-permute-start.6 = (bf16[128,320]{1,0:T(8,128)(2,1)S(1)}, bf16[128,320]{1,0:T(8,128)(2,1)S(1)}, u32[]{:S(2)}, u32[]{:S(2)}) collective-permute-start(bf16[128,320]{1,0:T(8,128)(2,1)S(1)} %get-tuple-element.73), channel_id=1, source_target_pairs={{16,24},{17,25},{18,26},{19,27},{20,28},{21,29},{22,30},{23,31}} | collective-permute-start | bytes 245768 | tf_op jit(solution)/shard_map/ppermute | solution.py:577
  17.2 8.7 %collective-permute-start.5 = (bf16[128,320]{1,0:T(8,128)(2,1)S(1)}, bf16[128,320]{1,0:T(8,128)(2,1)S(1)}, u32[]{:S(2)}, u32[]{:S(2)}) collective-permute-start(bf16[128,320]{1,0:T(8,128)(2,1)S(1)} %get-tuple-element.72), channel_id=1, source_target_pairs={{16,24},{17,25},{18,26},{19,27},{20,28},{21,29},{22,30},{23,31}} | collective-permute-start | bytes 245768 | tf_op jit(solution)/shard_map/ppermute | solution.py:577
  17.8 14.4 %collective-permute-start.7 = (bf16[2,160,256]{2,1,0:T(8,128)(2,1)S(1)}, bf16[2,160,256]{2,1,0:T(8,128)(2,1)S(1)}, u32[]{:S(2)}, u32[]{:S(2)}) collective-permute-start(bf16[2,160,256]{2,1,0:T(8,128)(2,1)S(1)} %shard_map.62), channel_id=1, source_target_pairs={{0,1},{1,2},{2,3},{3,0},{8,9},{9,10},{10,11},{11,8},{4,5},{5,6},{6... | collective-permute-start | bytes 491528 | tf_op jit(solution)/shard_map/ppermute | solution.py:586
  21.3 13.1 %collective-permute-start.8 = (bf16[2,160,256]{2,1,0:T(8,128)(2,1)S(1)}, bf16[2,160,256]{2,1,0:T(8,128)(2,1)S(1)}, u32[]{:S(2)}, u32[]{:S(2)}) collective-permute-start(bf16[2,160,256]{2,1,0:T(8,128)(2,1)S(1)} %shard_map.62), channel_id=1, source_target_pairs={{0,2},{1,3},{2,0},{3,1},{8,10},{9,11},{10,8},{11,9},{4,6},{5,7},{6... | collective-permute-start | bytes 491528 | tf_op jit(solution)/shard_map/ppermute | solution.py:586
  25.9 1.6 %collective-permute-start.11 = (bf16[128,320]{1,0:T(8,128)(2,1)S(1)}, bf16[128,320]{1,0:T(8,128)(2,1)S(1)}, u32[]{:S(2)}, u32[]{:S(2)}) collective-permute-start(bf16[128,320]{1,0:T(8,128)(2,1)S(1)} %get-tuple-element.83), channel_id=1, source_target_pairs={{24,16},{25,17},{26,18},{27,19},{28,20},{29,21},{30,22},{31,23}} | collective-permute-start | bytes 245768 | tf_op jit(solution)/shard_map/ppermute | solution.py:577
  26.8 4.7 %collective-permute-start.10 = (bf16[128,320]{1,0:T(8,128)(2,1)S(1)}, bf16[128,320]{1,0:T(8,128)(2,1)S(1)}, u32[]{:S(2)}, u32[]{:S(2)}) collective-permute-start(bf16[128,320]{1,0:T(8,128)(2,1)S(1)} %get-tuple-element.82), channel_id=1, source_target_pairs={{24,16},{25,17},{26,18},{27,19},{28,20},{29,21},{30,22},{31,23}} | collective-permute-start | bytes 245768 | tf_op jit(solution)/shard_map/ppermute | solution.py:577
  27.5 7.6 %collective-permute-start.17 = (bf16[128,320]{1,0:T(8,128)(2,1)S(1)}, bf16[128,320]{1,0:T(8,128)(2,1)S(1)}, u32[]{:S(2)}, u32[]{:S(2)}) collective-permute-start(bf16[128,320]{1,0:T(8,128)(2,1)S(1)} %get-tuple-element.91), channel_id=1, source_target_pairs={{16,8},{17,9},{18,10},{19,11},{20,12},{21,13},{22,14},{23,15}} | collective-permute-start | bytes 245768 | tf_op jit(solution)/shard_map/ppermute | solution.py:577
  28.2 9.7 %collective-permute-start.9 = (bf16[2,160,256]{2,1,0:T(8,128)(2,1)S(1)}, bf16[2,160,256]{2,1,0:T(8,128)(2,1)S(1)}, u32[]{:S(2)}, u32[]{:S(2)}) collective-permute-start(bf16[2,160,256]{2,1,0:T(8,128)(2,1)S(1)} %shard_map.62), channel_id=1, source_target_pairs={{0,3},{1,0},{2,1},{3,2},{8,11},{9,8},{10,9},{11,10},{4,7},{5,4},{6... | collective-permute-start | bytes 491528 | tf_op jit(solution)/shard_map/ppermute | solution.py:586
  31.6 7.5 %collective-permute-start.12 = (bf16[2,160,256]{2,1,0:T(8,128)(2,1)S(1)}, bf16[2,160,256]{2,1,0:T(8,128)(2,1)S(1)}, u32[]{:S(2)}, u32[]{:S(2)}) collective-permute-start(bf16[2,160,256]{2,1,0:T(8,128)(2,1)S(1)} %shard_map.67), channel_id=1, source_target_pairs={{16,17},{17,18},{18,19},{19,16},{24,25},{25,26},{26,27},{27,24},{2... | collective-permute-start | bytes 491528 | tf_op jit(solution)/shard_map/ppermute | solution.py:586
  32.3 6.8 %collective-permute-start.13 = (bf16[2,160,256]{2,1,0:T(8,128)(2,1)S(1)}, bf16[2,160,256]{2,1,0:T(8,128)(2,1)S(1)}, u32[]{:S(2)}, u32[]{:S(2)}) collective-permute-start(bf16[2,160,256]{2,1,0:T(8,128)(2,1)S(1)} %shard_map.67), channel_id=1, source_target_pairs={{16,18},{17,19},{18,16},{19,17},{24,26},{25,27},{26,24},{27,25},{2... | collective-permute-start | bytes 491528 | tf_op jit(solution)/shard_map/ppermute | solution.py:586
  34.4 4.7 %collective-permute-start.14 = (bf16[2,160,256]{2,1,0:T(8,128)(2,1)S(1)}, bf16[2,160,256]{2,1,0:T(8,128)(2,1)S(1)}, u32[]{:S(2)}, u32[]{:S(2)}) collective-permute-start(bf16[2,160,256]{2,1,0:T(8,128)(2,1)S(1)} %shard_map.67), channel_id=1, source_target_pairs={{16,19},{17,16},{18,17},{19,18},{24,27},{25,24},{26,25},{27,26},{2... | collective-permute-start | bytes 491528 | tf_op jit(solution)/shard_map/ppermute | solution.py:586
  35.1 0.7 collective-permute-start.16
  35.8 26.3 %collective-permute-start.19 = (bf16[128,320]{1,0:T(8,128)(2,1)S(1)}, bf16[128,320]{1,0:T(8,128)(2,1)S(1)}, u32[]{:S(2)}, u32[]{:S(2)}) collective-permute-start(bf16[128,320]{1,0:T(8,128)(2,1)S(1)} %get-tuple-element.97), channel_id=1, source_target_pairs={{8,0},{9,1},{10,2},{11,3},{12,4},{13,5},{14,6},{15,7}} | collective-permute-start | bytes 245768 | tf_op jit(solution)/shard_map/ppermute | solution.py:577
  37.8 26.8 %collective-permute-start.18 = (bf16[128,320]{1,0:T(8,128)(2,1)S(1)}, bf16[128,320]{1,0:T(8,128)(2,1)S(1)}, u32[]{:S(2)}, u32[]{:S(2)}) collective-permute-start(bf16[128,320]{1,0:T(8,128)(2,1)S(1)} %get-tuple-element.96), channel_id=1, source_target_pairs={{8,0},{9,1},{10,2},{11,3},{12,4},{13,5},{14,6},{15,7}} | collective-permute-start | bytes 245768 | tf_op jit(solution)/shard_map/ppermute | solution.py:577
  42.1 34.2 %collective-permute-start.15 = (bf16[2,4,160,256]{3,2,1,0:T(8,128)(2,1)S(1)}, bf16[2,4,160,256]{3,2,1,0:T(8,128)(2,1)S(1)}, u32[]{:S(2)}, u32[]{:S(2)}) collective-permute-start(bf16[2,4,160,256]{3,2,1,0:T(8,128)(2,1)S(1)} %get-tuple-element.89), channel_id=1, source_target_pairs={{0,4},{4,0},{1,5},{5,1},{2,6},{6,2},{3,7},{7,3},{8,12},{12,8},{9,1... | collective-permute-start | bytes 1966088 | tf_op jit(solution)/shard_map/ppermute | solution.py:559
  65.9 6.4 %collective-permute-start.20 = (bf16[2,80,256]{2,1,0:T(8,128)(2,1)S(1)}, bf16[2,80,256]{2,1,0:T(8,128)(2,1)S(1)}, u32[]{:S(2)}, u32[]{:S(2)}) collective-permute-start(bf16[2,80,256]{2,1,0:T(8,128)(2,1)S(1)} %get-tuple-element.108), channel_id=1, source_target_pairs={{0,1},{1,2},{2,3},{3,0},{8,9},{9,10},{10,11},{11,8},{16,17},{17,18... | collective-permute-start | bytes 245768 | tf_op jit(solution)/shard_map/ppermute | solution.py:586
  66.7 7.1 %collective-permute-start.21 = (bf16[2,80,256]{2,1,0:T(8,128)(2,1)S(1)}, bf16[2,80,256]{2,1,0:T(8,128)(2,1)S(1)}, u32[]{:S(2)}, u32[]{:S(2)}) collective-permute-start(bf16[2,80,256]{2,1,0:T(8,128)(2,1)S(1)} %get-tuple-element.107), channel_id=1, source_target_pairs={{0,2},{1,3},{2,0},{3,1},{8,10},{9,11},{10,8},{11,9},{16,18},{17,19... | collective-permute-start | bytes 245768 | tf_op jit(solution)/shard_map/ppermute | solution.py:586
  67.0 6.7 %collective-permute-start.22 = (bf16[2,80,256]{2,1,0:T(8,128)(2,1)S(1)}, bf16[2,80,256]{2,1,0:T(8,128)(2,1)S(1)}, u32[]{:S(2)}, u32[]{:S(2)}) collective-permute-start(bf16[2,80,256]{2,1,0:T(8,128)(2,1)S(1)} %get-tuple-element.106), channel_id=1, source_target_pairs={{0,3},{1,0},{2,1},{3,2},{8,11},{9,8},{10,9},{11,10},{16,19},{17,16... | collective-permute-start | bytes 245768 | tf_op jit(solution)/shard_map/ppermute | solution.py:586
  73.8 3.7 %collective-permute-start.23 = (bf16[4,2,80,256]{3,2,1,0:T(8,128)(2,1)S(1)}, bf16[4,2,80,256]{3,2,1,0:T(8,128)(2,1)S(1)}, u32[]{:S(2)}, u32[]{:S(2)}) collective-permute-start(bf16[4,2,80,256]{3,2,1,0:T(8,128)(2,1)S(1)} %shard_map.75.own_ref), channel_id=1, source_target_pairs={{0,4},{4,0},{1,5},{5,1},{2,6},{6,2},{3,7},{7,3},{8,12},{12,8},{9,1... | collective-permute-start | bytes 983048 | tf_op jit(solution)/shard_map/ppermute | solution.py:559
  73.9 1.7 %collective-permute-start.24 = (bf16[2,8,8,320]{3,2,1,0:T(8,128)(2,1)S(1)}, bf16[2,8,8,320]{3,2,1,0:T(8,128)(2,1)S(1)}, u32[]{:S(2)}, u32[]{:S(2)}) collective-permute-start(bf16[2,8,8,320]{3,2,1,0:T(8,128)(2,1)S(1)} %get-tuple-element.105), channel_id=1, source_target_pairs={{0,4},{4,0},{1,5},{5,1},{2,6},{6,2},{3,7},{7,3},{8,12},{12,8},{9,1... | collective-permute-start | bytes 245768 | tf_op jit(solution)/shard_map/ppermute | solution.py:559

commit v6 on v5

--- a/solution.py
+++ b/solution.py
@@ -453,14 +453,15 @@
     return stacked
 
 
-def remake_call(saved, weights, soon, late, late_from, width):
+def remake_call(saved, weights, blocks, width, sections):
     _, crops, count, channels = saved.shape
     share = channels // 2
-    each = len(soon)
+    each = len(blocks)
 
     def kernel(saved_ref, weights_ref, *refs):
         home_ref, outer_ref, taps, shifted = refs[-4:]
         is_left = lax.axis_index("slab") == 0
+        section = lax.axis_index("section")
 
         def put(kind, block, crop, value):
             cells = slice(crop * count, (crop + 1) * count)
@@ -469,61 +470,66 @@
             home_ref[kind, block, :, cells] = jnp.where(is_left, low, high)
             outer_ref[kind, block, :, cells] = jnp.where(is_left, high, low)
 
-        for crop in range(crops):
-            for kind in range(2):
-                put(kind, 0, crop, saved_ref[kind, crop])
-        is_late = lax.axis_index("section") >= late_from
-        for block in range(each):
-            for slot, ref in enumerate((home_ref, outer_ref)):
-                ref[0, 1 + block] = jnp.where(
-                    is_late, refs[each + block][slot], refs[block][slot]
-                )
-        for block in range(1, 1 + each):
+        @pl.when((section >= sections[0]) & (section <= sections[1]))
+        def _():
             for crop in range(crops):
-                cells = slice(crop * count, (crop + 1) * count)
-                mine, theirs = home_ref[0, block, :, cells], outer_ref[0, block, :, cells]
-                low, high = jnp.where(is_left, mine, theirs), jnp.where(is_left, theirs, mine)
-                field = jnp.concatenate([low, high], axis=0).T.astype(jnp.float32)
-                hidden = convolved(field, weights_ref.at[0], taps, shifted, width)
-                put(1, block, crop, (hidden * jax.nn.sigmoid(hidden)).astype(jnp.bfloat16))
+                for kind in range(2):
+                    put(kind, 0, crop, saved_ref[kind, crop])
+            for block in range(each):
+                home_ref[0, 1 + block] = refs[block][0]
+                outer_ref[0, 1 + block] = refs[block][1]
+                for crop in range(crops):
+                    cells = slice(crop * count, (crop + 1) * count)
+                    mine, theirs = refs[block][0, :, cells], refs[block][1, :, cells]
+                    low, high = jnp.where(is_left, mine, theirs), jnp.where(is_left, theirs, mine)
+                    field = jnp.concatenate([low, high], axis=0).T.astype(jnp.float32)
+                    hidden = convolved(field, weights_ref.at[0], taps, shifted, width)
+                    active = (hidden * jax.nn.sigmoid(hidden)).astype(jnp.bfloat16)
+                    put(1, 1 + block, crop, active)
 
     out = jax.ShapeDtypeStruct((2, 1 + each, share, crops * count), saved.dtype)
     scratch = [
         pltpu.VMEM((count + 2 * width, 3 * channels), jnp.bfloat16),
         pltpu.VMEM((count + 16, channels), jnp.float32),
     ]
-    operands = [saved, weights, *soon, *late]
-    return call(kernel, [out, out], operands, (), scratch, {})
-
-
-def spread_call(cells_of, around, place, count, width):
+    return call(kernel, [out, out], [saved, weights, *blocks], (), scratch, {})
+
+
+def spread_call(cells_of, around, place, count, width, sections):
     two, blocks, share, cells = cells_of.shape
     crops = cells // count
     stride = count + width
     total = 2 * blocks * crops * stride + width
 
     def kernel(cells_ref, *refs):
-        out_ref, shifted = refs[-2:]
-        edge = jnp.zeros((width, 3 * share), jnp.bfloat16)
-        for kind in range(two):
-            out_ref[kind, total - width : total, :] = edge
-            for block in range(blocks):
-                for crop in range(crops):
-                    cell = slice(crop * count, (crop + 1) * count)
-                    value = cells_ref[kind, block, :, cell].T.astype(jnp.float32)
-                    before, after = neighbours(value, shifted, width)
-                    at = ((place * blocks + block) * crops + crop) * stride
-                    out_ref[kind, at : at + width, :] = edge
-                    for side, part in enumerate((before, value, after)):
-                        lanes = slice(side * share, (side + 1) * share)
-                        out_ref[kind, at + width : at + stride, lanes] = part.astype(jnp.bfloat16)
+        out_ref, done_ref, shifted = refs[-3:]
+        section = lax.axis_index("section")
+        done_ref[...] = jnp.zeros_like(done_ref)
+
+        @pl.when((section >= sections[0]) & (section <= sections[1]))
+        def _():
+            edge = jnp.zeros((width, 3 * share), jnp.bfloat16)
+            for kind in range(two):
+                out_ref[kind, total - width : total, :] = edge
+                for block in range(blocks):
+                    for crop in range(crops):
+                        cell = slice(crop * count, (crop + 1) * count)
+                        value = cells_ref[kind, block, :, cell].T.astype(jnp.float32)
+                        before, after = neighbours(value, shifted, width)
+                        at = ((place * blocks + block) * crops + crop) * stride
+                        out_ref[kind, at : at + width, :] = edge
+                        for side, part in enumerate((before, value, after)):
+                            lanes = slice(side * share, (side + 1) * share)
+                            out_ref[kind, at + width : at + stride, lanes] = part.astype(
+                                jnp.bfloat16
+                            )
 
     out = jax.ShapeDtypeStruct((two, total, 3 * share), jnp.bfloat16)
     scratch = [pltpu.VMEM((count + 16, share), jnp.float32)]
     operands = [cells_of] if around is None else [cells_of, around]
     aliases = {} if around is None else {1: 0}
-    (spread,) = call(kernel, [out], operands, (), scratch, aliases)
-    return spread
+    token = jax.ShapeDtypeStruct((8, 128), jnp.float32)
+    return call(kernel, [out, token], operands, (), scratch, aliases)
 
 
 def terms_call(around, own, other, count, width, scaling):
@@ -567,7 +573,7 @@
     count = row_count * width
     crops = images * strip_count // slabs
     last = sections - 1
-    early, middle, late_from = min(1, last - 1), min(2, last), max(1, sections - 2)
+    early = min(1, last - 1)
     steps = range(1, groups)
     scaling = 1.0 / math.sqrt(images * groups * strip_count * count)
 
@@ -614,7 +620,7 @@
             incoming = hop(outgoing, place, place + 1)
         if place == early:
             inputs = flipped(state[0], state[1])
-            soon = [shared(inputs, step, range(late_from)) for step in steps]
+            soon = [shared(inputs, step, [0]) for step in steps]
             turned = turn_call(weights, state[0])
             after = turned
     saved, hidden = state
@@ -630,17 +636,22 @@
             outgoing.append(out)
         if place:
             incoming = hop(outgoing, place, place - 1)
-        if place == middle:
+        if place == last:
             inputs = flipped(saved, outgoing[-1])
-            late = [shared(inputs, step, range(late_from, sections)) for step in steps]
+            late = [shared(inputs, step, range(sections)) for step in steps]
+        if place == 1:
+            home, outer = remake_call(saved, weights, soon, width, (0, 0))
+            outer = swapped(outer)
+            around, after = spread_call(home, None, 0, count, width, (0, 0))
+            around, after = spread_call(outer, around, 1, count, width, (0, 0))
     kept, sent = grads
     own = [sent[0]]
     for step in steps:
         own.append(shared(sent[step], step, range(sections)))
-    home, outer = remake_call(saved, weights, soon, late, late_from, width)
+    home, outer = remake_call(saved, weights, late, width, (1, last))
     outer = swapped(outer)
-    around = spread_call(home, None, 0, count, width)
-    around = spread_call(outer, around, 1, count, width)
+    around, _ = spread_call(home, around, 0, count, width, (1, last))
+    around, _ = spread_call(outer, around, 1, count, width, (1, last))
     own = stack_call(own)
     other = swapped(own)
     terms = terms_call(around, own, other, count, width, scaling)

time: 81.5 us -> 80.2 us (0.984)
  waiting for transfers between devices: 29.4 us -> 25.5 us
  Pallas kernels: 19.9 us -> 21.4 us
  starting transfers between devices: 30.7 us -> 31.9 us
    ppermute x12, waiting for transfers between devices: 23.3 us -> 2.06 us  [hop(): arrived.append(lax.ppermute(value, 'section', [(source, target)]))]
    ppermute x9, waiting for transfers between devices: 6.12 us -> 22.9 us  [shared(): return lax.ppermute(values, ('section', 'img'), pairs)]
    pallas_call x29 -> x32, Pallas kernels: 19.9 us -> 21.4 us  [call(): pl.pallas_call(kernel, out_shape=outs, in_specs=[pl.BlockSpec(memory_spac...]
    ppermute x9, starting transfers between devices: 17.1 us -> 18.3 us  [shared(): return lax.ppermute(values, ('section', 'img'), pairs)]
  transfers between devices with their start and end apart: 25 -> 26, of which waited for: 8 -> 7; matrix products, arithmetic and copies ran while one was open for 0% -> 0% of each run, Pallas kernels for 17% -> 16%
where the time goes in v6:
time: 80.2 us; the launch traced here: 79.8 us
  starting transfers between devices  31.9 us (40%)
  waiting for transfers between devices  25.5 us (32%)
  Pallas kernels  21.4 us (27%)
  between operations  1.04 us (1%)
    ppermute x9, waiting for transfers between devices, shared(): return lax.ppermute(values, ('section', 'img'), pairs)  22.9 us
    pallas_call x32, Pallas kernels, call(): pl.pallas_call(kernel, out_shape=outs, in_specs=[pl.BlockSpec(memory_spac...  21.4 us
    ppermute x9, starting transfers between devices, shared(): return lax.ppermute(values, ('section', 'img'), pairs)  18.3 us
    ppermute x12, starting transfers between devices, hop(): arrived.append(lax.ppermute(value, 'section', [(source, target)]))  12.3 us
    ppermute x12, waiting for transfers between devices, hop(): arrived.append(lax.ppermute(value, 'section', [(source, target)]))  2.06 us
  transfers between devices with their start and end apart: 26, of which 7 were waited for; matrix products, arithmetic and copies ran while one was open for 0% of the time, Pallas kernels for 16%

profile of v6, /device:TPU:0, one launch (start us, length us, event | category | flops | bytes accessed | tf_op | source)
XLA Modules:
  0.0 79.8 jit_solution(5117039808157431229)
XLA Ops:
  0.6 1.0 %shard_map.50 = (bf16[2,8,8,320]{3,2,1,0:T(8,128)(2,1)S(1)}, bf16[2,8,8,320]{3,2,1,0:T(8,128)(2,1)S(1)}) custom-call(bf16[1,4,8,8,320]{4,3,2,1,0:T(8,128)(2,1)} %strips_ref.1, bf16[1,4,8,8,320]{4,3,2,1,0:T(8,128)(2,1)} %cotangent_ref.1), custom_call_target="tpu_custom_call" | custom-call | tf_op jit(solution)/shard_map/pallas_call | solution.py:177
  1.6 0.6 collective-permute-start
  2.2 2.3 %shard_map.52.weights_ref.after_ref = bf16[2,3,960,320]{3,2,1,0:T(8,128)(2,1)S(1)} custom-call(bf16[2,3,960,320]{3,2,1,0:T(8,128)(2,1)} %bitcast.11), custom_call_target="tpu_custom_call" | custom-call | tf_op jit(solution)/shard_map/pallas_call | solution.py:177
  4.5 0.0 collective-permute-done.other_ref
  4.5 0.1 shard_map.51
  4.6 1.3 %shard_map.53 = (bf16[128,320]{1,0:T(8,128)(2,1)S(1)}, bf16[2,2,128,320]{3,2,1,0:T(8,128)(2,1)S(1)}, f32[2,128,320]{2,1,0:T(8,128)S(1)}) custom-call(bf16[128,320]{1,0:T(8,128)(2,1)S(1)} %get-tuple-element.64.field_ref.grad_ref, bf16[2,3,960,320]{3,2,1,0:T(8,128)(2,1)S(1)} %shard_map.52.weights_ref.after_ref, ...), custom_call_target="tpu_custom_call" | custom-call | tf_op jit(solution)/shard_map/pallas_call | solution.py:177
  5.9 3.1 %collective-permute-start.2 = (bf16[128,320]{1,0:T(8,128)(2,1)S(1)}, bf16[128,320]{1,0:T(8,128)(2,1)S(1)}, u32[]{:S(2)}, u32[]{:S(2)}) collective-permute-start(bf16[128,320]{1,0:T(8,128)(2,1)S(1)} %get-tuple-element.68), channel_id=1, source_target_pairs={{0,8},{1,9},{2,10},{3,11},{4,12},{5,13},{6,14},{7,15}} | collective-permute-start | bytes 245768 | tf_op jit(solution)/shard_map/ppermute | solution.py:583
  9.0 1.3 %shard_map.54 = (bf16[128,320]{1,0:T(8,128)(2,1)S(1)}, bf16[2,2,128,320]{3,2,1,0:T(8,128)(2,1)S(1)}, f32[2,128,320]{2,1,0:T(8,128)S(1)}) custom-call(bf16[128,320]{1,0:T(8,128)(2,1)S(1)} %get-tuple-element.63.field_ref.grad_ref, bf16[2,3,960,320]{3,2,1,0:T(8,128)(2,1)S(1)} %shard_map.52.weights_ref.after_ref, ...), custom_call_target="tpu_custom_call", output_to_operand_aliasing={{1}: (3, {}), {2}: (4, {})} | custom-call | tf_op jit(solution)/shard_map/pallas_call | solution.py:177
  10.3 1.3 %collective-permute-start.1 = (bf16[128,320]{1,0:T(8,128)(2,1)S(1)}, bf16[128,320]{1,0:T(8,128)(2,1)S(1)}, u32[]{:S(2)}, u32[]{:S(2)}) collective-permute-start(bf16[128,320]{1,0:T(8,128)(2,1)S(1)} %get-tuple-element.67), channel_id=1, source_target_pairs={{0,8},{1,9},{2,10},{3,11},{4,12},{5,13},{6,14},{7,15}} | collective-permute-start | bytes 245768 | tf_op jit(solution)/shard_map/ppermute | solution.py:583
  11.6 0.1 collective-permute-done.2.field_ref
  11.7 0.7 collective-permute-start.4
  12.3 1.9 %collective-permute-done.1.field_ref = bf16[128,320]{1,0:T(8,128)(2,1)S(1)} collective-permute-done((bf16[128,320]{1,0:T(8,128)(2,1)S(1)}, bf16[128,320]{1,0:T(8,128)(2,1)S(1)}, u32[]{:S(2)}, u32[]{:S(2)}) %collective-permute-start.1) | collective-permute-done | bytes 81952 | tf_op jit(solution)/shard_map/ppermute | solution.py:583
  14.3 0.7 collective-permute-start.3
  15.0 0.1 shard_map.66
  15.1 5.5 %collective-permute-start.13 = (bf16[2,160,256]{2,1,0:T(8,128)(2,1)S(1)}, bf16[2,160,256]{2,1,0:T(8,128)(2,1)S(1)}, u32[]{:S(2)}, u32[]{:S(2)}) collective-permute-start(bf16[2,160,256]{2,1,0:T(8,128)(2,1)S(1)} %shard_map.66), channel_id=1, source_target_pairs={{0,3},{1,0},{2,1},{3,2},{4,7},{5,4},{6,5},{7,6}} | collective-permute-start | bytes 491528 | tf_op jit(solution)/shard_map/ppermute | solution.py:592
  20.5 1.9 %collective-permute-start.12 = (bf16[2,160,256]{2,1,0:T(8,128)(2,1)S(1)}, bf16[2,160,256]{2,1,0:T(8,128)(2,1)S(1)}, u32[]{:S(2)}, u32[]{:S(2)}) collective-permute-start(bf16[2,160,256]{2,1,0:T(8,128)(2,1)S(1)} %shard_map.66), channel_id=1, source_target_pairs={{0,2},{1,3},{2,0},{3,1},{4,6},{5,7},{6,4},{7,5}} | collective-permute-start | bytes 491528 | tf_op jit(solution)/shard_map/ppermute | solution.py:592
  22.5 2.9 %collective-permute-start.11 = (bf16[2,160,256]{2,1,0:T(8,128)(2,1)S(1)}, bf16[2,160,256]{2,1,0:T(8,128)(2,1)S(1)}, u32[]{:S(2)}, u32[]{:S(2)}) collective-permute-start(bf16[2,160,256]{2,1,0:T(8,128)(2,1)S(1)} %shard_map.66), channel_id=1, source_target_pairs={{0,1},{1,2},{2,3},{3,0},{4,5},{5,6},{6,7},{7,4}} | collective-permute-start | bytes 491528 | tf_op jit(solution)/shard_map/ppermute | solution.py:592
  25.4 1.4 %shard_map.57.after_ref.turned_ref = bf16[2,3,960,320]{3,2,1,0:T(8,128)(2,1)S(1)} custom-call(bf16[2,3,960,320]{3,2,1,0:T(8,128)(2,1)S(1)} %shard_map.52.weights_ref.after_ref, bf16[2,2,128,320]{3,2,1,0:T(8,128)(2,1)S(1)} %get-tuple-element.74.after_ref.refs_0_), custom_call_target="tpu_custom_call" | custom-call | tf_op jit(solution)/shard_map/pallas_call | solution.py:177
  26.8 0.0 collective-permute-done.4.field_ref
  26.8 0.7 collective-permute-start.6
  27.5 0.0 collective-permute-done.3.field_ref
  27.5 0.7 collective-permute-start.5
  28.2 0.0 collective-permute-done.6.field_ref
  28.2 0.0 collective-permute-done.5.field_ref
  28.3 0.0 collective-permute-done.13.refs_2_
  28.3 6.6 %collective-permute-done.12.refs_1_ = bf16[2,160,256]{2,1,0:T(8,128)(2,1)S(1)} collective-permute-done((bf16[2,160,256]{2,1,0:T(8,128)(2,1)S(1)}, bf16[2,160,256]{2,1,0:T(8,128)(2,1)S(1)}, u32[]{:S(2)}, u32[]{:S(2)}) %collective-permute-start.12) | collective-permute-done | bytes 163872 | tf_op jit(solution)/shard_map/ppermute | solution.py:592
  34.9 2.9 %shard_map.67 = (bf16[2,4,160,256]{3,2,1,0:T(8,128)(2,1)S(1)}, bf16[2,4,160,256]{3,2,1,0:T(8,128)(2,1)S(1)}) custom-call(bf16[2,2,128,320]{3,2,1,0:T(8,128)(2,1)S(1)} %get-tuple-element.85.refs_0_.saved_ref, bf16[2,3,960,320]{3,2,1,0:T(8,128)(2,1)S(1)} %shard_map.52.weights_ref.after_ref, bf16[2,160,256]{2,1,0:T(8,128)(2,1)S(1)} %collective-permute-done.11.refs_0_, ...), custom_call_target="tpu_custom_call" | custom-call | tf_op jit(solution)/shard_map/pallas_call | solution.py:177
  37.8 0.1 collective-permute-start.14
  37.9 0.7 collective-permute-start.16
  38.6 0.7 collective-permute-start.15
  39.2 0.0 collective-permute-done.16.grad_ref
  39.3 0.7 collective-permute-start.18
  39.9 0.1 shard_map.64
  40.1 1.2 %collective-permute-start.9 = (bf16[2,160,256]{2,1,0:T(8,128)(2,1)S(1)}, bf16[2,160,256]{2,1,0:T(8,128)(2,1)S(1)}, u32[]{:S(2)}, u32[]{:S(2)}) collective-permute-start(bf16[2,160,256]{2,1,0:T(8,128)(2,1)S(1)} %shard_map.64), channel_id=1, source_target_pairs={{0,3},{1,0},{2,1},{3,2},{8,11},{9,8},{10,9},{11,10},{16,19},{17,16... | collective-permute-start | bytes 491528 | tf_op jit(solution)/shard_map/ppermute | solution.py:592
  41.2 1.8 %collective-permute-start.8 = (bf16[2,160,256]{2,1,0:T(8,128)(2,1)S(1)}, bf16[2,160,256]{2,1,0:T(8,128)(2,1)S(1)}, u32[]{:S(2)}, u32[]{:S(2)}) collective-permute-start(bf16[2,160,256]{2,1,0:T(8,128)(2,1)S(1)} %shard_map.64), channel_id=1, source_target_pairs={{0,2},{1,3},{2,0},{3,1},{8,10},{9,11},{10,8},{11,9},{16,18},{17,19... | collective-permute-start | bytes 491528 | tf_op jit(solution)/shard_map/ppermute | solution.py:592
  43.0 0.0 collective-permute-done.15.grad_ref
  43.0 1.9 %collective-permute-start.7 = (bf16[2,160,256]{2,1,0:T(8,128)(2,1)S(1)}, bf16[2,160,256]{2,1,0:T(8,128)(2,1)S(1)}, u32[]{:S(2)}, u32[]{:S(2)}) collective-permute-start(bf16[2,160,256]{2,1,0:T(8,128)(2,1)S(1)} %shard_map.64), channel_id=1, source_target_pairs={{0,1},{1,2},{2,3},{3,0},{8,9},{9,10},{10,11},{11,8},{16,17},{17,18... | collective-permute-start | bytes 491528 | tf_op jit(solution)/shard_map/ppermute | solution.py:592
  45.0 0.7 collective-permute-start.17
  45.7 0.0 collective-permute-done.17.grad_ref
  45.7 1.3 %collective-permute-start.20 = (bf16[128,320]{1,0:T(8,128)(2,1)S(1)}, bf16[128,320]{1,0:T(8,128)(2,1)S(1)}, u32[]{:S(2)}, u32[]{:S(2)}) collective-permute-start(bf16[128,320]{1,0:T(8,128)(2,1)S(1)} %get-tuple-element.111), channel_id=1, source_target_pairs={{8,0},{9,1},{10,2},{11,3},{12,4},{13,5},{14,6},{15,7}} | collective-permute-start | bytes 245768 | tf_op jit(solution)/shard_map/ppermute | solution.py:583
  47.0 0.0 collective-permute-done.9.refs_2_
  47.0 1.3 %collective-permute-start.19 = (bf16[128,320]{1,0:T(8,128)(2,1)S(1)}, bf16[128,320]{1,0:T(8,128)(2,1)S(1)}, u32[]{:S(2)}, u32[]{:S(2)}) collective-permute-start(bf16[128,320]{1,0:T(8,128)(2,1)S(1)} %get-tuple-element.109), channel_id=1, source_target_pairs={{8,0},{9,1},{10,2},{11,3},{12,4},{13,5},{14,6},{15,7}} | collective-permute-start | bytes 245768 | tf_op jit(solution)/shard_map/ppermute | solution.py:583
  48.3 10.0 %collective-permute-done.8.refs_1_ = bf16[2,160,256]{2,1,0:T(8,128)(2,1)S(1)} collective-permute-done((bf16[2,160,256]{2,1,0:T(8,128)(2,1)S(1)}, bf16[2,160,256]{2,1,0:T(8,128)(2,1)S(1)}, u32[]{:S(2)}, u32[]{:S(2)}) %collective-permute-start.8) | collective-permute-done | bytes 163872 | tf_op jit(solution)/shard_map/ppermute | solution.py:592
  58.3 1.7 %shard_map.68 = (bf16[2,2320,480]{2,1,0:T(8,128)(2,1)S(1)}, f32[8,128]{1,0:T(8,128)}) custom-call(bf16[2,4,160,256]{3,2,1,0:T(8,128)(2,1)S(1)} %get-tuple-element.93.cells_ref), custom_call_target="tpu_custom_call" | custom-call | tf_op jit(solution)/shard_map/pallas_call | solution.py:177
  60.0 0.0 collective-permute-done.14.cells_ref
  60.1 1.1 %shard_map.69 = (bf16[2,2320,480]{2,1,0:T(8,128)(2,1)S(1)}, f32[8,128]{1,0:T(8,128)S(1)}) custom-call(bf16[2,4,160,256]{3,2,1,0:T(8,128)(2,1)S(1)} %collective-permute-done.14.cells_ref, bf16[2,2320,480]{2,1,0:T(8,128)(2,1)S(1)} %get-tuple-element.94.refs_0_), custom_call_target="tpu_custom_call", output_to_operand_aliasing={{0}: (1, {})} | custom-call | tf_op jit(solution)/shard_map/pallas_call | solution.py:177
  61.2 1.2 %shard_map.76 = (bf16[2,128,320]{2,1,0:T(8,128)(2,1)S(1)}, bf16[4,2,80,256]{3,2,1,0:T(8,128)(2,1)S(1)}) custom-call(bf16[128,320]{1,0:T(8,128)(2,1)S(1)} %collective-permute-done.20.grad_ref, bf16[2,3,960,320]{3,2,1,0:T(8,128)(2,1)S(1)} %shard_map.57.after_ref.turned_ref, ...), custom_call_target="tpu_custom_call", output_to_operand_aliasing={{0}: (4, {}), {1}: (5, {})} | custom-call | tf_op jit(solution)/shard_map/pallas_call | solution.py:177
  62.4 0.0 collective-permute-done.19.grad_ref
  62.4 1.2 %shard_map.77 = (bf16[2,128,320]{2,1,0:T(8,128)(2,1)S(1)}, bf16[4,2,80,256]{3,2,1,0:T(8,128)(2,1)S(1)}) custom-call(bf16[128,320]{1,0:T(8,128)(2,1)S(1)} %collective-permute-done.19.grad_ref, bf16[2,3,960,320]{3,2,1,0:T(8,128)(2,1)S(1)} %shard_map.57.after_ref.turned_ref, ...), custom_call_target="tpu_custom_call", output_to_operand_aliasing={{0}: (4, {}), {1}: (5, {})} | custom-call | tf_op jit(solution)/shard_map/pallas_call | solution.py:177
  63.7 0.1 collective-permute-start.23
  63.8 1.1 %collective-permute-start.22 = (bf16[2,80,256]{2,1,0:T(8,128)(2,1)S(1)}, bf16[2,80,256]{2,1,0:T(8,128)(2,1)S(1)}, u32[]{:S(2)}, u32[]{:S(2)}) collective-permute-start(bf16[2,80,256]{2,1,0:T(8,128)(2,1)S(1)} %get-tuple-element.121), channel_id=1, source_target_pairs={{0,2},{1,3},{2,0},{3,1},{8,10},{9,11},{10,8},{11,9},{16,18},{17,19... | collective-permute-start | bytes 245768 | tf_op jit(solution)/shard_map/ppermute | solution.py:592
  64.8 1.9 %collective-permute-start.21 = (bf16[2,80,256]{2,1,0:T(8,128)(2,1)S(1)}, bf16[2,80,256]{2,1,0:T(8,128)(2,1)S(1)}, u32[]{:S(2)}, u32[]{:S(2)}) collective-permute-start(bf16[2,80,256]{2,1,0:T(8,128)(2,1)S(1)} %get-tuple-element.122), channel_id=1, source_target_pairs={{0,1},{1,2},{2,3},{3,0},{8,9},{9,10},{10,11},{11,8},{16,17},{17,18... | collective-permute-start | bytes 245768 | tf_op jit(solution)/shard_map/ppermute | solution.py:592
  66.8 3.1 %collective-permute-done.23.refs_3_ = bf16[2,80,256]{2,1,0:T(8,128)(2,1)S(1)} collective-permute-done((bf16[2,80,256]{2,1,0:T(8,128)(2,1)S(1)}, bf16[2,80,256]{2,1,0:T(8,128)(2,1)S(1)}, u32[]{:S(2)}, u32[]{:S(2)}) %collective-permute-start.23) | collective-permute-done | bytes 81952 | tf_op jit(solution)/shard_map/ppermute | solution.py:592
  69.8 3.3 %collective-permute-done.22.refs_2_ = bf16[2,80,256]{2,1,0:T(8,128)(2,1)S(1)} collective-permute-done((bf16[2,80,256]{2,1,0:T(8,128)(2,1)S(1)}, bf16[2,80,256]{2,1,0:T(8,128)(2,1)S(1)}, u32[]{:S(2)}, u32[]{:S(2)}) %collective-permute-start.22) | collective-permute-done | bytes 81952 | tf_op jit(solution)/shard_map/ppermute | solution.py:592
  73.2 0.0 collective-permute-done.21.refs_1_
  73.2 0.1 collective-permute-start.24
  73.3 0.1 shard_map.80
  73.3 0.6 collective-permute-start.25
  73.9 0.6 shard_map.70
  74.5 0.5 collective-permute-done.25.other_ref
  75.0 0.7 shard_map.81
  75.7 0.0 collective-permute-done.10.cells_ref
  75.7 0.6 shard_map.71
  76.3 3.5 %shard_map.79 = f32[2,9,160,80]{3,2,1,0:T(8,128)} custom-call(bf16[2,2320,480]{2,1,0:T(8,128)(2,1)S(1)} %get-tuple-element.97.around_ref, bf16[4,2,80,256]{3,2,1,0:T(8,128)(2,1)S(1)} %shard_map.78.own_ref, bf16[4,2,80,256]{3,2,1,0:T(8,128)(2,1)S(1)} %collective-permute-done.24.other_ref), custom_call_target="tpu_custom_call" | custom-call | tf_op jit(solution)/shard_map/pallas_call | solution.py:177
  (21 shorter events, 0.2 us)
Async XLA Ops:
  1.6 2.9 %collective-permute-start = (bf16[2,8,8,320]{3,2,1,0:T(8,128)(2,1)S(1)}, bf16[2,8,8,320]{3,2,1,0:T(8,128)(2,1)S(1)}, u32[]{:S(2)}, u32[]{:S(2)}) collective-permute-start(bf16[2,8,8,320]{3,2,1,0:T(8,128)(2,1)S(1)} %get-tuple-element.62), channel_id=1, source_target_pairs={{0,4},{4,0},{1,5},{5,1},{2,6},{6,2},{3,7},{7,3},{8,12},{12,8},{9,1... | collective-permute-start | bytes 245768 | tf_op jit(solution)/shard_map/ppermute | solution.py:565
  5.9 5.8 %collective-permute-start.2 = (bf16[128,320]{1,0:T(8,128)(2,1)S(1)}, bf16[128,320]{1,0:T(8,128)(2,1)S(1)}, u32[]{:S(2)}, u32[]{:S(2)}) collective-permute-start(bf16[128,320]{1,0:T(8,128)(2,1)S(1)} %get-tuple-element.68), channel_id=1, source_target_pairs={{0,8},{1,9},{2,10},{3,11},{4,12},{5,13},{6,14},{7,15}} | collective-permute-start | bytes 245768 | tf_op jit(solution)/shard_map/ppermute | solution.py:583
  10.3 4.0 %collective-permute-start.1 = (bf16[128,320]{1,0:T(8,128)(2,1)S(1)}, bf16[128,320]{1,0:T(8,128)(2,1)S(1)}, u32[]{:S(2)}, u32[]{:S(2)}) collective-permute-start(bf16[128,320]{1,0:T(8,128)(2,1)S(1)} %get-tuple-element.67), channel_id=1, source_target_pairs={{0,8},{1,9},{2,10},{3,11},{4,12},{5,13},{6,14},{7,15}} | collective-permute-start | bytes 245768 | tf_op jit(solution)/shard_map/ppermute | solution.py:583
  11.7 15.1 %collective-permute-start.4 = (bf16[128,320]{1,0:T(8,128)(2,1)S(1)}, bf16[128,320]{1,0:T(8,128)(2,1)S(1)}, u32[]{:S(2)}, u32[]{:S(2)}) collective-permute-start(bf16[128,320]{1,0:T(8,128)(2,1)S(1)} %get-tuple-element.75), channel_id=1, source_target_pairs={{8,16},{9,17},{10,18},{11,19},{12,20},{13,21},{14,22},{15,23}} | collective-permute-start | bytes 245768 | tf_op jit(solution)/shard_map/ppermute | solution.py:583
  14.3 13.2 %collective-permute-start.3 = (bf16[128,320]{1,0:T(8,128)(2,1)S(1)}, bf16[128,320]{1,0:T(8,128)(2,1)S(1)}, u32[]{:S(2)}, u32[]{:S(2)}) collective-permute-start(bf16[128,320]{1,0:T(8,128)(2,1)S(1)} %get-tuple-element.73), channel_id=1, source_target_pairs={{8,16},{9,17},{10,18},{11,19},{12,20},{13,21},{14,22},{15,23}} | collective-permute-start | bytes 245768 | tf_op jit(solution)/shard_map/ppermute | solution.py:583
  15.1 13.2 %collective-permute-start.13 = (bf16[2,160,256]{2,1,0:T(8,128)(2,1)S(1)}, bf16[2,160,256]{2,1,0:T(8,128)(2,1)S(1)}, u32[]{:S(2)}, u32[]{:S(2)}) collective-permute-start(bf16[2,160,256]{2,1,0:T(8,128)(2,1)S(1)} %shard_map.66), channel_id=1, source_target_pairs={{0,3},{1,0},{2,1},{3,2},{4,7},{5,4},{6,5},{7,6}} | collective-permute-start | bytes 491528 | tf_op jit(solution)/shard_map/ppermute | solution.py:592
  20.5 14.3 %collective-permute-start.12 = (bf16[2,160,256]{2,1,0:T(8,128)(2,1)S(1)}, bf16[2,160,256]{2,1,0:T(8,128)(2,1)S(1)}, u32[]{:S(2)}, u32[]{:S(2)}) collective-permute-start(bf16[2,160,256]{2,1,0:T(8,128)(2,1)S(1)} %shard_map.66), channel_id=1, source_target_pairs={{0,2},{1,3},{2,0},{3,1},{4,6},{5,7},{6,4},{7,5}} | collective-permute-start | bytes 491528 | tf_op jit(solution)/shard_map/ppermute | solution.py:592
  22.5 12.4 %collective-permute-start.11 = (bf16[2,160,256]{2,1,0:T(8,128)(2,1)S(1)}, bf16[2,160,256]{2,1,0:T(8,128)(2,1)S(1)}, u32[]{:S(2)}, u32[]{:S(2)}) collective-permute-start(bf16[2,160,256]{2,1,0:T(8,128)(2,1)S(1)} %shard_map.66), channel_id=1, source_target_pairs={{0,1},{1,2},{2,3},{3,0},{4,5},{5,6},{6,7},{7,4}} | collective-permute-start | bytes 491528 | tf_op jit(solution)/shard_map/ppermute | solution.py:592
  26.8 1.4 %collective-permute-start.6 = (bf16[128,320]{1,0:T(8,128)(2,1)S(1)}, bf16[128,320]{1,0:T(8,128)(2,1)S(1)}, u32[]{:S(2)}, u32[]{:S(2)}) collective-permute-start(bf16[128,320]{1,0:T(8,128)(2,1)S(1)} %get-tuple-element.80), channel_id=1, source_target_pairs={{16,24},{17,25},{18,26},{19,27},{20,28},{21,29},{22,30},{23,31}} | collective-permute-start | bytes 245768 | tf_op jit(solution)/shard_map/ppermute | solution.py:583
  27.5 0.7 collective-permute-start.5
  37.8 22.3 %collective-permute-start.14 = (bf16[2,4,160,256]{3,2,1,0:T(8,128)(2,1)S(1)}, bf16[2,4,160,256]{3,2,1,0:T(8,128)(2,1)S(1)}, u32[]{:S(2)}, u32[]{:S(2)}) collective-permute-start(bf16[2,4,160,256]{3,2,1,0:T(8,128)(2,1)S(1)} %get-tuple-element.92), channel_id=1, source_target_pairs={{0,4},{4,0},{1,5},{5,1},{2,6},{6,2},{3,7},{7,3},{8,12},{12,8},{9,1... | collective-permute-start | bytes 1966088 | tf_op jit(solution)/shard_map/ppermute | solution.py:565
  37.9 1.4 %collective-permute-start.16 = (bf16[128,320]{1,0:T(8,128)(2,1)S(1)}, bf16[128,320]{1,0:T(8,128)(2,1)S(1)}, u32[]{:S(2)}, u32[]{:S(2)}) collective-permute-start(bf16[128,320]{1,0:T(8,128)(2,1)S(1)} %get-tuple-element.98), channel_id=1, source_target_pairs={{24,16},{25,17},{26,18},{27,19},{28,20},{29,21},{30,22},{31,23}} | collective-permute-start | bytes 245768 | tf_op jit(solution)/shard_map/ppermute | solution.py:583
  38.6 4.5 %collective-permute-start.15 = (bf16[128,320]{1,0:T(8,128)(2,1)S(1)}, bf16[128,320]{1,0:T(8,128)(2,1)S(1)}, u32[]{:S(2)}, u32[]{:S(2)}) collective-permute-start(bf16[128,320]{1,0:T(8,128)(2,1)S(1)} %get-tuple-element.89.refs_1_), channel_id=1, source_target_pairs={{24,16},{25,17},{26,18},{27,19},{28,20},{29,21},{30,22},{31,23}} | collective-permute-start | bytes 245768 | tf_op jit(solution)/shard_map/ppermute | solution.py:583
  39.3 5.7 %collective-permute-start.18 = (bf16[128,320]{1,0:T(8,128)(2,1)S(1)}, bf16[128,320]{1,0:T(8,128)(2,1)S(1)}, u32[]{:S(2)}, u32[]{:S(2)}) collective-permute-start(bf16[128,320]{1,0:T(8,128)(2,1)S(1)} %get-tuple-element.104), channel_id=1, source_target_pairs={{16,8},{17,9},{18,10},{19,11},{20,12},{21,13},{22,14},{23,15}} | collective-permute-start | bytes 245768 | tf_op jit(solution)/shard_map/ppermute | solution.py:583
  40.1 7.0 %collective-permute-start.9 = (bf16[2,160,256]{2,1,0:T(8,128)(2,1)S(1)}, bf16[2,160,256]{2,1,0:T(8,128)(2,1)S(1)}, u32[]{:S(2)}, u32[]{:S(2)}) collective-permute-start(bf16[2,160,256]{2,1,0:T(8,128)(2,1)S(1)} %shard_map.64), channel_id=1, source_target_pairs={{0,3},{1,0},{2,1},{3,2},{8,11},{9,8},{10,9},{11,10},{16,19},{17,16... | collective-permute-start | bytes 491528 | tf_op jit(solution)/shard_map/ppermute | solution.py:592
  41.2 17.1 %collective-permute-start.8 = (bf16[2,160,256]{2,1,0:T(8,128)(2,1)S(1)}, bf16[2,160,256]{2,1,0:T(8,128)(2,1)S(1)}, u32[]{:S(2)}, u32[]{:S(2)}) collective-permute-start(bf16[2,160,256]{2,1,0:T(8,128)(2,1)S(1)} %shard_map.64), channel_id=1, source_target_pairs={{0,2},{1,3},{2,0},{3,1},{8,10},{9,11},{10,8},{11,9},{16,18},{17,19... | collective-permute-start | bytes 491528 | tf_op jit(solution)/shard_map/ppermute | solution.py:592
  43.0 15.3 %collective-permute-start.7 = (bf16[2,160,256]{2,1,0:T(8,128)(2,1)S(1)}, bf16[2,160,256]{2,1,0:T(8,128)(2,1)S(1)}, u32[]{:S(2)}, u32[]{:S(2)}) collective-permute-start(bf16[2,160,256]{2,1,0:T(8,128)(2,1)S(1)} %shard_map.64), channel_id=1, source_target_pairs={{0,1},{1,2},{2,3},{3,0},{8,9},{9,10},{10,11},{11,8},{16,17},{17,18... | collective-permute-start | bytes 491528 | tf_op jit(solution)/shard_map/ppermute | solution.py:592
  45.0 0.7 collective-permute-start.17
  45.7 15.5 %collective-permute-start.20 = (bf16[128,320]{1,0:T(8,128)(2,1)S(1)}, bf16[128,320]{1,0:T(8,128)(2,1)S(1)}, u32[]{:S(2)}, u32[]{:S(2)}) collective-permute-start(bf16[128,320]{1,0:T(8,128)(2,1)S(1)} %get-tuple-element.111), channel_id=1, source_target_pairs={{8,0},{9,1},{10,2},{11,3},{12,4},{13,5},{14,6},{15,7}} | collective-permute-start | bytes 245768 | tf_op jit(solution)/shard_map/ppermute | solution.py:583
  47.0 15.4 %collective-permute-start.19 = (bf16[128,320]{1,0:T(8,128)(2,1)S(1)}, bf16[128,320]{1,0:T(8,128)(2,1)S(1)}, u32[]{:S(2)}, u32[]{:S(2)}) collective-permute-start(bf16[128,320]{1,0:T(8,128)(2,1)S(1)} %get-tuple-element.109), channel_id=1, source_target_pairs={{8,0},{9,1},{10,2},{11,3},{12,4},{13,5},{14,6},{15,7}} | collective-permute-start | bytes 245768 | tf_op jit(solution)/shard_map/ppermute | solution.py:583
  58.3 17.4 %collective-permute-start.10 = (bf16[2,4,160,256]{3,2,1,0:T(8,128)(2,1)S(1)}, bf16[2,4,160,256]{3,2,1,0:T(8,128)(2,1)S(1)}, u32[]{:S(2)}, u32[]{:S(2)}) collective-permute-start(bf16[2,4,160,256]{3,2,1,0:T(8,128)(2,1)S(1)} %get-tuple-element.90), channel_id=1, source_target_pairs={{0,4},{4,0},{1,5},{5,1},{2,6},{6,2},{3,7},{7,3},{8,12},{12,8},{9,1... | collective-permute-start | bytes 1966088 | tf_op jit(solution)/shard_map/ppermute | solution.py:565
  63.7 6.1 %collective-permute-start.23 = (bf16[2,80,256]{2,1,0:T(8,128)(2,1)S(1)}, bf16[2,80,256]{2,1,0:T(8,128)(2,1)S(1)}, u32[]{:S(2)}, u32[]{:S(2)}) collective-permute-start(bf16[2,80,256]{2,1,0:T(8,128)(2,1)S(1)} %get-tuple-element.120), channel_id=1, source_target_pairs={{0,3},{1,0},{2,1},{3,2},{8,11},{9,8},{10,9},{11,10},{16,19},{17,16... | collective-permute-start | bytes 245768 | tf_op jit(solution)/shard_map/ppermute | solution.py:592
  63.8 9.4 %collective-permute-start.22 = (bf16[2,80,256]{2,1,0:T(8,128)(2,1)S(1)}, bf16[2,80,256]{2,1,0:T(8,128)(2,1)S(1)}, u32[]{:S(2)}, u32[]{:S(2)}) collective-permute-start(bf16[2,80,256]{2,1,0:T(8,128)(2,1)S(1)} %get-tuple-element.121), channel_id=1, source_target_pairs={{0,2},{1,3},{2,0},{3,1},{8,10},{9,11},{10,8},{11,9},{16,18},{17,19... | collective-permute-start | bytes 245768 | tf_op jit(solution)/shard_map/ppermute | solution.py:592
  64.8 8.3 %collective-permute-start.21 = (bf16[2,80,256]{2,1,0:T(8,128)(2,1)S(1)}, bf16[2,80,256]{2,1,0:T(8,128)(2,1)S(1)}, u32[]{:S(2)}, u32[]{:S(2)}) collective-permute-start(bf16[2,80,256]{2,1,0:T(8,128)(2,1)S(1)} %get-tuple-element.122), channel_id=1, source_target_pairs={{0,1},{1,2},{2,3},{3,0},{8,9},{9,10},{10,11},{11,8},{16,17},{17,18... | collective-permute-start | bytes 245768 | tf_op jit(solution)/shard_map/ppermute | solution.py:592
  73.2 3.1 %collective-permute-start.24 = (bf16[4,2,80,256]{3,2,1,0:T(8,128)(2,1)S(1)}, bf16[4,2,80,256]{3,2,1,0:T(8,128)(2,1)S(1)}, u32[]{:S(2)}, u32[]{:S(2)}) collective-permute-start(bf16[4,2,80,256]{3,2,1,0:T(8,128)(2,1)S(1)} %shard_map.78.own_ref), channel_id=1, source_target_pairs={{0,4},{4,0},{1,5},{5,1},{2,6},{6,2},{3,7},{7,3},{8,12},{12,8},{9,1... | collective-permute-start | bytes 983048 | tf_op jit(solution)/shard_map/ppermute | solution.py:565
  73.3 1.7 %collective-permute-start.25 = (bf16[2,8,8,320]{3,2,1,0:T(8,128)(2,1)S(1)}, bf16[2,8,8,320]{3,2,1,0:T(8,128)(2,1)S(1)}, u32[]{:S(2)}, u32[]{:S(2)}) collective-permute-start(bf16[2,8,8,320]{3,2,1,0:T(8,128)(2,1)S(1)} %get-tuple-element.119), channel_id=1, source_target_pairs={{0,4},{4,0},{1,5},{5,1},{2,6},{6,2},{3,7},{7,3},{8,12},{12,8},{9,1... | collective-permute-start | bytes 245768 | tf_op jit(solution)/shard_map/ppermute | solution.py:565

commit v7 on v6

--- a/solution.py
+++ b/solution.py
@@ -188,6 +188,34 @@
     )(*operands)
 
 
+def half_lanes(count, channels):
+    return channels % 128 == 64 and count % 32 == 0
+
+
+def packed_shape(count, channels):
+    return (count * channels // 128, 128) if half_lanes(count, channels) else (count, channels)
+
+
+def pack(value):
+    count, channels = value.shape
+    if not half_lanes(count, channels):
+        return value
+    parts = [value[:, at : at + 128] for at in range(0, channels - 64, 128)]
+    rest = value[:, channels - 64 :]
+    parts.append(jnp.concatenate([rest[: count // 2], rest[count // 2 :]], axis=1))
+    return jnp.concatenate(parts, axis=0)
+
+
+def unpack(value, count, channels):
+    if not half_lanes(count, channels):
+        return value
+    whole = channels // 128
+    parts = [value[k * count : (k + 1) * count] for k in range(whole)]
+    rest = value[whole * count :]
+    parts.append(jnp.concatenate([rest[:, :64], rest[:, 64:]], axis=0))
+    return jnp.concatenate(parts, axis=1)
+
+
 def neighbours(value, shifted, width):
     count, channels = value.shape
     shifted[8 : 8 + count, :] = value
@@ -217,8 +245,8 @@
     return total
 
 
-def forward_call(field, weights, state, section, crop, crops, width, last, after):
-    count, channels = field.shape
+def forward_call(field, weights, state, section, crop, crops, shape, width, last, after):
+    count, channels = shape
 
     def kernel(field_ref, weights_ref, after_ref, *refs):
         *_, saved_ref, hidden_ref, taps, shifted = refs
@@ -226,6 +254,8 @@
         @pl.when(lax.axis_index("section") == section)
         def _():
             field_in = field_ref[...]
+            if section:
+                field_in = unpack(field_in, count, channels)
             wide = field_in.astype(jnp.float32)
             saved_ref[0, crop] = field_in
             hidden = convolved(wide, weights_ref.at[0], taps, shifted, width)
@@ -236,10 +266,10 @@
                 added = convolved(
                     active.astype(jnp.float32), weights_ref.at[1], taps, shifted, width
                 )
-                refs[-5][...] = (wide + added).astype(jnp.bfloat16)
+                refs[-5][...] = pack((wide + added).astype(jnp.bfloat16))
 
     outs = [
-        jax.ShapeDtypeStruct((count, channels), jnp.bfloat16),
+        jax.ShapeDtypeStruct(packed_shape(count, channels), jnp.bfloat16),
         jax.ShapeDtypeStruct((2, crops, count, channels), jnp.bfloat16),
         jax.ShapeDtypeStruct((crops, count, channels), jnp.float32),
     ][1 if last else 0 :]
@@ -253,9 +283,9 @@
 
 
 def backward_call(
-    grad, turned, hidden, state, section, crop, crops, width, parts, after
+    grad, turned, hidden, state, section, crop, crops, shape, width, last, parts, after
 ):
-    count, channels = grad.shape
+    count, channels = shape
     share = channels // parts
     first = section == 0
 
@@ -264,9 +294,12 @@
 
         @pl.when(lax.axis_index("section") == section)
         def _():
-            wide = grad_ref[...].astype(jnp.float32)
+            grad = grad_ref[...]
+            if not last:
+                grad = unpack(grad, count, channels)
+            wide = grad.astype(jnp.float32)
             own = lax.axis_index("img")
-            place_parts(sent_ref, (0,), grad_ref[...], crop, parts, own)
+            place_parts(sent_ref, (0,), grad, crop, parts, own)
             grad_active = convolved(wide, turned_ref.at[1], taps, shifted, width)
             hidden = hidden_ref[crop]
             gate = jax.nn.sigmoid(hidden)
@@ -280,10 +313,10 @@
             result = (wide + added).astype(jnp.bfloat16)
             kept_ref[crop] = result
             if not first:
-                refs[-5][...] = result
+                refs[-5][...] = pack(result)
 
     outs = [
-        jax.ShapeDtypeStruct((count, channels), jnp.bfloat16),
+        jax.ShapeDtypeStruct(packed_shape(count, channels), jnp.bfloat16),
         jax.ShapeDtypeStruct((crops, count, channels), jnp.bfloat16),
         jax.ShapeDtypeStruct((parts, 2, share, crops * count), jnp.bfloat16),
     ][1 if first else 0 :]
@@ -377,20 +410,24 @@
     return call(kernel, [out, out], [strips, cotangent], (), sems, {}, (0, 1))
 
 
-def load_call(weights):
-    def kernel(weights_ref, out_ref, sems):
-        copies = [
-            pltpu.make_async_copy(weights_ref.at[which], out_ref.at[which], sems.at[which])
-            for which in range(2)
-        ]
-        for copy in copies:
-            copy.start()
-        for copy in copies:
-            copy.wait()
+def load_call(weights, first, after):
+    def kernel(weights_ref, after_ref, *refs):
+        out_ref, sems = refs[-2:]
+
+        @pl.when((lax.axis_index("section") == 0) | (not first))
+        def _():
+            copies = [
+                pltpu.make_async_copy(weights_ref.at[which], out_ref.at[which], sems.at[which])
+                for which in range(2)
+            ]
+            for copy in copies:
+                copy.start()
+            for copy in copies:
+                copy.wait()
 
     out = jax.ShapeDtypeStruct(weights.shape, weights.dtype)
     sems = [pltpu.SemaphoreType.DMA((2,))]
-    (loaded,) = call(kernel, [out], [weights], (), sems, {}, (0,))
+    (loaded,) = call(kernel, [out], [weights, after], (1,), sems, {}, (0,))
     return loaded
 
 
@@ -495,16 +532,17 @@
     return call(kernel, [out, out], [saved, weights, *blocks], (), scratch, {})
 
 
-def spread_call(cells_of, around, place, count, width, sections):
+def spread_call(cells_of, around, place, count, width, sections, marked=False):
     two, blocks, share, cells = cells_of.shape
     crops = cells // count
     stride = count + width
     total = 2 * blocks * crops * stride + width
 
     def kernel(cells_ref, *refs):
-        out_ref, done_ref, shifted = refs[-3:]
+        out_ref, shifted = refs[-3 if marked else -2], refs[-1]
         section = lax.axis_index("section")
-        done_ref[...] = jnp.zeros_like(done_ref)
+        if marked:
+            refs[-2][...] = jnp.zeros_like(refs[-2])
 
         @pl.when((section >= sections[0]) & (section <= sections[1]))
         def _():
@@ -529,7 +567,8 @@
     operands = [cells_of] if around is None else [cells_of, around]
     aliases = {} if around is None else {1: 0}
     token = jax.ShapeDtypeStruct((8, 128), jnp.float32)
-    return call(kernel, [out, token], operands, (), scratch, aliases)
+    outs = [out, token] if marked else [out]
+    return call(kernel, outs, operands, (), scratch, aliases)
 
 
 def terms_call(around, own, other, count, width, scaling):
@@ -538,8 +577,9 @@
     stride = count + width
     crops = cells // count
 
-    def kernel(around_ref, own_ref, other_ref, out_ref):
-        for kind in range(2):
+    def kernel(around_ref, own_ref, other_ref, out_ref, held, sems):
+        copies = []
+        for kind in (1, 0):
             for down in range(3):
                 total = None
                 for block in range(2 * blocks):
@@ -552,12 +592,27 @@
                     term = jnp.dot(left, right, preferred_element_type=jnp.float32)
                     total = term if total is None else total + term
                 total = (total * scaling).T.reshape(3, rows, columns)
+                third = pl.ds(3 * down, 3)
                 for place in range(3):
-                    out_ref[kind, 3 * down + place] = total[place]
-
-    out = jax.ShapeDtypeStruct((2, 9, rows, columns), jnp.float32)
-    (terms,) = call(kernel, [out], [around, own, other], (), [], {})
-    return terms
+                    held[kind, 3 * down + place] = total[place]
+                copy = pltpu.make_async_copy(
+                    held.at[kind, third], out_ref.at[kind, third], sems.at[3 * kind + down]
+                )
+                copy.start()
+                copies.append(copy)
+        for copy in copies:
+            copy.wait()
+
+    shape = (2, 9, rows, columns)
+    return pl.pallas_call(
+        kernel,
+        out_shape=jax.ShapeDtypeStruct(shape, jnp.float32),
+        in_specs=[pl.BlockSpec(memory_space=pltpu.VMEM)] * 3,
+        out_specs=pl.BlockSpec(memory_space=pltpu.HBM),
+        scratch_shapes=[pltpu.VMEM(shape, jnp.float32), pltpu.SemaphoreType.DMA((6,))],
+        compiler_params=pltpu.CompilerParams(vmem_limit_bytes=8 << 20),
+        name="terms",
+    )(around, own, other)
 
 
 def rotated(value, axis, steps):
@@ -572,6 +627,7 @@
     width = col_count * slabs
     count = row_count * width
     crops = images * strip_count // slabs
+    shape = (count, channels)
     last = sections - 1
     early = min(1, last - 1)
     steps = range(1, groups)
@@ -604,7 +660,8 @@
     )
     other = swapped(other)
     weights = kernels[0].reshape(2, 3, 3 * channels, channels)
-    weights = load_call(pltpu.with_memory_space_constraint(weights, pltpu.HBM))
+    stored = pltpu.with_memory_space_constraint(weights, pltpu.HBM)
+    weights = load_call(stored, True, own)
     fields = join_call(own, other)
     incoming = fields
     state = []
@@ -613,9 +670,11 @@
         outgoing = []
         for crop in range(crops):
             out, state = forward_call(
-                incoming[crop], weights, state, place, crop, crops, width, place == last, after
+                incoming[crop], weights, state, place, crop, crops, shape, width, place == last, after
             )
             outgoing.append(out)
+        if place == 0:
+            weights = load_call(stored, False, state[0])
         if place < last:
             incoming = hop(outgoing, place, place + 1)
         if place == early:
@@ -631,7 +690,18 @@
         outgoing = []
         for crop in range(crops):
             out, grads = backward_call(
-                incoming[crop], turned, hidden, grads, place, crop, crops, width, groups, after
+                incoming[crop],
+                turned,
+                hidden,
+                grads,
+                place,
+                crop,
+                crops,
+                shape,
+                width,
+                place == last,
+                groups,
+                after,
             )
             outgoing.append(out)
         if place:
@@ -641,17 +711,19 @@
             late = [shared(inputs, step, range(sections)) for step in steps]
         if place == 1:
             home, outer = remake_call(saved, weights, soon, width, (0, 0))
-            outer = swapped(outer)
-            around, after = spread_call(home, None, 0, count, width, (0, 0))
-            around, after = spread_call(outer, around, 1, count, width, (0, 0))
+            outer = lax.ppermute(
+                outer, ("section", "slab"), [(i, (i + 1) % slabs) for i in range(slabs)]
+            )
+            (around,) = spread_call(home, None, 0, count, width, (0, 0))
+            around, after = spread_call(outer, around, 1, count, width, (0, 0), True)
     kept, sent = grads
     own = [sent[0]]
     for step in steps:
         own.append(shared(sent[step], step, range(sections)))
     home, outer = remake_call(saved, weights, late, width, (1, last))
     outer = swapped(outer)
-    around, _ = spread_call(home, around, 0, count, width, (1, last))
-    around, _ = spread_call(outer, around, 1, count, width, (1, last))
+    (around,) = spread_call(home, around, 0, count, width, (1, last))
+    (around,) = spread_call(outer, around, 1, count, width, (1, last))
     own = stack_call(own)
     other = swapped(own)
     terms = terms_call(around, own, other, count, width, scaling)

time: 80.2 us -> 81.4 us (1.015)
    pallas_call x0 -> x1, Pallas kernels: none -> 3.18 us  [terms_call(): pl.pallas_call(kernel, out_shape=jax.ShapeDtypeStruct(shape, jnp.float32)...]
    pallas_call x32, Pallas kernels: 21.4 us -> 18.6 us  [call(): pl.pallas_call(kernel, out_shape=outs, in_specs=[pl.BlockSpec(memory_spac...]
    ppermute x12, waiting for transfers between devices: 2.06 us -> 0.03 us  [hop(): arrived.append(lax.ppermute(value, 'section', [(source, target)]))]
    ppermute x0 -> x1, starting transfers between devices: none -> 1.95 us  [crop_shards(): lax.ppermute(outer, ('section', 'slab'), [(i, (i + 1) % slabs) for i in r...]
    ppermute x9, waiting for transfers between devices: 22.9 us -> 24.7 us  [shared(): return lax.ppermute(values, ('section', 'img'), pairs)]
    ppermute x12, starting transfers between devices: 12.3 us -> 11.2 us  [hop(): arrived.append(lax.ppermute(value, 'section', [(source, target)]))]
  transfers between devices with their start and end apart: 26 -> 26, of which waited for: 7 -> 5; matrix products, arithmetic and copies ran while one was open for 0% -> 0% of each run, Pallas kernels for 16% -> 16%
where the time goes in v7:
time: 81.4 us; the launch traced here: 81 us
  starting transfers between devices  32.1 us (39%)
  waiting for transfers between devices  25.8 us (32%)
  Pallas kernels  21.8 us (27%)
  between operations  1.26 us (2%)
    ppermute x9, waiting for transfers between devices, shared(): return lax.ppermute(values, ('section', 'img'), pairs)  24.7 us
    pallas_call x32, Pallas kernels, call(): pl.pallas_call(kernel, out_shape=outs, in_specs=[pl.BlockSpec(memory_spac...  18.6 us
    ppermute x9, starting transfers between devices, shared(): return lax.ppermute(values, ('section', 'img'), pairs)  17.8 us
    ppermute x12, starting transfers between devices, hop(): arrived.append(lax.ppermute(value, 'section', [(source, target)]))  11.2 us
    pallas_call x1, Pallas kernels, terms_call(): pl.pallas_call(kernel, out_shape=jax.ShapeDtypeStruct(shape, jnp.float32)...  3.18 us
    ppermute x1, starting transfers between devices, crop_shards(): lax.ppermute(outer, ('section', 'slab'), [(i, (i + 1) % slabs) for i in r...  1.95 us
  transfers between devices with their start and end apart: 26, of which 5 were waited for; matrix products, arithmetic and copies ran while one was open for 0% of the time, Pallas kernels for 16%

profile of v7, /device:TPU:0, one launch (start us, length us, event | category | flops | bytes accessed | tf_op | source)
XLA Modules:
  0.0 81.0 jit_solution(13389949930367709732)
XLA Ops:
  0.6 1.0 %shard_map.50 = (bf16[2,8,8,320]{3,2,1,0:T(8,128)(2,1)S(1)}, bf16[2,8,8,320]{3,2,1,0:T(8,128)(2,1)S(1)}) custom-call(bf16[1,4,8,8,320]{4,3,2,1,0:T(8,128)(2,1)} %strips_ref.1, bf16[1,4,8,8,320]{4,3,2,1,0:T(8,128)(2,1)} %cotangent_ref.1), custom_call_target="tpu_custom_call" | custom-call | tf_op jit(solution)/shard_map/pallas_call | solution.py:177
  1.6 0.6 collective-permute-start
  2.2 2.3 %shard_map.52.weights_ref.after_ref = bf16[2,3,960,320]{3,2,1,0:T(8,128)(2,1)S(1)} custom-call(bf16[2,3,960,320]{3,2,1,0:T(8,128)(2,1)} %bitcast.11, bf16[2,8,8,320]{3,2,1,0:T(8,128)(2,1)S(1)} %get-tuple-element.58.own_ref.after_ref), custom_call_target="tpu_custom_call" | custom-call | tf_op jit(solution)/shard_map/pallas_call | solution.py:177
  4.5 0.0 collective-permute-done.other_ref
  4.5 0.1 shard_map.51
  4.6 1.4 %shard_map.53 = (bf16[320,128]{1,0:T(8,128)(2,1)S(1)}, bf16[2,2,128,320]{3,2,1,0:T(8,128)(2,1)S(1)}, f32[2,128,320]{2,1,0:T(8,128)S(1)}) custom-call(bf16[128,320]{1,0:T(8,128)(2,1)S(1)} %get-tuple-element.61.field_ref.grad_ref, bf16[2,3,960,320]{3,2,1,0:T(8,128)(2,1)S(1)} %shard_map.52.weights_ref.after_ref, ...), custom_call_target="tpu_custom_call" | custom-call | tf_op jit(solution)/shard_map/pallas_call | solution.py:177
  5.9 2.0 %collective-permute-start.2 = (bf16[320,128]{1,0:T(8,128)(2,1)S(1)}, bf16[320,128]{1,0:T(8,128)(2,1)S(1)}, u32[]{:S(2)}, u32[]{:S(2)}) collective-permute-start(bf16[320,128]{1,0:T(8,128)(2,1)S(1)} %get-tuple-element.66), channel_id=1, source_target_pairs={{0,8},{1,9},{2,10},{3,11},{4,12},{5,13},{6,14},{7,15}} | collective-permute-start | bytes 245768 | tf_op jit(solution)/shard_map/ppermute | solution.py:639
  7.9 1.4 %shard_map.54 = (bf16[320,128]{1,0:T(8,128)(2,1)S(1)}, bf16[2,2,128,320]{3,2,1,0:T(8,128)(2,1)S(1)}, f32[2,128,320]{2,1,0:T(8,128)S(1)}) custom-call(bf16[128,320]{1,0:T(8,128)(2,1)S(1)} %get-tuple-element.60.field_ref.grad_ref, bf16[2,3,960,320]{3,2,1,0:T(8,128)(2,1)S(1)} %shard_map.52.weights_ref.after_ref, ...), custom_call_target="tpu_custom_call", output_to_operand_aliasing={{1}: (3, {}), {2}: (4, {})} | custom-call | tf_op jit(solution)/shard_map/pallas_call | solution.py:177
  9.3 1.3 %collective-permute-start.1 = (bf16[320,128]{1,0:T(8,128)(2,1)S(1)}, bf16[320,128]{1,0:T(8,128)(2,1)S(1)}, u32[]{:S(2)}, u32[]{:S(2)}) collective-permute-start(bf16[320,128]{1,0:T(8,128)(2,1)S(1)} %get-tuple-element.64), channel_id=1, source_target_pairs={{0,8},{1,9},{2,10},{3,11},{4,12},{5,13},{6,14},{7,15}} | collective-permute-start | bytes 245768 | tf_op jit(solution)/shard_map/ppermute | solution.py:639
  10.6 2.3 %shard_map.55.weights_ref = bf16[2,3,960,320]{3,2,1,0:T(8,128)(2,1)S(1)} custom-call(bf16[2,3,960,320]{3,2,1,0:T(8,128)(2,1)} %bitcast.12, bf16[2,2,128,320]{3,2,1,0:T(8,128)(2,1)S(1)} %get-tuple-element.65.after_ref.refs_0_), custom_call_target="tpu_custom_call" | custom-call | tf_op jit(solution)/shard_map/pallas_call | solution.py:177
  12.9 0.0 collective-permute-done.2.field_ref
  13.0 0.7 collective-permute-start.4
  13.6 0.0 collective-permute-done.1.field_ref
  13.7 0.7 collective-permute-start.3
  14.3 0.1 shard_map.67
  14.4 5.8 %collective-permute-start.13 = (bf16[2,160,256]{2,1,0:T(8,128)(2,1)S(1)}, bf16[2,160,256]{2,1,0:T(8,128)(2,1)S(1)}, u32[]{:S(2)}, u32[]{:S(2)}) collective-permute-start(bf16[2,160,256]{2,1,0:T(8,128)(2,1)S(1)} %shard_map.67), channel_id=1, source_target_pairs={{0,3},{1,0},{2,1},{3,2},{4,7},{5,4},{6,5},{7,6}} | collective-permute-start | bytes 491528 | tf_op jit(solution)/shard_map/ppermute | solution.py:648
  20.2 1.9 %collective-permute-start.12 = (bf16[2,160,256]{2,1,0:T(8,128)(2,1)S(1)}, bf16[2,160,256]{2,1,0:T(8,128)(2,1)S(1)}, u32[]{:S(2)}, u32[]{:S(2)}) collective-permute-start(bf16[2,160,256]{2,1,0:T(8,128)(2,1)S(1)} %shard_map.67), channel_id=1, source_target_pairs={{0,2},{1,3},{2,0},{3,1},{4,6},{5,7},{6,4},{7,5}} | collective-permute-start | bytes 491528 | tf_op jit(solution)/shard_map/ppermute | solution.py:648
  22.2 2.9 %collective-permute-start.11 = (bf16[2,160,256]{2,1,0:T(8,128)(2,1)S(1)}, bf16[2,160,256]{2,1,0:T(8,128)(2,1)S(1)}, u32[]{:S(2)}, u32[]{:S(2)}) collective-permute-start(bf16[2,160,256]{2,1,0:T(8,128)(2,1)S(1)} %shard_map.67), channel_id=1, source_target_pairs={{0,1},{1,2},{2,3},{3,0},{4,5},{5,6},{6,7},{7,4}} | collective-permute-start | bytes 491528 | tf_op jit(solution)/shard_map/ppermute | solution.py:648
  25.1 1.4 %shard_map.58.after_ref.turned_ref = bf16[2,3,960,320]{3,2,1,0:T(8,128)(2,1)S(1)} custom-call(bf16[2,3,960,320]{3,2,1,0:T(8,128)(2,1)S(1)} %shard_map.55.weights_ref, bf16[2,2,128,320]{3,2,1,0:T(8,128)(2,1)S(1)} %get-tuple-element.71.after_ref.refs_0_), custom_call_target="tpu_custom_call" | custom-call | tf_op jit(solution)/shard_map/pallas_call | solution.py:177
  26.4 0.0 collective-permute-done.4.field_ref
  26.4 0.7 collective-permute-start.6
  27.1 0.0 collective-permute-done.3.field_ref
  27.2 0.7 collective-permute-start.5
  27.8 0.0 collective-permute-done.6.field_ref
  27.9 0.0 collective-permute-done.5.field_ref
  27.9 0.0 collective-permute-done.13.refs_2_
  27.9 7.8 %collective-permute-done.12.refs_1_ = bf16[2,160,256]{2,1,0:T(8,128)(2,1)S(1)} collective-permute-done((bf16[2,160,256]{2,1,0:T(8,128)(2,1)S(1)}, bf16[2,160,256]{2,1,0:T(8,128)(2,1)S(1)}, u32[]{:S(2)}, u32[]{:S(2)}) %collective-permute-start.12) | collective-permute-done | bytes 163872 | tf_op jit(solution)/shard_map/ppermute | solution.py:648
  35.7 0.0 collective-permute-done.11.refs_0_
  35.7 2.9 %shard_map.68 = (bf16[2,4,160,256]{3,2,1,0:T(8,128)(2,1)S(1)}, bf16[2,4,160,256]{3,2,1,0:T(8,128)(2,1)S(1)}) custom-call(bf16[2,2,128,320]{3,2,1,0:T(8,128)(2,1)S(1)} %get-tuple-element.82.refs_0_.saved_ref, bf16[2,3,960,320]{3,2,1,0:T(8,128)(2,1)S(1)} %shard_map.55.weights_ref, bf16[2,160,256]{2,1,0:T(8,128)(2,1)S(1)} %collective-permute-done.11.refs_0_, ...), custom_call_target="tpu_custom_call" | custom-call | tf_op jit(solution)/shard_map/pallas_call | solution.py:177
  38.6 2.0 %collective-permute-start.14 = (bf16[2,4,160,256]{3,2,1,0:T(8,128)(2,1)S(1)}, bf16[2,4,160,256]{3,2,1,0:T(8,128)(2,1)S(1)}, u32[]{:S(2)}, u32[]{:S(2)}) collective-permute-start(bf16[2,4,160,256]{3,2,1,0:T(8,128)(2,1)S(1)} %get-tuple-element.89), channel_id=1, source_target_pairs={{0,4},{4,0},{1,5},{5,1},{2,6},{6,2},{3,7},{7,3}} | collective-permute-start | bytes 1966088 | tf_op jit(solution)/shard_map/ppermute | solution.py:714
  40.6 0.7 collective-permute-start.16
  41.3 0.7 collective-permute-start.15
  42.0 0.0 collective-permute-done.16.grad_ref
  42.0 0.7 collective-permute-start.18
  42.7 0.1 shard_map.65
  42.8 0.4 collective-permute-start.9
  43.2 2.3 %collective-permute-start.8 = (bf16[2,160,256]{2,1,0:T(8,128)(2,1)S(1)}, bf16[2,160,256]{2,1,0:T(8,128)(2,1)S(1)}, u32[]{:S(2)}, u32[]{:S(2)}) collective-permute-start(bf16[2,160,256]{2,1,0:T(8,128)(2,1)S(1)} %shard_map.65), channel_id=1, source_target_pairs={{0,2},{1,3},{2,0},{3,1},{8,10},{9,11},{10,8},{11,9},{16,18},{17,19... | collective-permute-start | bytes 491528 | tf_op jit(solution)/shard_map/ppermute | solution.py:648
  45.5 0.0 collective-permute-done.15.grad_ref
  45.5 1.9 %collective-permute-start.7 = (bf16[2,160,256]{2,1,0:T(8,128)(2,1)S(1)}, bf16[2,160,256]{2,1,0:T(8,128)(2,1)S(1)}, u32[]{:S(2)}, u32[]{:S(2)}) collective-permute-start(bf16[2,160,256]{2,1,0:T(8,128)(2,1)S(1)} %shard_map.65), channel_id=1, source_target_pairs={{0,1},{1,2},{2,3},{3,0},{8,9},{9,10},{10,11},{11,8},{16,17},{17,18... | collective-permute-start | bytes 491528 | tf_op jit(solution)/shard_map/ppermute | solution.py:648
  47.4 0.0 collective-permute-done.18.grad_ref
  47.4 0.7 collective-permute-start.17
  48.1 1.3 %collective-permute-start.20 = (bf16[320,128]{1,0:T(8,128)(2,1)S(1)}, bf16[320,128]{1,0:T(8,128)(2,1)S(1)}, u32[]{:S(2)}, u32[]{:S(2)}) collective-permute-start(bf16[320,128]{1,0:T(8,128)(2,1)S(1)} %get-tuple-element.105), channel_id=1, source_target_pairs={{8,0},{9,1},{10,2},{11,3},{12,4},{13,5},{14,6},{15,7}} | collective-permute-start | bytes 245768 | tf_op jit(solution)/shard_map/ppermute | solution.py:639
  49.5 0.0 collective-permute-done.9.refs_2_
  49.5 1.3 %collective-permute-start.19 = (bf16[320,128]{1,0:T(8,128)(2,1)S(1)}, bf16[320,128]{1,0:T(8,128)(2,1)S(1)}, u32[]{:S(2)}, u32[]{:S(2)}) collective-permute-start(bf16[320,128]{1,0:T(8,128)(2,1)S(1)} %get-tuple-element.103), channel_id=1, source_target_pairs={{8,0},{9,1},{10,2},{11,3},{12,4},{13,5},{14,6},{15,7}} | collective-permute-start | bytes 245768 | tf_op jit(solution)/shard_map/ppermute | solution.py:639
  50.8 10.0 %collective-permute-done.8.refs_1_ = bf16[2,160,256]{2,1,0:T(8,128)(2,1)S(1)} collective-permute-done((bf16[2,160,256]{2,1,0:T(8,128)(2,1)S(1)}, bf16[2,160,256]{2,1,0:T(8,128)(2,1)S(1)}, u32[]{:S(2)}, u32[]{:S(2)}) %collective-permute-start.8) | collective-permute-done | bytes 163872 | tf_op jit(solution)/shard_map/ppermute | solution.py:648
  60.8 0.0 collective-permute-start.10
  60.8 1.1 %shard_map.69.refs_0_ = bf16[2,2320,480]{2,1,0:T(8,128)(2,1)S(1)} custom-call(bf16[2,4,160,256]{3,2,1,0:T(8,128)(2,1)S(1)} %get-tuple-element.90.cells_ref), custom_call_target="tpu_custom_call" | custom-call | tf_op jit(solution)/shard_map/pallas_call | solution.py:177
  61.9 1.1 %shard_map.70 = (bf16[2,2320,480]{2,1,0:T(8,128)(2,1)S(1)}, f32[8,128]{1,0:T(8,128)S(1)}) custom-call(bf16[2,4,160,256]{3,2,1,0:T(8,128)(2,1)S(1)} %collective-permute-done.14.cells_ref, bf16[2,2320,480]{2,1,0:T(8,128)(2,1)S(1)} %shard_map.69.refs_0_), custom_call_target="tpu_custom_call", output_to_operand_aliasing={{0}: (1, {})} | custom-call | tf_op jit(solution)/shard_map/pallas_call | solution.py:177
  63.1 0.0 collective-permute-done.20.grad_ref
  63.1 1.3 %shard_map.77 = (bf16[2,128,320]{2,1,0:T(8,128)(2,1)S(1)}, bf16[4,2,80,256]{3,2,1,0:T(8,128)(2,1)S(1)}) custom-call(bf16[320,128]{1,0:T(8,128)(2,1)S(1)} %collective-permute-done.20.grad_ref, bf16[2,3,960,320]{3,2,1,0:T(8,128)(2,1)S(1)} %shard_map.58.after_ref.turned_ref, ...), custom_call_target="tpu_custom_call", output_to_operand_aliasing={{0}: (4, {}), {1}: (5, {})} | custom-call | tf_op jit(solution)/shard_map/pallas_call | solution.py:177
  64.4 0.0 collective-permute-done.19.grad_ref
  64.4 1.3 %shard_map.78 = (bf16[2,128,320]{2,1,0:T(8,128)(2,1)S(1)}, bf16[4,2,80,256]{3,2,1,0:T(8,128)(2,1)S(1)}) custom-call(bf16[320,128]{1,0:T(8,128)(2,1)S(1)} %collective-permute-done.19.grad_ref, bf16[2,3,960,320]{3,2,1,0:T(8,128)(2,1)S(1)} %shard_map.58.after_ref.turned_ref, ...), custom_call_target="tpu_custom_call", output_to_operand_aliasing={{0}: (4, {}), {1}: (5, {})} | custom-call | tf_op jit(solution)/shard_map/pallas_call | solution.py:177
  65.7 0.1 collective-permute-start.23
  65.7 0.6 collective-permute-start.22
  66.3 1.9 %collective-permute-start.21 = (bf16[2,80,256]{2,1,0:T(8,128)(2,1)S(1)}, bf16[2,80,256]{2,1,0:T(8,128)(2,1)S(1)}, u32[]{:S(2)}, u32[]{:S(2)}) collective-permute-start(bf16[2,80,256]{2,1,0:T(8,128)(2,1)S(1)} %get-tuple-element.116), channel_id=1, source_target_pairs={{0,1},{1,2},{2,3},{3,0},{8,9},{9,10},{10,11},{11,8},{16,17},{17,18... | collective-permute-start | bytes 245768 | tf_op jit(solution)/shard_map/ppermute | solution.py:648
  68.2 3.5 %collective-permute-done.23.refs_3_ = bf16[2,80,256]{2,1,0:T(8,128)(2,1)S(1)} collective-permute-done((bf16[2,80,256]{2,1,0:T(8,128)(2,1)S(1)}, bf16[2,80,256]{2,1,0:T(8,128)(2,1)S(1)}, u32[]{:S(2)}, u32[]{:S(2)}) %collective-permute-start.23) | collective-permute-done | bytes 81952 | tf_op jit(solution)/shard_map/ppermute | solution.py:648
  71.7 3.4 %collective-permute-done.22.refs_2_ = bf16[2,80,256]{2,1,0:T(8,128)(2,1)S(1)} collective-permute-done((bf16[2,80,256]{2,1,0:T(8,128)(2,1)S(1)}, bf16[2,80,256]{2,1,0:T(8,128)(2,1)S(1)}, u32[]{:S(2)}, u32[]{:S(2)}) %collective-permute-start.22) | collective-permute-done | bytes 81952 | tf_op jit(solution)/shard_map/ppermute | solution.py:648
  75.1 0.1 collective-permute-start.24
  75.2 0.1 shard_map.80
  75.3 0.6 collective-permute-start.25
  75.8 1.1 %collective-permute-done.25.other_ref = bf16[2,8,8,320]{3,2,1,0:T(8,128)(2,1)S(1)} collective-permute-done((bf16[2,8,8,320]{3,2,1,0:T(8,128)(2,1)S(1)}, bf16[2,8,8,320]{3,2,1,0:T(8,128)(2,1)S(1)}, u32[]{:S(2)}, u32[]{:S(2)}) %collective-permute-start.25) | collective-permute-done | bytes 81952 | tf_op jit(solution)/shard_map/ppermute | solution.py:620
  77.0 0.7 shard_map.81
  77.7 0.0 collective-permute-done.10.cells_ref
  77.7 3.2 %terms.1 = f32[2,9,160,80]{3,2,1,0:T(8,128)} custom-call(bf16[2,2320,480]{2,1,0:T(8,128)(2,1)S(1)} %shard_map.72.around_ref, bf16[4,2,80,256]{3,2,1,0:T(8,128)(2,1)S(1)} %shard_map.79.own_ref, bf16[4,2,80,256]{3,2,1,0:T(8,128)(2,1)S(1)} %collective-permute-done.24.other_ref), custom_call_target="tpu_custom_call" | custom-call | tf_op jit(solution)/shard_map/terms/pallas_call | solution.py:607
  (22 shorter events, 0.3 us)
Async XLA Ops:
  1.6 2.9 %collective-permute-start = (bf16[2,8,8,320]{3,2,1,0:T(8,128)(2,1)S(1)}, bf16[2,8,8,320]{3,2,1,0:T(8,128)(2,1)S(1)}, u32[]{:S(2)}, u32[]{:S(2)}) collective-permute-start(bf16[2,8,8,320]{3,2,1,0:T(8,128)(2,1)S(1)} %get-tuple-element.59), channel_id=1, source_target_pairs={{0,4},{4,0},{1,5},{5,1},{2,6},{6,2},{3,7},{7,3},{8,12},{12,8},{9,1... | collective-permute-start | bytes 245768 | tf_op jit(solution)/shard_map/ppermute | solution.py:620
  5.9 7.0 %collective-permute-start.2 = (bf16[320,128]{1,0:T(8,128)(2,1)S(1)}, bf16[320,128]{1,0:T(8,128)(2,1)S(1)}, u32[]{:S(2)}, u32[]{:S(2)}) collective-permute-start(bf16[320,128]{1,0:T(8,128)(2,1)S(1)} %get-tuple-element.66), channel_id=1, source_target_pairs={{0,8},{1,9},{2,10},{3,11},{4,12},{5,13},{6,14},{7,15}} | collective-permute-start | bytes 245768 | tf_op jit(solution)/shard_map/ppermute | solution.py:639
  9.3 4.3 %collective-permute-start.1 = (bf16[320,128]{1,0:T(8,128)(2,1)S(1)}, bf16[320,128]{1,0:T(8,128)(2,1)S(1)}, u32[]{:S(2)}, u32[]{:S(2)}) collective-permute-start(bf16[320,128]{1,0:T(8,128)(2,1)S(1)} %get-tuple-element.64), channel_id=1, source_target_pairs={{0,8},{1,9},{2,10},{3,11},{4,12},{5,13},{6,14},{7,15}} | collective-permute-start | bytes 245768 | tf_op jit(solution)/shard_map/ppermute | solution.py:639
  13.0 13.5 %collective-permute-start.4 = (bf16[320,128]{1,0:T(8,128)(2,1)S(1)}, bf16[320,128]{1,0:T(8,128)(2,1)S(1)}, u32[]{:S(2)}, u32[]{:S(2)}) collective-permute-start(bf16[320,128]{1,0:T(8,128)(2,1)S(1)} %get-tuple-element.72), channel_id=1, source_target_pairs={{8,16},{9,17},{10,18},{11,19},{12,20},{13,21},{14,22},{15,23}} | collective-permute-start | bytes 245768 | tf_op jit(solution)/shard_map/ppermute | solution.py:639
  13.7 13.5 %collective-permute-start.3 = (bf16[320,128]{1,0:T(8,128)(2,1)S(1)}, bf16[320,128]{1,0:T(8,128)(2,1)S(1)}, u32[]{:S(2)}, u32[]{:S(2)}) collective-permute-start(bf16[320,128]{1,0:T(8,128)(2,1)S(1)} %get-tuple-element.70), channel_id=1, source_target_pairs={{8,16},{9,17},{10,18},{11,19},{12,20},{13,21},{14,22},{15,23}} | collective-permute-start | bytes 245768 | tf_op jit(solution)/shard_map/ppermute | solution.py:639
  14.4 13.5 %collective-permute-start.13 = (bf16[2,160,256]{2,1,0:T(8,128)(2,1)S(1)}, bf16[2,160,256]{2,1,0:T(8,128)(2,1)S(1)}, u32[]{:S(2)}, u32[]{:S(2)}) collective-permute-start(bf16[2,160,256]{2,1,0:T(8,128)(2,1)S(1)} %shard_map.67), channel_id=1, source_target_pairs={{0,3},{1,0},{2,1},{3,2},{4,7},{5,4},{6,5},{7,6}} | collective-permute-start | bytes 491528 | tf_op jit(solution)/shard_map/ppermute | solution.py:648
  20.2 15.5 %collective-permute-start.12 = (bf16[2,160,256]{2,1,0:T(8,128)(2,1)S(1)}, bf16[2,160,256]{2,1,0:T(8,128)(2,1)S(1)}, u32[]{:S(2)}, u32[]{:S(2)}) collective-permute-start(bf16[2,160,256]{2,1,0:T(8,128)(2,1)S(1)} %shard_map.67), channel_id=1, source_target_pairs={{0,2},{1,3},{2,0},{3,1},{4,6},{5,7},{6,4},{7,5}} | collective-permute-start | bytes 491528 | tf_op jit(solution)/shard_map/ppermute | solution.py:648
  22.2 13.6 %collective-permute-start.11 = (bf16[2,160,256]{2,1,0:T(8,128)(2,1)S(1)}, bf16[2,160,256]{2,1,0:T(8,128)(2,1)S(1)}, u32[]{:S(2)}, u32[]{:S(2)}) collective-permute-start(bf16[2,160,256]{2,1,0:T(8,128)(2,1)S(1)} %shard_map.67), channel_id=1, source_target_pairs={{0,1},{1,2},{2,3},{3,0},{4,5},{5,6},{6,7},{7,4}} | collective-permute-start | bytes 491528 | tf_op jit(solution)/shard_map/ppermute | solution.py:648
  26.4 1.4 %collective-permute-start.6 = (bf16[320,128]{1,0:T(8,128)(2,1)S(1)}, bf16[320,128]{1,0:T(8,128)(2,1)S(1)}, u32[]{:S(2)}, u32[]{:S(2)}) collective-permute-start(bf16[320,128]{1,0:T(8,128)(2,1)S(1)} %get-tuple-element.77), channel_id=1, source_target_pairs={{16,24},{17,25},{18,26},{19,27},{20,28},{21,29},{22,30},{23,31}} | collective-permute-start | bytes 245768 | tf_op jit(solution)/shard_map/ppermute | solution.py:639
  27.2 0.7 collective-permute-start.5
  38.6 23.3 %collective-permute-start.14 = (bf16[2,4,160,256]{3,2,1,0:T(8,128)(2,1)S(1)}, bf16[2,4,160,256]{3,2,1,0:T(8,128)(2,1)S(1)}, u32[]{:S(2)}, u32[]{:S(2)}) collective-permute-start(bf16[2,4,160,256]{3,2,1,0:T(8,128)(2,1)S(1)} %get-tuple-element.89), channel_id=1, source_target_pairs={{0,4},{4,0},{1,5},{5,1},{2,6},{6,2},{3,7},{7,3}} | collective-permute-start | bytes 1966088 | tf_op jit(solution)/shard_map/ppermute | solution.py:714
  40.6 1.4 %collective-permute-start.16 = (bf16[320,128]{1,0:T(8,128)(2,1)S(1)}, bf16[320,128]{1,0:T(8,128)(2,1)S(1)}, u32[]{:S(2)}, u32[]{:S(2)}) collective-permute-start(bf16[320,128]{1,0:T(8,128)(2,1)S(1)} %get-tuple-element.92), channel_id=1, source_target_pairs={{24,16},{25,17},{26,18},{27,19},{28,20},{29,21},{30,22},{31,23}} | collective-permute-start | bytes 245768 | tf_op jit(solution)/shard_map/ppermute | solution.py:639
  41.3 4.2 %collective-permute-start.15 = (bf16[320,128]{1,0:T(8,128)(2,1)S(1)}, bf16[320,128]{1,0:T(8,128)(2,1)S(1)}, u32[]{:S(2)}, u32[]{:S(2)}) collective-permute-start(bf16[320,128]{1,0:T(8,128)(2,1)S(1)} %get-tuple-element.86.refs_1_), channel_id=1, source_target_pairs={{24,16},{25,17},{26,18},{27,19},{28,20},{29,21},{30,22},{31,23}} | collective-permute-start | bytes 245768 | tf_op jit(solution)/shard_map/ppermute | solution.py:639
  42.0 5.4 %collective-permute-start.18 = (bf16[320,128]{1,0:T(8,128)(2,1)S(1)}, bf16[320,128]{1,0:T(8,128)(2,1)S(1)}, u32[]{:S(2)}, u32[]{:S(2)}) collective-permute-start(bf16[320,128]{1,0:T(8,128)(2,1)S(1)} %get-tuple-element.98), channel_id=1, source_target_pairs={{16,8},{17,9},{18,10},{19,11},{20,12},{21,13},{22,14},{23,15}} | collective-permute-start | bytes 245768 | tf_op jit(solution)/shard_map/ppermute | solution.py:639
  42.8 6.7 %collective-permute-start.9 = (bf16[2,160,256]{2,1,0:T(8,128)(2,1)S(1)}, bf16[2,160,256]{2,1,0:T(8,128)(2,1)S(1)}, u32[]{:S(2)}, u32[]{:S(2)}) collective-permute-start(bf16[2,160,256]{2,1,0:T(8,128)(2,1)S(1)} %shard_map.65), channel_id=1, source_target_pairs={{0,3},{1,0},{2,1},{3,2},{8,11},{9,8},{10,9},{11,10},{16,19},{17,16... | collective-permute-start | bytes 491528 | tf_op jit(solution)/shard_map/ppermute | solution.py:648
  43.2 17.5 %collective-permute-start.8 = (bf16[2,160,256]{2,1,0:T(8,128)(2,1)S(1)}, bf16[2,160,256]{2,1,0:T(8,128)(2,1)S(1)}, u32[]{:S(2)}, u32[]{:S(2)}) collective-permute-start(bf16[2,160,256]{2,1,0:T(8,128)(2,1)S(1)} %shard_map.65), channel_id=1, source_target_pairs={{0,2},{1,3},{2,0},{3,1},{8,10},{9,11},{10,8},{11,9},{16,18},{17,19... | collective-permute-start | bytes 491528 | tf_op jit(solution)/shard_map/ppermute | solution.py:648
  45.5 15.3 %collective-permute-start.7 = (bf16[2,160,256]{2,1,0:T(8,128)(2,1)S(1)}, bf16[2,160,256]{2,1,0:T(8,128)(2,1)S(1)}, u32[]{:S(2)}, u32[]{:S(2)}) collective-permute-start(bf16[2,160,256]{2,1,0:T(8,128)(2,1)S(1)} %shard_map.65), channel_id=1, source_target_pairs={{0,1},{1,2},{2,3},{3,0},{8,9},{9,10},{10,11},{11,8},{16,17},{17,18... | collective-permute-start | bytes 491528 | tf_op jit(solution)/shard_map/ppermute | solution.py:648
  47.4 0.7 collective-permute-start.17
  48.1 14.9 %collective-permute-start.20 = (bf16[320,128]{1,0:T(8,128)(2,1)S(1)}, bf16[320,128]{1,0:T(8,128)(2,1)S(1)}, u32[]{:S(2)}, u32[]{:S(2)}) collective-permute-start(bf16[320,128]{1,0:T(8,128)(2,1)S(1)} %get-tuple-element.105), channel_id=1, source_target_pairs={{8,0},{9,1},{10,2},{11,3},{12,4},{13,5},{14,6},{15,7}} | collective-permute-start | bytes 245768 | tf_op jit(solution)/shard_map/ppermute | solution.py:639
  49.5 14.9 %collective-permute-start.19 = (bf16[320,128]{1,0:T(8,128)(2,1)S(1)}, bf16[320,128]{1,0:T(8,128)(2,1)S(1)}, u32[]{:S(2)}, u32[]{:S(2)}) collective-permute-start(bf16[320,128]{1,0:T(8,128)(2,1)S(1)} %get-tuple-element.103), channel_id=1, source_target_pairs={{8,0},{9,1},{10,2},{11,3},{12,4},{13,5},{14,6},{15,7}} | collective-permute-start | bytes 245768 | tf_op jit(solution)/shard_map/ppermute | solution.py:639
  60.8 16.9 %collective-permute-start.10 = (bf16[2,4,160,256]{3,2,1,0:T(8,128)(2,1)S(1)}, bf16[2,4,160,256]{3,2,1,0:T(8,128)(2,1)S(1)}, u32[]{:S(2)}, u32[]{:S(2)}) collective-permute-start(bf16[2,4,160,256]{3,2,1,0:T(8,128)(2,1)S(1)} %get-tuple-element.87), channel_id=1, source_target_pairs={{0,4},{4,0},{1,5},{5,1},{2,6},{6,2},{3,7},{7,3},{8,12},{12,8},{9,1... | collective-permute-start | bytes 1966088 | tf_op jit(solution)/shard_map/ppermute | solution.py:620
  65.7 6.1 %collective-permute-start.23 = (bf16[2,80,256]{2,1,0:T(8,128)(2,1)S(1)}, bf16[2,80,256]{2,1,0:T(8,128)(2,1)S(1)}, u32[]{:S(2)}, u32[]{:S(2)}) collective-permute-start(bf16[2,80,256]{2,1,0:T(8,128)(2,1)S(1)} %get-tuple-element.114), channel_id=1, source_target_pairs={{0,3},{1,0},{2,1},{3,2},{8,11},{9,8},{10,9},{11,10},{16,19},{17,16... | collective-permute-start | bytes 245768 | tf_op jit(solution)/shard_map/ppermute | solution.py:648
  65.7 9.4 %collective-permute-start.22 = (bf16[2,80,256]{2,1,0:T(8,128)(2,1)S(1)}, bf16[2,80,256]{2,1,0:T(8,128)(2,1)S(1)}, u32[]{:S(2)}, u32[]{:S(2)}) collective-permute-start(bf16[2,80,256]{2,1,0:T(8,128)(2,1)S(1)} %get-tuple-element.115), channel_id=1, source_target_pairs={{0,2},{1,3},{2,0},{3,1},{8,10},{9,11},{10,8},{11,9},{16,18},{17,19... | collective-permute-start | bytes 245768 | tf_op jit(solution)/shard_map/ppermute | solution.py:648
  66.3 8.8 %collective-permute-start.21 = (bf16[2,80,256]{2,1,0:T(8,128)(2,1)S(1)}, bf16[2,80,256]{2,1,0:T(8,128)(2,1)S(1)}, u32[]{:S(2)}, u32[]{:S(2)}) collective-permute-start(bf16[2,80,256]{2,1,0:T(8,128)(2,1)S(1)} %get-tuple-element.116), channel_id=1, source_target_pairs={{0,1},{1,2},{2,3},{3,0},{8,9},{9,10},{10,11},{11,8},{16,17},{17,18... | collective-permute-start | bytes 245768 | tf_op jit(solution)/shard_map/ppermute | solution.py:648
  75.1 2.5 %collective-permute-start.24 = (bf16[4,2,80,256]{3,2,1,0:T(8,128)(2,1)S(1)}, bf16[4,2,80,256]{3,2,1,0:T(8,128)(2,1)S(1)}, u32[]{:S(2)}, u32[]{:S(2)}) collective-permute-start(bf16[4,2,80,256]{3,2,1,0:T(8,128)(2,1)S(1)} %shard_map.79.own_ref), channel_id=1, source_target_pairs={{0,4},{4,0},{1,5},{5,1},{2,6},{6,2},{3,7},{7,3},{8,12},{12,8},{9,1... | collective-permute-start | bytes 983048 | tf_op jit(solution)/shard_map/ppermute | solution.py:620
  75.3 1.7 %collective-permute-start.25 = (bf16[2,8,8,320]{3,2,1,0:T(8,128)(2,1)S(1)}, bf16[2,8,8,320]{3,2,1,0:T(8,128)(2,1)S(1)}, u32[]{:S(2)}, u32[]{:S(2)}) collective-permute-start(bf16[2,8,8,320]{3,2,1,0:T(8,128)(2,1)S(1)} %get-tuple-element.113), channel_id=1, source_target_pairs={{0,4},{4,0},{1,5},{5,1},{2,6},{6,2},{3,7},{7,3},{8,12},{12,8},{9,1... | collective-permute-start | bytes 245768 | tf_op jit(solution)/shard_map/ppermute | solution.py:620

commit v8 on v7

--- a/solution.py
+++ b/solution.py
@@ -532,74 +532,72 @@
     return call(kernel, [out, out], [saved, weights, *blocks], (), scratch, {})
 
 
-def spread_call(cells_of, around, place, count, width, sections, marked=False):
+def spread_call(first, cells_of, around, place, count, width):
     two, blocks, share, cells = cells_of.shape
     crops = cells // count
-    stride = count + width
-    total = 2 * blocks * crops * stride + width
-
-    def kernel(cells_ref, *refs):
-        out_ref, shifted = refs[-3 if marked else -2], refs[-1]
-        section = lax.axis_index("section")
-        if marked:
-            refs[-2][...] = jnp.zeros_like(refs[-2])
-
-        @pl.when((section >= sections[0]) & (section <= sections[1]))
-        def _():
-            edge = jnp.zeros((width, 3 * share), jnp.bfloat16)
-            for kind in range(two):
-                out_ref[kind, total - width : total, :] = edge
-                for block in range(blocks):
-                    for crop in range(crops):
-                        cell = slice(crop * count, (crop + 1) * count)
-                        value = cells_ref[kind, block, :, cell].T.astype(jnp.float32)
-                        before, after = neighbours(value, shifted, width)
-                        at = ((place * blocks + block) * crops + crop) * stride
-                        out_ref[kind, at : at + width, :] = edge
-                        for side, part in enumerate((before, value, after)):
-                            lanes = slice(side * share, (side + 1) * share)
-                            out_ref[kind, at + width : at + stride, lanes] = part.astype(
-                                jnp.bfloat16
-                            )
+    total = 2 * blocks * cells
+
+    def kernel(first_ref, cells_ref, *refs):
+        out_ref, shifted = refs[-2:]
+        is_first = lax.axis_index("section") == 0
+        for kind in range(two):
+            for block in range(blocks):
+                for crop in range(crops):
+                    cell = slice(crop * count, (crop + 1) * count)
+                    value = jnp.where(
+                        is_first, first_ref[kind, block, :, cell], cells_ref[kind, block, :, cell]
+                    )
+                    value = value.T.astype(jnp.float32)
+                    before, after = neighbours(value, shifted, width)
+                    at = (place * blocks + block) * cells + crop * count
+                    for side, part in enumerate((before, value, after)):
+                        lanes = slice(side * share, (side + 1) * share)
+                        out_ref[kind, at : at + count, lanes] = part.astype(jnp.bfloat16)
 
     out = jax.ShapeDtypeStruct((two, total, 3 * share), jnp.bfloat16)
     scratch = [pltpu.VMEM((count + 16, share), jnp.float32)]
-    operands = [cells_of] if around is None else [cells_of, around]
-    aliases = {} if around is None else {1: 0}
-    token = jax.ShapeDtypeStruct((8, 128), jnp.float32)
-    outs = [out, token] if marked else [out]
-    return call(kernel, outs, operands, (), scratch, aliases)
+    operands = [first, cells_of] if around is None else [first, cells_of, around]
+    aliases = {} if around is None else {2: 0}
+    (spread,) = call(kernel, [out], operands, (), scratch, aliases)
+    return spread
 
 
 def terms_call(around, own, other, count, width, scaling):
     blocks, _, columns, cells = own.shape
     rows = around.shape[2] // 3
-    stride = count + width
     crops = cells // count
+
+    def moved(value, down):
+        parts = []
+        edge = jnp.zeros((columns, width), value.dtype)
+        for crop in range(crops):
+            part = value[:, crop * count : (crop + 1) * count]
+            if down == 0:
+                part = jnp.concatenate([part[:, width:], edge], axis=1)
+            elif down == 2:
+                part = jnp.concatenate([edge, part[:, : count - width]], axis=1)
+            parts.append(part)
+        return jnp.concatenate(parts, axis=1)
 
     def kernel(around_ref, own_ref, other_ref, out_ref, held, sems):
         copies = []
         for kind in (1, 0):
+            total = None
+            for block in range(2 * blocks):
+                left = own_ref if block < blocks else other_ref
+                left = left[block % blocks, 1 - kind]
+                left = jnp.concatenate([moved(left, down) for down in range(3)], axis=0)
+                right = around_ref[kind, block * cells : (block + 1) * cells, :]
+                term = jnp.dot(left, right, preferred_element_type=jnp.float32)
+                total = term if total is None else total + term
             for down in range(3):
-                total = None
-                for block in range(2 * blocks):
-                    left = own_ref if block < blocks else other_ref
-                    left = left[block % blocks, 1 - kind]
-                    at = [(block * crops + k) * stride + down * width for k in range(crops)]
-                    right = jnp.concatenate(
-                        [around_ref[kind, start : start + count, :] for start in at], axis=0
-                    )
-                    term = jnp.dot(left, right, preferred_element_type=jnp.float32)
-                    total = term if total is None else total + term
-                total = (total * scaling).T.reshape(3, rows, columns)
-                third = pl.ds(3 * down, 3)
+                part = total[down * columns : (down + 1) * columns] * scaling
+                part = part.T.reshape(3, rows, columns)
                 for place in range(3):
-                    held[kind, 3 * down + place] = total[place]
-                copy = pltpu.make_async_copy(
-                    held.at[kind, third], out_ref.at[kind, third], sems.at[3 * kind + down]
-                )
-                copy.start()
-                copies.append(copy)
+                    held[kind, 3 * down + place] = part[place]
+            copy = pltpu.make_async_copy(held.at[kind], out_ref.at[kind], sems.at[kind])
+            copy.start()
+            copies.append(copy)
         for copy in copies:
             copy.wait()
 
@@ -609,7 +607,7 @@
         out_shape=jax.ShapeDtypeStruct(shape, jnp.float32),
         in_specs=[pl.BlockSpec(memory_space=pltpu.VMEM)] * 3,
         out_specs=pl.BlockSpec(memory_space=pltpu.HBM),
-        scratch_shapes=[pltpu.VMEM(shape, jnp.float32), pltpu.SemaphoreType.DMA((6,))],
+        scratch_shapes=[pltpu.VMEM(shape, jnp.float32), pltpu.SemaphoreType.DMA((2,))],
         compiler_params=pltpu.CompilerParams(vmem_limit_bytes=8 << 20),
         name="terms",
     )(around, own, other)
@@ -710,20 +708,17 @@
             inputs = flipped(saved, outgoing[-1])
             late = [shared(inputs, step, range(sections)) for step in steps]
         if place == 1:
-            home, outer = remake_call(saved, weights, soon, width, (0, 0))
-            outer = lax.ppermute(
-                outer, ("section", "slab"), [(i, (i + 1) % slabs) for i in range(slabs)]
-            )
-            (around,) = spread_call(home, None, 0, count, width, (0, 0))
-            around, after = spread_call(outer, around, 1, count, width, (0, 0), True)
+            first, early_outer = remake_call(saved, weights, soon, width, (0, 0))
+            after = first
+            early_outer = lax.ppermute(early_outer, ("section", "slab"), [(i, (i + 1) % slabs) for i in range(slabs)])
     kept, sent = grads
     own = [sent[0]]
     for step in steps:
         own.append(shared(sent[step], step, range(sections)))
     home, outer = remake_call(saved, weights, late, width, (1, last))
     outer = swapped(outer)
-    (around,) = spread_call(home, around, 0, count, width, (1, last))
-    (around,) = spread_call(outer, around, 1, count, width, (1, last))
+    around = spread_call(first, home, None, 0, count, width)
+    around = spread_call(early_outer, outer, around, 1, count, width)
     own = stack_call(own)
     other = swapped(own)
     terms = terms_call(around, own, other, count, width, scaling)

time: 81.4 us -> 73.8 us (0.907)
  the two profiles are of different devices: /device:TPU:0 before, /device:TPU:11 now
where the time goes in v8:
time: 73.8 us; the launch traced here: 73.4 us
  starting transfers between devices  29.6 us (40%)
  waiting for transfers between devices  23.2 us (31%)
  Pallas kernels  19.4 us (26%)
  between operations  1.22 us (2%)
    pallas_call x30, Pallas kernels, call(): pl.pallas_call(kernel, out_shape=outs, in_specs=[pl.BlockSpec(memory_spac...  17.1 us
    ppermute x12, waiting for transfers between devices, hop(): arrived.append(lax.ppermute(value, 'section', [(source, target)]))  15 us
    ppermute x12, starting transfers between devices, hop(): arrived.append(lax.ppermute(value, 'section', [(source, target)]))  13 us
    ppermute x9, starting transfers between devices, shared(): return lax.ppermute(values, ('section', 'img'), pairs)  9.02 us
    ppermute x9, waiting for transfers between devices, shared(): return lax.ppermute(values, ('section', 'img'), pairs)  7.2 us
    ppermute x4, starting transfers between devices, rotated(): lax.ppermute(value, axis, [(source, (source + steps) % count) for source...  6.85 us
    pallas_call x1, Pallas kernels, terms_call(): pl.pallas_call(kernel, out_shape=jax.ShapeDtypeStruct(shape, jnp.float32)...  2.31 us
  transfers between devices with their start and end apart: 26, of which 8 were waited for; matrix products, arithmetic and copies ran while one was open for 0% of the time, Pallas kernels for 22%

profile of v8, /device:TPU:11, one launch (start us, length us, event | category | flops | bytes accessed | tf_op | source)
XLA Modules:
  0.0 73.4 jit_solution(15913088605856043017)
XLA Ops:
  0.6 1.0 %shard_map.50 = (bf16[2,8,8,320]{3,2,1,0:T(8,128)(2,1)S(1)}, bf16[2,8,8,320]{3,2,1,0:T(8,128)(2,1)S(1)}) custom-call(bf16[1,4,8,8,320]{4,3,2,1,0:T(8,128)(2,1)} %strips_ref.1, bf16[1,4,8,8,320]{4,3,2,1,0:T(8,128)(2,1)} %cotangent_ref.1), custom_call_target="tpu_custom_call" | custom-call | tf_op jit(solution)/shard_map/pallas_call | solution.py:177
  1.6 0.7 %collective-permute-start = (bf16[2,8,8,320]{3,2,1,0:T(8,128)(2,1)S(1)}, bf16[2,8,8,320]{3,2,1,0:T(8,128)(2,1)S(1)}, u32[]{:S(2)}, u32[]{:S(2)}) collective-permute-start(bf16[2,8,8,320]{3,2,1,0:T(8,128)(2,1)S(1)} %get-tuple-element.57), channel_id=1, source_target_pairs={{0,4},{4,0},{1,5},{5,1},{2,6},{6,2},{3,7},{7,3},{8,12},{12,8},{9,1... | collective-permute-start | bytes 245768 | tf_op jit(solution)/shard_map/ppermute | solution.py:618
  2.4 0.9 %collective-permute-done.other_ref = bf16[2,8,8,320]{3,2,1,0:T(8,128)(2,1)S(1)} collective-permute-done((bf16[2,8,8,320]{3,2,1,0:T(8,128)(2,1)S(1)}, bf16[2,8,8,320]{3,2,1,0:T(8,128)(2,1)S(1)}, u32[]{:S(2)}, u32[]{:S(2)}) %collective-permute-start) | collective-permute-done | bytes 81952 | tf_op jit(solution)/shard_map/ppermute | solution.py:618
  3.3 0.1 shard_map.51
  3.4 1.3 %collective-permute-start.2 = (bf16[320,128]{1,0:T(8,128)(2,1)S(1)}, bf16[320,128]{1,0:T(8,128)(2,1)S(1)}, u32[]{:S(2)}, u32[]{:S(2)}) collective-permute-start(bf16[320,128]{1,0:T(8,128)(2,1)S(1)} %get-tuple-element.64), channel_id=1, source_target_pairs={{0,8},{1,9},{2,10},{3,11},{4,12},{5,13},{6,14},{7,15}} | collective-permute-start | bytes 245768 | tf_op jit(solution)/shard_map/ppermute | solution.py:637
  4.7 1.3 %collective-permute-start.1 = (bf16[320,128]{1,0:T(8,128)(2,1)S(1)}, bf16[320,128]{1,0:T(8,128)(2,1)S(1)}, u32[]{:S(2)}, u32[]{:S(2)}) collective-permute-start(bf16[320,128]{1,0:T(8,128)(2,1)S(1)} %get-tuple-element.62), channel_id=1, source_target_pairs={{0,8},{1,9},{2,10},{3,11},{4,12},{5,13},{6,14},{7,15}} | collective-permute-start | bytes 245768 | tf_op jit(solution)/shard_map/ppermute | solution.py:637
  6.0 2.3 %shard_map.55.weights_ref = bf16[2,3,960,320]{3,2,1,0:T(8,128)(2,1)S(1)} custom-call(bf16[2,3,960,320]{3,2,1,0:T(8,128)(2,1)} %bitcast.12, bf16[2,2,128,320]{3,2,1,0:T(8,128)(2,1)S(1)} %get-tuple-element.63.after_ref.refs_0_), custom_call_target="tpu_custom_call" | custom-call | tf_op jit(solution)/shard_map/pallas_call | solution.py:177
  8.3 2.1 %collective-permute-done.2.field_ref = bf16[320,128]{1,0:T(8,128)(2,1)S(1)} collective-permute-done((bf16[320,128]{1,0:T(8,128)(2,1)S(1)}, bf16[320,128]{1,0:T(8,128)(2,1)S(1)}, u32[]{:S(2)}, u32[]{:S(2)}) %collective-permute-start.2) | collective-permute-done | bytes 81952 | tf_op jit(solution)/shard_map/ppermute | solution.py:637
  10.4 1.4 %shard_map.56 = (bf16[320,128]{1,0:T(8,128)(2,1)S(1)}, bf16[2,2,128,320]{3,2,1,0:T(8,128)(2,1)S(1)}, f32[2,128,320]{2,1,0:T(8,128)S(1)}) custom-call(bf16[320,128]{1,0:T(8,128)(2,1)S(1)} %collective-permute-done.2.field_ref, bf16[2,3,960,320]{3,2,1,0:T(8,128)(2,1)S(1)} %shard_map.55.weights_ref, ...), custom_call_target="tpu_custom_call", output_to_operand_aliasing={{1}: (3, {}), {2}: (4, {})} | custom-call | tf_op jit(solution)/shard_map/pallas_call | solution.py:177
  11.8 1.3 %collective-permute-start.4 = (bf16[320,128]{1,0:T(8,128)(2,1)S(1)}, bf16[320,128]{1,0:T(8,128)(2,1)S(1)}, u32[]{:S(2)}, u32[]{:S(2)}) collective-permute-start(bf16[320,128]{1,0:T(8,128)(2,1)S(1)} %get-tuple-element.70), channel_id=1, source_target_pairs={{8,16},{9,17},{10,18},{11,19},{12,20},{13,21},{14,22},{15,23}} | collective-permute-start | bytes 245768 | tf_op jit(solution)/shard_map/ppermute | solution.py:637
  13.1 0.0 collective-permute-done.1.field_ref
  13.1 1.4 %shard_map.57 = (bf16[320,128]{1,0:T(8,128)(2,1)S(1)}, bf16[2,2,128,320]{3,2,1,0:T(8,128)(2,1)S(1)}, f32[2,128,320]{2,1,0:T(8,128)S(1)}) custom-call(bf16[320,128]{1,0:T(8,128)(2,1)S(1)} %collective-permute-done.1.field_ref, bf16[2,3,960,320]{3,2,1,0:T(8,128)(2,1)S(1)} %shard_map.55.weights_ref, ...), custom_call_target="tpu_custom_call", output_to_operand_aliasing={{1}: (3, {}), {2}: (4, {})} | custom-call | tf_op jit(solution)/shard_map/pallas_call | solution.py:177
  14.5 1.3 %collective-permute-start.3 = (bf16[320,128]{1,0:T(8,128)(2,1)S(1)}, bf16[320,128]{1,0:T(8,128)(2,1)S(1)}, u32[]{:S(2)}, u32[]{:S(2)}) collective-permute-start(bf16[320,128]{1,0:T(8,128)(2,1)S(1)} %get-tuple-element.68), channel_id=1, source_target_pairs={{8,16},{9,17},{10,18},{11,19},{12,20},{13,21},{14,22},{15,23}} | collective-permute-start | bytes 245768 | tf_op jit(solution)/shard_map/ppermute | solution.py:637
  15.8 1.4 %shard_map.58.after_ref.turned_ref = bf16[2,3,960,320]{3,2,1,0:T(8,128)(2,1)S(1)} custom-call(bf16[2,3,960,320]{3,2,1,0:T(8,128)(2,1)S(1)} %shard_map.55.weights_ref, bf16[2,2,128,320]{3,2,1,0:T(8,128)(2,1)S(1)} %get-tuple-element.69.after_ref.refs_0_), custom_call_target="tpu_custom_call" | custom-call | tf_op jit(solution)/shard_map/pallas_call | solution.py:177
  17.1 0.1 shard_map.63
  17.2 0.0 collective-permute-done.4.field_ref
  17.3 0.7 collective-permute-start.6
  18.0 0.0 collective-permute-done.3.field_ref
  18.0 0.7 collective-permute-start.5
  18.7 0.7 collective-permute-start.7
  19.3 0.7 collective-permute-start.8
  20.0 0.0 collective-permute-done.6.field_ref
  20.1 0.0 collective-permute-done.5.field_ref
  20.1 0.7 collective-permute-start.16
  20.8 0.2 shard_map.66
  21.0 0.7 collective-permute-start.15
  21.7 0.0 collective-permute-done.16.grad_ref
  21.7 1.3 %collective-permute-start.18 = (bf16[320,128]{1,0:T(8,128)(2,1)S(1)}, bf16[320,128]{1,0:T(8,128)(2,1)S(1)}, u32[]{:S(2)}, u32[]{:S(2)}) collective-permute-start(bf16[320,128]{1,0:T(8,128)(2,1)S(1)} %get-tuple-element.95), channel_id=1, source_target_pairs={{16,8},{17,9},{18,10},{19,11},{20,12},{21,13},{22,14},{23,15}} | collective-permute-start | bytes 245768 | tf_op jit(solution)/shard_map/ppermute | solution.py:637
  23.0 0.7 collective-permute-start.9
  23.7 0.1 shard_map.67
  23.8 0.0 collective-permute-done.7.refs_0_
  23.8 1.3 %collective-permute-start.11 = (bf16[2,160,256]{2,1,0:T(8,128)(2,1)S(1)}, bf16[2,160,256]{2,1,0:T(8,128)(2,1)S(1)}, u32[]{:S(2)}, u32[]{:S(2)}) collective-permute-start(bf16[2,160,256]{2,1,0:T(8,128)(2,1)S(1)} %shard_map.67), channel_id=1, source_target_pairs={{0,1},{1,2},{2,3},{3,0},{8,9},{9,10},{10,11},{11,8},{16,17},{17,18... | collective-permute-start | bytes 491528 | tf_op jit(solution)/shard_map/ppermute | solution.py:646
  25.1 0.0 collective-permute-done.8.refs_1_
  25.1 1.1 %collective-permute-start.12 = (bf16[2,160,256]{2,1,0:T(8,128)(2,1)S(1)}, bf16[2,160,256]{2,1,0:T(8,128)(2,1)S(1)}, u32[]{:S(2)}, u32[]{:S(2)}) collective-permute-start(bf16[2,160,256]{2,1,0:T(8,128)(2,1)S(1)} %shard_map.67), channel_id=1, source_target_pairs={{0,2},{1,3},{2,0},{3,1},{8,10},{9,11},{10,8},{11,9},{16,18},{17,19... | collective-permute-start | bytes 491528 | tf_op jit(solution)/shard_map/ppermute | solution.py:646
  26.2 0.0 collective-permute-done.15.grad_ref
  26.3 1.4 %collective-permute-start.13 = (bf16[2,160,256]{2,1,0:T(8,128)(2,1)S(1)}, bf16[2,160,256]{2,1,0:T(8,128)(2,1)S(1)}, u32[]{:S(2)}, u32[]{:S(2)}) collective-permute-start(bf16[2,160,256]{2,1,0:T(8,128)(2,1)S(1)} %shard_map.67), channel_id=1, source_target_pairs={{0,3},{1,0},{2,1},{3,2},{8,11},{9,8},{10,9},{11,10},{16,19},{17,16... | collective-permute-start | bytes 491528 | tf_op jit(solution)/shard_map/ppermute | solution.py:646
  27.6 8.2 %collective-permute-done.18.grad_ref = bf16[320,128]{1,0:T(8,128)(2,1)S(1)} collective-permute-done((bf16[320,128]{1,0:T(8,128)(2,1)S(1)}, bf16[320,128]{1,0:T(8,128)(2,1)S(1)}, u32[]{:S(2)}, u32[]{:S(2)}) %collective-permute-start.18) | collective-permute-done | bytes 81952 | tf_op jit(solution)/shard_map/ppermute | solution.py:637
  35.9 1.3 %collective-permute-start.17 = (bf16[320,128]{1,0:T(8,128)(2,1)S(1)}, bf16[320,128]{1,0:T(8,128)(2,1)S(1)}, u32[]{:S(2)}, u32[]{:S(2)}) collective-permute-start(bf16[320,128]{1,0:T(8,128)(2,1)S(1)} %get-tuple-element.94), channel_id=1, source_target_pairs={{16,8},{17,9},{18,10},{19,11},{20,12},{21,13},{22,14},{23,15}} | collective-permute-start | bytes 245768 | tf_op jit(solution)/shard_map/ppermute | solution.py:637
  37.1 1.4 %shard_map.73 = (bf16[320,128]{1,0:T(8,128)(2,1)S(1)}, bf16[2,128,320]{2,1,0:T(8,128)(2,1)S(1)}, bf16[4,2,80,256]{3,2,1,0:T(8,128)(2,1)S(1)}) custom-call(bf16[320,128]{1,0:T(8,128)(2,1)S(1)} %collective-permute-done.18.grad_ref, bf16[2,3,960,320]{3,2,1,0:T(8,128)(2,1)S(1)} %shard_map.58.after_ref.turned_ref, ...), custom_call_target="tpu_custom_call", output_to_operand_aliasing={{1}: (4, {}), {2}: (5, {})} | custom-call | tf_op jit(solution)/shard_map/pallas_call | solution.py:177
  38.5 4.6 %collective-permute-done.17.grad_ref = bf16[320,128]{1,0:T(8,128)(2,1)S(1)} collective-permute-done((bf16[320,128]{1,0:T(8,128)(2,1)S(1)}, bf16[320,128]{1,0:T(8,128)(2,1)S(1)}, u32[]{:S(2)}, u32[]{:S(2)}) %collective-permute-start.17) | collective-permute-done | bytes 81952 | tf_op jit(solution)/shard_map/ppermute | solution.py:637
  43.2 1.3 %collective-permute-start.20 = (bf16[320,128]{1,0:T(8,128)(2,1)S(1)}, bf16[320,128]{1,0:T(8,128)(2,1)S(1)}, u32[]{:S(2)}, u32[]{:S(2)}) collective-permute-start(bf16[320,128]{1,0:T(8,128)(2,1)S(1)} %get-tuple-element.101), channel_id=1, source_target_pairs={{8,0},{9,1},{10,2},{11,3},{12,4},{13,5},{14,6},{15,7}} | collective-permute-start | bytes 245768 | tf_op jit(solution)/shard_map/ppermute | solution.py:637
  44.5 1.4 %shard_map.74 = (bf16[320,128]{1,0:T(8,128)(2,1)S(1)}, bf16[2,128,320]{2,1,0:T(8,128)(2,1)S(1)}, bf16[4,2,80,256]{3,2,1,0:T(8,128)(2,1)S(1)}) custom-call(bf16[320,128]{1,0:T(8,128)(2,1)S(1)} %collective-permute-done.17.grad_ref, bf16[2,3,960,320]{3,2,1,0:T(8,128)(2,1)S(1)} %shard_map.58.after_ref.turned_ref, ...), custom_call_target="tpu_custom_call", output_to_operand_aliasing={{1}: (4, {}), {2}: (5, {})} | custom-call | tf_op jit(solution)/shard_map/pallas_call | solution.py:177
  45.8 0.0 collective-permute-done.9.refs_2_
  45.8 1.3 %collective-permute-start.19 = (bf16[320,128]{1,0:T(8,128)(2,1)S(1)}, bf16[320,128]{1,0:T(8,128)(2,1)S(1)}, u32[]{:S(2)}, u32[]{:S(2)}) collective-permute-start(bf16[320,128]{1,0:T(8,128)(2,1)S(1)} %get-tuple-element.100), channel_id=1, source_target_pairs={{8,0},{9,1},{10,2},{11,3},{12,4},{13,5},{14,6},{15,7}} | collective-permute-start | bytes 245768 | tf_op jit(solution)/shard_map/ppermute | solution.py:637
  47.2 0.0 collective-permute-done.11.refs_0_
  47.2 0.7 collective-permute-start.10
  47.9 3.2 %shard_map.68 = (bf16[2,4,160,256]{3,2,1,0:T(8,128)(2,1)S(1)}, bf16[2,4,160,256]{3,2,1,0:T(8,128)(2,1)S(1)}) custom-call(bf16[2,2,128,320]{3,2,1,0:T(8,128)(2,1)S(1)} %get-tuple-element.80.saved_ref.refs_0_, bf16[2,3,960,320]{3,2,1,0:T(8,128)(2,1)S(1)} %shard_map.55.weights_ref, bf16[2,160,256]{2,1,0:T(8,128)(2,1)S(1)} %collective-permute-done.11.refs_0_, ...), custom_call_target="tpu_custom_call" | custom-call | tf_op jit(solution)/shard_map/pallas_call | solution.py:177
  51.1 5.0 %collective-permute-start.14 = (bf16[2,4,160,256]{3,2,1,0:T(8,128)(2,1)S(1)}, bf16[2,4,160,256]{3,2,1,0:T(8,128)(2,1)S(1)}, u32[]{:S(2)}, u32[]{:S(2)}) collective-permute-start(bf16[2,4,160,256]{3,2,1,0:T(8,128)(2,1)S(1)} %get-tuple-element.86), channel_id=1, source_target_pairs={{0,4},{4,0},{1,5},{5,1},{2,6},{6,2},{3,7},{7,3},{8,12},{12,8},{9,1... | collective-permute-start | bytes 1966088 | tf_op jit(solution)/shard_map/ppermute | solution.py:618
  56.1 0.0 collective-permute-done.20.grad_ref
  56.1 0.0 collective-permute-done.19.grad_ref
  56.1 0.4 collective-permute-start.21
  56.5 2.8 %collective-permute-start.22 = (bf16[2,80,256]{2,1,0:T(8,128)(2,1)S(1)}, bf16[2,80,256]{2,1,0:T(8,128)(2,1)S(1)}, u32[]{:S(2)}, u32[]{:S(2)}) collective-permute-start(bf16[2,80,256]{2,1,0:T(8,128)(2,1)S(1)} %get-tuple-element.111), channel_id=1, source_target_pairs={{0,2},{1,3},{2,0},{3,1},{8,10},{9,11},{10,8},{11,9},{16,18},{17,19... | collective-permute-start | bytes 245768 | tf_op jit(solution)/shard_map/ppermute | solution.py:646
  59.3 0.8 %collective-permute-done.21.refs_1_ = bf16[2,80,256]{2,1,0:T(8,128)(2,1)S(1)} collective-permute-done((bf16[2,80,256]{2,1,0:T(8,128)(2,1)S(1)}, bf16[2,80,256]{2,1,0:T(8,128)(2,1)S(1)}, u32[]{:S(2)}, u32[]{:S(2)}) %collective-permute-start.21) | collective-permute-done | bytes 81952 | tf_op jit(solution)/shard_map/ppermute | solution.py:646
  60.1 4.5 %collective-permute-done.22.refs_2_ = bf16[2,80,256]{2,1,0:T(8,128)(2,1)S(1)} collective-permute-done((bf16[2,80,256]{2,1,0:T(8,128)(2,1)S(1)}, bf16[2,80,256]{2,1,0:T(8,128)(2,1)S(1)}, u32[]{:S(2)}, u32[]{:S(2)}) %collective-permute-start.22) | collective-permute-done | bytes 81952 | tf_op jit(solution)/shard_map/ppermute | solution.py:646
  64.6 1.9 %collective-permute-done.23.refs_3_ = bf16[2,80,256]{2,1,0:T(8,128)(2,1)S(1)} collective-permute-done((bf16[2,80,256]{2,1,0:T(8,128)(2,1)S(1)}, bf16[2,80,256]{2,1,0:T(8,128)(2,1)S(1)}, u32[]{:S(2)}, u32[]{:S(2)}) %collective-permute-start.23) | collective-permute-done | bytes 81952 | tf_op jit(solution)/shard_map/ppermute | solution.py:646
  66.5 1.0 %collective-permute-start.24 = (bf16[4,2,80,256]{3,2,1,0:T(8,128)(2,1)S(1)}, bf16[4,2,80,256]{3,2,1,0:T(8,128)(2,1)S(1)}, u32[]{:S(2)}, u32[]{:S(2)}) collective-permute-start(bf16[4,2,80,256]{3,2,1,0:T(8,128)(2,1)S(1)} %shard_map.77.own_ref), channel_id=1, source_target_pairs={{0,4},{4,0},{1,5},{5,1},{2,6},{6,2},{3,7},{7,3},{8,12},{12,8},{9,1... | collective-permute-start | bytes 983048 | tf_op jit(solution)/shard_map/ppermute | solution.py:618
  67.6 0.1 shard_map.78
  67.6 0.1 collective-permute-start.25
  67.7 1.2 %shard_map.69.refs_0_ = bf16[2,2048,480]{2,1,0:T(8,128)(2,1)S(1)} custom-call(bf16[2,4,160,256]{3,2,1,0:T(8,128)(2,1)S(1)} %get-tuple-element.87.first_ref.after_ref, bf16[2,4,160,256]{3,2,1,0:T(8,128)(2,1)S(1)} %get-tuple-element.88.cells_ref), custom_call_target="tpu_custom_call" | custom-call | tf_op jit(solution)/shard_map/pallas_call | solution.py:177
  68.9 0.1 collective-permute-done.25.other_ref
  69.0 0.7 shard_map.79
  69.7 1.2 %shard_map.70.around_ref = bf16[2,2048,480]{2,1,0:T(8,128)(2,1)S(1)} custom-call(bf16[2,4,160,256]{3,2,1,0:T(8,128)(2,1)S(1)} %collective-permute-done.10.first_ref, bf16[2,4,160,256]{3,2,1,0:T(8,128)(2,1)S(1)} %collective-permute-done.14.cells_ref, bf16[2,2048,480]{2,1,0:T(8,128)(2,1)S(1)} %shard_map.69.refs_0_), custom_call_target="tpu_custom_call", output_to_operand_aliasing={{}: (2, {})} | custom-call | tf_op jit(solution)/shard_map/pallas_call | solution.py:177
  70.9 0.0 collective-permute-done.24.other_ref
  70.9 2.3 %terms.1 = f32[2,9,160,80]{3,2,1,0:T(8,128)} custom-call(bf16[2,2048,480]{2,1,0:T(8,128)(2,1)S(1)} %shard_map.70.around_ref, bf16[4,2,80,256]{3,2,1,0:T(8,128)(2,1)S(1)} %shard_map.77.own_ref, bf16[4,2,80,256]{3,2,1,0:T(8,128)(2,1)S(1)} %collective-permute-done.24.other_ref), custom_call_target="tpu_custom_call" | custom-call | tf_op jit(solution)/shard_map/terms/pallas_call | solution.py:605
  (20 shorter events, 0.2 us)
Async XLA Ops:
  1.6 1.7 %collective-permute-start = (bf16[2,8,8,320]{3,2,1,0:T(8,128)(2,1)S(1)}, bf16[2,8,8,320]{3,2,1,0:T(8,128)(2,1)S(1)}, u32[]{:S(2)}, u32[]{:S(2)}) collective-permute-start(bf16[2,8,8,320]{3,2,1,0:T(8,128)(2,1)S(1)} %get-tuple-element.57), channel_id=1, source_target_pairs={{0,4},{4,0},{1,5},{5,1},{2,6},{6,2},{3,7},{7,3},{8,12},{12,8},{9,1... | collective-permute-start | bytes 245768 | tf_op jit(solution)/shard_map/ppermute | solution.py:618
  3.4 7.0 %collective-permute-start.2 = (bf16[320,128]{1,0:T(8,128)(2,1)S(1)}, bf16[320,128]{1,0:T(8,128)(2,1)S(1)}, u32[]{:S(2)}, u32[]{:S(2)}) collective-permute-start(bf16[320,128]{1,0:T(8,128)(2,1)S(1)} %get-tuple-element.64), channel_id=1, source_target_pairs={{0,8},{1,9},{2,10},{3,11},{4,12},{5,13},{6,14},{7,15}} | collective-permute-start | bytes 245768 | tf_op jit(solution)/shard_map/ppermute | solution.py:637
  4.7 8.4 %collective-permute-start.1 = (bf16[320,128]{1,0:T(8,128)(2,1)S(1)}, bf16[320,128]{1,0:T(8,128)(2,1)S(1)}, u32[]{:S(2)}, u32[]{:S(2)}) collective-permute-start(bf16[320,128]{1,0:T(8,128)(2,1)S(1)} %get-tuple-element.62), channel_id=1, source_target_pairs={{0,8},{1,9},{2,10},{3,11},{4,12},{5,13},{6,14},{7,15}} | collective-permute-start | bytes 245768 | tf_op jit(solution)/shard_map/ppermute | solution.py:637
  11.8 5.5 %collective-permute-start.4 = (bf16[320,128]{1,0:T(8,128)(2,1)S(1)}, bf16[320,128]{1,0:T(8,128)(2,1)S(1)}, u32[]{:S(2)}, u32[]{:S(2)}) collective-permute-start(bf16[320,128]{1,0:T(8,128)(2,1)S(1)} %get-tuple-element.70), channel_id=1, source_target_pairs={{8,16},{9,17},{10,18},{11,19},{12,20},{13,21},{14,22},{15,23}} | collective-permute-start | bytes 245768 | tf_op jit(solution)/shard_map/ppermute | solution.py:637
  14.5 3.5 %collective-permute-start.3 = (bf16[320,128]{1,0:T(8,128)(2,1)S(1)}, bf16[320,128]{1,0:T(8,128)(2,1)S(1)}, u32[]{:S(2)}, u32[]{:S(2)}) collective-permute-start(bf16[320,128]{1,0:T(8,128)(2,1)S(1)} %get-tuple-element.68), channel_id=1, source_target_pairs={{8,16},{9,17},{10,18},{11,19},{12,20},{13,21},{14,22},{15,23}} | collective-permute-start | bytes 245768 | tf_op jit(solution)/shard_map/ppermute | solution.py:637
  17.3 2.7 %collective-permute-start.6 = (bf16[320,128]{1,0:T(8,128)(2,1)S(1)}, bf16[320,128]{1,0:T(8,128)(2,1)S(1)}, u32[]{:S(2)}, u32[]{:S(2)}) collective-permute-start(bf16[320,128]{1,0:T(8,128)(2,1)S(1)} %get-tuple-element.75), channel_id=1, source_target_pairs={{16,24},{17,25},{18,26},{19,27},{20,28},{21,29},{22,30},{23,31}} | collective-permute-start | bytes 245768 | tf_op jit(solution)/shard_map/ppermute | solution.py:637
  18.0 2.1 %collective-permute-start.5 = (bf16[320,128]{1,0:T(8,128)(2,1)S(1)}, bf16[320,128]{1,0:T(8,128)(2,1)S(1)}, u32[]{:S(2)}, u32[]{:S(2)}) collective-permute-start(bf16[320,128]{1,0:T(8,128)(2,1)S(1)} %get-tuple-element.74), channel_id=1, source_target_pairs={{16,24},{17,25},{18,26},{19,27},{20,28},{21,29},{22,30},{23,31}} | collective-permute-start | bytes 245768 | tf_op jit(solution)/shard_map/ppermute | solution.py:637
  18.7 5.1 %collective-permute-start.7 = (bf16[2,160,256]{2,1,0:T(8,128)(2,1)S(1)}, bf16[2,160,256]{2,1,0:T(8,128)(2,1)S(1)}, u32[]{:S(2)}, u32[]{:S(2)}) collective-permute-start(bf16[2,160,256]{2,1,0:T(8,128)(2,1)S(1)} %shard_map.63), channel_id=1, source_target_pairs={{0,1},{1,2},{2,3},{3,0},{4,5},{5,6},{6,7},{7,4}} | collective-permute-start | bytes 491528 | tf_op jit(solution)/shard_map/ppermute | solution.py:646
  19.3 5.8 %collective-permute-start.8 = (bf16[2,160,256]{2,1,0:T(8,128)(2,1)S(1)}, bf16[2,160,256]{2,1,0:T(8,128)(2,1)S(1)}, u32[]{:S(2)}, u32[]{:S(2)}) collective-permute-start(bf16[2,160,256]{2,1,0:T(8,128)(2,1)S(1)} %shard_map.63), channel_id=1, source_target_pairs={{0,2},{1,3},{2,0},{3,1},{4,6},{5,7},{6,4},{7,5}} | collective-permute-start | bytes 491528 | tf_op jit(solution)/shard_map/ppermute | solution.py:646
  20.1 1.6 %collective-permute-start.16 = (bf16[320,128]{1,0:T(8,128)(2,1)S(1)}, bf16[320,128]{1,0:T(8,128)(2,1)S(1)}, u32[]{:S(2)}, u32[]{:S(2)}) collective-permute-start(bf16[320,128]{1,0:T(8,128)(2,1)S(1)} %get-tuple-element.89), channel_id=1, source_target_pairs={{24,16},{25,17},{26,18},{27,19},{28,20},{29,21},{30,22},{31,23}} | collective-permute-start | bytes 245768 | tf_op jit(solution)/shard_map/ppermute | solution.py:637
  21.0 5.3 %collective-permute-start.15 = (bf16[320,128]{1,0:T(8,128)(2,1)S(1)}, bf16[320,128]{1,0:T(8,128)(2,1)S(1)}, u32[]{:S(2)}, u32[]{:S(2)}) collective-permute-start(bf16[320,128]{1,0:T(8,128)(2,1)S(1)} %get-tuple-element.85.refs_1_), channel_id=1, source_target_pairs={{24,16},{25,17},{26,18},{27,19},{28,20},{29,21},{30,22},{31,23}} | collective-permute-start | bytes 245768 | tf_op jit(solution)/shard_map/ppermute | solution.py:637
  21.7 14.1 %collective-permute-start.18 = (bf16[320,128]{1,0:T(8,128)(2,1)S(1)}, bf16[320,128]{1,0:T(8,128)(2,1)S(1)}, u32[]{:S(2)}, u32[]{:S(2)}) collective-permute-start(bf16[320,128]{1,0:T(8,128)(2,1)S(1)} %get-tuple-element.95), channel_id=1, source_target_pairs={{16,8},{17,9},{18,10},{19,11},{20,12},{21,13},{22,14},{23,15}} | collective-permute-start | bytes 245768 | tf_op jit(solution)/shard_map/ppermute | solution.py:637
  23.0 22.8 %collective-permute-start.9 = (bf16[2,160,256]{2,1,0:T(8,128)(2,1)S(1)}, bf16[2,160,256]{2,1,0:T(8,128)(2,1)S(1)}, u32[]{:S(2)}, u32[]{:S(2)}) collective-permute-start(bf16[2,160,256]{2,1,0:T(8,128)(2,1)S(1)} %shard_map.63), channel_id=1, source_target_pairs={{0,3},{1,0},{2,1},{3,2},{4,7},{5,4},{6,5},{7,6}} | collective-permute-start | bytes 491528 | tf_op jit(solution)/shard_map/ppermute | solution.py:646
  23.8 23.4 %collective-permute-start.11 = (bf16[2,160,256]{2,1,0:T(8,128)(2,1)S(1)}, bf16[2,160,256]{2,1,0:T(8,128)(2,1)S(1)}, u32[]{:S(2)}, u32[]{:S(2)}) collective-permute-start(bf16[2,160,256]{2,1,0:T(8,128)(2,1)S(1)} %shard_map.67), channel_id=1, source_target_pairs={{0,1},{1,2},{2,3},{3,0},{8,9},{9,10},{10,11},{11,8},{16,17},{17,18... | collective-permute-start | bytes 491528 | tf_op jit(solution)/shard_map/ppermute | solution.py:646
  25.1 22.8 %collective-permute-start.12 = (bf16[2,160,256]{2,1,0:T(8,128)(2,1)S(1)}, bf16[2,160,256]{2,1,0:T(8,128)(2,1)S(1)}, u32[]{:S(2)}, u32[]{:S(2)}) collective-permute-start(bf16[2,160,256]{2,1,0:T(8,128)(2,1)S(1)} %shard_map.67), channel_id=1, source_target_pairs={{0,2},{1,3},{2,0},{3,1},{8,10},{9,11},{10,8},{11,9},{16,18},{17,19... | collective-permute-start | bytes 491528 | tf_op jit(solution)/shard_map/ppermute | solution.py:646
  26.3 21.7 %collective-permute-start.13 = (bf16[2,160,256]{2,1,0:T(8,128)(2,1)S(1)}, bf16[2,160,256]{2,1,0:T(8,128)(2,1)S(1)}, u32[]{:S(2)}, u32[]{:S(2)}) collective-permute-start(bf16[2,160,256]{2,1,0:T(8,128)(2,1)S(1)} %shard_map.67), channel_id=1, source_target_pairs={{0,3},{1,0},{2,1},{3,2},{8,11},{9,8},{10,9},{11,10},{16,19},{17,16... | collective-permute-start | bytes 491528 | tf_op jit(solution)/shard_map/ppermute | solution.py:646
  35.9 7.3 %collective-permute-start.17 = (bf16[320,128]{1,0:T(8,128)(2,1)S(1)}, bf16[320,128]{1,0:T(8,128)(2,1)S(1)}, u32[]{:S(2)}, u32[]{:S(2)}) collective-permute-start(bf16[320,128]{1,0:T(8,128)(2,1)S(1)} %get-tuple-element.94), channel_id=1, source_target_pairs={{16,8},{17,9},{18,10},{19,11},{20,12},{21,13},{22,14},{23,15}} | collective-permute-start | bytes 245768 | tf_op jit(solution)/shard_map/ppermute | solution.py:637
  43.2 12.9 %collective-permute-start.20 = (bf16[320,128]{1,0:T(8,128)(2,1)S(1)}, bf16[320,128]{1,0:T(8,128)(2,1)S(1)}, u32[]{:S(2)}, u32[]{:S(2)}) collective-permute-start(bf16[320,128]{1,0:T(8,128)(2,1)S(1)} %get-tuple-element.101), channel_id=1, source_target_pairs={{8,0},{9,1},{10,2},{11,3},{12,4},{13,5},{14,6},{15,7}} | collective-permute-start | bytes 245768 | tf_op jit(solution)/shard_map/ppermute | solution.py:637
  45.8 10.2 %collective-permute-start.19 = (bf16[320,128]{1,0:T(8,128)(2,1)S(1)}, bf16[320,128]{1,0:T(8,128)(2,1)S(1)}, u32[]{:S(2)}, u32[]{:S(2)}) collective-permute-start(bf16[320,128]{1,0:T(8,128)(2,1)S(1)} %get-tuple-element.100), channel_id=1, source_target_pairs={{8,0},{9,1},{10,2},{11,3},{12,4},{13,5},{14,6},{15,7}} | collective-permute-start | bytes 245768 | tf_op jit(solution)/shard_map/ppermute | solution.py:637
  47.2 22.5 %collective-permute-start.10 = (bf16[2,4,160,256]{3,2,1,0:T(8,128)(2,1)S(1)}, bf16[2,4,160,256]{3,2,1,0:T(8,128)(2,1)S(1)}, u32[]{:S(2)}, u32[]{:S(2)}) collective-permute-start(bf16[2,4,160,256]{3,2,1,0:T(8,128)(2,1)S(1)} %get-tuple-element.81), channel_id=1, source_target_pairs={{0,4},{4,0},{1,5},{5,1},{2,6},{6,2},{3,7},{7,3}} | collective-permute-start | bytes 1966088 | tf_op jit(solution)/shard_map/ppermute | solution.py:713
  51.1 18.6 %collective-permute-start.14 = (bf16[2,4,160,256]{3,2,1,0:T(8,128)(2,1)S(1)}, bf16[2,4,160,256]{3,2,1,0:T(8,128)(2,1)S(1)}, u32[]{:S(2)}, u32[]{:S(2)}) collective-permute-start(bf16[2,4,160,256]{3,2,1,0:T(8,128)(2,1)S(1)} %get-tuple-element.86), channel_id=1, source_target_pairs={{0,4},{4,0},{1,5},{5,1},{2,6},{6,2},{3,7},{7,3},{8,12},{12,8},{9,1... | collective-permute-start | bytes 1966088 | tf_op jit(solution)/shard_map/ppermute | solution.py:618
  56.1 4.0 %collective-permute-start.21 = (bf16[2,80,256]{2,1,0:T(8,128)(2,1)S(1)}, bf16[2,80,256]{2,1,0:T(8,128)(2,1)S(1)}, u32[]{:S(2)}, u32[]{:S(2)}) collective-permute-start(bf16[2,80,256]{2,1,0:T(8,128)(2,1)S(1)} %get-tuple-element.112), channel_id=1, source_target_pairs={{0,1},{1,2},{2,3},{3,0},{8,9},{9,10},{10,11},{11,8},{16,17},{17,18... | collective-permute-start | bytes 245768 | tf_op jit(solution)/shard_map/ppermute | solution.py:646
  56.5 8.1 %collective-permute-start.22 = (bf16[2,80,256]{2,1,0:T(8,128)(2,1)S(1)}, bf16[2,80,256]{2,1,0:T(8,128)(2,1)S(1)}, u32[]{:S(2)}, u32[]{:S(2)}) collective-permute-start(bf16[2,80,256]{2,1,0:T(8,128)(2,1)S(1)} %get-tuple-element.111), channel_id=1, source_target_pairs={{0,2},{1,3},{2,0},{3,1},{8,10},{9,11},{10,8},{11,9},{16,18},{17,19... | collective-permute-start | bytes 245768 | tf_op jit(solution)/shard_map/ppermute | solution.py:646
  59.3 7.2 %collective-permute-start.23 = (bf16[2,80,256]{2,1,0:T(8,128)(2,1)S(1)}, bf16[2,80,256]{2,1,0:T(8,128)(2,1)S(1)}, u32[]{:S(2)}, u32[]{:S(2)}) collective-permute-start(bf16[2,80,256]{2,1,0:T(8,128)(2,1)S(1)} %get-tuple-element.110), channel_id=1, source_target_pairs={{0,3},{1,0},{2,1},{3,2},{8,11},{9,8},{10,9},{11,10},{16,19},{17,16... | collective-permute-start | bytes 245768 | tf_op jit(solution)/shard_map/ppermute | solution.py:646
  66.5 4.4 %collective-permute-start.24 = (bf16[4,2,80,256]{3,2,1,0:T(8,128)(2,1)S(1)}, bf16[4,2,80,256]{3,2,1,0:T(8,128)(2,1)S(1)}, u32[]{:S(2)}, u32[]{:S(2)}) collective-permute-start(bf16[4,2,80,256]{3,2,1,0:T(8,128)(2,1)S(1)} %shard_map.77.own_ref), channel_id=1, source_target_pairs={{0,4},{4,0},{1,5},{5,1},{2,6},{6,2},{3,7},{7,3},{8,12},{12,8},{9,1... | collective-permute-start | bytes 983048 | tf_op jit(solution)/shard_map/ppermute | solution.py:618
  67.6 1.4 %collective-permute-start.25 = (bf16[2,8,8,320]{3,2,1,0:T(8,128)(2,1)S(1)}, bf16[2,8,8,320]{3,2,1,0:T(8,128)(2,1)S(1)}, u32[]{:S(2)}, u32[]{:S(2)}) collective-permute-start(bf16[2,8,8,320]{3,2,1,0:T(8,128)(2,1)S(1)} %get-tuple-element.109), channel_id=1, source_target_pairs={{0,4},{4,0},{1,5},{5,1},{2,6},{6,2},{3,7},{7,3},{8,12},{12,8},{9,1... | collective-permute-start | bytes 245768 | tf_op jit(solution)/shard_map/ppermute | solution.py:618

commit v9 on v8

--- a/solution.py
+++ b/solution.py
@@ -307,12 +307,14 @@
                 jnp.bfloat16
             )
             place_parts(sent_ref, (1,), grad_hidden, crop, parts, own)
-            added = convolved(
-                grad_hidden.astype(jnp.float32), turned_ref.at[0], taps, shifted, width
-            )
-            result = (wide + added).astype(jnp.bfloat16)
-            kept_ref[crop] = result
-            if not first:
+            if first:
+                kept_ref[crop] = grad_hidden
+            else:
+                added = convolved(
+                    grad_hidden.astype(jnp.float32), turned_ref.at[0], taps, shifted, width
+                )
+                result = (wide + added).astype(jnp.bfloat16)
+                kept_ref[crop] = result
                 refs[-5][...] = pack(result)
 
     outs = [
@@ -328,6 +330,30 @@
     operands = [grad, turned, hidden, after, *state]
     outputs = call(kernel, outs, operands, (3,), scratch, aliases)
     return (None if first else outputs[0]), outputs[-2:]
+
+
+def finish_call(grads, turned, kept, width):
+    crops, count, channels = kept.shape
+
+    def kernel(turned_ref, *refs):
+        kept_ref, taps, shifted = refs[-3:]
+
+        @pl.when(lax.axis_index("section") == 0)
+        def _():
+            for crop in range(crops):
+                wide = unpack(refs[crop][...], count, channels).astype(jnp.float32)
+                grad_hidden = kept_ref[crop].astype(jnp.float32)
+                added = convolved(grad_hidden, turned_ref.at[0], taps, shifted, width)
+                kept_ref[crop] = (wide + added).astype(jnp.bfloat16)
+
+    out = jax.ShapeDtypeStruct(kept.shape, kept.dtype)
+    scratch = [
+        pltpu.VMEM((count + 2 * width, 3 * channels), jnp.bfloat16),
+        pltpu.VMEM((count + 16, channels), jnp.float32),
+    ]
+    operands = [turned, *grads, kept]
+    (kept,) = call(kernel, [out], operands, (), scratch, {len(operands) - 1: 0})
+    return kept
 
 
 def place_parts(target, lead, value, crop, parts, own):
@@ -664,54 +690,75 @@
     incoming = fields
     state = []
     turned, after = None, weights
-    for place in range(sections):
+    grads = []
+
+    def forward(place, crop):
+        return forward_call(
+            incoming[crop],
+            weights,
+            state,
+            place,
+            crop,
+            crops,
+            shape,
+            width,
+            place == last,
+            after,
+        )
+
+    def backward(place, crop, incoming):
+        return backward_call(
+            incoming[crop],
+            turned,
+            state[1],
+            grads,
+            place,
+            crop,
+            crops,
+            shape,
+            width,
+            place == last,
+            groups,
+            after,
+        )
+
+    for place in range(last):
         outgoing = []
         for crop in range(crops):
-            out, state = forward_call(
-                incoming[crop], weights, state, place, crop, crops, shape, width, place == last, after
-            )
+            out, state = forward(place, crop)
             outgoing.append(out)
         if place == 0:
             weights = load_call(stored, False, state[0])
-        if place < last:
-            incoming = hop(outgoing, place, place + 1)
+        incoming = hop(outgoing, place, place + 1)
         if place == early:
             inputs = flipped(state[0], state[1])
             soon = [shared(inputs, step, [0]) for step in steps]
             turned = turn_call(weights, state[0])
             after = turned
+    outgoing = []
+    for crop in range(crops):
+        _, state = forward(last, crop)
+        out, grads = backward(last, crop, fields)
+        after = out
+        outgoing.append(out)
     saved, hidden = state
-    incoming = fields
-    grads = []
+    incoming = hop(outgoing, last, last - 1)
+    inputs = flipped(saved, outgoing[-1])
+    late = [shared(inputs, step, range(sections)) for step in steps]
     after = hidden
-    for place in reversed(range(sections)):
+    for place in reversed(range(last)):
+        if place == 0:
+            first, early_outer = remake_call(saved, weights, soon, width, (0, 0))
+            after = first
+            early_outer = lax.ppermute(early_outer, ("section", "slab"), [(i, (i + 1) % slabs) for i in range(slabs)])
         outgoing = []
         for crop in range(crops):
-            out, grads = backward_call(
-                incoming[crop],
-                turned,
-                hidden,
-                grads,
-                place,
-                crop,
-                crops,
-                shape,
-                width,
-                place == last,
-                groups,
-                after,
-            )
+            out, grads = backward(place, crop, incoming)
             outgoing.append(out)
         if place:
             incoming = hop(outgoing, place, place - 1)
-        if place == last:
-            inputs = flipped(saved, outgoing[-1])
-            late = [shared(inputs, step, range(sections)) for step in steps]
-        if place == 1:
-            first, early_outer = remake_call(saved, weights, soon, width, (0, 0))
-            after = first
-            early_outer = lax.ppermute(early_outer, ("section", "slab"), [(i, (i + 1) % slabs) for i in range(slabs)])
     kept, sent = grads
+    kept = finish_call(incoming, turned, kept, width)
     own = [sent[0]]
     for step in steps:
         own.append(shared(sent[step], step, range(sections)))

time: 73.8 us -> 71.4 us (0.967)
  the two profiles are of different devices: /device:TPU:11 before, /device:TPU:0 now
where the time goes in v9:
time: 71.4 us; the launch traced here: 71 us
  starting transfers between devices  36.5 us (51%)
  Pallas kernels  21.2 us (30%)
  waiting for transfers between devices  12 us (17%)
  between operations  1.26 us (2%)
    ppermute x9, starting transfers between devices, shared(): return lax.ppermute(values, ('section', 'img'), pairs)  21.6 us
    pallas_call x31, Pallas kernels, call(): pl.pallas_call(kernel, out_shape=outs, in_specs=[pl.BlockSpec(memory_spac...  18.9 us
    ppermute x12, starting transfers between devices, hop(): arrived.append(lax.ppermute(value, 'section', [(source, target)]))  11.2 us
    ppermute x9, waiting for transfers between devices, shared(): return lax.ppermute(values, ('section', 'img'), pairs)  7.26 us
    ppermute x12, waiting for transfers between devices, hop(): arrived.append(lax.ppermute(value, 'section', [(source, target)]))  4.72 us
    pallas_call x1, Pallas kernels, terms_call(): pl.pallas_call(kernel, out_shape=jax.ShapeDtypeStruct(shape, jnp.float32)...  2.31 us
    ppermute x1, starting transfers between devices, crop_shards(): lax.ppermute(early_outer, ('section', 'slab'), [(i, (i + 1) % slabs) for...  1.92 us
    ppermute x4, starting transfers between devices, rotated(): lax.ppermute(value, axis, [(source, (source + steps) % count) for source...  1.73 us
  transfers between devices with their start and end apart: 26, of which 6 were waited for; matrix products, arithmetic and copies ran while one was open for 0% of the time, Pallas kernels for 23%

profile of v9, /device:TPU:0, one launch (start us, length us, event | category | flops | bytes accessed | tf_op | source)
XLA Modules:
  0.0 71.0 jit_solution(5322934803444610185)
XLA Ops:
  0.6 1.0 %shard_map.50 = (bf16[2,8,8,320]{3,2,1,0:T(8,128)(2,1)S(1)}, bf16[2,8,8,320]{3,2,1,0:T(8,128)(2,1)S(1)}) custom-call(bf16[1,4,8,8,320]{4,3,2,1,0:T(8,128)(2,1)} %strips_ref.1, bf16[1,4,8,8,320]{4,3,2,1,0:T(8,128)(2,1)} %cotangent_ref.1), custom_call_target="tpu_custom_call" | custom-call | tf_op jit(solution)/shard_map/pallas_call | solution.py:177
  1.6 0.6 collective-permute-start
  2.2 2.3 %shard_map.52.weights_ref.after_ref = bf16[2,3,960,320]{3,2,1,0:T(8,128)(2,1)S(1)} custom-call(bf16[2,3,960,320]{3,2,1,0:T(8,128)(2,1)} %bitcast.11, bf16[2,8,8,320]{3,2,1,0:T(8,128)(2,1)S(1)} %get-tuple-element.56.own_ref.after_ref), custom_call_target="tpu_custom_call" | custom-call | tf_op jit(solution)/shard_map/pallas_call | solution.py:177
  4.5 0.0 collective-permute-done.other_ref
  4.5 0.1 shard_map.51
  4.6 1.4 %shard_map.53 = (bf16[320,128]{1,0:T(8,128)(2,1)S(1)}, bf16[2,2,128,320]{3,2,1,0:T(8,128)(2,1)S(1)}, f32[2,128,320]{2,1,0:T(8,128)S(1)}) custom-call(bf16[128,320]{1,0:T(8,128)(2,1)S(1)} %get-tuple-element.59.field_ref.grad_ref, bf16[2,3,960,320]{3,2,1,0:T(8,128)(2,1)S(1)} %shard_map.52.weights_ref.after_ref, ...), custom_call_target="tpu_custom_call" | custom-call | tf_op jit(solution)/shard_map/pallas_call | solution.py:177
  5.9 2.0 %collective-permute-start.2 = (bf16[320,128]{1,0:T(8,128)(2,1)S(1)}, bf16[320,128]{1,0:T(8,128)(2,1)S(1)}, u32[]{:S(2)}, u32[]{:S(2)}) collective-permute-start(bf16[320,128]{1,0:T(8,128)(2,1)S(1)} %get-tuple-element.64), channel_id=1, source_target_pairs={{0,8},{1,9},{2,10},{3,11},{4,12},{5,13},{6,14},{7,15}} | collective-permute-start | bytes 245768 | tf_op jit(solution)/shard_map/ppermute | solution.py:663
  7.9 1.4 %shard_map.54 = (bf16[320,128]{1,0:T(8,128)(2,1)S(1)}, bf16[2,2,128,320]{3,2,1,0:T(8,128)(2,1)S(1)}, f32[2,128,320]{2,1,0:T(8,128)S(1)}) custom-call(bf16[128,320]{1,0:T(8,128)(2,1)S(1)} %get-tuple-element.58.field_ref.grad_ref, bf16[2,3,960,320]{3,2,1,0:T(8,128)(2,1)S(1)} %shard_map.52.weights_ref.after_ref, ...), custom_call_target="tpu_custom_call", output_to_operand_aliasing={{1}: (3, {}), {2}: (4, {})} | custom-call | tf_op jit(solution)/shard_map/pallas_call | solution.py:177
  9.3 1.3 %collective-permute-start.1 = (bf16[320,128]{1,0:T(8,128)(2,1)S(1)}, bf16[320,128]{1,0:T(8,128)(2,1)S(1)}, u32[]{:S(2)}, u32[]{:S(2)}) collective-permute-start(bf16[320,128]{1,0:T(8,128)(2,1)S(1)} %get-tuple-element.62), channel_id=1, source_target_pairs={{0,8},{1,9},{2,10},{3,11},{4,12},{5,13},{6,14},{7,15}} | collective-permute-start | bytes 245768 | tf_op jit(solution)/shard_map/ppermute | solution.py:663
  10.6 2.3 %shard_map.55.weights_ref = bf16[2,3,960,320]{3,2,1,0:T(8,128)(2,1)S(1)} custom-call(bf16[2,3,960,320]{3,2,1,0:T(8,128)(2,1)} %bitcast.12, bf16[2,2,128,320]{3,2,1,0:T(8,128)(2,1)S(1)} %get-tuple-element.63.after_ref.refs_0_), custom_call_target="tpu_custom_call" | custom-call | tf_op jit(solution)/shard_map/pallas_call | solution.py:177
  12.9 0.0 collective-permute-done.2.field_ref
  13.0 0.7 collective-permute-start.4
  13.6 0.0 collective-permute-done.1.field_ref
  13.7 0.7 collective-permute-start.3
  14.3 1.4 %shard_map.58.after_ref.turned_ref = bf16[2,3,960,320]{3,2,1,0:T(8,128)(2,1)S(1)} custom-call(bf16[2,3,960,320]{3,2,1,0:T(8,128)(2,1)S(1)} %shard_map.55.weights_ref, bf16[2,2,128,320]{3,2,1,0:T(8,128)(2,1)S(1)} %get-tuple-element.69.after_ref.refs_0_), custom_call_target="tpu_custom_call" | custom-call | tf_op jit(solution)/shard_map/pallas_call | solution.py:177
  15.7 0.1 shard_map.64
  15.8 0.0 collective-permute-done.4.field_ref
  15.8 0.7 collective-permute-start.6
  16.5 0.0 collective-permute-done.3.field_ref
  16.5 0.7 collective-permute-start.5
  17.2 3.8 %collective-permute-start.7 = (bf16[2,160,256]{2,1,0:T(8,128)(2,1)S(1)}, bf16[2,160,256]{2,1,0:T(8,128)(2,1)S(1)}, u32[]{:S(2)}, u32[]{:S(2)}) collective-permute-start(bf16[2,160,256]{2,1,0:T(8,128)(2,1)S(1)} %shard_map.64), channel_id=1, source_target_pairs={{0,1},{1,2},{2,3},{3,0},{4,5},{5,6},{6,7},{7,4}} | collective-permute-start | bytes 491528 | tf_op jit(solution)/shard_map/ppermute | solution.py:672
  21.0 4.5 %collective-permute-start.8 = (bf16[2,160,256]{2,1,0:T(8,128)(2,1)S(1)}, bf16[2,160,256]{2,1,0:T(8,128)(2,1)S(1)}, u32[]{:S(2)}, u32[]{:S(2)}) collective-permute-start(bf16[2,160,256]{2,1,0:T(8,128)(2,1)S(1)} %shard_map.64), channel_id=1, source_target_pairs={{0,2},{1,3},{2,0},{3,1},{4,6},{5,7},{6,4},{7,5}} | collective-permute-start | bytes 491528 | tf_op jit(solution)/shard_map/ppermute | solution.py:672
  25.5 0.0 collective-permute-done.6.field_ref
  25.5 0.7 collective-permute-start.16
  26.3 0.2 shard_map.66
  26.5 0.7 collective-permute-start.15
  27.2 0.7 collective-permute-start.18
  27.8 3.2 %collective-permute-start.9 = (bf16[2,160,256]{2,1,0:T(8,128)(2,1)S(1)}, bf16[2,160,256]{2,1,0:T(8,128)(2,1)S(1)}, u32[]{:S(2)}, u32[]{:S(2)}) collective-permute-start(bf16[2,160,256]{2,1,0:T(8,128)(2,1)S(1)} %shard_map.64), channel_id=1, source_target_pairs={{0,3},{1,0},{2,1},{3,2},{4,7},{5,4},{6,5},{7,6}} | collective-permute-start | bytes 491528 | tf_op jit(solution)/shard_map/ppermute | solution.py:672
  31.1 0.1 shard_map.67
  31.2 0.7 %collective-permute-start.11 = (bf16[2,160,256]{2,1,0:T(8,128)(2,1)S(1)}, bf16[2,160,256]{2,1,0:T(8,128)(2,1)S(1)}, u32[]{:S(2)}, u32[]{:S(2)}) collective-permute-start(bf16[2,160,256]{2,1,0:T(8,128)(2,1)S(1)} %shard_map.67), channel_id=1, source_target_pairs={{0,1},{1,2},{2,3},{3,0},{8,9},{9,10},{10,11},{11,8},{16,17},{17,18... | collective-permute-start | bytes 491528 | tf_op jit(solution)/shard_map/ppermute | solution.py:672
  32.0 3.0 %collective-permute-done.8.refs_1_ = bf16[2,160,256]{2,1,0:T(8,128)(2,1)S(1)} collective-permute-done((bf16[2,160,256]{2,1,0:T(8,128)(2,1)S(1)}, bf16[2,160,256]{2,1,0:T(8,128)(2,1)S(1)}, u32[]{:S(2)}, u32[]{:S(2)}) %collective-permute-start.8) | collective-permute-done | bytes 163872 | tf_op jit(solution)/shard_map/ppermute | solution.py:672
  35.0 0.0 collective-permute-start.12
  35.0 0.0 collective-permute-done.15.grad_ref
  35.0 5.5 %collective-permute-start.13 = (bf16[2,160,256]{2,1,0:T(8,128)(2,1)S(1)}, bf16[2,160,256]{2,1,0:T(8,128)(2,1)S(1)}, u32[]{:S(2)}, u32[]{:S(2)}) collective-permute-start(bf16[2,160,256]{2,1,0:T(8,128)(2,1)S(1)} %shard_map.67), channel_id=1, source_target_pairs={{0,3},{1,0},{2,1},{3,2},{8,11},{9,8},{10,9},{11,10},{16,19},{17,16... | collective-permute-start | bytes 491528 | tf_op jit(solution)/shard_map/ppermute | solution.py:672
  40.5 0.7 collective-permute-start.17
  41.2 1.3 %collective-permute-start.20 = (bf16[320,128]{1,0:T(8,128)(2,1)S(1)}, bf16[320,128]{1,0:T(8,128)(2,1)S(1)}, u32[]{:S(2)}, u32[]{:S(2)}) collective-permute-start(bf16[320,128]{1,0:T(8,128)(2,1)S(1)} %get-tuple-element.101), channel_id=1, source_target_pairs={{8,0},{9,1},{10,2},{11,3},{12,4},{13,5},{14,6},{15,7}} | collective-permute-start | bytes 245768 | tf_op jit(solution)/shard_map/ppermute | solution.py:663
  42.5 0.0 collective-permute-done.9.refs_2_
  42.5 1.3 %collective-permute-start.19 = (bf16[320,128]{1,0:T(8,128)(2,1)S(1)}, bf16[320,128]{1,0:T(8,128)(2,1)S(1)}, u32[]{:S(2)}, u32[]{:S(2)}) collective-permute-start(bf16[320,128]{1,0:T(8,128)(2,1)S(1)} %get-tuple-element.100), channel_id=1, source_target_pairs={{8,0},{9,1},{10,2},{11,3},{12,4},{13,5},{14,6},{15,7}} | collective-permute-start | bytes 245768 | tf_op jit(solution)/shard_map/ppermute | solution.py:663
  43.8 2.9 %shard_map.65 = (bf16[2,4,160,256]{3,2,1,0:T(8,128)(2,1)S(1)}, bf16[2,4,160,256]{3,2,1,0:T(8,128)(2,1)S(1)}) custom-call(bf16[2,2,128,320]{3,2,1,0:T(8,128)(2,1)S(1)} %get-tuple-element.81.saved_ref.refs_0_, bf16[2,3,960,320]{3,2,1,0:T(8,128)(2,1)S(1)} %shard_map.55.weights_ref, bf16[2,160,256]{2,1,0:T(8,128)(2,1)S(1)} %collective-permute-done.7.refs_0_, ...), custom_call_target="tpu_custom_call" | custom-call | tf_op jit(solution)/shard_map/pallas_call | solution.py:177
  46.8 0.0 collective-permute-done.11.refs_0_
  46.8 1.9 %collective-permute-start.10 = (bf16[2,4,160,256]{3,2,1,0:T(8,128)(2,1)S(1)}, bf16[2,4,160,256]{3,2,1,0:T(8,128)(2,1)S(1)}, u32[]{:S(2)}, u32[]{:S(2)}) collective-permute-start(bf16[2,4,160,256]{3,2,1,0:T(8,128)(2,1)S(1)} %get-tuple-element.82), channel_id=1, source_target_pairs={{0,4},{4,0},{1,5},{5,1},{2,6},{6,2},{3,7},{7,3}} | collective-permute-start | bytes 1966088 | tf_op jit(solution)/shard_map/ppermute | solution.py:753
  48.7 0.3 collective-permute-done.12.refs_1_
  49.0 0.0 collective-permute-done.13.refs_2_
  49.0 0.6 collective-permute-start.14
  49.6 2.7 %collective-permute-done.20.grad_ref.refs_0_ = bf16[320,128]{1,0:T(8,128)(2,1)S(1)} collective-permute-done((bf16[320,128]{1,0:T(8,128)(2,1)S(1)}, bf16[320,128]{1,0:T(8,128)(2,1)S(1)}, u32[]{:S(2)}, u32[]{:S(2)}) %collective-permute-start.20) | collective-permute-done | bytes 81952 | tf_op jit(solution)/shard_map/ppermute | solution.py:663
  52.3 0.7 %shard_map.75 = (bf16[2,128,320]{2,1,0:T(8,128)(2,1)S(1)}, bf16[4,2,80,256]{3,2,1,0:T(8,128)(2,1)S(1)}) custom-call(bf16[320,128]{1,0:T(8,128)(2,1)S(1)} %collective-permute-done.20.grad_ref.refs_0_, bf16[2,3,960,320]{3,2,1,0:T(8,128)(2,1)S(1)} %shard_map.58.after_ref.turned_ref, ...), custom_call_target="tpu_custom_call", output_to_operand_aliasing={{0}: (4, {}), {1}: (5, {})} | custom-call | tf_op jit(solution)/shard_map/pallas_call | solution.py:177
  53.0 2.0 %collective-permute-done.19.grad_ref.refs_1_ = bf16[320,128]{1,0:T(8,128)(2,1)S(1)} collective-permute-done((bf16[320,128]{1,0:T(8,128)(2,1)S(1)}, bf16[320,128]{1,0:T(8,128)(2,1)S(1)}, u32[]{:S(2)}, u32[]{:S(2)}) %collective-permute-start.19) | collective-permute-done | bytes 81952 | tf_op jit(solution)/shard_map/ppermute | solution.py:663
  55.0 0.7 %shard_map.76 = (bf16[2,128,320]{2,1,0:T(8,128)(2,1)S(1)}, bf16[4,2,80,256]{3,2,1,0:T(8,128)(2,1)S(1)}) custom-call(bf16[320,128]{1,0:T(8,128)(2,1)S(1)} %collective-permute-done.19.grad_ref.refs_1_, bf16[2,3,960,320]{3,2,1,0:T(8,128)(2,1)S(1)} %shard_map.58.after_ref.turned_ref, ...), custom_call_target="tpu_custom_call", output_to_operand_aliasing={{0}: (4, {}), {1}: (5, {})} | custom-call | tf_op jit(solution)/shard_map/pallas_call | solution.py:177
  55.7 0.7 %collective-permute-start.21 = (bf16[2,80,256]{2,1,0:T(8,128)(2,1)S(1)}, bf16[2,80,256]{2,1,0:T(8,128)(2,1)S(1)}, u32[]{:S(2)}, u32[]{:S(2)}) collective-permute-start(bf16[2,80,256]{2,1,0:T(8,128)(2,1)S(1)} %get-tuple-element.112), channel_id=1, source_target_pairs={{0,1},{1,2},{2,3},{3,0},{8,9},{9,10},{10,11},{11,8},{16,17},{17,18... | collective-permute-start | bytes 245768 | tf_op jit(solution)/shard_map/ppermute | solution.py:672
  56.5 1.7 %collective-permute-start.22 = (bf16[2,80,256]{2,1,0:T(8,128)(2,1)S(1)}, bf16[2,80,256]{2,1,0:T(8,128)(2,1)S(1)}, u32[]{:S(2)}, u32[]{:S(2)}) collective-permute-start(bf16[2,80,256]{2,1,0:T(8,128)(2,1)S(1)} %get-tuple-element.111), channel_id=1, source_target_pairs={{0,2},{1,3},{2,0},{3,1},{8,10},{9,11},{10,8},{11,9},{16,18},{17,19... | collective-permute-start | bytes 245768 | tf_op jit(solution)/shard_map/ppermute | solution.py:672
  58.2 1.5 %collective-permute-start.23 = (bf16[2,80,256]{2,1,0:T(8,128)(2,1)S(1)}, bf16[2,80,256]{2,1,0:T(8,128)(2,1)S(1)}, u32[]{:S(2)}, u32[]{:S(2)}) collective-permute-start(bf16[2,80,256]{2,1,0:T(8,128)(2,1)S(1)} %get-tuple-element.110), channel_id=1, source_target_pairs={{0,3},{1,0},{2,1},{3,2},{8,11},{9,8},{10,9},{11,10},{16,19},{17,16... | collective-permute-start | bytes 245768 | tf_op jit(solution)/shard_map/ppermute | solution.py:672
  59.6 2.6 %collective-permute-done.21.refs_1_ = bf16[2,80,256]{2,1,0:T(8,128)(2,1)S(1)} collective-permute-done((bf16[2,80,256]{2,1,0:T(8,128)(2,1)S(1)}, bf16[2,80,256]{2,1,0:T(8,128)(2,1)S(1)}, u32[]{:S(2)}, u32[]{:S(2)}) %collective-permute-start.21) | collective-permute-done | bytes 81952 | tf_op jit(solution)/shard_map/ppermute | solution.py:672
  62.2 1.4 %collective-permute-done.22.refs_2_ = bf16[2,80,256]{2,1,0:T(8,128)(2,1)S(1)} collective-permute-done((bf16[2,80,256]{2,1,0:T(8,128)(2,1)S(1)}, bf16[2,80,256]{2,1,0:T(8,128)(2,1)S(1)}, u32[]{:S(2)}, u32[]{:S(2)}) %collective-permute-start.22) | collective-permute-done | bytes 81952 | tf_op jit(solution)/shard_map/ppermute | solution.py:672
  63.6 0.0 collective-permute-done.23.refs_3_
  63.6 0.1 collective-permute-start.24
  63.7 1.1 %shard_map.78.kept_ref = bf16[2,128,320]{2,1,0:T(8,128)(2,1)S(1)} custom-call(bf16[2,3,960,320]{3,2,1,0:T(8,128)(2,1)S(1)} %shard_map.58.after_ref.turned_ref, bf16[320,128]{1,0:T(8,128)(2,1)S(1)} %collective-permute-done.20.grad_ref.refs_0_, bf16[320,128]{1,0:T(8,128)(2,1)S(1)} %collective-permute-done.19.grad_ref.refs_1_, ...), custom_call_target="tpu_custom_call", output_to_operand_aliasing={{}: (3, {})} | custom-call | tf_op jit(solution)/shard_map/pallas_call | solution.py:177
  64.8 0.1 shard_map.79
  64.9 0.5 collective-permute-start.25
  65.4 1.2 %shard_map.69.refs_0_ = bf16[2,2048,480]{2,1,0:T(8,128)(2,1)S(1)} custom-call(bf16[2,4,160,256]{3,2,1,0:T(8,128)(2,1)S(1)} %get-tuple-element.88.first_ref.after_ref, bf16[2,4,160,256]{3,2,1,0:T(8,128)(2,1)S(1)} %get-tuple-element.89.cells_ref), custom_call_target="tpu_custom_call" | custom-call | tf_op jit(solution)/shard_map/pallas_call | solution.py:177
  66.6 0.0 collective-permute-done.25.other_ref
  66.6 0.7 shard_map.80
  67.3 1.2 %shard_map.70.around_ref = bf16[2,2048,480]{2,1,0:T(8,128)(2,1)S(1)} custom-call(bf16[2,4,160,256]{3,2,1,0:T(8,128)(2,1)S(1)} %collective-permute-done.10.first_ref, bf16[2,4,160,256]{3,2,1,0:T(8,128)(2,1)S(1)} %collective-permute-done.14.cells_ref, bf16[2,2048,480]{2,1,0:T(8,128)(2,1)S(1)} %shard_map.69.refs_0_), custom_call_target="tpu_custom_call", output_to_operand_aliasing={{}: (2, {})} | custom-call | tf_op jit(solution)/shard_map/pallas_call | solution.py:177
  68.5 0.0 collective-permute-done.24.other_ref
  68.5 2.3 %terms.1 = f32[2,9,160,80]{3,2,1,0:T(8,128)} custom-call(bf16[2,2048,480]{2,1,0:T(8,128)(2,1)S(1)} %shard_map.70.around_ref, bf16[4,2,80,256]{3,2,1,0:T(8,128)(2,1)S(1)} %shard_map.77.own_ref, bf16[4,2,80,256]{3,2,1,0:T(8,128)(2,1)S(1)} %collective-permute-done.24.other_ref), custom_call_target="tpu_custom_call" | custom-call | tf_op jit(solution)/shard_map/terms/pallas_call | solution.py:631
  (21 shorter events, 0.2 us)
Async XLA Ops:
  1.6 2.9 %collective-permute-start = (bf16[2,8,8,320]{3,2,1,0:T(8,128)(2,1)S(1)}, bf16[2,8,8,320]{3,2,1,0:T(8,128)(2,1)S(1)}, u32[]{:S(2)}, u32[]{:S(2)}) collective-permute-start(bf16[2,8,8,320]{3,2,1,0:T(8,128)(2,1)S(1)} %get-tuple-element.57), channel_id=1, source_target_pairs={{0,4},{4,0},{1,5},{5,1},{2,6},{6,2},{3,7},{7,3},{8,12},{12,8},{9,1... | collective-permute-start | bytes 245768 | tf_op jit(solution)/shard_map/ppermute | solution.py:644
  5.9 7.0 %collective-permute-start.2 = (bf16[320,128]{1,0:T(8,128)(2,1)S(1)}, bf16[320,128]{1,0:T(8,128)(2,1)S(1)}, u32[]{:S(2)}, u32[]{:S(2)}) collective-permute-start(bf16[320,128]{1,0:T(8,128)(2,1)S(1)} %get-tuple-element.64), channel_id=1, source_target_pairs={{0,8},{1,9},{2,10},{3,11},{4,12},{5,13},{6,14},{7,15}} | collective-permute-start | bytes 245768 | tf_op jit(solution)/shard_map/ppermute | solution.py:663
  9.3 4.3 %collective-permute-start.1 = (bf16[320,128]{1,0:T(8,128)(2,1)S(1)}, bf16[320,128]{1,0:T(8,128)(2,1)S(1)}, u32[]{:S(2)}, u32[]{:S(2)}) collective-permute-start(bf16[320,128]{1,0:T(8,128)(2,1)S(1)} %get-tuple-element.62), channel_id=1, source_target_pairs={{0,8},{1,9},{2,10},{3,11},{4,12},{5,13},{6,14},{7,15}} | collective-permute-start | bytes 245768 | tf_op jit(solution)/shard_map/ppermute | solution.py:663
  13.0 2.9 %collective-permute-start.4 = (bf16[320,128]{1,0:T(8,128)(2,1)S(1)}, bf16[320,128]{1,0:T(8,128)(2,1)S(1)}, u32[]{:S(2)}, u32[]{:S(2)}) collective-permute-start(bf16[320,128]{1,0:T(8,128)(2,1)S(1)} %get-tuple-element.70), channel_id=1, source_target_pairs={{8,16},{9,17},{10,18},{11,19},{12,20},{13,21},{14,22},{15,23}} | collective-permute-start | bytes 245768 | tf_op jit(solution)/shard_map/ppermute | solution.py:663
  13.7 2.9 %collective-permute-start.3 = (bf16[320,128]{1,0:T(8,128)(2,1)S(1)}, bf16[320,128]{1,0:T(8,128)(2,1)S(1)}, u32[]{:S(2)}, u32[]{:S(2)}) collective-permute-start(bf16[320,128]{1,0:T(8,128)(2,1)S(1)} %get-tuple-element.68), channel_id=1, source_target_pairs={{8,16},{9,17},{10,18},{11,19},{12,20},{13,21},{14,22},{15,23}} | collective-permute-start | bytes 245768 | tf_op jit(solution)/shard_map/ppermute | solution.py:663
  15.8 9.6 %collective-permute-start.6 = (bf16[320,128]{1,0:T(8,128)(2,1)S(1)}, bf16[320,128]{1,0:T(8,128)(2,1)S(1)}, u32[]{:S(2)}, u32[]{:S(2)}) collective-permute-start(bf16[320,128]{1,0:T(8,128)(2,1)S(1)} %get-tuple-element.75), channel_id=1, source_target_pairs={{16,24},{17,25},{18,26},{19,27},{20,28},{21,29},{22,30},{23,31}} | collective-permute-start | bytes 245768 | tf_op jit(solution)/shard_map/ppermute | solution.py:663
  16.5 9.7 %collective-permute-start.5 = (bf16[320,128]{1,0:T(8,128)(2,1)S(1)}, bf16[320,128]{1,0:T(8,128)(2,1)S(1)}, u32[]{:S(2)}, u32[]{:S(2)}) collective-permute-start(bf16[320,128]{1,0:T(8,128)(2,1)S(1)} %get-tuple-element.74), channel_id=1, source_target_pairs={{16,24},{17,25},{18,26},{19,27},{20,28},{21,29},{22,30},{23,31}} | collective-permute-start | bytes 245768 | tf_op jit(solution)/shard_map/ppermute | solution.py:663
  17.2 14.0 %collective-permute-start.7 = (bf16[2,160,256]{2,1,0:T(8,128)(2,1)S(1)}, bf16[2,160,256]{2,1,0:T(8,128)(2,1)S(1)}, u32[]{:S(2)}, u32[]{:S(2)}) collective-permute-start(bf16[2,160,256]{2,1,0:T(8,128)(2,1)S(1)} %shard_map.64), channel_id=1, source_target_pairs={{0,1},{1,2},{2,3},{3,0},{4,5},{5,6},{6,7},{7,4}} | collective-permute-start | bytes 491528 | tf_op jit(solution)/shard_map/ppermute | solution.py:672
  21.0 14.0 %collective-permute-start.8 = (bf16[2,160,256]{2,1,0:T(8,128)(2,1)S(1)}, bf16[2,160,256]{2,1,0:T(8,128)(2,1)S(1)}, u32[]{:S(2)}, u32[]{:S(2)}) collective-permute-start(bf16[2,160,256]{2,1,0:T(8,128)(2,1)S(1)} %shard_map.64), channel_id=1, source_target_pairs={{0,2},{1,3},{2,0},{3,1},{4,6},{5,7},{6,4},{7,5}} | collective-permute-start | bytes 491528 | tf_op jit(solution)/shard_map/ppermute | solution.py:672
  25.5 1.6 %collective-permute-start.16 = (bf16[320,128]{1,0:T(8,128)(2,1)S(1)}, bf16[320,128]{1,0:T(8,128)(2,1)S(1)}, u32[]{:S(2)}, u32[]{:S(2)}) collective-permute-start(bf16[320,128]{1,0:T(8,128)(2,1)S(1)} %get-tuple-element.79.after_ref), channel_id=1, source_target_pairs={{24,16},{25,17},{26,18},{27,19},{28,20},{29,21},{30,22},{31,23}} | collective-permute-start | bytes 245768 | tf_op jit(solution)/shard_map/ppermute | solution.py:663
  26.5 8.5 %collective-permute-start.15 = (bf16[320,128]{1,0:T(8,128)(2,1)S(1)}, bf16[320,128]{1,0:T(8,128)(2,1)S(1)}, u32[]{:S(2)}, u32[]{:S(2)}) collective-permute-start(bf16[320,128]{1,0:T(8,128)(2,1)S(1)} %get-tuple-element.86.refs_1_), channel_id=1, source_target_pairs={{24,16},{25,17},{26,18},{27,19},{28,20},{29,21},{30,22},{31,23}} | collective-permute-start | bytes 245768 | tf_op jit(solution)/shard_map/ppermute | solution.py:663
  27.2 13.3 %collective-permute-start.18 = (bf16[320,128]{1,0:T(8,128)(2,1)S(1)}, bf16[320,128]{1,0:T(8,128)(2,1)S(1)}, u32[]{:S(2)}, u32[]{:S(2)}) collective-permute-start(bf16[320,128]{1,0:T(8,128)(2,1)S(1)} %get-tuple-element.95), channel_id=1, source_target_pairs={{16,8},{17,9},{18,10},{19,11},{20,12},{21,13},{22,14},{23,15}} | collective-permute-start | bytes 245768 | tf_op jit(solution)/shard_map/ppermute | solution.py:663
  27.8 14.7 %collective-permute-start.9 = (bf16[2,160,256]{2,1,0:T(8,128)(2,1)S(1)}, bf16[2,160,256]{2,1,0:T(8,128)(2,1)S(1)}, u32[]{:S(2)}, u32[]{:S(2)}) collective-permute-start(bf16[2,160,256]{2,1,0:T(8,128)(2,1)S(1)} %shard_map.64), channel_id=1, source_target_pairs={{0,3},{1,0},{2,1},{3,2},{4,7},{5,4},{6,5},{7,6}} | collective-permute-start | bytes 491528 | tf_op jit(solution)/shard_map/ppermute | solution.py:672
  31.2 15.6 %collective-permute-start.11 = (bf16[2,160,256]{2,1,0:T(8,128)(2,1)S(1)}, bf16[2,160,256]{2,1,0:T(8,128)(2,1)S(1)}, u32[]{:S(2)}, u32[]{:S(2)}) collective-permute-start(bf16[2,160,256]{2,1,0:T(8,128)(2,1)S(1)} %shard_map.67), channel_id=1, source_target_pairs={{0,1},{1,2},{2,3},{3,0},{8,9},{9,10},{10,11},{11,8},{16,17},{17,18... | collective-permute-start | bytes 491528 | tf_op jit(solution)/shard_map/ppermute | solution.py:672
  35.0 14.0 %collective-permute-start.12 = (bf16[2,160,256]{2,1,0:T(8,128)(2,1)S(1)}, bf16[2,160,256]{2,1,0:T(8,128)(2,1)S(1)}, u32[]{:S(2)}, u32[]{:S(2)}) collective-permute-start(bf16[2,160,256]{2,1,0:T(8,128)(2,1)S(1)} %shard_map.67), channel_id=1, source_target_pairs={{0,2},{1,3},{2,0},{3,1},{8,10},{9,11},{10,8},{11,9},{16,18},{17,19... | collective-permute-start | bytes 491528 | tf_op jit(solution)/shard_map/ppermute | solution.py:672
  35.0 14.0 %collective-permute-start.13 = (bf16[2,160,256]{2,1,0:T(8,128)(2,1)S(1)}, bf16[2,160,256]{2,1,0:T(8,128)(2,1)S(1)}, u32[]{:S(2)}, u32[]{:S(2)}) collective-permute-start(bf16[2,160,256]{2,1,0:T(8,128)(2,1)S(1)} %shard_map.67), channel_id=1, source_target_pairs={{0,3},{1,0},{2,1},{3,2},{8,11},{9,8},{10,9},{11,10},{16,19},{17,16... | collective-permute-start | bytes 491528 | tf_op jit(solution)/shard_map/ppermute | solution.py:672
  40.5 0.7 collective-permute-start.17
  41.2 11.1 %collective-permute-start.20 = (bf16[320,128]{1,0:T(8,128)(2,1)S(1)}, bf16[320,128]{1,0:T(8,128)(2,1)S(1)}, u32[]{:S(2)}, u32[]{:S(2)}) collective-permute-start(bf16[320,128]{1,0:T(8,128)(2,1)S(1)} %get-tuple-element.101), channel_id=1, source_target_pairs={{8,0},{9,1},{10,2},{11,3},{12,4},{13,5},{14,6},{15,7}} | collective-permute-start | bytes 245768 | tf_op jit(solution)/shard_map/ppermute | solution.py:663
  42.5 12.4 %collective-permute-start.19 = (bf16[320,128]{1,0:T(8,128)(2,1)S(1)}, bf16[320,128]{1,0:T(8,128)(2,1)S(1)}, u32[]{:S(2)}, u32[]{:S(2)}) collective-permute-start(bf16[320,128]{1,0:T(8,128)(2,1)S(1)} %get-tuple-element.100), channel_id=1, source_target_pairs={{8,0},{9,1},{10,2},{11,3},{12,4},{13,5},{14,6},{15,7}} | collective-permute-start | bytes 245768 | tf_op jit(solution)/shard_map/ppermute | solution.py:663
  46.8 20.5 %collective-permute-start.10 = (bf16[2,4,160,256]{3,2,1,0:T(8,128)(2,1)S(1)}, bf16[2,4,160,256]{3,2,1,0:T(8,128)(2,1)S(1)}, u32[]{:S(2)}, u32[]{:S(2)}) collective-permute-start(bf16[2,4,160,256]{3,2,1,0:T(8,128)(2,1)S(1)} %get-tuple-element.82), channel_id=1, source_target_pairs={{0,4},{4,0},{1,5},{5,1},{2,6},{6,2},{3,7},{7,3}} | collective-permute-start | bytes 1966088 | tf_op jit(solution)/shard_map/ppermute | solution.py:753
  49.0 18.3 %collective-permute-start.14 = (bf16[2,4,160,256]{3,2,1,0:T(8,128)(2,1)S(1)}, bf16[2,4,160,256]{3,2,1,0:T(8,128)(2,1)S(1)}, u32[]{:S(2)}, u32[]{:S(2)}) collective-permute-start(bf16[2,4,160,256]{3,2,1,0:T(8,128)(2,1)S(1)} %get-tuple-element.87), channel_id=1, source_target_pairs={{0,4},{4,0},{1,5},{5,1},{2,6},{6,2},{3,7},{7,3},{8,12},{12,8},{9,1... | collective-permute-start | bytes 1966088 | tf_op jit(solution)/shard_map/ppermute | solution.py:644
  55.7 6.4 %collective-permute-start.21 = (bf16[2,80,256]{2,1,0:T(8,128)(2,1)S(1)}, bf16[2,80,256]{2,1,0:T(8,128)(2,1)S(1)}, u32[]{:S(2)}, u32[]{:S(2)}) collective-permute-start(bf16[2,80,256]{2,1,0:T(8,128)(2,1)S(1)} %get-tuple-element.112), channel_id=1, source_target_pairs={{0,1},{1,2},{2,3},{3,0},{8,9},{9,10},{10,11},{11,8},{16,17},{17,18... | collective-permute-start | bytes 245768 | tf_op jit(solution)/shard_map/ppermute | solution.py:672
  56.5 7.1 %collective-permute-start.22 = (bf16[2,80,256]{2,1,0:T(8,128)(2,1)S(1)}, bf16[2,80,256]{2,1,0:T(8,128)(2,1)S(1)}, u32[]{:S(2)}, u32[]{:S(2)}) collective-permute-start(bf16[2,80,256]{2,1,0:T(8,128)(2,1)S(1)} %get-tuple-element.111), channel_id=1, source_target_pairs={{0,2},{1,3},{2,0},{3,1},{8,10},{9,11},{10,8},{11,9},{16,18},{17,19... | collective-permute-start | bytes 245768 | tf_op jit(solution)/shard_map/ppermute | solution.py:672
  58.2 5.4 %collective-permute-start.23 = (bf16[2,80,256]{2,1,0:T(8,128)(2,1)S(1)}, bf16[2,80,256]{2,1,0:T(8,128)(2,1)S(1)}, u32[]{:S(2)}, u32[]{:S(2)}) collective-permute-start(bf16[2,80,256]{2,1,0:T(8,128)(2,1)S(1)} %get-tuple-element.110), channel_id=1, source_target_pairs={{0,3},{1,0},{2,1},{3,2},{8,11},{9,8},{10,9},{11,10},{16,19},{17,16... | collective-permute-start | bytes 245768 | tf_op jit(solution)/shard_map/ppermute | solution.py:672
  63.6 4.9 %collective-permute-start.24 = (bf16[4,2,80,256]{3,2,1,0:T(8,128)(2,1)S(1)}, bf16[4,2,80,256]{3,2,1,0:T(8,128)(2,1)S(1)}, u32[]{:S(2)}, u32[]{:S(2)}) collective-permute-start(bf16[4,2,80,256]{3,2,1,0:T(8,128)(2,1)S(1)} %shard_map.77.own_ref), channel_id=1, source_target_pairs={{0,4},{4,0},{1,5},{5,1},{2,6},{6,2},{3,7},{7,3},{8,12},{12,8},{9,1... | collective-permute-start | bytes 983048 | tf_op jit(solution)/shard_map/ppermute | solution.py:644
  64.9 1.7 %collective-permute-start.25 = (bf16[2,8,8,320]{3,2,1,0:T(8,128)(2,1)S(1)}, bf16[2,8,8,320]{3,2,1,0:T(8,128)(2,1)S(1)}, u32[]{:S(2)}, u32[]{:S(2)}) collective-permute-start(bf16[2,8,8,320]{3,2,1,0:T(8,128)(2,1)S(1)} %get-tuple-element.109), channel_id=1, source_target_pairs={{0,4},{4,0},{1,5},{5,1},{2,6},{6,2},{3,7},{7,3},{8,12},{12,8},{9,1... | collective-permute-start | bytes 245768 | tf_op jit(solution)/shard_map/ppermute | solution.py:644

commit v10 on v9

--- a/solution.py
+++ b/solution.py
@@ -387,19 +387,23 @@
     return flipped
 
 
-def turn_call(weights, after):
+def turn_call(loaded, weights, after):
     two, _, _, channels = weights.shape
 
-    def kernel(weights_ref, after_ref, turned_ref):
+    def kernel(loaded_ref, weights_ref, after_ref, turned_ref):
+        is_first = lax.axis_index("section") == 0
         for which in range(two):
             for tap in range(9):
                 down, right = divmod(tap, 3)
-                flipped = weights_ref[which, down, right * channels : (right + 1) * channels, :].T
+                rows = slice(right * channels, (right + 1) * channels)
+                value = jnp.where(
+                    is_first, loaded_ref[which, down, rows, :], weights_ref[which, down, rows, :]
+                )
                 down, right = divmod(8 - tap, 3)
-                turned_ref[which, down, right * channels : (right + 1) * channels, :] = flipped
+                turned_ref[which, down, right * channels : (right + 1) * channels, :] = value.T
 
     out = jax.ShapeDtypeStruct(weights.shape, weights.dtype)
-    (turned,) = call(kernel, [out], [weights, after], (1,), [], {})
+    (turned,) = call(kernel, [out], [loaded, weights, after], (2,), [], {})
     return turned
 
 
@@ -440,7 +444,7 @@
     def kernel(weights_ref, after_ref, *refs):
         out_ref, sems = refs[-2:]
 
-        @pl.when((lax.axis_index("section") == 0) | (not first))
+        @pl.when((lax.axis_index("section") == 0) == first)
         def _():
             copies = [
                 pltpu.make_async_copy(weights_ref.at[which], out_ref.at[which], sems.at[which])
@@ -685,7 +689,7 @@
     other = swapped(other)
     weights = kernels[0].reshape(2, 3, 3 * channels, channels)
     stored = pltpu.with_memory_space_constraint(weights, pltpu.HBM)
-    weights = load_call(stored, True, own)
+    loaded = weights = load_call(stored, True, own)
     fields = join_call(own, other)
     incoming = fields
     state = []
@@ -733,7 +737,7 @@
         if place == early:
             inputs = flipped(state[0], state[1])
             soon = [shared(inputs, step, [0]) for step in steps]
-            turned = turn_call(weights, state[0])
+            turned = turn_call(loaded, weights, state[0])
             after = turned
     outgoing = []
     for crop in range(crops):
@@ -748,7 +752,7 @@
     after = hidden
     for place in reversed(range(last)):
         if place == 0:
-            first, early_outer = remake_call(saved, weights, soon, width, (0, 0))
+            first, early_outer = remake_call(saved, loaded, soon, width, (0, 0))
             after = first
             early_outer = lax.ppermute(early_outer, ("section", "slab"), [(i, (i + 1) % slabs) for i in range(slabs)])
         outgoing = []

time: 71.4 us -> 72.9 us (1.021)
  waiting for transfers between devices: 12 us -> 18.5 us
  starting transfers between devices: 36.5 us -> 33.8 us
  Pallas kernels: 21.2 us -> 19 us
    ppermute x9, waiting for transfers between devices: 7.26 us -> 15.2 us  [shared(): return lax.ppermute(values, ('section', 'img'), pairs)]
    pallas_call x31, Pallas kernels: 18.9 us -> 16.7 us  [call(): pl.pallas_call(kernel, out_shape=outs, in_specs=[pl.BlockSpec(memory_spac...]
    ppermute x9, starting transfers between devices: 21.6 us -> 19.5 us  [shared(): return lax.ppermute(values, ('section', 'img'), pairs)]
    ppermute x12, waiting for transfers between devices: 4.72 us -> 3.3 us  [hop(): arrived.append(lax.ppermute(value, 'section', [(source, target)]))]
  transfers between devices with their start and end apart: 26 -> 26, of which waited for: 6 -> 7; matrix products, arithmetic and copies ran while one was open for 0% -> 0% of each run, Pallas kernels for 23% -> 20%
where the time goes in v10:
time: 72.9 us; the launch traced here: 72.5 us
  starting transfers between devices  33.8 us (46%)
  Pallas kernels  19 us (26%)
  waiting for transfers between devices  18.5 us (25%)
  between operations  1.24 us (2%)
    ppermute x9, starting transfers between devices, shared(): return lax.ppermute(values, ('section', 'img'), pairs)  19.5 us
    pallas_call x31, Pallas kernels, call(): pl.pallas_call(kernel, out_shape=outs, in_specs=[pl.BlockSpec(memory_spac...  16.7 us
    ppermute x9, waiting for transfers between devices, shared(): return lax.ppermute(values, ('section', 'img'), pairs)  15.2 us
    ppermute x12, starting transfers between devices, hop(): arrived.append(lax.ppermute(value, 'section', [(source, target)]))  11.2 us
    ppermute x12, waiting for transfers between devices, hop(): arrived.append(lax.ppermute(value, 'section', [(source, target)]))  3.3 us
    pallas_call x1, Pallas kernels, terms_call(): pl.pallas_call(kernel, out_shape=jax.ShapeDtypeStruct(shape, jnp.float32)...  2.31 us
    ppermute x1, starting transfers between devices, crop_shards(): lax.ppermute(early_outer, ('section', 'slab'), [(i, (i + 1) % slabs) for...  1.92 us
  transfers between devices with their start and end apart: 26, of which 7 were waited for; matrix products, arithmetic and copies ran while one was open for 0% of the time, Pallas kernels for 20%

profile of v10, /device:TPU:0, one launch (start us, length us, event | category | flops | bytes accessed | tf_op | source)
XLA Modules:
  0.0 72.5 jit_solution(8210892185627902402)
XLA Ops:
  0.6 1.0 %shard_map.50 = (bf16[2,8,8,320]{3,2,1,0:T(8,128)(2,1)S(1)}, bf16[2,8,8,320]{3,2,1,0:T(8,128)(2,1)S(1)}) custom-call(bf16[1,4,8,8,320]{4,3,2,1,0:T(8,128)(2,1)} %strips_ref.1, bf16[1,4,8,8,320]{4,3,2,1,0:T(8,128)(2,1)} %cotangent_ref.1), custom_call_target="tpu_custom_call" | custom-call | tf_op jit(solution)/shard_map/pallas_call | solution.py:177
  1.6 0.6 collective-permute-start
  2.2 2.3 %shard_map.52.weights_ref.after_ref.loaded_ref = bf16[2,3,960,320]{3,2,1,0:T(8,128)(2,1)S(1)} custom-call(bf16[2,3,960,320]{3,2,1,0:T(8,128)(2,1)} %bitcast.11, bf16[2,8,8,320]{3,2,1,0:T(8,128)(2,1)S(1)} %get-tuple-element.56.own_ref.after_ref), custom_call_target="tpu_custom_call" | custom-call | tf_op jit(solution)/shard_map/pallas_call | solution.py:177
  4.5 0.0 collective-permute-done.other_ref
  4.5 0.1 shard_map.51
  4.6 1.4 %shard_map.53 = (bf16[320,128]{1,0:T(8,128)(2,1)S(1)}, bf16[2,2,128,320]{3,2,1,0:T(8,128)(2,1)S(1)}, f32[2,128,320]{2,1,0:T(8,128)S(1)}) custom-call(bf16[128,320]{1,0:T(8,128)(2,1)S(1)} %get-tuple-element.59.field_ref.grad_ref, bf16[2,3,960,320]{3,2,1,0:T(8,128)(2,1)S(1)} %shard_map.52.weights_ref.after_ref.loaded_ref, ...), custom_call_target="tpu_custom_call" | custom-call | tf_op jit(solution)/shard_map/pallas_call | solution.py:177
  5.9 2.0 %collective-permute-start.2 = (bf16[320,128]{1,0:T(8,128)(2,1)S(1)}, bf16[320,128]{1,0:T(8,128)(2,1)S(1)}, u32[]{:S(2)}, u32[]{:S(2)}) collective-permute-start(bf16[320,128]{1,0:T(8,128)(2,1)S(1)} %get-tuple-element.64), channel_id=1, source_target_pairs={{0,8},{1,9},{2,10},{3,11},{4,12},{5,13},{6,14},{7,15}} | collective-permute-start | bytes 245768 | tf_op jit(solution)/shard_map/ppermute | solution.py:667
  7.9 1.4 %shard_map.54 = (bf16[320,128]{1,0:T(8,128)(2,1)S(1)}, bf16[2,2,128,320]{3,2,1,0:T(8,128)(2,1)S(1)}, f32[2,128,320]{2,1,0:T(8,128)S(1)}) custom-call(bf16[128,320]{1,0:T(8,128)(2,1)S(1)} %get-tuple-element.58.field_ref.grad_ref, ...), custom_call_target="tpu_custom_call", output_to_operand_aliasing={{1}: (3, {}), {2}: (4, {})} | custom-call | tf_op jit(solution)/shard_map/pallas_call | solution.py:177
  9.3 1.3 %collective-permute-start.1 = (bf16[320,128]{1,0:T(8,128)(2,1)S(1)}, bf16[320,128]{1,0:T(8,128)(2,1)S(1)}, u32[]{:S(2)}, u32[]{:S(2)}) collective-permute-start(bf16[320,128]{1,0:T(8,128)(2,1)S(1)} %get-tuple-element.62), channel_id=1, source_target_pairs={{0,8},{1,9},{2,10},{3,11},{4,12},{5,13},{6,14},{7,15}} | collective-permute-start | bytes 245768 | tf_op jit(solution)/shard_map/ppermute | solution.py:667
  10.6 0.0 collective-permute-done.2.field_ref
  10.7 0.7 collective-permute-start.4
  11.4 1.3 %collective-permute-done.1.field_ref = bf16[320,128]{1,0:T(8,128)(2,1)S(1)} collective-permute-done((bf16[320,128]{1,0:T(8,128)(2,1)S(1)}, bf16[320,128]{1,0:T(8,128)(2,1)S(1)}, u32[]{:S(2)}, u32[]{:S(2)}) %collective-permute-start.1) | collective-permute-done | bytes 81952 | tf_op jit(solution)/shard_map/ppermute | solution.py:667
  12.6 0.7 collective-permute-start.3
  13.3 1.4 %shard_map.58.after_ref.turned_ref = bf16[2,3,960,320]{3,2,1,0:T(8,128)(2,1)S(1)} custom-call(bf16[2,3,960,320]{3,2,1,0:T(8,128)(2,1)S(1)} %shard_map.52.weights_ref.after_ref.loaded_ref, bf16[2,3,960,320]{3,2,1,0:T(8,128)(2,1)S(1)} %shard_map.55.weights_ref, bf16[2,2,128,320]{3,2,1,0:T(8,128)(2,1)S(1)} %get-tuple-element.69.after_ref.refs_0_), custom_call_target="tpu_custom_call" | custom-call | tf_op jit(solution)/shard_map/pallas_call | solution.py:177
  14.7 0.1 shard_map.64
  14.8 0.0 collective-permute-done.4.field_ref
  14.8 0.7 collective-permute-start.6
  15.5 0.0 collective-permute-done.3.field_ref
  15.5 0.7 collective-permute-start.5
  16.2 6.3 %collective-permute-start.9 = (bf16[2,160,256]{2,1,0:T(8,128)(2,1)S(1)}, bf16[2,160,256]{2,1,0:T(8,128)(2,1)S(1)}, u32[]{:S(2)}, u32[]{:S(2)}) collective-permute-start(bf16[2,160,256]{2,1,0:T(8,128)(2,1)S(1)} %shard_map.64), channel_id=1, source_target_pairs={{0,3},{1,0},{2,1},{3,2},{4,7},{5,4},{6,5},{7,6}} | collective-permute-start | bytes 491528 | tf_op jit(solution)/shard_map/ppermute | solution.py:676
  22.6 1.9 %collective-permute-start.8 = (bf16[2,160,256]{2,1,0:T(8,128)(2,1)S(1)}, bf16[2,160,256]{2,1,0:T(8,128)(2,1)S(1)}, u32[]{:S(2)}, u32[]{:S(2)}) collective-permute-start(bf16[2,160,256]{2,1,0:T(8,128)(2,1)S(1)} %shard_map.64), channel_id=1, source_target_pairs={{0,2},{1,3},{2,0},{3,1},{4,6},{5,7},{6,4},{7,5}} | collective-permute-start | bytes 491528 | tf_op jit(solution)/shard_map/ppermute | solution.py:676
  24.5 0.0 collective-permute-done.6.field_ref
  24.5 0.7 collective-permute-start.16
  25.2 0.0 collective-permute-done.5.field_ref
  25.3 0.2 shard_map.66
  25.5 0.7 collective-permute-start.15
  26.1 0.0 collective-permute-done.16.grad_ref
  26.2 0.7 collective-permute-start.18
  26.8 2.9 %collective-permute-start.7 = (bf16[2,160,256]{2,1,0:T(8,128)(2,1)S(1)}, bf16[2,160,256]{2,1,0:T(8,128)(2,1)S(1)}, u32[]{:S(2)}, u32[]{:S(2)}) collective-permute-start(bf16[2,160,256]{2,1,0:T(8,128)(2,1)S(1)} %shard_map.64), channel_id=1, source_target_pairs={{0,1},{1,2},{2,3},{3,0},{4,5},{5,6},{6,7},{7,4}} | collective-permute-start | bytes 491528 | tf_op jit(solution)/shard_map/ppermute | solution.py:676
  29.7 0.1 shard_map.67
  29.9 2.9 %collective-permute-start.13 = (bf16[2,160,256]{2,1,0:T(8,128)(2,1)S(1)}, bf16[2,160,256]{2,1,0:T(8,128)(2,1)S(1)}, u32[]{:S(2)}, u32[]{:S(2)}) collective-permute-start(bf16[2,160,256]{2,1,0:T(8,128)(2,1)S(1)} %shard_map.67), channel_id=1, source_target_pairs={{0,3},{1,0},{2,1},{3,2},{8,11},{9,8},{10,9},{11,10},{16,19},{17,16... | collective-permute-start | bytes 491528 | tf_op jit(solution)/shard_map/ppermute | solution.py:676
  32.8 4.8 %collective-permute-done.8.refs_1_ = bf16[2,160,256]{2,1,0:T(8,128)(2,1)S(1)} collective-permute-done((bf16[2,160,256]{2,1,0:T(8,128)(2,1)S(1)}, bf16[2,160,256]{2,1,0:T(8,128)(2,1)S(1)}, u32[]{:S(2)}, u32[]{:S(2)}) %collective-permute-start.8) | collective-permute-done | bytes 163872 | tf_op jit(solution)/shard_map/ppermute | solution.py:676
  37.6 0.0 collective-permute-start.12
  37.6 0.0 collective-permute-done.15.grad_ref
  37.6 1.4 %collective-permute-start.11 = (bf16[2,160,256]{2,1,0:T(8,128)(2,1)S(1)}, bf16[2,160,256]{2,1,0:T(8,128)(2,1)S(1)}, u32[]{:S(2)}, u32[]{:S(2)}) collective-permute-start(bf16[2,160,256]{2,1,0:T(8,128)(2,1)S(1)} %shard_map.67), channel_id=1, source_target_pairs={{0,1},{1,2},{2,3},{3,0},{8,9},{9,10},{10,11},{11,8},{16,17},{17,18... | collective-permute-start | bytes 491528 | tf_op jit(solution)/shard_map/ppermute | solution.py:676
  39.0 0.7 collective-permute-start.17
  39.7 0.0 collective-permute-done.17.grad_ref
  39.7 1.3 %collective-permute-start.20 = (bf16[320,128]{1,0:T(8,128)(2,1)S(1)}, bf16[320,128]{1,0:T(8,128)(2,1)S(1)}, u32[]{:S(2)}, u32[]{:S(2)}) collective-permute-start(bf16[320,128]{1,0:T(8,128)(2,1)S(1)} %get-tuple-element.101), channel_id=1, source_target_pairs={{8,0},{9,1},{10,2},{11,3},{12,4},{13,5},{14,6},{15,7}} | collective-permute-start | bytes 245768 | tf_op jit(solution)/shard_map/ppermute | solution.py:667
  41.0 0.0 collective-permute-done.7.refs_0_
  41.0 1.3 %collective-permute-start.19 = (bf16[320,128]{1,0:T(8,128)(2,1)S(1)}, bf16[320,128]{1,0:T(8,128)(2,1)S(1)}, u32[]{:S(2)}, u32[]{:S(2)}) collective-permute-start(bf16[320,128]{1,0:T(8,128)(2,1)S(1)} %get-tuple-element.100), channel_id=1, source_target_pairs={{8,0},{9,1},{10,2},{11,3},{12,4},{13,5},{14,6},{15,7}} | collective-permute-start | bytes 245768 | tf_op jit(solution)/shard_map/ppermute | solution.py:667
  42.3 2.9 %shard_map.65 = (bf16[2,4,160,256]{3,2,1,0:T(8,128)(2,1)S(1)}, bf16[2,4,160,256]{3,2,1,0:T(8,128)(2,1)S(1)}) custom-call(bf16[2,2,128,320]{3,2,1,0:T(8,128)(2,1)S(1)} %get-tuple-element.81.saved_ref.refs_0_, bf16[2,3,960,320]{3,2,1,0:T(8,128)(2,1)S(1)} %shard_map.52.weights_ref.after_ref.loaded_ref, bf16[2,160,256]{2,1,0:T(8,128)(2,1)S(1)} %collective-permute-done.7.refs_0_, ...), custom_call_target="tpu_custom_call" | custom-call | tf_op jit(solution)/shard_map/pallas_call | solution.py:177
  45.3 1.9 %collective-permute-start.10 = (bf16[2,4,160,256]{3,2,1,0:T(8,128)(2,1)S(1)}, bf16[2,4,160,256]{3,2,1,0:T(8,128)(2,1)S(1)}, u32[]{:S(2)}, u32[]{:S(2)}) collective-permute-start(bf16[2,4,160,256]{3,2,1,0:T(8,128)(2,1)S(1)} %get-tuple-element.82), channel_id=1, source_target_pairs={{0,4},{4,0},{1,5},{5,1},{2,6},{6,2},{3,7},{7,3}} | collective-permute-start | bytes 1966088 | tf_op jit(solution)/shard_map/ppermute | solution.py:757
  47.2 4.1 %collective-permute-done.12.refs_1_ = bf16[2,160,256]{2,1,0:T(8,128)(2,1)S(1)} collective-permute-done((bf16[2,160,256]{2,1,0:T(8,128)(2,1)S(1)}, bf16[2,160,256]{2,1,0:T(8,128)(2,1)S(1)}, u32[]{:S(2)}, u32[]{:S(2)}) %collective-permute-start.12) | collective-permute-done | bytes 163872 | tf_op jit(solution)/shard_map/ppermute | solution.py:676
  51.4 0.0 collective-permute-done.20.grad_ref.refs_0_
  51.4 0.7 %shard_map.75 = (bf16[2,128,320]{2,1,0:T(8,128)(2,1)S(1)}, bf16[4,2,80,256]{3,2,1,0:T(8,128)(2,1)S(1)}) custom-call(bf16[320,128]{1,0:T(8,128)(2,1)S(1)} %collective-permute-done.20.grad_ref.refs_0_, bf16[2,3,960,320]{3,2,1,0:T(8,128)(2,1)S(1)} %shard_map.58.after_ref.turned_ref, ...), custom_call_target="tpu_custom_call", output_to_operand_aliasing={{0}: (4, {}), {1}: (5, {})} | custom-call | tf_op jit(solution)/shard_map/pallas_call | solution.py:177
  52.1 2.0 %collective-permute-done.19.grad_ref.refs_1_ = bf16[320,128]{1,0:T(8,128)(2,1)S(1)} collective-permute-done((bf16[320,128]{1,0:T(8,128)(2,1)S(1)}, bf16[320,128]{1,0:T(8,128)(2,1)S(1)}, u32[]{:S(2)}, u32[]{:S(2)}) %collective-permute-start.19) | collective-permute-done | bytes 81952 | tf_op jit(solution)/shard_map/ppermute | solution.py:667
  54.1 0.7 shard_map.76
  54.8 2.9 %collective-permute-start.23 = (bf16[2,80,256]{2,1,0:T(8,128)(2,1)S(1)}, bf16[2,80,256]{2,1,0:T(8,128)(2,1)S(1)}, u32[]{:S(2)}, u32[]{:S(2)}) collective-permute-start(bf16[2,80,256]{2,1,0:T(8,128)(2,1)S(1)} %get-tuple-element.110), channel_id=1, source_target_pairs={{0,3},{1,0},{2,1},{3,2},{8,11},{9,8},{10,9},{11,10},{16,19},{17,16... | collective-permute-start | bytes 245768 | tf_op jit(solution)/shard_map/ppermute | solution.py:676
  57.8 1.1 %collective-permute-start.22 = (bf16[2,80,256]{2,1,0:T(8,128)(2,1)S(1)}, bf16[2,80,256]{2,1,0:T(8,128)(2,1)S(1)}, u32[]{:S(2)}, u32[]{:S(2)}) collective-permute-start(bf16[2,80,256]{2,1,0:T(8,128)(2,1)S(1)} %get-tuple-element.111), channel_id=1, source_target_pairs={{0,2},{1,3},{2,0},{3,1},{8,10},{9,11},{10,8},{11,9},{16,18},{17,19... | collective-permute-start | bytes 245768 | tf_op jit(solution)/shard_map/ppermute | solution.py:676
  58.9 0.0 collective-permute-start.21
  58.9 1.0 %collective-permute-done.23.refs_3_ = bf16[2,80,256]{2,1,0:T(8,128)(2,1)S(1)} collective-permute-done((bf16[2,80,256]{2,1,0:T(8,128)(2,1)S(1)}, bf16[2,80,256]{2,1,0:T(8,128)(2,1)S(1)}, u32[]{:S(2)}, u32[]{:S(2)}) %collective-permute-start.23) | collective-permute-done | bytes 81952 | tf_op jit(solution)/shard_map/ppermute | solution.py:676
  59.8 4.0 %collective-permute-done.22.refs_2_ = bf16[2,80,256]{2,1,0:T(8,128)(2,1)S(1)} collective-permute-done((bf16[2,80,256]{2,1,0:T(8,128)(2,1)S(1)}, bf16[2,80,256]{2,1,0:T(8,128)(2,1)S(1)}, u32[]{:S(2)}, u32[]{:S(2)}) %collective-permute-start.22) | collective-permute-done | bytes 81952 | tf_op jit(solution)/shard_map/ppermute | solution.py:676
  63.9 1.2 %collective-permute-done.21.refs_1_ = bf16[2,80,256]{2,1,0:T(8,128)(2,1)S(1)} collective-permute-done((bf16[2,80,256]{2,1,0:T(8,128)(2,1)S(1)}, bf16[2,80,256]{2,1,0:T(8,128)(2,1)S(1)}, u32[]{:S(2)}, u32[]{:S(2)}) %collective-permute-start.21) | collective-permute-done | bytes 81952 | tf_op jit(solution)/shard_map/ppermute | solution.py:676
  65.1 0.1 collective-permute-start.24
  65.2 1.1 %shard_map.78.kept_ref = bf16[2,128,320]{2,1,0:T(8,128)(2,1)S(1)} custom-call(bf16[2,3,960,320]{3,2,1,0:T(8,128)(2,1)S(1)} %shard_map.58.after_ref.turned_ref, bf16[320,128]{1,0:T(8,128)(2,1)S(1)} %collective-permute-done.20.grad_ref.refs_0_, bf16[320,128]{1,0:T(8,128)(2,1)S(1)} %collective-permute-done.19.grad_ref.refs_1_, ...), custom_call_target="tpu_custom_call", output_to_operand_aliasing={{}: (3, {})} | custom-call | tf_op jit(solution)/shard_map/pallas_call | solution.py:177
  66.3 0.1 shard_map.79
  66.4 0.6 collective-permute-start.25
  66.9 1.2 %shard_map.69.refs_0_ = bf16[2,2048,480]{2,1,0:T(8,128)(2,1)S(1)} custom-call(bf16[2,4,160,256]{3,2,1,0:T(8,128)(2,1)S(1)} %get-tuple-element.88.first_ref.after_ref, bf16[2,4,160,256]{3,2,1,0:T(8,128)(2,1)S(1)} %get-tuple-element.89.cells_ref), custom_call_target="tpu_custom_call" | custom-call | tf_op jit(solution)/shard_map/pallas_call | solution.py:177
  68.1 0.0 collective-permute-done.25.other_ref
  68.1 0.7 shard_map.80
  68.8 0.0 collective-permute-done.10.first_ref
  68.8 1.2 %shard_map.70.around_ref = bf16[2,2048,480]{2,1,0:T(8,128)(2,1)S(1)} custom-call(bf16[2,4,160,256]{3,2,1,0:T(8,128)(2,1)S(1)} %collective-permute-done.10.first_ref, bf16[2,4,160,256]{3,2,1,0:T(8,128)(2,1)S(1)} %collective-permute-done.14.cells_ref, bf16[2,2048,480]{2,1,0:T(8,128)(2,1)S(1)} %shard_map.69.refs_0_), custom_call_target="tpu_custom_call", output_to_operand_aliasing={{}: (2, {})} | custom-call | tf_op jit(solution)/shard_map/pallas_call | solution.py:177
  70.0 0.0 collective-permute-done.24.other_ref
  70.0 2.3 %terms.1 = f32[2,9,160,80]{3,2,1,0:T(8,128)} custom-call(bf16[2,2048,480]{2,1,0:T(8,128)(2,1)S(1)} %shard_map.70.around_ref, bf16[4,2,80,256]{3,2,1,0:T(8,128)(2,1)S(1)} %shard_map.77.own_ref, bf16[4,2,80,256]{3,2,1,0:T(8,128)(2,1)S(1)} %collective-permute-done.24.other_ref), custom_call_target="tpu_custom_call" | custom-call | tf_op jit(solution)/shard_map/terms/pallas_call | solution.py:635
  (21 shorter events, 0.3 us)
Async XLA Ops:
  1.6 2.9 %collective-permute-start = (bf16[2,8,8,320]{3,2,1,0:T(8,128)(2,1)S(1)}, bf16[2,8,8,320]{3,2,1,0:T(8,128)(2,1)S(1)}, u32[]{:S(2)}, u32[]{:S(2)}) collective-permute-start(bf16[2,8,8,320]{3,2,1,0:T(8,128)(2,1)S(1)} %get-tuple-element.57), channel_id=1, source_target_pairs={{0,4},{4,0},{1,5},{5,1},{2,6},{6,2},{3,7},{7,3},{8,12},{12,8},{9,1... | collective-permute-start | bytes 245768 | tf_op jit(solution)/shard_map/ppermute | solution.py:648
  5.9 4.7 %collective-permute-start.2 = (bf16[320,128]{1,0:T(8,128)(2,1)S(1)}, bf16[320,128]{1,0:T(8,128)(2,1)S(1)}, u32[]{:S(2)}, u32[]{:S(2)}) collective-permute-start(bf16[320,128]{1,0:T(8,128)(2,1)S(1)} %get-tuple-element.64), channel_id=1, source_target_pairs={{0,8},{1,9},{2,10},{3,11},{4,12},{5,13},{6,14},{7,15}} | collective-permute-start | bytes 245768 | tf_op jit(solution)/shard_map/ppermute | solution.py:667
  9.3 3.3 %collective-permute-start.1 = (bf16[320,128]{1,0:T(8,128)(2,1)S(1)}, bf16[320,128]{1,0:T(8,128)(2,1)S(1)}, u32[]{:S(2)}, u32[]{:S(2)}) collective-permute-start(bf16[320,128]{1,0:T(8,128)(2,1)S(1)} %get-tuple-element.62), channel_id=1, source_target_pairs={{0,8},{1,9},{2,10},{3,11},{4,12},{5,13},{6,14},{7,15}} | collective-permute-start | bytes 245768 | tf_op jit(solution)/shard_map/ppermute | solution.py:667
  10.7 4.1 %collective-permute-start.4 = (bf16[320,128]{1,0:T(8,128)(2,1)S(1)}, bf16[320,128]{1,0:T(8,128)(2,1)S(1)}, u32[]{:S(2)}, u32[]{:S(2)}) collective-permute-start(bf16[320,128]{1,0:T(8,128)(2,1)S(1)} %get-tuple-element.70), channel_id=1, source_target_pairs={{8,16},{9,17},{10,18},{11,19},{12,20},{13,21},{14,22},{15,23}} | collective-permute-start | bytes 245768 | tf_op jit(solution)/shard_map/ppermute | solution.py:667
  12.6 2.9 %collective-permute-start.3 = (bf16[320,128]{1,0:T(8,128)(2,1)S(1)}, bf16[320,128]{1,0:T(8,128)(2,1)S(1)}, u32[]{:S(2)}, u32[]{:S(2)}) collective-permute-start(bf16[320,128]{1,0:T(8,128)(2,1)S(1)} %get-tuple-element.68), channel_id=1, source_target_pairs={{8,16},{9,17},{10,18},{11,19},{12,20},{13,21},{14,22},{15,23}} | collective-permute-start | bytes 245768 | tf_op jit(solution)/shard_map/ppermute | solution.py:667
  14.8 9.7 %collective-permute-start.6 = (bf16[320,128]{1,0:T(8,128)(2,1)S(1)}, bf16[320,128]{1,0:T(8,128)(2,1)S(1)}, u32[]{:S(2)}, u32[]{:S(2)}) collective-permute-start(bf16[320,128]{1,0:T(8,128)(2,1)S(1)} %get-tuple-element.75), channel_id=1, source_target_pairs={{16,24},{17,25},{18,26},{19,27},{20,28},{21,29},{22,30},{23,31}} | collective-permute-start | bytes 245768 | tf_op jit(solution)/shard_map/ppermute | solution.py:667
  15.5 9.7 %collective-permute-start.5 = (bf16[320,128]{1,0:T(8,128)(2,1)S(1)}, bf16[320,128]{1,0:T(8,128)(2,1)S(1)}, u32[]{:S(2)}, u32[]{:S(2)}) collective-permute-start(bf16[320,128]{1,0:T(8,128)(2,1)S(1)} %get-tuple-element.74), channel_id=1, source_target_pairs={{16,24},{17,25},{18,26},{19,27},{20,28},{21,29},{22,30},{23,31}} | collective-permute-start | bytes 245768 | tf_op jit(solution)/shard_map/ppermute | solution.py:667
  16.2 13.7 %collective-permute-start.9 = (bf16[2,160,256]{2,1,0:T(8,128)(2,1)S(1)}, bf16[2,160,256]{2,1,0:T(8,128)(2,1)S(1)}, u32[]{:S(2)}, u32[]{:S(2)}) collective-permute-start(bf16[2,160,256]{2,1,0:T(8,128)(2,1)S(1)} %shard_map.64), channel_id=1, source_target_pairs={{0,3},{1,0},{2,1},{3,2},{4,7},{5,4},{6,5},{7,6}} | collective-permute-start | bytes 491528 | tf_op jit(solution)/shard_map/ppermute | solution.py:676
  22.6 15.0 %collective-permute-start.8 = (bf16[2,160,256]{2,1,0:T(8,128)(2,1)S(1)}, bf16[2,160,256]{2,1,0:T(8,128)(2,1)S(1)}, u32[]{:S(2)}, u32[]{:S(2)}) collective-permute-start(bf16[2,160,256]{2,1,0:T(8,128)(2,1)S(1)} %shard_map.64), channel_id=1, source_target_pairs={{0,2},{1,3},{2,0},{3,1},{4,6},{5,7},{6,4},{7,5}} | collective-permute-start | bytes 491528 | tf_op jit(solution)/shard_map/ppermute | solution.py:676
  24.5 1.6 %collective-permute-start.16 = (bf16[320,128]{1,0:T(8,128)(2,1)S(1)}, bf16[320,128]{1,0:T(8,128)(2,1)S(1)}, u32[]{:S(2)}, u32[]{:S(2)}) collective-permute-start(bf16[320,128]{1,0:T(8,128)(2,1)S(1)} %get-tuple-element.79.after_ref), channel_id=1, source_target_pairs={{24,16},{25,17},{26,18},{27,19},{28,20},{29,21},{30,22},{31,23}} | collective-permute-start | bytes 245768 | tf_op jit(solution)/shard_map/ppermute | solution.py:667
  25.5 12.1 %collective-permute-start.15 = (bf16[320,128]{1,0:T(8,128)(2,1)S(1)}, bf16[320,128]{1,0:T(8,128)(2,1)S(1)}, u32[]{:S(2)}, u32[]{:S(2)}) collective-permute-start(bf16[320,128]{1,0:T(8,128)(2,1)S(1)} %get-tuple-element.86.refs_1_), channel_id=1, source_target_pairs={{24,16},{25,17},{26,18},{27,19},{28,20},{29,21},{30,22},{31,23}} | collective-permute-start | bytes 245768 | tf_op jit(solution)/shard_map/ppermute | solution.py:667
  26.2 12.8 %collective-permute-start.18 = (bf16[320,128]{1,0:T(8,128)(2,1)S(1)}, bf16[320,128]{1,0:T(8,128)(2,1)S(1)}, u32[]{:S(2)}, u32[]{:S(2)}) collective-permute-start(bf16[320,128]{1,0:T(8,128)(2,1)S(1)} %get-tuple-element.95), channel_id=1, source_target_pairs={{16,8},{17,9},{18,10},{19,11},{20,12},{21,13},{22,14},{23,15}} | collective-permute-start | bytes 245768 | tf_op jit(solution)/shard_map/ppermute | solution.py:667
  26.8 14.2 %collective-permute-start.7 = (bf16[2,160,256]{2,1,0:T(8,128)(2,1)S(1)}, bf16[2,160,256]{2,1,0:T(8,128)(2,1)S(1)}, u32[]{:S(2)}, u32[]{:S(2)}) collective-permute-start(bf16[2,160,256]{2,1,0:T(8,128)(2,1)S(1)} %shard_map.64), channel_id=1, source_target_pairs={{0,1},{1,2},{2,3},{3,0},{4,5},{5,6},{6,7},{7,4}} | collective-permute-start | bytes 491528 | tf_op jit(solution)/shard_map/ppermute | solution.py:676
  29.9 15.4 %collective-permute-start.13 = (bf16[2,160,256]{2,1,0:T(8,128)(2,1)S(1)}, bf16[2,160,256]{2,1,0:T(8,128)(2,1)S(1)}, u32[]{:S(2)}, u32[]{:S(2)}) collective-permute-start(bf16[2,160,256]{2,1,0:T(8,128)(2,1)S(1)} %shard_map.67), channel_id=1, source_target_pairs={{0,3},{1,0},{2,1},{3,2},{8,11},{9,8},{10,9},{11,10},{16,19},{17,16... | collective-permute-start | bytes 491528 | tf_op jit(solution)/shard_map/ppermute | solution.py:676
  37.6 13.7 %collective-permute-start.12 = (bf16[2,160,256]{2,1,0:T(8,128)(2,1)S(1)}, bf16[2,160,256]{2,1,0:T(8,128)(2,1)S(1)}, u32[]{:S(2)}, u32[]{:S(2)}) collective-permute-start(bf16[2,160,256]{2,1,0:T(8,128)(2,1)S(1)} %shard_map.67), channel_id=1, source_target_pairs={{0,2},{1,3},{2,0},{3,1},{8,10},{9,11},{10,8},{11,9},{16,18},{17,19... | collective-permute-start | bytes 491528 | tf_op jit(solution)/shard_map/ppermute | solution.py:676
  37.6 13.7 %collective-permute-start.11 = (bf16[2,160,256]{2,1,0:T(8,128)(2,1)S(1)}, bf16[2,160,256]{2,1,0:T(8,128)(2,1)S(1)}, u32[]{:S(2)}, u32[]{:S(2)}) collective-permute-start(bf16[2,160,256]{2,1,0:T(8,128)(2,1)S(1)} %shard_map.67), channel_id=1, source_target_pairs={{0,1},{1,2},{2,3},{3,0},{8,9},{9,10},{10,11},{11,8},{16,17},{17,18... | collective-permute-start | bytes 491528 | tf_op jit(solution)/shard_map/ppermute | solution.py:676
  39.0 0.7 collective-permute-start.17
  39.7 11.7 %collective-permute-start.20 = (bf16[320,128]{1,0:T(8,128)(2,1)S(1)}, bf16[320,128]{1,0:T(8,128)(2,1)S(1)}, u32[]{:S(2)}, u32[]{:S(2)}) collective-permute-start(bf16[320,128]{1,0:T(8,128)(2,1)S(1)} %get-tuple-element.101), channel_id=1, source_target_pairs={{8,0},{9,1},{10,2},{11,3},{12,4},{13,5},{14,6},{15,7}} | collective-permute-start | bytes 245768 | tf_op jit(solution)/shard_map/ppermute | solution.py:667
  41.0 13.1 %collective-permute-start.19 = (bf16[320,128]{1,0:T(8,128)(2,1)S(1)}, bf16[320,128]{1,0:T(8,128)(2,1)S(1)}, u32[]{:S(2)}, u32[]{:S(2)}) collective-permute-start(bf16[320,128]{1,0:T(8,128)(2,1)S(1)} %get-tuple-element.100), channel_id=1, source_target_pairs={{8,0},{9,1},{10,2},{11,3},{12,4},{13,5},{14,6},{15,7}} | collective-permute-start | bytes 245768 | tf_op jit(solution)/shard_map/ppermute | solution.py:667
  45.3 23.5 %collective-permute-start.10 = (bf16[2,4,160,256]{3,2,1,0:T(8,128)(2,1)S(1)}, bf16[2,4,160,256]{3,2,1,0:T(8,128)(2,1)S(1)}, u32[]{:S(2)}, u32[]{:S(2)}) collective-permute-start(bf16[2,4,160,256]{3,2,1,0:T(8,128)(2,1)S(1)} %get-tuple-element.82), channel_id=1, source_target_pairs={{0,4},{4,0},{1,5},{5,1},{2,6},{6,2},{3,7},{7,3}} | collective-permute-start | bytes 1966088 | tf_op jit(solution)/shard_map/ppermute | solution.py:757
  51.4 17.5 %collective-permute-start.14 = (bf16[2,4,160,256]{3,2,1,0:T(8,128)(2,1)S(1)}, bf16[2,4,160,256]{3,2,1,0:T(8,128)(2,1)S(1)}, u32[]{:S(2)}, u32[]{:S(2)}) collective-permute-start(bf16[2,4,160,256]{3,2,1,0:T(8,128)(2,1)S(1)} %get-tuple-element.87), channel_id=1, source_target_pairs={{0,4},{4,0},{1,5},{5,1},{2,6},{6,2},{3,7},{7,3},{8,12},{12,8},{9,1... | collective-permute-start | bytes 1966088 | tf_op jit(solution)/shard_map/ppermute | solution.py:648
  54.8 5.0 %collective-permute-start.23 = (bf16[2,80,256]{2,1,0:T(8,128)(2,1)S(1)}, bf16[2,80,256]{2,1,0:T(8,128)(2,1)S(1)}, u32[]{:S(2)}, u32[]{:S(2)}) collective-permute-start(bf16[2,80,256]{2,1,0:T(8,128)(2,1)S(1)} %get-tuple-element.110), channel_id=1, source_target_pairs={{0,3},{1,0},{2,1},{3,2},{8,11},{9,8},{10,9},{11,10},{16,19},{17,16... | collective-permute-start | bytes 245768 | tf_op jit(solution)/shard_map/ppermute | solution.py:676
  57.8 6.1 %collective-permute-start.22 = (bf16[2,80,256]{2,1,0:T(8,128)(2,1)S(1)}, bf16[2,80,256]{2,1,0:T(8,128)(2,1)S(1)}, u32[]{:S(2)}, u32[]{:S(2)}) collective-permute-start(bf16[2,80,256]{2,1,0:T(8,128)(2,1)S(1)} %get-tuple-element.111), channel_id=1, source_target_pairs={{0,2},{1,3},{2,0},{3,1},{8,10},{9,11},{10,8},{11,9},{16,18},{17,19... | collective-permute-start | bytes 245768 | tf_op jit(solution)/shard_map/ppermute | solution.py:676
  58.9 6.2 %collective-permute-start.21 = (bf16[2,80,256]{2,1,0:T(8,128)(2,1)S(1)}, bf16[2,80,256]{2,1,0:T(8,128)(2,1)S(1)}, u32[]{:S(2)}, u32[]{:S(2)}) collective-permute-start(bf16[2,80,256]{2,1,0:T(8,128)(2,1)S(1)} %get-tuple-element.112), channel_id=1, source_target_pairs={{0,1},{1,2},{2,3},{3,0},{8,9},{9,10},{10,11},{11,8},{16,17},{17,18... | collective-permute-start | bytes 245768 | tf_op jit(solution)/shard_map/ppermute | solution.py:676
  65.1 4.9 %collective-permute-start.24 = (bf16[4,2,80,256]{3,2,1,0:T(8,128)(2,1)S(1)}, bf16[4,2,80,256]{3,2,1,0:T(8,128)(2,1)S(1)}, u32[]{:S(2)}, u32[]{:S(2)}) collective-permute-start(bf16[4,2,80,256]{3,2,1,0:T(8,128)(2,1)S(1)} %shard_map.77.own_ref), channel_id=1, source_target_pairs={{0,4},{4,0},{1,5},{5,1},{2,6},{6,2},{3,7},{7,3},{8,12},{12,8},{9,1... | collective-permute-start | bytes 983048 | tf_op jit(solution)/shard_map/ppermute | solution.py:648
  66.4 1.7 %collective-permute-start.25 = (bf16[2,8,8,320]{3,2,1,0:T(8,128)(2,1)S(1)}, bf16[2,8,8,320]{3,2,1,0:T(8,128)(2,1)S(1)}, u32[]{:S(2)}, u32[]{:S(2)}) collective-permute-start(bf16[2,8,8,320]{3,2,1,0:T(8,128)(2,1)S(1)} %get-tuple-element.109), channel_id=1, source_target_pairs={{0,4},{4,0},{1,5},{5,1},{2,6},{6,2},{3,7},{7,3},{8,12},{12,8},{9,1... | collective-permute-start | bytes 245768 | tf_op jit(solution)/shard_map/ppermute | solution.py:648

commit v11 on v10

--- a/solution.py
+++ b/solution.py
@@ -520,7 +520,7 @@
     return stacked
 
 
-def remake_call(saved, weights, blocks, width, sections):
+def remake_call(saved, weights, blocks, width, sections, earlier=None):
     _, crops, count, channels = saved.shape
     share = channels // 2
     each = len(blocks)
@@ -537,7 +537,14 @@
             home_ref[kind, block, :, cells] = jnp.where(is_left, low, high)
             outer_ref[kind, block, :, cells] = jnp.where(is_left, high, low)
 
-        @pl.when((section >= sections[0]) & (section <= sections[1]))
+        is_active = (section >= sections[0]) & (section <= sections[1])
+        if earlier is not None:
+
+            @pl.when(jnp.logical_not(is_active))
+            def _():
+                outer_ref[...] = refs[each][...]
+
+        @pl.when(is_active)
         def _():
             for crop in range(crops):
                 for kind in range(2):
@@ -559,7 +566,8 @@
         pltpu.VMEM((count + 2 * width, 3 * channels), jnp.bfloat16),
         pltpu.VMEM((count + 16, channels), jnp.float32),
     ]
-    return call(kernel, [out, out], [saved, weights, *blocks], (), scratch, {})
+    operands = [saved, weights, *blocks] + ([] if earlier is None else [earlier])
+    return call(kernel, [out, out], operands, (), scratch, {})
 
 
 def spread_call(first, cells_of, around, place, count, width):
@@ -754,7 +762,6 @@
         if place == 0:
             first, early_outer = remake_call(saved, loaded, soon, width, (0, 0))
             after = first
-            early_outer = lax.ppermute(early_outer, ("section", "slab"), [(i, (i + 1) % slabs) for i in range(slabs)])
         outgoing = []
         for crop in range(crops):
             out, grads = backward(place, crop, incoming)
@@ -766,10 +773,10 @@
     own = [sent[0]]
     for step in steps:
         own.append(shared(sent[step], step, range(sections)))
-    home, outer = remake_call(saved, weights, late, width, (1, last))
+    home, outer = remake_call(saved, weights, late, width, (1, last), early_outer)
     outer = swapped(outer)
     around = spread_call(first, home, None, 0, count, width)
-    around = spread_call(early_outer, outer, around, 1, count, width)
+    around = spread_call(outer, outer, around, 1, count, width)
     own = stack_call(own)
     other = swapped(own)
     terms = terms_call(around, own, other, count, width, scaling)

time: 72.9 us -> 72.9 us (level)
  starting transfers between devices: 33.8 us -> 31.9 us
  waiting for transfers between devices: 18.5 us -> 20.3 us
    ppermute x1 -> x0, starting transfers between devices: 1.92 us -> none  [crop_shards(): lax.ppermute(early_outer, ('section', 'slab'), [(i, (i + 1) % slabs) for...]
    ppermute x9, waiting for transfers between devices: 15.2 us -> 17.1 us  [shared(): return lax.ppermute(values, ('section', 'img'), pairs)]
  transfers between devices with their start and end apart: 26 -> 25, of which waited for: 7 -> 7; matrix products, arithmetic and copies ran while one was open for 0% -> 0% of each run, Pallas kernels for 20% -> 20%
where the time goes in v11:
time: 72.9 us; the launch traced here: 72.5 us
  starting transfers between devices  31.9 us (44%)
  waiting for transfers between devices  20.3 us (28%)
  Pallas kernels  19 us (26%)
  between operations  1.25 us (2%)
    ppermute x9, starting transfers between devices, shared(): return lax.ppermute(values, ('section', 'img'), pairs)  19.5 us
    ppermute x9, waiting for transfers between devices, shared(): return lax.ppermute(values, ('section', 'img'), pairs)  17.1 us
    pallas_call x31, Pallas kernels, call(): pl.pallas_call(kernel, out_shape=outs, in_specs=[pl.BlockSpec(memory_spac...  16.7 us
    ppermute x12, starting transfers between devices, hop(): arrived.append(lax.ppermute(value, 'section', [(source, target)]))  11.2 us
    ppermute x12, waiting for transfers between devices, hop(): arrived.append(lax.ppermute(value, 'section', [(source, target)]))  3.17 us
    pallas_call x1, Pallas kernels, terms_call(): pl.pallas_call(kernel, out_shape=jax.ShapeDtypeStruct(shape, jnp.float32)...  2.31 us
  transfers between devices with their start and end apart: 25, of which 7 were waited for; matrix products, arithmetic and copies ran while one was open for 0% of the time, Pallas kernels for 20%

profile of v11, /device:TPU:0, one launch (start us, length us, event | category | flops | bytes accessed | tf_op | source)
XLA Modules:
  0.0 72.5 jit_solution(12915642503781191231)
XLA Ops:
  0.6 1.0 %shard_map.50 = (bf16[2,8,8,320]{3,2,1,0:T(8,128)(2,1)S(1)}, bf16[2,8,8,320]{3,2,1,0:T(8,128)(2,1)S(1)}) custom-call(bf16[1,4,8,8,320]{4,3,2,1,0:T(8,128)(2,1)} %strips_ref.1, bf16[1,4,8,8,320]{4,3,2,1,0:T(8,128)(2,1)} %cotangent_ref.1), custom_call_target="tpu_custom_call" | custom-call | tf_op jit(solution)/shard_map/pallas_call | solution.py:177
  1.6 0.6 collective-permute-start
  2.2 2.3 %shard_map.52.weights_ref.after_ref.loaded_ref = bf16[2,3,960,320]{3,2,1,0:T(8,128)(2,1)S(1)} custom-call(bf16[2,3,960,320]{3,2,1,0:T(8,128)(2,1)} %bitcast.11, bf16[2,8,8,320]{3,2,1,0:T(8,128)(2,1)S(1)} %get-tuple-element.56.own_ref.after_ref), custom_call_target="tpu_custom_call" | custom-call | tf_op jit(solution)/shard_map/pallas_call | solution.py:177
  4.5 0.0 collective-permute-done.other_ref
  4.5 0.1 shard_map.51
  4.6 1.4 %shard_map.53 = (bf16[320,128]{1,0:T(8,128)(2,1)S(1)}, bf16[2,2,128,320]{3,2,1,0:T(8,128)(2,1)S(1)}, f32[2,128,320]{2,1,0:T(8,128)S(1)}) custom-call(bf16[128,320]{1,0:T(8,128)(2,1)S(1)} %get-tuple-element.59.field_ref.grad_ref, bf16[2,3,960,320]{3,2,1,0:T(8,128)(2,1)S(1)} %shard_map.52.weights_ref.after_ref.loaded_ref, ...), custom_call_target="tpu_custom_call" | custom-call | tf_op jit(solution)/shard_map/pallas_call | solution.py:177
  5.9 2.0 %collective-permute-start.2 = (bf16[320,128]{1,0:T(8,128)(2,1)S(1)}, bf16[320,128]{1,0:T(8,128)(2,1)S(1)}, u32[]{:S(2)}, u32[]{:S(2)}) collective-permute-start(bf16[320,128]{1,0:T(8,128)(2,1)S(1)} %get-tuple-element.64), channel_id=1, source_target_pairs={{0,8},{1,9},{2,10},{3,11},{4,12},{5,13},{6,14},{7,15}} | collective-permute-start | bytes 245768 | tf_op jit(solution)/shard_map/ppermute | solution.py:675
  7.9 1.4 %shard_map.54 = (bf16[320,128]{1,0:T(8,128)(2,1)S(1)}, bf16[2,2,128,320]{3,2,1,0:T(8,128)(2,1)S(1)}, f32[2,128,320]{2,1,0:T(8,128)S(1)}) custom-call(bf16[128,320]{1,0:T(8,128)(2,1)S(1)} %get-tuple-element.58.field_ref.grad_ref, ...), custom_call_target="tpu_custom_call", output_to_operand_aliasing={{1}: (3, {}), {2}: (4, {})} | custom-call | tf_op jit(solution)/shard_map/pallas_call | solution.py:177
  9.3 1.3 %collective-permute-start.1 = (bf16[320,128]{1,0:T(8,128)(2,1)S(1)}, bf16[320,128]{1,0:T(8,128)(2,1)S(1)}, u32[]{:S(2)}, u32[]{:S(2)}) collective-permute-start(bf16[320,128]{1,0:T(8,128)(2,1)S(1)} %get-tuple-element.62), channel_id=1, source_target_pairs={{0,8},{1,9},{2,10},{3,11},{4,12},{5,13},{6,14},{7,15}} | collective-permute-start | bytes 245768 | tf_op jit(solution)/shard_map/ppermute | solution.py:675
  10.6 0.0 collective-permute-done.2.field_ref
  10.7 0.7 collective-permute-start.4
  11.4 1.3 %collective-permute-done.1.field_ref = bf16[320,128]{1,0:T(8,128)(2,1)S(1)} collective-permute-done((bf16[320,128]{1,0:T(8,128)(2,1)S(1)}, bf16[320,128]{1,0:T(8,128)(2,1)S(1)}, u32[]{:S(2)}, u32[]{:S(2)}) %collective-permute-start.1) | collective-permute-done | bytes 81952 | tf_op jit(solution)/shard_map/ppermute | solution.py:675
  12.6 0.7 collective-permute-start.3
  13.3 1.4 %shard_map.58.after_ref.turned_ref = bf16[2,3,960,320]{3,2,1,0:T(8,128)(2,1)S(1)} custom-call(bf16[2,3,960,320]{3,2,1,0:T(8,128)(2,1)S(1)} %shard_map.52.weights_ref.after_ref.loaded_ref, bf16[2,3,960,320]{3,2,1,0:T(8,128)(2,1)S(1)} %shard_map.55.weights_ref, bf16[2,2,128,320]{3,2,1,0:T(8,128)(2,1)S(1)} %get-tuple-element.69.after_ref.refs_0_), custom_call_target="tpu_custom_call" | custom-call | tf_op jit(solution)/shard_map/pallas_call | solution.py:177
  14.7 0.1 shard_map.66
  14.8 0.0 collective-permute-done.4.field_ref
  14.8 0.7 collective-permute-start.6
  15.5 0.0 collective-permute-done.3.field_ref
  15.5 0.7 collective-permute-start.5
  16.2 6.3 %collective-permute-start.12 = (bf16[2,160,256]{2,1,0:T(8,128)(2,1)S(1)}, bf16[2,160,256]{2,1,0:T(8,128)(2,1)S(1)}, u32[]{:S(2)}, u32[]{:S(2)}) collective-permute-start(bf16[2,160,256]{2,1,0:T(8,128)(2,1)S(1)} %shard_map.66), channel_id=1, source_target_pairs={{0,3},{1,0},{2,1},{3,2},{4,7},{5,4},{6,5},{7,6}} | collective-permute-start | bytes 491528 | tf_op jit(solution)/shard_map/ppermute | solution.py:684
  22.6 1.9 %collective-permute-start.11 = (bf16[2,160,256]{2,1,0:T(8,128)(2,1)S(1)}, bf16[2,160,256]{2,1,0:T(8,128)(2,1)S(1)}, u32[]{:S(2)}, u32[]{:S(2)}) collective-permute-start(bf16[2,160,256]{2,1,0:T(8,128)(2,1)S(1)} %shard_map.66), channel_id=1, source_target_pairs={{0,2},{1,3},{2,0},{3,1},{4,6},{5,7},{6,4},{7,5}} | collective-permute-start | bytes 491528 | tf_op jit(solution)/shard_map/ppermute | solution.py:684
  24.5 0.0 collective-permute-done.6.field_ref
  24.5 0.7 collective-permute-start.15
  25.2 0.0 collective-permute-done.5.field_ref
  25.3 0.2 shard_map.64
  25.5 0.7 collective-permute-start.14
  26.1 0.0 collective-permute-done.15.grad_ref
  26.2 0.7 collective-permute-start.17
  26.8 2.9 %collective-permute-start.10 = (bf16[2,160,256]{2,1,0:T(8,128)(2,1)S(1)}, bf16[2,160,256]{2,1,0:T(8,128)(2,1)S(1)}, u32[]{:S(2)}, u32[]{:S(2)}) collective-permute-start(bf16[2,160,256]{2,1,0:T(8,128)(2,1)S(1)} %shard_map.66), channel_id=1, source_target_pairs={{0,1},{1,2},{2,3},{3,0},{4,5},{5,6},{6,7},{7,4}} | collective-permute-start | bytes 491528 | tf_op jit(solution)/shard_map/ppermute | solution.py:684
  29.7 0.1 shard_map.65
  29.9 2.9 %collective-permute-start.9 = (bf16[2,160,256]{2,1,0:T(8,128)(2,1)S(1)}, bf16[2,160,256]{2,1,0:T(8,128)(2,1)S(1)}, u32[]{:S(2)}, u32[]{:S(2)}) collective-permute-start(bf16[2,160,256]{2,1,0:T(8,128)(2,1)S(1)} %shard_map.65), channel_id=1, source_target_pairs={{0,3},{1,0},{2,1},{3,2},{8,11},{9,8},{10,9},{11,10},{16,19},{17,16... | collective-permute-start | bytes 491528 | tf_op jit(solution)/shard_map/ppermute | solution.py:684
  32.8 4.8 %collective-permute-done.11.refs_1_ = bf16[2,160,256]{2,1,0:T(8,128)(2,1)S(1)} collective-permute-done((bf16[2,160,256]{2,1,0:T(8,128)(2,1)S(1)}, bf16[2,160,256]{2,1,0:T(8,128)(2,1)S(1)}, u32[]{:S(2)}, u32[]{:S(2)}) %collective-permute-start.11) | collective-permute-done | bytes 163872 | tf_op jit(solution)/shard_map/ppermute | solution.py:684
  37.6 0.0 collective-permute-start.8
  37.6 0.0 collective-permute-done.14.grad_ref
  37.6 1.4 %collective-permute-start.7 = (bf16[2,160,256]{2,1,0:T(8,128)(2,1)S(1)}, bf16[2,160,256]{2,1,0:T(8,128)(2,1)S(1)}, u32[]{:S(2)}, u32[]{:S(2)}) collective-permute-start(bf16[2,160,256]{2,1,0:T(8,128)(2,1)S(1)} %shard_map.65), channel_id=1, source_target_pairs={{0,1},{1,2},{2,3},{3,0},{8,9},{9,10},{10,11},{11,8},{16,17},{17,18... | collective-permute-start | bytes 491528 | tf_op jit(solution)/shard_map/ppermute | solution.py:684
  39.0 0.7 collective-permute-start.16
  39.7 0.0 collective-permute-done.16.grad_ref
  39.7 1.3 %collective-permute-start.19 = (bf16[320,128]{1,0:T(8,128)(2,1)S(1)}, bf16[320,128]{1,0:T(8,128)(2,1)S(1)}, u32[]{:S(2)}, u32[]{:S(2)}) collective-permute-start(bf16[320,128]{1,0:T(8,128)(2,1)S(1)} %get-tuple-element.101), channel_id=1, source_target_pairs={{8,0},{9,1},{10,2},{11,3},{12,4},{13,5},{14,6},{15,7}} | collective-permute-start | bytes 245768 | tf_op jit(solution)/shard_map/ppermute | solution.py:675
  41.0 0.0 collective-permute-done.10.refs_0_
  41.0 1.3 %collective-permute-start.18 = (bf16[320,128]{1,0:T(8,128)(2,1)S(1)}, bf16[320,128]{1,0:T(8,128)(2,1)S(1)}, u32[]{:S(2)}, u32[]{:S(2)}) collective-permute-start(bf16[320,128]{1,0:T(8,128)(2,1)S(1)} %get-tuple-element.100), channel_id=1, source_target_pairs={{8,0},{9,1},{10,2},{11,3},{12,4},{13,5},{14,6},{15,7}} | collective-permute-start | bytes 245768 | tf_op jit(solution)/shard_map/ppermute | solution.py:675
  42.3 2.9 %shard_map.67 = (bf16[2,4,160,256]{3,2,1,0:T(8,128)(2,1)S(1)}, bf16[2,4,160,256]{3,2,1,0:T(8,128)(2,1)S(1)}) custom-call(bf16[2,2,128,320]{3,2,1,0:T(8,128)(2,1)S(1)} %get-tuple-element.81.refs_0_.saved_ref, bf16[2,3,960,320]{3,2,1,0:T(8,128)(2,1)S(1)} %shard_map.52.weights_ref.after_ref.loaded_ref, ...), custom_call_target="tpu_custom_call" | custom-call | tf_op jit(solution)/shard_map/pallas_call | solution.py:177
  45.3 0.0 collective-permute-done.9.refs_2_
  45.3 6.0 %collective-permute-done.8.refs_1_ = bf16[2,160,256]{2,1,0:T(8,128)(2,1)S(1)} collective-permute-done((bf16[2,160,256]{2,1,0:T(8,128)(2,1)S(1)}, bf16[2,160,256]{2,1,0:T(8,128)(2,1)S(1)}, u32[]{:S(2)}, u32[]{:S(2)}) %collective-permute-start.8) | collective-permute-done | bytes 163872 | tf_op jit(solution)/shard_map/ppermute | solution.py:684
  51.4 0.1 collective-permute-start.13
  51.5 0.0 collective-permute-done.19.grad_ref.refs_0_
  51.5 0.7 %shard_map.75 = (bf16[2,128,320]{2,1,0:T(8,128)(2,1)S(1)}, bf16[4,2,80,256]{3,2,1,0:T(8,128)(2,1)S(1)}) custom-call(bf16[320,128]{1,0:T(8,128)(2,1)S(1)} %collective-permute-done.19.grad_ref.refs_0_, bf16[2,3,960,320]{3,2,1,0:T(8,128)(2,1)S(1)} %shard_map.58.after_ref.turned_ref, ...), custom_call_target="tpu_custom_call", output_to_operand_aliasing={{0}: (4, {}), {1}: (5, {})} | custom-call | tf_op jit(solution)/shard_map/pallas_call | solution.py:177
  52.2 1.9 %collective-permute-done.18.grad_ref.refs_1_ = bf16[320,128]{1,0:T(8,128)(2,1)S(1)} collective-permute-done((bf16[320,128]{1,0:T(8,128)(2,1)S(1)}, bf16[320,128]{1,0:T(8,128)(2,1)S(1)}, u32[]{:S(2)}, u32[]{:S(2)}) %collective-permute-start.18) | collective-permute-done | bytes 81952 | tf_op jit(solution)/shard_map/ppermute | solution.py:675
  54.1 0.7 shard_map.76
  54.8 2.9 %collective-permute-start.22 = (bf16[2,80,256]{2,1,0:T(8,128)(2,1)S(1)}, bf16[2,80,256]{2,1,0:T(8,128)(2,1)S(1)}, u32[]{:S(2)}, u32[]{:S(2)}) collective-permute-start(bf16[2,80,256]{2,1,0:T(8,128)(2,1)S(1)} %get-tuple-element.110), channel_id=1, source_target_pairs={{0,3},{1,0},{2,1},{3,2},{8,11},{9,8},{10,9},{11,10},{16,19},{17,16... | collective-permute-start | bytes 245768 | tf_op jit(solution)/shard_map/ppermute | solution.py:684
  57.8 1.1 %collective-permute-start.21 = (bf16[2,80,256]{2,1,0:T(8,128)(2,1)S(1)}, bf16[2,80,256]{2,1,0:T(8,128)(2,1)S(1)}, u32[]{:S(2)}, u32[]{:S(2)}) collective-permute-start(bf16[2,80,256]{2,1,0:T(8,128)(2,1)S(1)} %get-tuple-element.111), channel_id=1, source_target_pairs={{0,2},{1,3},{2,0},{3,1},{8,10},{9,11},{10,8},{11,9},{16,18},{17,19... | collective-permute-start | bytes 245768 | tf_op jit(solution)/shard_map/ppermute | solution.py:684
  58.9 0.0 collective-permute-start.20
  58.9 1.0 %collective-permute-done.22.refs_3_ = bf16[2,80,256]{2,1,0:T(8,128)(2,1)S(1)} collective-permute-done((bf16[2,80,256]{2,1,0:T(8,128)(2,1)S(1)}, bf16[2,80,256]{2,1,0:T(8,128)(2,1)S(1)}, u32[]{:S(2)}, u32[]{:S(2)}) %collective-permute-start.22) | collective-permute-done | bytes 81952 | tf_op jit(solution)/shard_map/ppermute | solution.py:684
  59.8 4.1 %collective-permute-done.21.refs_2_ = bf16[2,80,256]{2,1,0:T(8,128)(2,1)S(1)} collective-permute-done((bf16[2,80,256]{2,1,0:T(8,128)(2,1)S(1)}, bf16[2,80,256]{2,1,0:T(8,128)(2,1)S(1)}, u32[]{:S(2)}, u32[]{:S(2)}) %collective-permute-start.21) | collective-permute-done | bytes 81952 | tf_op jit(solution)/shard_map/ppermute | solution.py:684
  63.9 1.2 %collective-permute-done.20.refs_1_ = bf16[2,80,256]{2,1,0:T(8,128)(2,1)S(1)} collective-permute-done((bf16[2,80,256]{2,1,0:T(8,128)(2,1)S(1)}, bf16[2,80,256]{2,1,0:T(8,128)(2,1)S(1)}, u32[]{:S(2)}, u32[]{:S(2)}) %collective-permute-start.20) | collective-permute-done | bytes 81952 | tf_op jit(solution)/shard_map/ppermute | solution.py:684
  65.1 0.1 collective-permute-start.23
  65.2 1.1 %shard_map.78.kept_ref = bf16[2,128,320]{2,1,0:T(8,128)(2,1)S(1)} custom-call(bf16[2,3,960,320]{3,2,1,0:T(8,128)(2,1)S(1)} %shard_map.58.after_ref.turned_ref, bf16[320,128]{1,0:T(8,128)(2,1)S(1)} %collective-permute-done.19.grad_ref.refs_0_, bf16[320,128]{1,0:T(8,128)(2,1)S(1)} %collective-permute-done.18.grad_ref.refs_1_, ...), custom_call_target="tpu_custom_call", output_to_operand_aliasing={{}: (3, {})} | custom-call | tf_op jit(solution)/shard_map/pallas_call | solution.py:177
  66.3 0.1 shard_map.79
  66.4 0.6 collective-permute-start.24
  66.9 1.2 %shard_map.69.refs_0_ = bf16[2,2048,480]{2,1,0:T(8,128)(2,1)S(1)} custom-call(bf16[2,4,160,256]{3,2,1,0:T(8,128)(2,1)S(1)} %get-tuple-element.88.first_ref.after_ref, bf16[2,4,160,256]{3,2,1,0:T(8,128)(2,1)S(1)} %get-tuple-element.89.cells_ref), custom_call_target="tpu_custom_call" | custom-call | tf_op jit(solution)/shard_map/pallas_call | solution.py:177
  68.1 0.0 collective-permute-done.24.other_ref
  68.1 0.7 shard_map.80
  68.8 1.2 %shard_map.70.around_ref = bf16[2,2048,480]{2,1,0:T(8,128)(2,1)S(1)} custom-call(bf16[2,4,160,256]{3,2,1,0:T(8,128)(2,1)S(1)} %collective-permute-done.13.first_ref.cells_ref, bf16[2,4,160,256]{3,2,1,0:T(8,128)(2,1)S(1)} %collective-permute-done.13.first_ref.cells_ref, bf16[2,2048,480]{2,1,0:T(8,128)(2,1)S(1)} %shard_map.69.refs_0_), custom_call_target="tpu_custom_call", output_to_operand_aliasing={{}: (2, {})} | custom-call | tf_op jit(solution)/shard_map/pallas_call | solution.py:177
  70.0 0.0 collective-permute-done.23.other_ref
  70.0 2.3 %terms.1 = f32[2,9,160,80]{3,2,1,0:T(8,128)} custom-call(bf16[2,2048,480]{2,1,0:T(8,128)(2,1)S(1)} %shard_map.70.around_ref, bf16[4,2,80,256]{3,2,1,0:T(8,128)(2,1)S(1)} %shard_map.77.own_ref, bf16[4,2,80,256]{3,2,1,0:T(8,128)(2,1)S(1)} %collective-permute-done.23.other_ref), custom_call_target="tpu_custom_call" | custom-call | tf_op jit(solution)/shard_map/terms/pallas_call | solution.py:643
  (19 shorter events, 0.3 us)
Async XLA Ops:
  1.6 2.9 %collective-permute-start = (bf16[2,8,8,320]{3,2,1,0:T(8,128)(2,1)S(1)}, bf16[2,8,8,320]{3,2,1,0:T(8,128)(2,1)S(1)}, u32[]{:S(2)}, u32[]{:S(2)}) collective-permute-start(bf16[2,8,8,320]{3,2,1,0:T(8,128)(2,1)S(1)} %get-tuple-element.57), channel_id=1, source_target_pairs={{0,4},{4,0},{1,5},{5,1},{2,6},{6,2},{3,7},{7,3},{8,12},{12,8},{9,1... | collective-permute-start | bytes 245768 | tf_op jit(solution)/shard_map/ppermute | solution.py:656
  5.9 4.7 %collective-permute-start.2 = (bf16[320,128]{1,0:T(8,128)(2,1)S(1)}, bf16[320,128]{1,0:T(8,128)(2,1)S(1)}, u32[]{:S(2)}, u32[]{:S(2)}) collective-permute-start(bf16[320,128]{1,0:T(8,128)(2,1)S(1)} %get-tuple-element.64), channel_id=1, source_target_pairs={{0,8},{1,9},{2,10},{3,11},{4,12},{5,13},{6,14},{7,15}} | collective-permute-start | bytes 245768 | tf_op jit(solution)/shard_map/ppermute | solution.py:675
  9.3 3.3 %collective-permute-start.1 = (bf16[320,128]{1,0:T(8,128)(2,1)S(1)}, bf16[320,128]{1,0:T(8,128)(2,1)S(1)}, u32[]{:S(2)}, u32[]{:S(2)}) collective-permute-start(bf16[320,128]{1,0:T(8,128)(2,1)S(1)} %get-tuple-element.62), channel_id=1, source_target_pairs={{0,8},{1,9},{2,10},{3,11},{4,12},{5,13},{6,14},{7,15}} | collective-permute-start | bytes 245768 | tf_op jit(solution)/shard_map/ppermute | solution.py:675
  10.7 4.1 %collective-permute-start.4 = (bf16[320,128]{1,0:T(8,128)(2,1)S(1)}, bf16[320,128]{1,0:T(8,128)(2,1)S(1)}, u32[]{:S(2)}, u32[]{:S(2)}) collective-permute-start(bf16[320,128]{1,0:T(8,128)(2,1)S(1)} %get-tuple-element.70), channel_id=1, source_target_pairs={{8,16},{9,17},{10,18},{11,19},{12,20},{13,21},{14,22},{15,23}} | collective-permute-start | bytes 245768 | tf_op jit(solution)/shard_map/ppermute | solution.py:675
  12.6 2.9 %collective-permute-start.3 = (bf16[320,128]{1,0:T(8,128)(2,1)S(1)}, bf16[320,128]{1,0:T(8,128)(2,1)S(1)}, u32[]{:S(2)}, u32[]{:S(2)}) collective-permute-start(bf16[320,128]{1,0:T(8,128)(2,1)S(1)} %get-tuple-element.68), channel_id=1, source_target_pairs={{8,16},{9,17},{10,18},{11,19},{12,20},{13,21},{14,22},{15,23}} | collective-permute-start | bytes 245768 | tf_op jit(solution)/shard_map/ppermute | solution.py:675
  14.8 9.7 %collective-permute-start.6 = (bf16[320,128]{1,0:T(8,128)(2,1)S(1)}, bf16[320,128]{1,0:T(8,128)(2,1)S(1)}, u32[]{:S(2)}, u32[]{:S(2)}) collective-permute-start(bf16[320,128]{1,0:T(8,128)(2,1)S(1)} %get-tuple-element.75), channel_id=1, source_target_pairs={{16,24},{17,25},{18,26},{19,27},{20,28},{21,29},{22,30},{23,31}} | collective-permute-start | bytes 245768 | tf_op jit(solution)/shard_map/ppermute | solution.py:675
  15.5 9.7 %collective-permute-start.5 = (bf16[320,128]{1,0:T(8,128)(2,1)S(1)}, bf16[320,128]{1,0:T(8,128)(2,1)S(1)}, u32[]{:S(2)}, u32[]{:S(2)}) collective-permute-start(bf16[320,128]{1,0:T(8,128)(2,1)S(1)} %get-tuple-element.74), channel_id=1, source_target_pairs={{16,24},{17,25},{18,26},{19,27},{20,28},{21,29},{22,30},{23,31}} | collective-permute-start | bytes 245768 | tf_op jit(solution)/shard_map/ppermute | solution.py:675
  16.2 13.7 %collective-permute-start.12 = (bf16[2,160,256]{2,1,0:T(8,128)(2,1)S(1)}, bf16[2,160,256]{2,1,0:T(8,128)(2,1)S(1)}, u32[]{:S(2)}, u32[]{:S(2)}) collective-permute-start(bf16[2,160,256]{2,1,0:T(8,128)(2,1)S(1)} %shard_map.66), channel_id=1, source_target_pairs={{0,3},{1,0},{2,1},{3,2},{4,7},{5,4},{6,5},{7,6}} | collective-permute-start | bytes 491528 | tf_op jit(solution)/shard_map/ppermute | solution.py:684
  22.6 15.0 %collective-permute-start.11 = (bf16[2,160,256]{2,1,0:T(8,128)(2,1)S(1)}, bf16[2,160,256]{2,1,0:T(8,128)(2,1)S(1)}, u32[]{:S(2)}, u32[]{:S(2)}) collective-permute-start(bf16[2,160,256]{2,1,0:T(8,128)(2,1)S(1)} %shard_map.66), channel_id=1, source_target_pairs={{0,2},{1,3},{2,0},{3,1},{4,6},{5,7},{6,4},{7,5}} | collective-permute-start | bytes 491528 | tf_op jit(solution)/shard_map/ppermute | solution.py:684
  24.5 1.6 %collective-permute-start.15 = (bf16[320,128]{1,0:T(8,128)(2,1)S(1)}, bf16[320,128]{1,0:T(8,128)(2,1)S(1)}, u32[]{:S(2)}, u32[]{:S(2)}) collective-permute-start(bf16[320,128]{1,0:T(8,128)(2,1)S(1)} %get-tuple-element.79.after_ref), channel_id=1, source_target_pairs={{24,16},{25,17},{26,18},{27,19},{28,20},{29,21},{30,22},{31,23}} | collective-permute-start | bytes 245768 | tf_op jit(solution)/shard_map/ppermute | solution.py:675
  25.5 12.1 %collective-permute-start.14 = (bf16[320,128]{1,0:T(8,128)(2,1)S(1)}, bf16[320,128]{1,0:T(8,128)(2,1)S(1)}, u32[]{:S(2)}, u32[]{:S(2)}) collective-permute-start(bf16[320,128]{1,0:T(8,128)(2,1)S(1)} %get-tuple-element.85.refs_1_), channel_id=1, source_target_pairs={{24,16},{25,17},{26,18},{27,19},{28,20},{29,21},{30,22},{31,23}} | collective-permute-start | bytes 245768 | tf_op jit(solution)/shard_map/ppermute | solution.py:675
  26.2 12.8 %collective-permute-start.17 = (bf16[320,128]{1,0:T(8,128)(2,1)S(1)}, bf16[320,128]{1,0:T(8,128)(2,1)S(1)}, u32[]{:S(2)}, u32[]{:S(2)}) collective-permute-start(bf16[320,128]{1,0:T(8,128)(2,1)S(1)} %get-tuple-element.95), channel_id=1, source_target_pairs={{16,8},{17,9},{18,10},{19,11},{20,12},{21,13},{22,14},{23,15}} | collective-permute-start | bytes 245768 | tf_op jit(solution)/shard_map/ppermute | solution.py:675
  26.8 14.2 %collective-permute-start.10 = (bf16[2,160,256]{2,1,0:T(8,128)(2,1)S(1)}, bf16[2,160,256]{2,1,0:T(8,128)(2,1)S(1)}, u32[]{:S(2)}, u32[]{:S(2)}) collective-permute-start(bf16[2,160,256]{2,1,0:T(8,128)(2,1)S(1)} %shard_map.66), channel_id=1, source_target_pairs={{0,1},{1,2},{2,3},{3,0},{4,5},{5,6},{6,7},{7,4}} | collective-permute-start | bytes 491528 | tf_op jit(solution)/shard_map/ppermute | solution.py:684
  29.9 15.4 %collective-permute-start.9 = (bf16[2,160,256]{2,1,0:T(8,128)(2,1)S(1)}, bf16[2,160,256]{2,1,0:T(8,128)(2,1)S(1)}, u32[]{:S(2)}, u32[]{:S(2)}) collective-permute-start(bf16[2,160,256]{2,1,0:T(8,128)(2,1)S(1)} %shard_map.65), channel_id=1, source_target_pairs={{0,3},{1,0},{2,1},{3,2},{8,11},{9,8},{10,9},{11,10},{16,19},{17,16... | collective-permute-start | bytes 491528 | tf_op jit(solution)/shard_map/ppermute | solution.py:684
  37.6 13.7 %collective-permute-start.8 = (bf16[2,160,256]{2,1,0:T(8,128)(2,1)S(1)}, bf16[2,160,256]{2,1,0:T(8,128)(2,1)S(1)}, u32[]{:S(2)}, u32[]{:S(2)}) collective-permute-start(bf16[2,160,256]{2,1,0:T(8,128)(2,1)S(1)} %shard_map.65), channel_id=1, source_target_pairs={{0,2},{1,3},{2,0},{3,1},{8,10},{9,11},{10,8},{11,9},{16,18},{17,19... | collective-permute-start | bytes 491528 | tf_op jit(solution)/shard_map/ppermute | solution.py:684
  37.6 13.7 %collective-permute-start.7 = (bf16[2,160,256]{2,1,0:T(8,128)(2,1)S(1)}, bf16[2,160,256]{2,1,0:T(8,128)(2,1)S(1)}, u32[]{:S(2)}, u32[]{:S(2)}) collective-permute-start(bf16[2,160,256]{2,1,0:T(8,128)(2,1)S(1)} %shard_map.65), channel_id=1, source_target_pairs={{0,1},{1,2},{2,3},{3,0},{8,9},{9,10},{10,11},{11,8},{16,17},{17,18... | collective-permute-start | bytes 491528 | tf_op jit(solution)/shard_map/ppermute | solution.py:684
  39.0 0.7 collective-permute-start.16
  39.7 11.8 %collective-permute-start.19 = (bf16[320,128]{1,0:T(8,128)(2,1)S(1)}, bf16[320,128]{1,0:T(8,128)(2,1)S(1)}, u32[]{:S(2)}, u32[]{:S(2)}) collective-permute-start(bf16[320,128]{1,0:T(8,128)(2,1)S(1)} %get-tuple-element.101), channel_id=1, source_target_pairs={{8,0},{9,1},{10,2},{11,3},{12,4},{13,5},{14,6},{15,7}} | collective-permute-start | bytes 245768 | tf_op jit(solution)/shard_map/ppermute | solution.py:675
  41.0 13.1 %collective-permute-start.18 = (bf16[320,128]{1,0:T(8,128)(2,1)S(1)}, bf16[320,128]{1,0:T(8,128)(2,1)S(1)}, u32[]{:S(2)}, u32[]{:S(2)}) collective-permute-start(bf16[320,128]{1,0:T(8,128)(2,1)S(1)} %get-tuple-element.100), channel_id=1, source_target_pairs={{8,0},{9,1},{10,2},{11,3},{12,4},{13,5},{14,6},{15,7}} | collective-permute-start | bytes 245768 | tf_op jit(solution)/shard_map/ppermute | solution.py:675
  51.4 17.4 %collective-permute-start.13 = (bf16[2,4,160,256]{3,2,1,0:T(8,128)(2,1)S(1)}, bf16[2,4,160,256]{3,2,1,0:T(8,128)(2,1)S(1)}, u32[]{:S(2)}, u32[]{:S(2)}) collective-permute-start(bf16[2,4,160,256]{3,2,1,0:T(8,128)(2,1)S(1)} %get-tuple-element.87), channel_id=1, source_target_pairs={{0,4},{4,0},{1,5},{5,1},{2,6},{6,2},{3,7},{7,3},{8,12},{12,8},{9,1... | collective-permute-start | bytes 1966088 | tf_op jit(solution)/shard_map/ppermute | solution.py:656
  54.8 5.0 %collective-permute-start.22 = (bf16[2,80,256]{2,1,0:T(8,128)(2,1)S(1)}, bf16[2,80,256]{2,1,0:T(8,128)(2,1)S(1)}, u32[]{:S(2)}, u32[]{:S(2)}) collective-permute-start(bf16[2,80,256]{2,1,0:T(8,128)(2,1)S(1)} %get-tuple-element.110), channel_id=1, source_target_pairs={{0,3},{1,0},{2,1},{3,2},{8,11},{9,8},{10,9},{11,10},{16,19},{17,16... | collective-permute-start | bytes 245768 | tf_op jit(solution)/shard_map/ppermute | solution.py:684
  57.8 6.1 %collective-permute-start.21 = (bf16[2,80,256]{2,1,0:T(8,128)(2,1)S(1)}, bf16[2,80,256]{2,1,0:T(8,128)(2,1)S(1)}, u32[]{:S(2)}, u32[]{:S(2)}) collective-permute-start(bf16[2,80,256]{2,1,0:T(8,128)(2,1)S(1)} %get-tuple-element.111), channel_id=1, source_target_pairs={{0,2},{1,3},{2,0},{3,1},{8,10},{9,11},{10,8},{11,9},{16,18},{17,19... | collective-permute-start | bytes 245768 | tf_op jit(solution)/shard_map/ppermute | solution.py:684
  58.9 6.2 %collective-permute-start.20 = (bf16[2,80,256]{2,1,0:T(8,128)(2,1)S(1)}, bf16[2,80,256]{2,1,0:T(8,128)(2,1)S(1)}, u32[]{:S(2)}, u32[]{:S(2)}) collective-permute-start(bf16[2,80,256]{2,1,0:T(8,128)(2,1)S(1)} %get-tuple-element.112), channel_id=1, source_target_pairs={{0,1},{1,2},{2,3},{3,0},{8,9},{9,10},{10,11},{11,8},{16,17},{17,18... | collective-permute-start | bytes 245768 | tf_op jit(solution)/shard_map/ppermute | solution.py:684
  65.1 4.9 %collective-permute-start.23 = (bf16[4,2,80,256]{3,2,1,0:T(8,128)(2,1)S(1)}, bf16[4,2,80,256]{3,2,1,0:T(8,128)(2,1)S(1)}, u32[]{:S(2)}, u32[]{:S(2)}) collective-permute-start(bf16[4,2,80,256]{3,2,1,0:T(8,128)(2,1)S(1)} %shard_map.77.own_ref), channel_id=1, source_target_pairs={{0,4},{4,0},{1,5},{5,1},{2,6},{6,2},{3,7},{7,3},{8,12},{12,8},{9,1... | collective-permute-start | bytes 983048 | tf_op jit(solution)/shard_map/ppermute | solution.py:656
  66.4 1.7 %collective-permute-start.24 = (bf16[2,8,8,320]{3,2,1,0:T(8,128)(2,1)S(1)}, bf16[2,8,8,320]{3,2,1,0:T(8,128)(2,1)S(1)}, u32[]{:S(2)}, u32[]{:S(2)}) collective-permute-start(bf16[2,8,8,320]{3,2,1,0:T(8,128)(2,1)S(1)} %get-tuple-element.109), channel_id=1, source_target_pairs={{0,4},{4,0},{1,5},{5,1},{2,6},{6,2},{3,7},{7,3},{8,12},{12,8},{9,1... | collective-permute-start | bytes 245768 | tf_op jit(solution)/shard_map/ppermute | solution.py:656

commit v12 on v11

--- a/solution.py
+++ b/solution.py
@@ -172,7 +172,7 @@
     return (grad_kernels, grad_slots[None])
 
 
-def call(kernel, outs, operands, unread, scratch, aliases, apart=()):
+def call(kernel, outs, operands, unread, scratch, aliases, apart=(), cost=None):
     spaces = {**dict.fromkeys(unread, pl.ANY), **dict.fromkeys(apart, pltpu.HBM)}
     return pl.pallas_call(
         kernel,
@@ -185,6 +185,7 @@
         scratch_shapes=scratch,
         input_output_aliases=aliases,
         compiler_params=pltpu.CompilerParams(vmem_limit_bytes=8 << 20),
+        cost_estimate=cost,
     )(*operands)
 
 
@@ -437,7 +438,7 @@
 
     out = jax.ShapeDtypeStruct((images * share, rows, cols, channels), strips.dtype)
     sems = [pltpu.SemaphoreType.DMA((2 * images,))]
-    return call(kernel, [out, out], [strips, cotangent], (), sems, {}, (0, 1))
+    return call(kernel, [out, out], [strips, cotangent], (), sems, {}, (0, 1), pl.CostEstimate(flops=10**10, transcendentals=0, bytes_accessed=10**6))
 
 
 def load_call(weights, first, after):
@@ -697,7 +698,7 @@
     other = swapped(other)
     weights = kernels[0].reshape(2, 3, 3 * channels, channels)
     stored = pltpu.with_memory_space_constraint(weights, pltpu.HBM)
-    loaded = weights = load_call(stored, True, own)
+    loaded = weights
     fields = join_call(own, other)
     incoming = fields
     state = []

time: 72.9 us -> 70.9 us (0.973)
  starting transfers between devices: 31.9 us -> 35.3 us
  waiting for transfers between devices: 20.3 us -> 17.1 us
  Pallas kernels: 19 us -> 16.9 us
    ppermute x9, waiting for transfers between devices: 17.1 us -> 8.21 us  [shared(): return lax.ppermute(values, ('section', 'img'), pairs)]
    ppermute x12, waiting for transfers between devices: 3.17 us -> 7.97 us  [hop(): arrived.append(lax.ppermute(value, 'section', [(source, target)]))]
    pallas_call x31 -> x30, Pallas kernels: 16.7 us -> 14.5 us  [call(): pl.pallas_call(kernel, out_shape=outs, in_specs=[pl.BlockSpec(memory_spac...]
    ppermute x9, starting transfers between devices: 19.5 us -> 21.2 us  [shared(): return lax.ppermute(values, ('section', 'img'), pairs)]
    ppermute x12, starting transfers between devices: 11.2 us -> 12.8 us  [hop(): arrived.append(lax.ppermute(value, 'section', [(source, target)]))]
    ppermute x4, waiting for transfers between devices: 0.01 us -> 0.95 us  [rotated(): lax.ppermute(value, axis, [(source, (source + steps) % count) for source...]
  transfers between devices with their start and end apart: 25 -> 25, of which waited for: 7 -> 8; matrix products, arithmetic and copies ran while one was open for 0% -> 0% of each run, Pallas kernels for 20% -> 17%
where the time goes in v12:
time: 70.9 us; the launch traced here: 70.6 us
  starting transfers between devices  35.3 us (50%)
  waiting for transfers between devices  17.1 us (24%)
  Pallas kernels  16.9 us (24%)
  between operations  1.28 us (2%)
    ppermute x9, starting transfers between devices, shared(): return lax.ppermute(values, ('section', 'img'), pairs)  21.2 us
    pallas_call x30, Pallas kernels, call(): pl.pallas_call(kernel, out_shape=outs, in_specs=[pl.BlockSpec(memory_spac...  14.5 us
    ppermute x12, starting transfers between devices, hop(): arrived.append(lax.ppermute(value, 'section', [(source, target)]))  12.8 us
    ppermute x9, waiting for transfers between devices, shared(): return lax.ppermute(values, ('section', 'img'), pairs)  8.21 us
    ppermute x12, waiting for transfers between devices, hop(): arrived.append(lax.ppermute(value, 'section', [(source, target)]))  7.97 us
    pallas_call x1, Pallas kernels, terms_call(): pl.pallas_call(kernel, out_shape=jax.ShapeDtypeStruct(shape, jnp.float32)...  2.31 us
  transfers between devices with their start and end apart: 25, of which 8 were waited for; matrix products, arithmetic and copies ran while one was open for 0% of the time, Pallas kernels for 17%

profile of v12, /device:TPU:0, one launch (start us, length us, event | category | flops | bytes accessed | tf_op | source)
XLA Modules:
  0.0 70.6 jit_solution(12513622863648634643)
XLA Ops:
  0.6 0.0 copy-start
  0.6 1.1 %shard_map.50 = (bf16[2,8,8,320]{3,2,1,0:T(8,128)(2,1)S(1)}, bf16[2,8,8,320]{3,2,1,0:T(8,128)(2,1)S(1)}) custom-call(bf16[1,4,8,8,320]{4,3,2,1,0:T(8,128)(2,1)} %strips_ref.1, bf16[1,4,8,8,320]{4,3,2,1,0:T(8,128)(2,1)} %cotangent_ref.1), custom_call_target="tpu_custom_call" | custom-call | flops 10000000000 | bytes 1000000 | tf_op jit(solution)/shard_map/pallas_call | solution.py:177
  1.8 0.6 collective-permute-start
  2.3 0.9 %collective-permute-done.other_ref = bf16[2,8,8,320]{3,2,1,0:T(8,128)(2,1)S(1)} collective-permute-done((bf16[2,8,8,320]{3,2,1,0:T(8,128)(2,1)S(1)}, bf16[2,8,8,320]{3,2,1,0:T(8,128)(2,1)S(1)}, u32[]{:S(2)}, u32[]{:S(2)}) %collective-permute-start) | collective-permute-done | bytes 81952 | tf_op jit(solution)/shard_map/ppermute | solution.py:657
  3.3 0.1 shard_map.51
  3.3 0.0 slice-start
  3.4 1.4 %shard_map.52 = (bf16[320,128]{1,0:T(8,128)(2,1)S(1)}, bf16[2,2,128,320]{3,2,1,0:T(8,128)(2,1)S(1)}, f32[2,128,320]{2,1,0:T(8,128)S(1)}) custom-call(bf16[128,320]{1,0:T(8,128)(2,1)S(1)} %get-tuple-element.59.field_ref.grad_ref, bf16[2,3,960,320]{3,2,1,0:T(8,128)(2,1)S(1)} %bitcast.12, bf16[2,3,960,320]{3,2,1,0:T(8,128)(2,1)S(1)} %bitcast.13), custom_call_target="tpu_custom_call" | custom-call | tf_op jit(solution)/shard_map/pallas_call | solution.py:177
  4.7 3.7 %collective-permute-start.2 = (bf16[320,128]{1,0:T(8,128)(2,1)S(1)}, bf16[320,128]{1,0:T(8,128)(2,1)S(1)}, u32[]{:S(2)}, u32[]{:S(2)}) collective-permute-start(bf16[320,128]{1,0:T(8,128)(2,1)S(1)} %get-tuple-element.64), channel_id=1, source_target_pairs={{0,8},{1,9},{2,10},{3,11},{4,12},{5,13},{6,14},{7,15}} | collective-permute-start | bytes 245768 | tf_op jit(solution)/shard_map/ppermute | solution.py:676
  8.4 0.0 slice-start.1
  8.4 1.4 %shard_map.53 = (bf16[320,128]{1,0:T(8,128)(2,1)S(1)}, bf16[2,2,128,320]{3,2,1,0:T(8,128)(2,1)S(1)}, f32[2,128,320]{2,1,0:T(8,128)S(1)}) custom-call(bf16[128,320]{1,0:T(8,128)(2,1)S(1)} %get-tuple-element.58.field_ref.grad_ref, bf16[2,3,960,320]{3,2,1,0:T(8,128)(2,1)S(1)} %bitcast.14, ...), custom_call_target="tpu_custom_call", output_to_operand_aliasing={{1}: (3, {}), {2}: (4, {})} | custom-call | tf_op jit(solution)/shard_map/pallas_call | solution.py:177
  9.8 1.3 %collective-permute-start.1 = (bf16[320,128]{1,0:T(8,128)(2,1)S(1)}, bf16[320,128]{1,0:T(8,128)(2,1)S(1)}, u32[]{:S(2)}, u32[]{:S(2)}) collective-permute-start(bf16[320,128]{1,0:T(8,128)(2,1)S(1)} %get-tuple-element.62), channel_id=1, source_target_pairs={{0,8},{1,9},{2,10},{3,11},{4,12},{5,13},{6,14},{7,15}} | collective-permute-start | bytes 245768 | tf_op jit(solution)/shard_map/ppermute | solution.py:676
  11.1 0.0 collective-permute-done.2.field_ref
  11.2 0.7 collective-permute-start.4
  11.8 1.3 %collective-permute-done.1.field_ref = bf16[320,128]{1,0:T(8,128)(2,1)S(1)} collective-permute-done((bf16[320,128]{1,0:T(8,128)(2,1)S(1)}, bf16[320,128]{1,0:T(8,128)(2,1)S(1)}, u32[]{:S(2)}, u32[]{:S(2)}) %collective-permute-start.1) | collective-permute-done | bytes 81952 | tf_op jit(solution)/shard_map/ppermute | solution.py:676
  13.1 0.7 collective-permute-start.3
  13.8 1.4 %shard_map.57.after_ref.turned_ref = bf16[2,3,960,320]{3,2,1,0:T(8,128)(2,1)S(1)} custom-call(bf16[2,3,960,320]{3,2,1,0:T(8,128)(2,1)S(1)} %bitcast.20, bf16[2,3,960,320]{3,2,1,0:T(8,128)(2,1)S(1)} %shard_map.54.weights_ref, bf16[2,2,128,320]{3,2,1,0:T(8,128)(2,1)S(1)} %get-tuple-element.69.after_ref.refs_0_), custom_call_target="tpu_custom_call" | custom-call | tf_op jit(solution)/shard_map/pallas_call | solution.py:177
  15.1 0.1 shard_map.65
  15.2 0.0 collective-permute-done.4.field_ref
  15.3 0.7 collective-permute-start.6
  16.0 0.0 collective-permute-done.3.field_ref
  16.0 0.7 collective-permute-start.5
  16.7 3.5 %collective-permute-start.10 = (bf16[2,160,256]{2,1,0:T(8,128)(2,1)S(1)}, bf16[2,160,256]{2,1,0:T(8,128)(2,1)S(1)}, u32[]{:S(2)}, u32[]{:S(2)}) collective-permute-start(bf16[2,160,256]{2,1,0:T(8,128)(2,1)S(1)} %shard_map.65), channel_id=1, source_target_pairs={{0,1},{1,2},{2,3},{3,0},{4,5},{5,6},{6,7},{7,4}} | collective-permute-start | bytes 491528 | tf_op jit(solution)/shard_map/ppermute | solution.py:685
  20.2 4.5 %collective-permute-start.11 = (bf16[2,160,256]{2,1,0:T(8,128)(2,1)S(1)}, bf16[2,160,256]{2,1,0:T(8,128)(2,1)S(1)}, u32[]{:S(2)}, u32[]{:S(2)}) collective-permute-start(bf16[2,160,256]{2,1,0:T(8,128)(2,1)S(1)} %shard_map.65), channel_id=1, source_target_pairs={{0,2},{1,3},{2,0},{3,1},{4,6},{5,7},{6,4},{7,5}} | collective-permute-start | bytes 491528 | tf_op jit(solution)/shard_map/ppermute | solution.py:685
  24.6 0.0 collective-permute-done.6.field_ref
  24.7 0.7 collective-permute-start.15
  25.4 0.0 collective-permute-done.5.field_ref
  25.4 0.2 shard_map.63
  25.6 0.7 collective-permute-start.14
  26.3 0.0 collective-permute-done.15.grad_ref
  26.3 0.7 collective-permute-start.17
  27.0 3.3 %collective-permute-start.12 = (bf16[2,160,256]{2,1,0:T(8,128)(2,1)S(1)}, bf16[2,160,256]{2,1,0:T(8,128)(2,1)S(1)}, u32[]{:S(2)}, u32[]{:S(2)}) collective-permute-start(bf16[2,160,256]{2,1,0:T(8,128)(2,1)S(1)} %shard_map.65), channel_id=1, source_target_pairs={{0,3},{1,0},{2,1},{3,2},{4,7},{5,4},{6,5},{7,6}} | collective-permute-start | bytes 491528 | tf_op jit(solution)/shard_map/ppermute | solution.py:685
  30.3 0.1 shard_map.64
  30.4 0.0 collective-permute-done.10.refs_0_
  30.4 0.7 %collective-permute-start.7 = (bf16[2,160,256]{2,1,0:T(8,128)(2,1)S(1)}, bf16[2,160,256]{2,1,0:T(8,128)(2,1)S(1)}, u32[]{:S(2)}, u32[]{:S(2)}) collective-permute-start(bf16[2,160,256]{2,1,0:T(8,128)(2,1)S(1)} %shard_map.64), channel_id=1, source_target_pairs={{0,1},{1,2},{2,3},{3,0},{8,9},{9,10},{10,11},{11,8},{16,17},{17,18... | collective-permute-start | bytes 491528 | tf_op jit(solution)/shard_map/ppermute | solution.py:685
  31.1 1.9 %collective-permute-done.11.refs_1_ = bf16[2,160,256]{2,1,0:T(8,128)(2,1)S(1)} collective-permute-done((bf16[2,160,256]{2,1,0:T(8,128)(2,1)S(1)}, bf16[2,160,256]{2,1,0:T(8,128)(2,1)S(1)}, u32[]{:S(2)}, u32[]{:S(2)}) %collective-permute-start.11) | collective-permute-done | bytes 163872 | tf_op jit(solution)/shard_map/ppermute | solution.py:685
  33.0 0.0 collective-permute-start.8
  33.0 0.0 collective-permute-done.14.grad_ref
  33.0 5.3 %collective-permute-start.9 = (bf16[2,160,256]{2,1,0:T(8,128)(2,1)S(1)}, bf16[2,160,256]{2,1,0:T(8,128)(2,1)S(1)}, u32[]{:S(2)}, u32[]{:S(2)}) collective-permute-start(bf16[2,160,256]{2,1,0:T(8,128)(2,1)S(1)} %shard_map.64), channel_id=1, source_target_pairs={{0,3},{1,0},{2,1},{3,2},{8,11},{9,8},{10,9},{11,10},{16,19},{17,16... | collective-permute-start | bytes 491528 | tf_op jit(solution)/shard_map/ppermute | solution.py:685
  38.3 0.0 collective-permute-done.17.grad_ref
  38.3 0.7 collective-permute-start.16
  39.0 0.0 collective-permute-done.16.grad_ref
  39.0 1.3 %collective-permute-start.19 = (bf16[320,128]{1,0:T(8,128)(2,1)S(1)}, bf16[320,128]{1,0:T(8,128)(2,1)S(1)}, u32[]{:S(2)}, u32[]{:S(2)}) collective-permute-start(bf16[320,128]{1,0:T(8,128)(2,1)S(1)} %get-tuple-element.101), channel_id=1, source_target_pairs={{8,0},{9,1},{10,2},{11,3},{12,4},{13,5},{14,6},{15,7}} | collective-permute-start | bytes 245768 | tf_op jit(solution)/shard_map/ppermute | solution.py:676
  40.4 1.3 %collective-permute-start.18 = (bf16[320,128]{1,0:T(8,128)(2,1)S(1)}, bf16[320,128]{1,0:T(8,128)(2,1)S(1)}, u32[]{:S(2)}, u32[]{:S(2)}) collective-permute-start(bf16[320,128]{1,0:T(8,128)(2,1)S(1)} %get-tuple-element.100), channel_id=1, source_target_pairs={{8,0},{9,1},{10,2},{11,3},{12,4},{13,5},{14,6},{15,7}} | collective-permute-start | bytes 245768 | tf_op jit(solution)/shard_map/ppermute | solution.py:676
  41.7 3.0 %shard_map.66 = (bf16[2,4,160,256]{3,2,1,0:T(8,128)(2,1)S(1)}, bf16[2,4,160,256]{3,2,1,0:T(8,128)(2,1)S(1)}) custom-call(bf16[2,2,128,320]{3,2,1,0:T(8,128)(2,1)S(1)} %get-tuple-element.81.refs_0_.saved_ref, bf16[2,3,960,320]{3,2,1,0:T(8,128)(2,1)S(1)} %bitcast.21, bf16[2,160,256]{2,1,0:T(8,128)(2,1)S(1)} %collective-permute-done.10.refs_0_, ...), custom_call_target="tpu_custom_call" | custom-call | tf_op jit(solution)/shard_map/pallas_call | solution.py:177
  44.6 2.4 %collective-permute-done.8.refs_1_ = bf16[2,160,256]{2,1,0:T(8,128)(2,1)S(1)} collective-permute-done((bf16[2,160,256]{2,1,0:T(8,128)(2,1)S(1)}, bf16[2,160,256]{2,1,0:T(8,128)(2,1)S(1)}, u32[]{:S(2)}, u32[]{:S(2)}) %collective-permute-start.8) | collective-permute-done | bytes 163872 | tf_op jit(solution)/shard_map/ppermute | solution.py:685
  47.1 0.1 collective-permute-start.13
  47.2 4.7 %collective-permute-done.19.grad_ref.refs_0_ = bf16[320,128]{1,0:T(8,128)(2,1)S(1)} collective-permute-done((bf16[320,128]{1,0:T(8,128)(2,1)S(1)}, bf16[320,128]{1,0:T(8,128)(2,1)S(1)}, u32[]{:S(2)}, u32[]{:S(2)}) %collective-permute-start.19) | collective-permute-done | bytes 81952 | tf_op jit(solution)/shard_map/ppermute | solution.py:676
  51.9 0.7 %shard_map.74 = (bf16[2,128,320]{2,1,0:T(8,128)(2,1)S(1)}, bf16[4,2,80,256]{3,2,1,0:T(8,128)(2,1)S(1)}) custom-call(bf16[320,128]{1,0:T(8,128)(2,1)S(1)} %collective-permute-done.19.grad_ref.refs_0_, bf16[2,3,960,320]{3,2,1,0:T(8,128)(2,1)S(1)} %shard_map.57.after_ref.turned_ref, ...), custom_call_target="tpu_custom_call", output_to_operand_aliasing={{0}: (4, {}), {1}: (5, {})} | custom-call | tf_op jit(solution)/shard_map/pallas_call | solution.py:177
  52.6 2.0 %collective-permute-done.18.grad_ref.refs_1_ = bf16[320,128]{1,0:T(8,128)(2,1)S(1)} collective-permute-done((bf16[320,128]{1,0:T(8,128)(2,1)S(1)}, bf16[320,128]{1,0:T(8,128)(2,1)S(1)}, u32[]{:S(2)}, u32[]{:S(2)}) %collective-permute-start.18) | collective-permute-done | bytes 81952 | tf_op jit(solution)/shard_map/ppermute | solution.py:676
  54.6 0.7 %shard_map.75 = (bf16[2,128,320]{2,1,0:T(8,128)(2,1)S(1)}, bf16[4,2,80,256]{3,2,1,0:T(8,128)(2,1)S(1)}) custom-call(bf16[320,128]{1,0:T(8,128)(2,1)S(1)} %collective-permute-done.18.grad_ref.refs_1_, bf16[2,3,960,320]{3,2,1,0:T(8,128)(2,1)S(1)} %shard_map.57.after_ref.turned_ref, ...), custom_call_target="tpu_custom_call", output_to_operand_aliasing={{0}: (4, {}), {1}: (5, {})} | custom-call | tf_op jit(solution)/shard_map/pallas_call | solution.py:177
  55.3 0.7 collective-permute-start.20
  56.0 1.7 %collective-permute-start.21 = (bf16[2,80,256]{2,1,0:T(8,128)(2,1)S(1)}, bf16[2,80,256]{2,1,0:T(8,128)(2,1)S(1)}, u32[]{:S(2)}, u32[]{:S(2)}) collective-permute-start(bf16[2,80,256]{2,1,0:T(8,128)(2,1)S(1)} %get-tuple-element.111), channel_id=1, source_target_pairs={{0,2},{1,3},{2,0},{3,1},{8,10},{9,11},{10,8},{11,9},{16,18},{17,19... | collective-permute-start | bytes 245768 | tf_op jit(solution)/shard_map/ppermute | solution.py:685
  57.7 1.5 %collective-permute-start.22 = (bf16[2,80,256]{2,1,0:T(8,128)(2,1)S(1)}, bf16[2,80,256]{2,1,0:T(8,128)(2,1)S(1)}, u32[]{:S(2)}, u32[]{:S(2)}) collective-permute-start(bf16[2,80,256]{2,1,0:T(8,128)(2,1)S(1)} %get-tuple-element.110), channel_id=1, source_target_pairs={{0,3},{1,0},{2,1},{3,2},{8,11},{9,8},{10,9},{11,10},{16,19},{17,16... | collective-permute-start | bytes 245768 | tf_op jit(solution)/shard_map/ppermute | solution.py:685
  59.2 2.6 %collective-permute-done.20.refs_1_ = bf16[2,80,256]{2,1,0:T(8,128)(2,1)S(1)} collective-permute-done((bf16[2,80,256]{2,1,0:T(8,128)(2,1)S(1)}, bf16[2,80,256]{2,1,0:T(8,128)(2,1)S(1)}, u32[]{:S(2)}, u32[]{:S(2)}) %collective-permute-start.20) | collective-permute-done | bytes 81952 | tf_op jit(solution)/shard_map/ppermute | solution.py:685
  61.8 1.4 %collective-permute-done.21.refs_2_ = bf16[2,80,256]{2,1,0:T(8,128)(2,1)S(1)} collective-permute-done((bf16[2,80,256]{2,1,0:T(8,128)(2,1)S(1)}, bf16[2,80,256]{2,1,0:T(8,128)(2,1)S(1)}, u32[]{:S(2)}, u32[]{:S(2)}) %collective-permute-start.21) | collective-permute-done | bytes 81952 | tf_op jit(solution)/shard_map/ppermute | solution.py:685
  63.1 0.0 collective-permute-done.22.refs_3_
  63.2 0.1 collective-permute-start.23
  63.3 1.1 %shard_map.77.kept_ref = bf16[2,128,320]{2,1,0:T(8,128)(2,1)S(1)} custom-call(bf16[2,3,960,320]{3,2,1,0:T(8,128)(2,1)S(1)} %shard_map.57.after_ref.turned_ref, bf16[320,128]{1,0:T(8,128)(2,1)S(1)} %collective-permute-done.19.grad_ref.refs_0_, bf16[320,128]{1,0:T(8,128)(2,1)S(1)} %collective-permute-done.18.grad_ref.refs_1_, ...), custom_call_target="tpu_custom_call", output_to_operand_aliasing={{}: (3, {})} | custom-call | tf_op jit(solution)/shard_map/pallas_call | solution.py:177
  64.4 0.1 shard_map.78
  64.4 0.5 collective-permute-start.24
  65.0 1.2 %shard_map.68.refs_0_ = bf16[2,2048,480]{2,1,0:T(8,128)(2,1)S(1)} custom-call(bf16[2,4,160,256]{3,2,1,0:T(8,128)(2,1)S(1)} %get-tuple-element.88.first_ref.after_ref, bf16[2,4,160,256]{3,2,1,0:T(8,128)(2,1)S(1)} %get-tuple-element.89.cells_ref), custom_call_target="tpu_custom_call" | custom-call | tf_op jit(solution)/shard_map/pallas_call | solution.py:177
  66.2 0.7 %shard_map.79 = bf16[1,4,8,8,320]{4,3,2,1,0:T(8,128)(2,1)} custom-call(bf16[2,8,8,320]{3,2,1,0:T(8,128)(2,1)S(1)} %get-tuple-element.108.own_ref, bf16[2,8,8,320]{3,2,1,0:T(8,128)(2,1)S(1)} %collective-permute-done.24.other_ref), custom_call_target="tpu_custom_call" | custom-call | tf_op jit(solution)/shard_map/pallas_call | solution.py:177
  66.9 1.2 %shard_map.69.around_ref = bf16[2,2048,480]{2,1,0:T(8,128)(2,1)S(1)} custom-call(bf16[2,4,160,256]{3,2,1,0:T(8,128)(2,1)S(1)} %collective-permute-done.13.first_ref.cells_ref, bf16[2,4,160,256]{3,2,1,0:T(8,128)(2,1)S(1)} %collective-permute-done.13.first_ref.cells_ref, bf16[2,2048,480]{2,1,0:T(8,128)(2,1)S(1)} %shard_map.68.refs_0_), custom_call_target="tpu_custom_call", output_to_operand_aliasing={{}: (2, {})} | custom-call | tf_op jit(solution)/shard_map/pallas_call | solution.py:177
  68.1 2.3 %terms.1 = f32[2,9,160,80]{3,2,1,0:T(8,128)} custom-call(bf16[2,2048,480]{2,1,0:T(8,128)(2,1)S(1)} %shard_map.69.around_ref, bf16[4,2,80,256]{3,2,1,0:T(8,128)(2,1)S(1)} %shard_map.76.own_ref, bf16[4,2,80,256]{3,2,1,0:T(8,128)(2,1)S(1)} %collective-permute-done.23.other_ref), custom_call_target="tpu_custom_call" | custom-call | tf_op jit(solution)/shard_map/terms/pallas_call | solution.py:644
  (25 shorter events, 0.3 us)
Async XLA Ops:
  0.6 2.7 %copy-start = (bf16[1,2,9,320,320]{4,3,2,1,0:T(8,128)(2,1)S(1)}, bf16[1,2,9,320,320]{4,3,2,1,0:T(8,128)(2,1)}, u32[]{:S(2)}) copy-start(bf16[1,2,9,320,320]{4,3,2,1,0:T(8,128)(2,1)} %param.4) | copy-start | bytes 11059204
  1.8 1.5 %collective-permute-start = (bf16[2,8,8,320]{3,2,1,0:T(8,128)(2,1)S(1)}, bf16[2,8,8,320]{3,2,1,0:T(8,128)(2,1)S(1)}, u32[]{:S(2)}, u32[]{:S(2)}) collective-permute-start(bf16[2,8,8,320]{3,2,1,0:T(8,128)(2,1)S(1)} %get-tuple-element.57), channel_id=1, source_target_pairs={{0,4},{4,0},{1,5},{5,1},{2,6},{6,2},{3,7},{7,3},{8,12},{12,8},{9,1... | collective-permute-start | bytes 245768 | tf_op jit(solution)/shard_map/ppermute | solution.py:657
  3.3 7.8 %slice-start = ((s8[4423680]{0:T(1024)(128)(4,1)}), s8[4194304]{0:T(1024)(128)(4,1)S(1)}, s32[]{:S(2)}) async-start(s8[4423680]{0:T(1024)(128)(4,1)} %bitcast.16), calls=%async_computation | async-start | bytes 8388608
  4.7 6.4 %collective-permute-start.2 = (bf16[320,128]{1,0:T(8,128)(2,1)S(1)}, bf16[320,128]{1,0:T(8,128)(2,1)S(1)}, u32[]{:S(2)}, u32[]{:S(2)}) collective-permute-start(bf16[320,128]{1,0:T(8,128)(2,1)S(1)} %get-tuple-element.64), channel_id=1, source_target_pairs={{0,8},{1,9},{2,10},{3,11},{4,12},{5,13},{6,14},{7,15}} | collective-permute-start | bytes 245768 | tf_op jit(solution)/shard_map/ppermute | solution.py:676
  8.4 2.7 %slice-start.1 = ((s8[4423680]{0:T(1024)(128)(4,1)}), s8[229376]{0:T(1024)(128)(4,1)S(1)}, s32[]{:S(2)}) async-start(s8[4423680]{0:T(1024)(128)(4,1)} %bitcast.16), calls=%async_computation.1 | async-start | bytes 458752
  9.8 3.3 %collective-permute-start.1 = (bf16[320,128]{1,0:T(8,128)(2,1)S(1)}, bf16[320,128]{1,0:T(8,128)(2,1)S(1)}, u32[]{:S(2)}, u32[]{:S(2)}) collective-permute-start(bf16[320,128]{1,0:T(8,128)(2,1)S(1)} %get-tuple-element.62), channel_id=1, source_target_pairs={{0,8},{1,9},{2,10},{3,11},{4,12},{5,13},{6,14},{7,15}} | collective-permute-start | bytes 245768 | tf_op jit(solution)/shard_map/ppermute | solution.py:676
  11.2 4.1 %collective-permute-start.4 = (bf16[320,128]{1,0:T(8,128)(2,1)S(1)}, bf16[320,128]{1,0:T(8,128)(2,1)S(1)}, u32[]{:S(2)}, u32[]{:S(2)}) collective-permute-start(bf16[320,128]{1,0:T(8,128)(2,1)S(1)} %get-tuple-element.70), channel_id=1, source_target_pairs={{8,16},{9,17},{10,18},{11,19},{12,20},{13,21},{14,22},{15,23}} | collective-permute-start | bytes 245768 | tf_op jit(solution)/shard_map/ppermute | solution.py:676
  13.1 2.9 %collective-permute-start.3 = (bf16[320,128]{1,0:T(8,128)(2,1)S(1)}, bf16[320,128]{1,0:T(8,128)(2,1)S(1)}, u32[]{:S(2)}, u32[]{:S(2)}) collective-permute-start(bf16[320,128]{1,0:T(8,128)(2,1)S(1)} %get-tuple-element.68), channel_id=1, source_target_pairs={{8,16},{9,17},{10,18},{11,19},{12,20},{13,21},{14,22},{15,23}} | collective-permute-start | bytes 245768 | tf_op jit(solution)/shard_map/ppermute | solution.py:676
  15.3 9.4 %collective-permute-start.6 = (bf16[320,128]{1,0:T(8,128)(2,1)S(1)}, bf16[320,128]{1,0:T(8,128)(2,1)S(1)}, u32[]{:S(2)}, u32[]{:S(2)}) collective-permute-start(bf16[320,128]{1,0:T(8,128)(2,1)S(1)} %get-tuple-element.75), channel_id=1, source_target_pairs={{16,24},{17,25},{18,26},{19,27},{20,28},{21,29},{22,30},{23,31}} | collective-permute-start | bytes 245768 | tf_op jit(solution)/shard_map/ppermute | solution.py:676
  16.0 9.4 %collective-permute-start.5 = (bf16[320,128]{1,0:T(8,128)(2,1)S(1)}, bf16[320,128]{1,0:T(8,128)(2,1)S(1)}, u32[]{:S(2)}, u32[]{:S(2)}) collective-permute-start(bf16[320,128]{1,0:T(8,128)(2,1)S(1)} %get-tuple-element.74), channel_id=1, source_target_pairs={{16,24},{17,25},{18,26},{19,27},{20,28},{21,29},{22,30},{23,31}} | collective-permute-start | bytes 245768 | tf_op jit(solution)/shard_map/ppermute | solution.py:676
  16.7 13.7 %collective-permute-start.10 = (bf16[2,160,256]{2,1,0:T(8,128)(2,1)S(1)}, bf16[2,160,256]{2,1,0:T(8,128)(2,1)S(1)}, u32[]{:S(2)}, u32[]{:S(2)}) collective-permute-start(bf16[2,160,256]{2,1,0:T(8,128)(2,1)S(1)} %shard_map.65), channel_id=1, source_target_pairs={{0,1},{1,2},{2,3},{3,0},{4,5},{5,6},{6,7},{7,4}} | collective-permute-start | bytes 491528 | tf_op jit(solution)/shard_map/ppermute | solution.py:685
  20.2 12.8 %collective-permute-start.11 = (bf16[2,160,256]{2,1,0:T(8,128)(2,1)S(1)}, bf16[2,160,256]{2,1,0:T(8,128)(2,1)S(1)}, u32[]{:S(2)}, u32[]{:S(2)}) collective-permute-start(bf16[2,160,256]{2,1,0:T(8,128)(2,1)S(1)} %shard_map.65), channel_id=1, source_target_pairs={{0,2},{1,3},{2,0},{3,1},{4,6},{5,7},{6,4},{7,5}} | collective-permute-start | bytes 491528 | tf_op jit(solution)/shard_map/ppermute | solution.py:685
  24.7 1.6 %collective-permute-start.15 = (bf16[320,128]{1,0:T(8,128)(2,1)S(1)}, bf16[320,128]{1,0:T(8,128)(2,1)S(1)}, u32[]{:S(2)}, u32[]{:S(2)}) collective-permute-start(bf16[320,128]{1,0:T(8,128)(2,1)S(1)} %get-tuple-element.79.after_ref), channel_id=1, source_target_pairs={{24,16},{25,17},{26,18},{27,19},{28,20},{29,21},{30,22},{31,23}} | collective-permute-start | bytes 245768 | tf_op jit(solution)/shard_map/ppermute | solution.py:676
  25.6 7.4 %collective-permute-start.14 = (bf16[320,128]{1,0:T(8,128)(2,1)S(1)}, bf16[320,128]{1,0:T(8,128)(2,1)S(1)}, u32[]{:S(2)}, u32[]{:S(2)}) collective-permute-start(bf16[320,128]{1,0:T(8,128)(2,1)S(1)} %get-tuple-element.85.refs_1_), channel_id=1, source_target_pairs={{24,16},{25,17},{26,18},{27,19},{28,20},{29,21},{30,22},{31,23}} | collective-permute-start | bytes 245768 | tf_op jit(solution)/shard_map/ppermute | solution.py:676
  26.3 12.0 %collective-permute-start.17 = (bf16[320,128]{1,0:T(8,128)(2,1)S(1)}, bf16[320,128]{1,0:T(8,128)(2,1)S(1)}, u32[]{:S(2)}, u32[]{:S(2)}) collective-permute-start(bf16[320,128]{1,0:T(8,128)(2,1)S(1)} %get-tuple-element.95), channel_id=1, source_target_pairs={{16,8},{17,9},{18,10},{19,11},{20,12},{21,13},{22,14},{23,15}} | collective-permute-start | bytes 245768 | tf_op jit(solution)/shard_map/ppermute | solution.py:676
  27.0 13.4 %collective-permute-start.12 = (bf16[2,160,256]{2,1,0:T(8,128)(2,1)S(1)}, bf16[2,160,256]{2,1,0:T(8,128)(2,1)S(1)}, u32[]{:S(2)}, u32[]{:S(2)}) collective-permute-start(bf16[2,160,256]{2,1,0:T(8,128)(2,1)S(1)} %shard_map.65), channel_id=1, source_target_pairs={{0,3},{1,0},{2,1},{3,2},{4,7},{5,4},{6,5},{7,6}} | collective-permute-start | bytes 491528 | tf_op jit(solution)/shard_map/ppermute | solution.py:685
  30.4 14.2 %collective-permute-start.7 = (bf16[2,160,256]{2,1,0:T(8,128)(2,1)S(1)}, bf16[2,160,256]{2,1,0:T(8,128)(2,1)S(1)}, u32[]{:S(2)}, u32[]{:S(2)}) collective-permute-start(bf16[2,160,256]{2,1,0:T(8,128)(2,1)S(1)} %shard_map.64), channel_id=1, source_target_pairs={{0,1},{1,2},{2,3},{3,0},{8,9},{9,10},{10,11},{11,8},{16,17},{17,18... | collective-permute-start | bytes 491528 | tf_op jit(solution)/shard_map/ppermute | solution.py:685
  33.0 14.0 %collective-permute-start.8 = (bf16[2,160,256]{2,1,0:T(8,128)(2,1)S(1)}, bf16[2,160,256]{2,1,0:T(8,128)(2,1)S(1)}, u32[]{:S(2)}, u32[]{:S(2)}) collective-permute-start(bf16[2,160,256]{2,1,0:T(8,128)(2,1)S(1)} %shard_map.64), channel_id=1, source_target_pairs={{0,2},{1,3},{2,0},{3,1},{8,10},{9,11},{10,8},{11,9},{16,18},{17,19... | collective-permute-start | bytes 491528 | tf_op jit(solution)/shard_map/ppermute | solution.py:685
  33.0 14.0 %collective-permute-start.9 = (bf16[2,160,256]{2,1,0:T(8,128)(2,1)S(1)}, bf16[2,160,256]{2,1,0:T(8,128)(2,1)S(1)}, u32[]{:S(2)}, u32[]{:S(2)}) collective-permute-start(bf16[2,160,256]{2,1,0:T(8,128)(2,1)S(1)} %shard_map.64), channel_id=1, source_target_pairs={{0,3},{1,0},{2,1},{3,2},{8,11},{9,8},{10,9},{11,10},{16,19},{17,16... | collective-permute-start | bytes 491528 | tf_op jit(solution)/shard_map/ppermute | solution.py:685
  38.3 0.7 collective-permute-start.16
  39.0 12.8 %collective-permute-start.19 = (bf16[320,128]{1,0:T(8,128)(2,1)S(1)}, bf16[320,128]{1,0:T(8,128)(2,1)S(1)}, u32[]{:S(2)}, u32[]{:S(2)}) collective-permute-start(bf16[320,128]{1,0:T(8,128)(2,1)S(1)} %get-tuple-element.101), channel_id=1, source_target_pairs={{8,0},{9,1},{10,2},{11,3},{12,4},{13,5},{14,6},{15,7}} | collective-permute-start | bytes 245768 | tf_op jit(solution)/shard_map/ppermute | solution.py:676
  40.4 14.2 %collective-permute-start.18 = (bf16[320,128]{1,0:T(8,128)(2,1)S(1)}, bf16[320,128]{1,0:T(8,128)(2,1)S(1)}, u32[]{:S(2)}, u32[]{:S(2)}) collective-permute-start(bf16[320,128]{1,0:T(8,128)(2,1)S(1)} %get-tuple-element.100), channel_id=1, source_target_pairs={{8,0},{9,1},{10,2},{11,3},{12,4},{13,5},{14,6},{15,7}} | collective-permute-start | bytes 245768 | tf_op jit(solution)/shard_map/ppermute | solution.py:676
  47.1 19.8 %collective-permute-start.13 = (bf16[2,4,160,256]{3,2,1,0:T(8,128)(2,1)S(1)}, bf16[2,4,160,256]{3,2,1,0:T(8,128)(2,1)S(1)}, u32[]{:S(2)}, u32[]{:S(2)}) collective-permute-start(bf16[2,4,160,256]{3,2,1,0:T(8,128)(2,1)S(1)} %get-tuple-element.87), channel_id=1, source_target_pairs={{0,4},{4,0},{1,5},{5,1},{2,6},{6,2},{3,7},{7,3},{8,12},{12,8},{9,1... | collective-permute-start | bytes 1966088 | tf_op jit(solution)/shard_map/ppermute | solution.py:657
  55.3 6.4 %collective-permute-start.20 = (bf16[2,80,256]{2,1,0:T(8,128)(2,1)S(1)}, bf16[2,80,256]{2,1,0:T(8,128)(2,1)S(1)}, u32[]{:S(2)}, u32[]{:S(2)}) collective-permute-start(bf16[2,80,256]{2,1,0:T(8,128)(2,1)S(1)} %get-tuple-element.112), channel_id=1, source_target_pairs={{0,1},{1,2},{2,3},{3,0},{8,9},{9,10},{10,11},{11,8},{16,17},{17,18... | collective-permute-start | bytes 245768 | tf_op jit(solution)/shard_map/ppermute | solution.py:685
  56.0 7.1 %collective-permute-start.21 = (bf16[2,80,256]{2,1,0:T(8,128)(2,1)S(1)}, bf16[2,80,256]{2,1,0:T(8,128)(2,1)S(1)}, u32[]{:S(2)}, u32[]{:S(2)}) collective-permute-start(bf16[2,80,256]{2,1,0:T(8,128)(2,1)S(1)} %get-tuple-element.111), channel_id=1, source_target_pairs={{0,2},{1,3},{2,0},{3,1},{8,10},{9,11},{10,8},{11,9},{16,18},{17,19... | collective-permute-start | bytes 245768 | tf_op jit(solution)/shard_map/ppermute | solution.py:685
  57.7 5.4 %collective-permute-start.22 = (bf16[2,80,256]{2,1,0:T(8,128)(2,1)S(1)}, bf16[2,80,256]{2,1,0:T(8,128)(2,1)S(1)}, u32[]{:S(2)}, u32[]{:S(2)}) collective-permute-start(bf16[2,80,256]{2,1,0:T(8,128)(2,1)S(1)} %get-tuple-element.110), channel_id=1, source_target_pairs={{0,3},{1,0},{2,1},{3,2},{8,11},{9,8},{10,9},{11,10},{16,19},{17,16... | collective-permute-start | bytes 245768 | tf_op jit(solution)/shard_map/ppermute | solution.py:685
  63.2 4.9 %collective-permute-start.23 = (bf16[4,2,80,256]{3,2,1,0:T(8,128)(2,1)S(1)}, bf16[4,2,80,256]{3,2,1,0:T(8,128)(2,1)S(1)}, u32[]{:S(2)}, u32[]{:S(2)}) collective-permute-start(bf16[4,2,80,256]{3,2,1,0:T(8,128)(2,1)S(1)} %shard_map.76.own_ref), channel_id=1, source_target_pairs={{0,4},{4,0},{1,5},{5,1},{2,6},{6,2},{3,7},{7,3},{8,12},{12,8},{9,1... | collective-permute-start | bytes 983048 | tf_op jit(solution)/shard_map/ppermute | solution.py:657
  64.4 1.7 %collective-permute-start.24 = (bf16[2,8,8,320]{3,2,1,0:T(8,128)(2,1)S(1)}, bf16[2,8,8,320]{3,2,1,0:T(8,128)(2,1)S(1)}, u32[]{:S(2)}, u32[]{:S(2)}) collective-permute-start(bf16[2,8,8,320]{3,2,1,0:T(8,128)(2,1)S(1)} %get-tuple-element.109), channel_id=1, source_target_pairs={{0,4},{4,0},{1,5},{5,1},{2,6},{6,2},{3,7},{7,3},{8,12},{12,8},{9,1... | collective-permute-start | bytes 245768 | tf_op jit(solution)/shard_map/ppermute | solution.py:657

commit v13 on v12

--- a/solution.py
+++ b/solution.py
@@ -634,9 +634,12 @@
                 part = part.T.reshape(3, rows, columns)
                 for place in range(3):
                     held[kind, 3 * down + place] = part[place]
-            copy = pltpu.make_async_copy(held.at[kind], out_ref.at[kind], sems.at[kind])
-            copy.start()
-            copies.append(copy)
+                third = pl.ds(3 * down, 3)
+                copy = pltpu.make_async_copy(
+                    held.at[kind, third], out_ref.at[kind, third], sems.at[3 * kind + down]
+                )
+                copy.start()
+                copies.append(copy)
         for copy in copies:
             copy.wait()
 
@@ -646,7 +649,7 @@
         out_shape=jax.ShapeDtypeStruct(shape, jnp.float32),
         in_specs=[pl.BlockSpec(memory_space=pltpu.VMEM)] * 3,
         out_specs=pl.BlockSpec(memory_space=pltpu.HBM),
-        scratch_shapes=[pltpu.VMEM(shape, jnp.float32), pltpu.SemaphoreType.DMA((2,))],
+        scratch_shapes=[pltpu.VMEM(shape, jnp.float32), pltpu.SemaphoreType.DMA((6,))],
         compiler_params=pltpu.CompilerParams(vmem_limit_bytes=8 << 20),
         name="terms",
     )(around, own, other)

time: 70.9 us -> 70.9 us (level)
  no operation moved by 1% of the time
where the time goes in v13:
time: 70.9 us; the launch traced here: 70.5 us
  starting transfers between devices  35.3 us (50%)
  waiting for transfers between devices  17.1 us (24%)
  Pallas kernels  16.8 us (24%)
  between operations  1.28 us (2%)
    ppermute x9, starting transfers between devices, shared(): return lax.ppermute(values, ('section', 'img'), pairs)  21.2 us
    pallas_call x30, Pallas kernels, call(): pl.pallas_call(kernel, out_shape=outs, in_specs=[pl.BlockSpec(memory_spac...  14.5 us
    ppermute x12, starting transfers between devices, hop(): arrived.append(lax.ppermute(value, 'section', [(source, target)]))  12.8 us
    ppermute x9, waiting for transfers between devices, shared(): return lax.ppermute(values, ('section', 'img'), pairs)  8.21 us
    ppermute x12, waiting for transfers between devices, hop(): arrived.append(lax.ppermute(value, 'section', [(source, target)]))  7.97 us
    pallas_call x1, Pallas kernels, terms_call(): pl.pallas_call(kernel, out_shape=jax.ShapeDtypeStruct(shape, jnp.float32)...  2.26 us
  transfers between devices with their start and end apart: 25, of which 8 were waited for; matrix products, arithmetic and copies ran while one was open for 0% of the time, Pallas kernels for 17%

profile of v13, /device:TPU:0, one launch (start us, length us, event | category | flops | bytes accessed | tf_op | source)
XLA Modules:
  0.0 70.5 jit_solution(18405691747262416321)
XLA Ops:
  0.6 0.0 copy-start
  0.6 1.1 %shard_map.50 = (bf16[2,8,8,320]{3,2,1,0:T(8,128)(2,1)S(1)}, bf16[2,8,8,320]{3,2,1,0:T(8,128)(2,1)S(1)}) custom-call(bf16[1,4,8,8,320]{4,3,2,1,0:T(8,128)(2,1)} %strips_ref.1, bf16[1,4,8,8,320]{4,3,2,1,0:T(8,128)(2,1)} %cotangent_ref.1), custom_call_target="tpu_custom_call" | custom-call | flops 10000000000 | bytes 1000000 | tf_op jit(solution)/shard_map/pallas_call | solution.py:177
  1.8 0.6 collective-permute-start
  2.3 0.9 %collective-permute-done.other_ref = bf16[2,8,8,320]{3,2,1,0:T(8,128)(2,1)S(1)} collective-permute-done((bf16[2,8,8,320]{3,2,1,0:T(8,128)(2,1)S(1)}, bf16[2,8,8,320]{3,2,1,0:T(8,128)(2,1)S(1)}, u32[]{:S(2)}, u32[]{:S(2)}) %collective-permute-start) | collective-permute-done | bytes 81952 | tf_op jit(solution)/shard_map/ppermute | solution.py:660
  3.3 0.1 shard_map.51
  3.3 0.0 slice-start
  3.4 1.4 %shard_map.52 = (bf16[320,128]{1,0:T(8,128)(2,1)S(1)}, bf16[2,2,128,320]{3,2,1,0:T(8,128)(2,1)S(1)}, f32[2,128,320]{2,1,0:T(8,128)S(1)}) custom-call(bf16[128,320]{1,0:T(8,128)(2,1)S(1)} %get-tuple-element.59.field_ref.grad_ref, bf16[2,3,960,320]{3,2,1,0:T(8,128)(2,1)S(1)} %bitcast.12, bf16[2,3,960,320]{3,2,1,0:T(8,128)(2,1)S(1)} %bitcast.13), custom_call_target="tpu_custom_call" | custom-call | tf_op jit(solution)/shard_map/pallas_call | solution.py:177
  4.7 3.7 %collective-permute-start.2 = (bf16[320,128]{1,0:T(8,128)(2,1)S(1)}, bf16[320,128]{1,0:T(8,128)(2,1)S(1)}, u32[]{:S(2)}, u32[]{:S(2)}) collective-permute-start(bf16[320,128]{1,0:T(8,128)(2,1)S(1)} %get-tuple-element.64), channel_id=1, source_target_pairs={{0,8},{1,9},{2,10},{3,11},{4,12},{5,13},{6,14},{7,15}} | collective-permute-start | bytes 245768 | tf_op jit(solution)/shard_map/ppermute | solution.py:679
  8.4 0.0 slice-start.1
  8.4 1.4 %shard_map.53 = (bf16[320,128]{1,0:T(8,128)(2,1)S(1)}, bf16[2,2,128,320]{3,2,1,0:T(8,128)(2,1)S(1)}, f32[2,128,320]{2,1,0:T(8,128)S(1)}) custom-call(bf16[128,320]{1,0:T(8,128)(2,1)S(1)} %get-tuple-element.58.field_ref.grad_ref, bf16[2,3,960,320]{3,2,1,0:T(8,128)(2,1)S(1)} %bitcast.14, ...), custom_call_target="tpu_custom_call", output_to_operand_aliasing={{1}: (3, {}), {2}: (4, {})} | custom-call | tf_op jit(solution)/shard_map/pallas_call | solution.py:177
  9.8 1.3 %collective-permute-start.1 = (bf16[320,128]{1,0:T(8,128)(2,1)S(1)}, bf16[320,128]{1,0:T(8,128)(2,1)S(1)}, u32[]{:S(2)}, u32[]{:S(2)}) collective-permute-start(bf16[320,128]{1,0:T(8,128)(2,1)S(1)} %get-tuple-element.62), channel_id=1, source_target_pairs={{0,8},{1,9},{2,10},{3,11},{4,12},{5,13},{6,14},{7,15}} | collective-permute-start | bytes 245768 | tf_op jit(solution)/shard_map/ppermute | solution.py:679
  11.1 0.0 collective-permute-done.2.field_ref
  11.2 0.7 collective-permute-start.4
  11.8 1.3 %collective-permute-done.1.field_ref = bf16[320,128]{1,0:T(8,128)(2,1)S(1)} collective-permute-done((bf16[320,128]{1,0:T(8,128)(2,1)S(1)}, bf16[320,128]{1,0:T(8,128)(2,1)S(1)}, u32[]{:S(2)}, u32[]{:S(2)}) %collective-permute-start.1) | collective-permute-done | bytes 81952 | tf_op jit(solution)/shard_map/ppermute | solution.py:679
  13.1 0.7 collective-permute-start.3
  13.8 1.4 %shard_map.57.after_ref.turned_ref = bf16[2,3,960,320]{3,2,1,0:T(8,128)(2,1)S(1)} custom-call(bf16[2,3,960,320]{3,2,1,0:T(8,128)(2,1)S(1)} %bitcast.20, bf16[2,3,960,320]{3,2,1,0:T(8,128)(2,1)S(1)} %shard_map.54.weights_ref, bf16[2,2,128,320]{3,2,1,0:T(8,128)(2,1)S(1)} %get-tuple-element.69.after_ref.refs_0_), custom_call_target="tpu_custom_call" | custom-call | tf_op jit(solution)/shard_map/pallas_call | solution.py:177
  15.1 0.1 shard_map.65
  15.2 0.0 collective-permute-done.4.field_ref
  15.3 0.7 collective-permute-start.6
  16.0 0.0 collective-permute-done.3.field_ref
  16.0 0.7 collective-permute-start.5
  16.7 3.5 %collective-permute-start.10 = (bf16[2,160,256]{2,1,0:T(8,128)(2,1)S(1)}, bf16[2,160,256]{2,1,0:T(8,128)(2,1)S(1)}, u32[]{:S(2)}, u32[]{:S(2)}) collective-permute-start(bf16[2,160,256]{2,1,0:T(8,128)(2,1)S(1)} %shard_map.65), channel_id=1, source_target_pairs={{0,1},{1,2},{2,3},{3,0},{4,5},{5,6},{6,7},{7,4}} | collective-permute-start | bytes 491528 | tf_op jit(solution)/shard_map/ppermute | solution.py:688
  20.2 4.5 %collective-permute-start.11 = (bf16[2,160,256]{2,1,0:T(8,128)(2,1)S(1)}, bf16[2,160,256]{2,1,0:T(8,128)(2,1)S(1)}, u32[]{:S(2)}, u32[]{:S(2)}) collective-permute-start(bf16[2,160,256]{2,1,0:T(8,128)(2,1)S(1)} %shard_map.65), channel_id=1, source_target_pairs={{0,2},{1,3},{2,0},{3,1},{4,6},{5,7},{6,4},{7,5}} | collective-permute-start | bytes 491528 | tf_op jit(solution)/shard_map/ppermute | solution.py:688
  24.6 0.0 collective-permute-done.6.field_ref
  24.7 0.7 collective-permute-start.15
  25.4 0.0 collective-permute-done.5.field_ref
  25.4 0.2 shard_map.63
  25.6 0.7 collective-permute-start.14
  26.3 0.0 collective-permute-done.15.grad_ref
  26.3 0.7 collective-permute-start.17
  27.0 3.3 %collective-permute-start.12 = (bf16[2,160,256]{2,1,0:T(8,128)(2,1)S(1)}, bf16[2,160,256]{2,1,0:T(8,128)(2,1)S(1)}, u32[]{:S(2)}, u32[]{:S(2)}) collective-permute-start(bf16[2,160,256]{2,1,0:T(8,128)(2,1)S(1)} %shard_map.65), channel_id=1, source_target_pairs={{0,3},{1,0},{2,1},{3,2},{4,7},{5,4},{6,5},{7,6}} | collective-permute-start | bytes 491528 | tf_op jit(solution)/shard_map/ppermute | solution.py:688
  30.3 0.1 shard_map.64
  30.4 0.0 collective-permute-done.10.refs_0_
  30.4 0.7 %collective-permute-start.7 = (bf16[2,160,256]{2,1,0:T(8,128)(2,1)S(1)}, bf16[2,160,256]{2,1,0:T(8,128)(2,1)S(1)}, u32[]{:S(2)}, u32[]{:S(2)}) collective-permute-start(bf16[2,160,256]{2,1,0:T(8,128)(2,1)S(1)} %shard_map.64), channel_id=1, source_target_pairs={{0,1},{1,2},{2,3},{3,0},{8,9},{9,10},{10,11},{11,8},{16,17},{17,18... | collective-permute-start | bytes 491528 | tf_op jit(solution)/shard_map/ppermute | solution.py:688
  31.1 1.9 %collective-permute-done.11.refs_1_ = bf16[2,160,256]{2,1,0:T(8,128)(2,1)S(1)} collective-permute-done((bf16[2,160,256]{2,1,0:T(8,128)(2,1)S(1)}, bf16[2,160,256]{2,1,0:T(8,128)(2,1)S(1)}, u32[]{:S(2)}, u32[]{:S(2)}) %collective-permute-start.11) | collective-permute-done | bytes 163872 | tf_op jit(solution)/shard_map/ppermute | solution.py:688
  33.0 0.0 collective-permute-start.8
  33.0 0.0 collective-permute-done.14.grad_ref
  33.0 5.3 %collective-permute-start.9 = (bf16[2,160,256]{2,1,0:T(8,128)(2,1)S(1)}, bf16[2,160,256]{2,1,0:T(8,128)(2,1)S(1)}, u32[]{:S(2)}, u32[]{:S(2)}) collective-permute-start(bf16[2,160,256]{2,1,0:T(8,128)(2,1)S(1)} %shard_map.64), channel_id=1, source_target_pairs={{0,3},{1,0},{2,1},{3,2},{8,11},{9,8},{10,9},{11,10},{16,19},{17,16... | collective-permute-start | bytes 491528 | tf_op jit(solution)/shard_map/ppermute | solution.py:688
  38.3 0.0 collective-permute-done.17.grad_ref
  38.3 0.7 collective-permute-start.16
  39.0 0.0 collective-permute-done.16.grad_ref
  39.0 1.3 %collective-permute-start.19 = (bf16[320,128]{1,0:T(8,128)(2,1)S(1)}, bf16[320,128]{1,0:T(8,128)(2,1)S(1)}, u32[]{:S(2)}, u32[]{:S(2)}) collective-permute-start(bf16[320,128]{1,0:T(8,128)(2,1)S(1)} %get-tuple-element.101), channel_id=1, source_target_pairs={{8,0},{9,1},{10,2},{11,3},{12,4},{13,5},{14,6},{15,7}} | collective-permute-start | bytes 245768 | tf_op jit(solution)/shard_map/ppermute | solution.py:679
  40.4 1.3 %collective-permute-start.18 = (bf16[320,128]{1,0:T(8,128)(2,1)S(1)}, bf16[320,128]{1,0:T(8,128)(2,1)S(1)}, u32[]{:S(2)}, u32[]{:S(2)}) collective-permute-start(bf16[320,128]{1,0:T(8,128)(2,1)S(1)} %get-tuple-element.100), channel_id=1, source_target_pairs={{8,0},{9,1},{10,2},{11,3},{12,4},{13,5},{14,6},{15,7}} | collective-permute-start | bytes 245768 | tf_op jit(solution)/shard_map/ppermute | solution.py:679
  41.7 3.0 %shard_map.66 = (bf16[2,4,160,256]{3,2,1,0:T(8,128)(2,1)S(1)}, bf16[2,4,160,256]{3,2,1,0:T(8,128)(2,1)S(1)}) custom-call(bf16[2,2,128,320]{3,2,1,0:T(8,128)(2,1)S(1)} %get-tuple-element.81.refs_0_.saved_ref, bf16[2,3,960,320]{3,2,1,0:T(8,128)(2,1)S(1)} %bitcast.21, bf16[2,160,256]{2,1,0:T(8,128)(2,1)S(1)} %collective-permute-done.10.refs_0_, ...), custom_call_target="tpu_custom_call" | custom-call | tf_op jit(solution)/shard_map/pallas_call | solution.py:177
  44.6 2.4 %collective-permute-done.8.refs_1_ = bf16[2,160,256]{2,1,0:T(8,128)(2,1)S(1)} collective-permute-done((bf16[2,160,256]{2,1,0:T(8,128)(2,1)S(1)}, bf16[2,160,256]{2,1,0:T(8,128)(2,1)S(1)}, u32[]{:S(2)}, u32[]{:S(2)}) %collective-permute-start.8) | collective-permute-done | bytes 163872 | tf_op jit(solution)/shard_map/ppermute | solution.py:688
  47.1 0.1 collective-permute-start.13
  47.2 4.7 %collective-permute-done.19.grad_ref.refs_0_ = bf16[320,128]{1,0:T(8,128)(2,1)S(1)} collective-permute-done((bf16[320,128]{1,0:T(8,128)(2,1)S(1)}, bf16[320,128]{1,0:T(8,128)(2,1)S(1)}, u32[]{:S(2)}, u32[]{:S(2)}) %collective-permute-start.19) | collective-permute-done | bytes 81952 | tf_op jit(solution)/shard_map/ppermute | solution.py:679
  51.9 0.7 %shard_map.74 = (bf16[2,128,320]{2,1,0:T(8,128)(2,1)S(1)}, bf16[4,2,80,256]{3,2,1,0:T(8,128)(2,1)S(1)}) custom-call(bf16[320,128]{1,0:T(8,128)(2,1)S(1)} %collective-permute-done.19.grad_ref.refs_0_, bf16[2,3,960,320]{3,2,1,0:T(8,128)(2,1)S(1)} %shard_map.57.after_ref.turned_ref, ...), custom_call_target="tpu_custom_call", output_to_operand_aliasing={{0}: (4, {}), {1}: (5, {})} | custom-call | tf_op jit(solution)/shard_map/pallas_call | solution.py:177
  52.6 2.0 %collective-permute-done.18.grad_ref.refs_1_ = bf16[320,128]{1,0:T(8,128)(2,1)S(1)} collective-permute-done((bf16[320,128]{1,0:T(8,128)(2,1)S(1)}, bf16[320,128]{1,0:T(8,128)(2,1)S(1)}, u32[]{:S(2)}, u32[]{:S(2)}) %collective-permute-start.18) | collective-permute-done | bytes 81952 | tf_op jit(solution)/shard_map/ppermute | solution.py:679
  54.6 0.7 %shard_map.75 = (bf16[2,128,320]{2,1,0:T(8,128)(2,1)S(1)}, bf16[4,2,80,256]{3,2,1,0:T(8,128)(2,1)S(1)}) custom-call(bf16[320,128]{1,0:T(8,128)(2,1)S(1)} %collective-permute-done.18.grad_ref.refs_1_, bf16[2,3,960,320]{3,2,1,0:T(8,128)(2,1)S(1)} %shard_map.57.after_ref.turned_ref, ...), custom_call_target="tpu_custom_call", output_to_operand_aliasing={{0}: (4, {}), {1}: (5, {})} | custom-call | tf_op jit(solution)/shard_map/pallas_call | solution.py:177
  55.3 0.7 collective-permute-start.20
  56.0 1.7 %collective-permute-start.21 = (bf16[2,80,256]{2,1,0:T(8,128)(2,1)S(1)}, bf16[2,80,256]{2,1,0:T(8,128)(2,1)S(1)}, u32[]{:S(2)}, u32[]{:S(2)}) collective-permute-start(bf16[2,80,256]{2,1,0:T(8,128)(2,1)S(1)} %get-tuple-element.111), channel_id=1, source_target_pairs={{0,2},{1,3},{2,0},{3,1},{8,10},{9,11},{10,8},{11,9},{16,18},{17,19... | collective-permute-start | bytes 245768 | tf_op jit(solution)/shard_map/ppermute | solution.py:688
  57.7 1.5 %collective-permute-start.22 = (bf16[2,80,256]{2,1,0:T(8,128)(2,1)S(1)}, bf16[2,80,256]{2,1,0:T(8,128)(2,1)S(1)}, u32[]{:S(2)}, u32[]{:S(2)}) collective-permute-start(bf16[2,80,256]{2,1,0:T(8,128)(2,1)S(1)} %get-tuple-element.110), channel_id=1, source_target_pairs={{0,3},{1,0},{2,1},{3,2},{8,11},{9,8},{10,9},{11,10},{16,19},{17,16... | collective-permute-start | bytes 245768 | tf_op jit(solution)/shard_map/ppermute | solution.py:688
  59.2 2.6 %collective-permute-done.20.refs_1_ = bf16[2,80,256]{2,1,0:T(8,128)(2,1)S(1)} collective-permute-done((bf16[2,80,256]{2,1,0:T(8,128)(2,1)S(1)}, bf16[2,80,256]{2,1,0:T(8,128)(2,1)S(1)}, u32[]{:S(2)}, u32[]{:S(2)}) %collective-permute-start.20) | collective-permute-done | bytes 81952 | tf_op jit(solution)/shard_map/ppermute | solution.py:688
  61.8 1.4 %collective-permute-done.21.refs_2_ = bf16[2,80,256]{2,1,0:T(8,128)(2,1)S(1)} collective-permute-done((bf16[2,80,256]{2,1,0:T(8,128)(2,1)S(1)}, bf16[2,80,256]{2,1,0:T(8,128)(2,1)S(1)}, u32[]{:S(2)}, u32[]{:S(2)}) %collective-permute-start.21) | collective-permute-done | bytes 81952 | tf_op jit(solution)/shard_map/ppermute | solution.py:688
  63.1 0.0 collective-permute-done.22.refs_3_
  63.2 0.1 collective-permute-start.23
  63.3 1.1 %shard_map.77.kept_ref = bf16[2,128,320]{2,1,0:T(8,128)(2,1)S(1)} custom-call(bf16[2,3,960,320]{3,2,1,0:T(8,128)(2,1)S(1)} %shard_map.57.after_ref.turned_ref, bf16[320,128]{1,0:T(8,128)(2,1)S(1)} %collective-permute-done.19.grad_ref.refs_0_, bf16[320,128]{1,0:T(8,128)(2,1)S(1)} %collective-permute-done.18.grad_ref.refs_1_, ...), custom_call_target="tpu_custom_call", output_to_operand_aliasing={{}: (3, {})} | custom-call | tf_op jit(solution)/shard_map/pallas_call | solution.py:177
  64.4 0.1 shard_map.78
  64.4 0.5 collective-permute-start.24
  65.0 1.2 %shard_map.68.refs_0_ = bf16[2,2048,480]{2,1,0:T(8,128)(2,1)S(1)} custom-call(bf16[2,4,160,256]{3,2,1,0:T(8,128)(2,1)S(1)} %get-tuple-element.88.first_ref.after_ref, bf16[2,4,160,256]{3,2,1,0:T(8,128)(2,1)S(1)} %get-tuple-element.89.cells_ref), custom_call_target="tpu_custom_call" | custom-call | tf_op jit(solution)/shard_map/pallas_call | solution.py:177
  66.2 0.7 %shard_map.79 = bf16[1,4,8,8,320]{4,3,2,1,0:T(8,128)(2,1)} custom-call(bf16[2,8,8,320]{3,2,1,0:T(8,128)(2,1)S(1)} %get-tuple-element.108.own_ref, bf16[2,8,8,320]{3,2,1,0:T(8,128)(2,1)S(1)} %collective-permute-done.24.other_ref), custom_call_target="tpu_custom_call" | custom-call | tf_op jit(solution)/shard_map/pallas_call | solution.py:177
  66.9 1.2 %shard_map.69.around_ref = bf16[2,2048,480]{2,1,0:T(8,128)(2,1)S(1)} custom-call(bf16[2,4,160,256]{3,2,1,0:T(8,128)(2,1)S(1)} %collective-permute-done.13.first_ref.cells_ref, bf16[2,4,160,256]{3,2,1,0:T(8,128)(2,1)S(1)} %collective-permute-done.13.first_ref.cells_ref, bf16[2,2048,480]{2,1,0:T(8,128)(2,1)S(1)} %shard_map.68.refs_0_), custom_call_target="tpu_custom_call", output_to_operand_aliasing={{}: (2, {})} | custom-call | tf_op jit(solution)/shard_map/pallas_call | solution.py:177
  68.1 2.3 %terms.1 = f32[2,9,160,80]{3,2,1,0:T(8,128)} custom-call(bf16[2,2048,480]{2,1,0:T(8,128)(2,1)S(1)} %shard_map.69.around_ref, bf16[4,2,80,256]{3,2,1,0:T(8,128)(2,1)S(1)} %shard_map.76.own_ref, bf16[4,2,80,256]{3,2,1,0:T(8,128)(2,1)S(1)} %collective-permute-done.23.other_ref), custom_call_target="tpu_custom_call" | custom-call | tf_op jit(solution)/shard_map/terms/pallas_call | solution.py:647
  (25 shorter events, 0.3 us)
Async XLA Ops:
  0.6 2.7 %copy-start = (bf16[1,2,9,320,320]{4,3,2,1,0:T(8,128)(2,1)S(1)}, bf16[1,2,9,320,320]{4,3,2,1,0:T(8,128)(2,1)}, u32[]{:S(2)}) copy-start(bf16[1,2,9,320,320]{4,3,2,1,0:T(8,128)(2,1)} %param.4) | copy-start | bytes 11059204
  1.8 1.5 %collective-permute-start = (bf16[2,8,8,320]{3,2,1,0:T(8,128)(2,1)S(1)}, bf16[2,8,8,320]{3,2,1,0:T(8,128)(2,1)S(1)}, u32[]{:S(2)}, u32[]{:S(2)}) collective-permute-start(bf16[2,8,8,320]{3,2,1,0:T(8,128)(2,1)S(1)} %get-tuple-element.57), channel_id=1, source_target_pairs={{0,4},{4,0},{1,5},{5,1},{2,6},{6,2},{3,7},{7,3},{8,12},{12,8},{9,1... | collective-permute-start | bytes 245768 | tf_op jit(solution)/shard_map/ppermute | solution.py:660
  3.3 7.8 %slice-start = ((s8[4423680]{0:T(1024)(128)(4,1)}), s8[4194304]{0:T(1024)(128)(4,1)S(1)}, s32[]{:S(2)}) async-start(s8[4423680]{0:T(1024)(128)(4,1)} %bitcast.16), calls=%async_computation | async-start | bytes 8388608
  4.7 6.4 %collective-permute-start.2 = (bf16[320,128]{1,0:T(8,128)(2,1)S(1)}, bf16[320,128]{1,0:T(8,128)(2,1)S(1)}, u32[]{:S(2)}, u32[]{:S(2)}) collective-permute-start(bf16[320,128]{1,0:T(8,128)(2,1)S(1)} %get-tuple-element.64), channel_id=1, source_target_pairs={{0,8},{1,9},{2,10},{3,11},{4,12},{5,13},{6,14},{7,15}} | collective-permute-start | bytes 245768 | tf_op jit(solution)/shard_map/ppermute | solution.py:679
  8.4 2.7 %slice-start.1 = ((s8[4423680]{0:T(1024)(128)(4,1)}), s8[229376]{0:T(1024)(128)(4,1)S(1)}, s32[]{:S(2)}) async-start(s8[4423680]{0:T(1024)(128)(4,1)} %bitcast.16), calls=%async_computation.1 | async-start | bytes 458752
  9.8 3.3 %collective-permute-start.1 = (bf16[320,128]{1,0:T(8,128)(2,1)S(1)}, bf16[320,128]{1,0:T(8,128)(2,1)S(1)}, u32[]{:S(2)}, u32[]{:S(2)}) collective-permute-start(bf16[320,128]{1,0:T(8,128)(2,1)S(1)} %get-tuple-element.62), channel_id=1, source_target_pairs={{0,8},{1,9},{2,10},{3,11},{4,12},{5,13},{6,14},{7,15}} | collective-permute-start | bytes 245768 | tf_op jit(solution)/shard_map/ppermute | solution.py:679
  11.2 4.1 %collective-permute-start.4 = (bf16[320,128]{1,0:T(8,128)(2,1)S(1)}, bf16[320,128]{1,0:T(8,128)(2,1)S(1)}, u32[]{:S(2)}, u32[]{:S(2)}) collective-permute-start(bf16[320,128]{1,0:T(8,128)(2,1)S(1)} %get-tuple-element.70), channel_id=1, source_target_pairs={{8,16},{9,17},{10,18},{11,19},{12,20},{13,21},{14,22},{15,23}} | collective-permute-start | bytes 245768 | tf_op jit(solution)/shard_map/ppermute | solution.py:679
  13.1 2.9 %collective-permute-start.3 = (bf16[320,128]{1,0:T(8,128)(2,1)S(1)}, bf16[320,128]{1,0:T(8,128)(2,1)S(1)}, u32[]{:S(2)}, u32[]{:S(2)}) collective-permute-start(bf16[320,128]{1,0:T(8,128)(2,1)S(1)} %get-tuple-element.68), channel_id=1, source_target_pairs={{8,16},{9,17},{10,18},{11,19},{12,20},{13,21},{14,22},{15,23}} | collective-permute-start | bytes 245768 | tf_op jit(solution)/shard_map/ppermute | solution.py:679
  15.3 9.4 %collective-permute-start.6 = (bf16[320,128]{1,0:T(8,128)(2,1)S(1)}, bf16[320,128]{1,0:T(8,128)(2,1)S(1)}, u32[]{:S(2)}, u32[]{:S(2)}) collective-permute-start(bf16[320,128]{1,0:T(8,128)(2,1)S(1)} %get-tuple-element.75), channel_id=1, source_target_pairs={{16,24},{17,25},{18,26},{19,27},{20,28},{21,29},{22,30},{23,31}} | collective-permute-start | bytes 245768 | tf_op jit(solution)/shard_map/ppermute | solution.py:679
  16.0 9.4 %collective-permute-start.5 = (bf16[320,128]{1,0:T(8,128)(2,1)S(1)}, bf16[320,128]{1,0:T(8,128)(2,1)S(1)}, u32[]{:S(2)}, u32[]{:S(2)}) collective-permute-start(bf16[320,128]{1,0:T(8,128)(2,1)S(1)} %get-tuple-element.74), channel_id=1, source_target_pairs={{16,24},{17,25},{18,26},{19,27},{20,28},{21,29},{22,30},{23,31}} | collective-permute-start | bytes 245768 | tf_op jit(solution)/shard_map/ppermute | solution.py:679
  16.7 13.7 %collective-permute-start.10 = (bf16[2,160,256]{2,1,0:T(8,128)(2,1)S(1)}, bf16[2,160,256]{2,1,0:T(8,128)(2,1)S(1)}, u32[]{:S(2)}, u32[]{:S(2)}) collective-permute-start(bf16[2,160,256]{2,1,0:T(8,128)(2,1)S(1)} %shard_map.65), channel_id=1, source_target_pairs={{0,1},{1,2},{2,3},{3,0},{4,5},{5,6},{6,7},{7,4}} | collective-permute-start | bytes 491528 | tf_op jit(solution)/shard_map/ppermute | solution.py:688
  20.2 12.8 %collective-permute-start.11 = (bf16[2,160,256]{2,1,0:T(8,128)(2,1)S(1)}, bf16[2,160,256]{2,1,0:T(8,128)(2,1)S(1)}, u32[]{:S(2)}, u32[]{:S(2)}) collective-permute-start(bf16[2,160,256]{2,1,0:T(8,128)(2,1)S(1)} %shard_map.65), channel_id=1, source_target_pairs={{0,2},{1,3},{2,0},{3,1},{4,6},{5,7},{6,4},{7,5}} | collective-permute-start | bytes 491528 | tf_op jit(solution)/shard_map/ppermute | solution.py:688
  24.7 1.6 %collective-permute-start.15 = (bf16[320,128]{1,0:T(8,128)(2,1)S(1)}, bf16[320,128]{1,0:T(8,128)(2,1)S(1)}, u32[]{:S(2)}, u32[]{:S(2)}) collective-permute-start(bf16[320,128]{1,0:T(8,128)(2,1)S(1)} %get-tuple-element.79.after_ref), channel_id=1, source_target_pairs={{24,16},{25,17},{26,18},{27,19},{28,20},{29,21},{30,22},{31,23}} | collective-permute-start | bytes 245768 | tf_op jit(solution)/shard_map/ppermute | solution.py:679
  25.6 7.4 %collective-permute-start.14 = (bf16[320,128]{1,0:T(8,128)(2,1)S(1)}, bf16[320,128]{1,0:T(8,128)(2,1)S(1)}, u32[]{:S(2)}, u32[]{:S(2)}) collective-permute-start(bf16[320,128]{1,0:T(8,128)(2,1)S(1)} %get-tuple-element.85.refs_1_), channel_id=1, source_target_pairs={{24,16},{25,17},{26,18},{27,19},{28,20},{29,21},{30,22},{31,23}} | collective-permute-start | bytes 245768 | tf_op jit(solution)/shard_map/ppermute | solution.py:679
  26.3 12.0 %collective-permute-start.17 = (bf16[320,128]{1,0:T(8,128)(2,1)S(1)}, bf16[320,128]{1,0:T(8,128)(2,1)S(1)}, u32[]{:S(2)}, u32[]{:S(2)}) collective-permute-start(bf16[320,128]{1,0:T(8,128)(2,1)S(1)} %get-tuple-element.95), channel_id=1, source_target_pairs={{16,8},{17,9},{18,10},{19,11},{20,12},{21,13},{22,14},{23,15}} | collective-permute-start | bytes 245768 | tf_op jit(solution)/shard_map/ppermute | solution.py:679
  27.0 13.4 %collective-permute-start.12 = (bf16[2,160,256]{2,1,0:T(8,128)(2,1)S(1)}, bf16[2,160,256]{2,1,0:T(8,128)(2,1)S(1)}, u32[]{:S(2)}, u32[]{:S(2)}) collective-permute-start(bf16[2,160,256]{2,1,0:T(8,128)(2,1)S(1)} %shard_map.65), channel_id=1, source_target_pairs={{0,3},{1,0},{2,1},{3,2},{4,7},{5,4},{6,5},{7,6}} | collective-permute-start | bytes 491528 | tf_op jit(solution)/shard_map/ppermute | solution.py:688
  30.4 14.2 %collective-permute-start.7 = (bf16[2,160,256]{2,1,0:T(8,128)(2,1)S(1)}, bf16[2,160,256]{2,1,0:T(8,128)(2,1)S(1)}, u32[]{:S(2)}, u32[]{:S(2)}) collective-permute-start(bf16[2,160,256]{2,1,0:T(8,128)(2,1)S(1)} %shard_map.64), channel_id=1, source_target_pairs={{0,1},{1,2},{2,3},{3,0},{8,9},{9,10},{10,11},{11,8},{16,17},{17,18... | collective-permute-start | bytes 491528 | tf_op jit(solution)/shard_map/ppermute | solution.py:688
  33.0 14.0 %collective-permute-start.8 = (bf16[2,160,256]{2,1,0:T(8,128)(2,1)S(1)}, bf16[2,160,256]{2,1,0:T(8,128)(2,1)S(1)}, u32[]{:S(2)}, u32[]{:S(2)}) collective-permute-start(bf16[2,160,256]{2,1,0:T(8,128)(2,1)S(1)} %shard_map.64), channel_id=1, source_target_pairs={{0,2},{1,3},{2,0},{3,1},{8,10},{9,11},{10,8},{11,9},{16,18},{17,19... | collective-permute-start | bytes 491528 | tf_op jit(solution)/shard_map/ppermute | solution.py:688
  33.0 14.0 %collective-permute-start.9 = (bf16[2,160,256]{2,1,0:T(8,128)(2,1)S(1)}, bf16[2,160,256]{2,1,0:T(8,128)(2,1)S(1)}, u32[]{:S(2)}, u32[]{:S(2)}) collective-permute-start(bf16[2,160,256]{2,1,0:T(8,128)(2,1)S(1)} %shard_map.64), channel_id=1, source_target_pairs={{0,3},{1,0},{2,1},{3,2},{8,11},{9,8},{10,9},{11,10},{16,19},{17,16... | collective-permute-start | bytes 491528 | tf_op jit(solution)/shard_map/ppermute | solution.py:688
  38.3 0.7 collective-permute-start.16
  39.0 12.8 %collective-permute-start.19 = (bf16[320,128]{1,0:T(8,128)(2,1)S(1)}, bf16[320,128]{1,0:T(8,128)(2,1)S(1)}, u32[]{:S(2)}, u32[]{:S(2)}) collective-permute-start(bf16[320,128]{1,0:T(8,128)(2,1)S(1)} %get-tuple-element.101), channel_id=1, source_target_pairs={{8,0},{9,1},{10,2},{11,3},{12,4},{13,5},{14,6},{15,7}} | collective-permute-start | bytes 245768 | tf_op jit(solution)/shard_map/ppermute | solution.py:679
  40.4 14.2 %collective-permute-start.18 = (bf16[320,128]{1,0:T(8,128)(2,1)S(1)}, bf16[320,128]{1,0:T(8,128)(2,1)S(1)}, u32[]{:S(2)}, u32[]{:S(2)}) collective-permute-start(bf16[320,128]{1,0:T(8,128)(2,1)S(1)} %get-tuple-element.100), channel_id=1, source_target_pairs={{8,0},{9,1},{10,2},{11,3},{12,4},{13,5},{14,6},{15,7}} | collective-permute-start | bytes 245768 | tf_op jit(solution)/shard_map/ppermute | solution.py:679
  47.1 19.8 %collective-permute-start.13 = (bf16[2,4,160,256]{3,2,1,0:T(8,128)(2,1)S(1)}, bf16[2,4,160,256]{3,2,1,0:T(8,128)(2,1)S(1)}, u32[]{:S(2)}, u32[]{:S(2)}) collective-permute-start(bf16[2,4,160,256]{3,2,1,0:T(8,128)(2,1)S(1)} %get-tuple-element.87), channel_id=1, source_target_pairs={{0,4},{4,0},{1,5},{5,1},{2,6},{6,2},{3,7},{7,3},{8,12},{12,8},{9,1... | collective-permute-start | bytes 1966088 | tf_op jit(solution)/shard_map/ppermute | solution.py:660
  55.3 6.4 %collective-permute-start.20 = (bf16[2,80,256]{2,1,0:T(8,128)(2,1)S(1)}, bf16[2,80,256]{2,1,0:T(8,128)(2,1)S(1)}, u32[]{:S(2)}, u32[]{:S(2)}) collective-permute-start(bf16[2,80,256]{2,1,0:T(8,128)(2,1)S(1)} %get-tuple-element.112), channel_id=1, source_target_pairs={{0,1},{1,2},{2,3},{3,0},{8,9},{9,10},{10,11},{11,8},{16,17},{17,18... | collective-permute-start | bytes 245768 | tf_op jit(solution)/shard_map/ppermute | solution.py:688
  56.0 7.1 %collective-permute-start.21 = (bf16[2,80,256]{2,1,0:T(8,128)(2,1)S(1)}, bf16[2,80,256]{2,1,0:T(8,128)(2,1)S(1)}, u32[]{:S(2)}, u32[]{:S(2)}) collective-permute-start(bf16[2,80,256]{2,1,0:T(8,128)(2,1)S(1)} %get-tuple-element.111), channel_id=1, source_target_pairs={{0,2},{1,3},{2,0},{3,1},{8,10},{9,11},{10,8},{11,9},{16,18},{17,19... | collective-permute-start | bytes 245768 | tf_op jit(solution)/shard_map/ppermute | solution.py:688
  57.7 5.4 %collective-permute-start.22 = (bf16[2,80,256]{2,1,0:T(8,128)(2,1)S(1)}, bf16[2,80,256]{2,1,0:T(8,128)(2,1)S(1)}, u32[]{:S(2)}, u32[]{:S(2)}) collective-permute-start(bf16[2,80,256]{2,1,0:T(8,128)(2,1)S(1)} %get-tuple-element.110), channel_id=1, source_target_pairs={{0,3},{1,0},{2,1},{3,2},{8,11},{9,8},{10,9},{11,10},{16,19},{17,16... | collective-permute-start | bytes 245768 | tf_op jit(solution)/shard_map/ppermute | solution.py:688
  63.2 4.9 %collective-permute-start.23 = (bf16[4,2,80,256]{3,2,1,0:T(8,128)(2,1)S(1)}, bf16[4,2,80,256]{3,2,1,0:T(8,128)(2,1)S(1)}, u32[]{:S(2)}, u32[]{:S(2)}) collective-permute-start(bf16[4,2,80,256]{3,2,1,0:T(8,128)(2,1)S(1)} %shard_map.76.own_ref), channel_id=1, source_target_pairs={{0,4},{4,0},{1,5},{5,1},{2,6},{6,2},{3,7},{7,3},{8,12},{12,8},{9,1... | collective-permute-start | bytes 983048 | tf_op jit(solution)/shard_map/ppermute | solution.py:660
  64.4 1.7 %collective-permute-start.24 = (bf16[2,8,8,320]{3,2,1,0:T(8,128)(2,1)S(1)}, bf16[2,8,8,320]{3,2,1,0:T(8,128)(2,1)S(1)}, u32[]{:S(2)}, u32[]{:S(2)}) collective-permute-start(bf16[2,8,8,320]{3,2,1,0:T(8,128)(2,1)S(1)} %get-tuple-element.109), channel_id=1, source_target_pairs={{0,4},{4,0},{1,5},{5,1},{2,6},{6,2},{3,7},{7,3},{8,12},{12,8},{9,1... | collective-permute-start | bytes 245768 | tf_op jit(solution)/shard_map/ppermute | solution.py:660
